TPU v7x, 32 devices: a whole 2x2x4 slice. The times are simulated.
32 devices in a mesh: rows: 8 (over z, y), cols: 4 (over x, core).
Axes of the slice: x: 2, y: 2, z: 4, core: 2. Of those that a mesh axis runs over, the one named last changes fastest.
Arguments:
- blocks: bfloat16 [32, 4, 3, 128, 128], P('rows', 'cols'), may hold values from -1.1953125 to 1.1953125
- block_cols: int32 [32, 4, 3], P('rows', 'cols'), may hold values from 0 to 31, as said below
Outputs:
- square_blocks: bfloat16 [32, 4, 36, 128, 128], P('rows', 'cols')
- square_cols: int32 [32, 4, 36], P('rows', 'cols')
- square_start: int32 [32, 4], P('rows', 'cols')
Inputs may be any that keep to these rules, and one draw needn't show every extreme that they name: Block-row i lies in panel p = i // 4; every block_cols[i, g, s] is a block-column congruent to g modulo 4 among block-rows 4 * (p - 4) to 4 * (p + 4) - 1, taken modulo 32; the three entries of one group differ; the block-columns i - 1, i and i + 1 (modulo 32) are always among a row's entries.
All inputs are finite; a program needn't handle non-finite values.
Results may differ from a plain program's by a relative error of at most 0.001.
Values may be sent and summed in bfloat16 or wider, within the bound.
No kernel may reach another device: no remote copies, remote signals or barrier semaphores. Data moves between devices by JAX's collectives and lax.ppermute only.
A program may use at most 64 MiB of HBM per device.

v0:
```python
import jax
import jax.numpy as jnp
from jax import lax
from jax.sharding import PartitionSpec as P

HP = 4


def shifted(block, axis, distance):
    devices = range(lax.axis_size(axis))
    route = [((i - distance) % len(devices), i) for i in devices]
    return lax.ppermute(block, axis, route)


def unique_slots(candidates):
    width = candidates.shape[-1]
    ordered = jnp.sort(candidates, axis=-1)
    firsts = jnp.concatenate(
        [jnp.ones(ordered.shape[:-1] + (1,), dtype=bool), ordered[..., 1:] != ordered[..., :-1]],
        axis=-1,
    )
    marks = firsts.astype(jnp.int32)
    totals = jnp.sum(marks, axis=-1)
    ranking = jnp.sum(
        marks[..., None, :] * (ordered[..., None, :] < candidates[..., :, None]).astype(jnp.int32),
        axis=-1,
    )
    places = jnp.cumsum(marks, axis=-1) - 1
    slot_ids = jnp.arange(width, dtype=jnp.int32)
    chosen = (places[..., None, :] == slot_ids[:, None]) & firsts[..., None, :]
    columns = jnp.sum(jnp.where(chosen, ordered[..., None, :], 0), axis=-1).astype(jnp.int32)
    columns = jnp.where(slot_ids < totals[..., None], columns, -1)
    onehot = (ranking[..., None, :] == slot_ids[:, None]).astype(jnp.float32)
    return (columns, onehot, totals)


def on_device(blocks, block_cols):
    panel_rows = block_cols.shape[0]
    per_group = block_cols.shape[2]
    block_size = blocks.shape[-1]
    cycle_size = lax.axis_size("rows")
    block_rows = panel_rows * cycle_size
    panel_id = lax.axis_index("rows")
    left_vals, left_cols = (
        lax.all_gather(blocks, "cols", axis=1, tiled=True),
        lax.all_gather(block_cols, "cols", axis=1, tiled=True),
    )
    groups = left_cols.shape[1]
    row_slots = groups * per_group
    left_vals = left_vals.reshape(panel_rows, row_slots, block_size, block_size)
    left_cols = left_cols.reshape(panel_rows, row_slots)
    own_panel = (blocks[:, 0], block_cols[:, 0])
    pieces = []
    for offset in range(-HP, HP):
        if offset == 0:
            pieces.append(own_panel)
        else:
            pieces.append(shifted((own_panel[0], own_panel[1]), "rows", -offset))
    win_vals = jnp.concatenate([piece[0] for piece in pieces], axis=0)
    win_cols = jnp.concatenate([piece[1] for piece in pieces], axis=0)
    window_base = (panel_id - HP) * panel_rows % block_rows
    local_index = ((left_cols - window_base) % block_rows).astype(jnp.int32)
    right_vals = win_vals[local_index]
    right_cols = win_cols[local_index]
    products = jnp.einsum(
        "ptab,ptsbc->ptsac", left_vals, right_vals, preferred_element_type=jnp.float32
    )
    candidates = right_cols.reshape(panel_rows, row_slots * per_group)
    columns, onehot, totals = unique_slots(candidates)
    merged = jnp.einsum(
        "poq,pqac->poac",
        onehot,
        products.reshape(panel_rows, row_slots * per_group, block_size, block_size),
        precision=lax.Precision.HIGHEST,
    )
    merged_blocks = merged.astype(jnp.bfloat16)
    panel_total = jnp.sum(totals)
    all_totals = lax.all_gather(panel_total.reshape(1), "rows", axis=0, tiled=True)
    earlier = jnp.sum(jnp.where(jnp.arange(cycle_size, dtype=jnp.int32) < panel_id, all_totals, 0))
    starts = earlier + jnp.cumsum(totals) - totals
    return (merged_blocks[:, None], columns[:, None], starts[:, None])


def solution(mesh):
    in_specs = (P("rows", "cols", None, None, None), P("rows", "cols", None))
    out_specs = (P("rows", "cols", None, None, None), P("rows", "cols", None), P("rows", "cols"))
    return jax.shard_map(
        on_device, mesh=mesh, in_specs=in_specs, out_specs=out_specs, check_vma=False
    )
```

profile of v0, /device:TPU:0, one launch (start us, length us, event | category | flops | bytes accessed | tf_op | source)
XLA Modules:
  0.0 152.6 jit_solution(1161392853445351504)
XLA Ops:
  7.2 0.8 copy.54
  8.0 5.0 %collective-permute-start.6 = (s32[4,3]{1,0:T(4,128)S(1)}, s32[4,3]{1,0:T(4,128)S(1)}, u32[]{:S(2)}, u32[]{:S(2)}) collective-permute-start(s32[4,3]{1,0:T(4,128)S(1)} %bitcast.40), channel_id=1, source_target_pairs={{12,0},{16,4},{20,8},{24,12},{28,16},{0,20},{4,24},{8,28},{13,1},{... | collective-permute-start | bytes 152 | tf_op jit(solution)/shard_map/ppermute | solution.py:12
  13.1 1.3 collective-permute-start.5
  14.4 0.5 collective-permute-start.4
  14.9 1.5 collective-permute-start.3
  16.4 0.7 collective-permute-start.2
  17.1 5.2 %all_gather.9 = s32[4,4,3]{2,0,1:T(4,128)S(1)} all-gather(s32[4,1,3]{2,0,1:T(4,128)S(1)} %copy.54), channel_id=1, replica_groups=mesh['rows'=8,'cols'=4] {'cols'}, dimensions={1}, use_global_device_ids=true | all-gather | bytes 240 | tf_op jit(solution)/shard_map/all_gather | solution.py:46
  22.3 0.1 copy.56
  22.5 0.1 copy.57
  22.6 0.1 sub.36
  22.7 0.1 reshape.143
  22.8 1.2 dynamic-slice
  24.0 1.9 %collective-permute-start.1 = (s32[4,3]{1,0:T(4,128)S(1)}, s32[4,3]{1,0:T(4,128)S(1)}, u32[]{:S(2)}, u32[]{:S(2)}) collective-permute-start(s32[4,3]{1,0:T(4,128)S(1)} %bitcast.45), channel_id=1, source_target_pairs={{20,0},{24,4},{28,8},{0,12},{4,16},{8,20},{12,24},{16,28},{21,1},{... | collective-permute-start | bytes 152 | tf_op jit(solution)/shard_map/ppermute | solution.py:12
  25.9 2.8 %collective-permute-start = (s32[4,3]{1,0:T(4,128)S(1)}, s32[4,3]{1,0:T(4,128)S(1)}, u32[]{:S(2)}, u32[]{:S(2)}) collective-permute-start(s32[4,3]{1,0:T(4,128)S(1)} %bitcast.46), channel_id=1, source_target_pairs={{16,0},{20,4},{24,8},{28,12},{0,16},{4,20},{8,24},{12,28},{17,1},{... | collective-permute-start | bytes 152 | tf_op jit(solution)/shard_map/ppermute | solution.py:12
  28.7 0.2 collective-permute-start.13
  28.9 2.6 %collective-permute-start.10 = (bf16[4,3,128,128]{3,2,1,0:T(8,128)(2,1)}, bf16[4,3,128,128]{3,2,1,0:T(8,128)(2,1)}, u32[]{:S(2)}, u32[]{:S(2)}) collective-permute-start(bf16[4,3,128,128]{3,2,1,0:T(8,128)(2,1)} %bitcast.34), channel_id=1, source_target_pairs={{28,0},{0,4},{4,8},{8,12},{12,16},{16,20},{20,24},{24,28},{29,1},{... | collective-permute-start | bytes 1179656 | tf_op jit(solution)/shard_map/ppermute | solution.py:12
  31.5 0.7 collective-permute-start.9
  32.2 1.6 %collective-permute-start.8 = (bf16[4,3,128,128]{3,2,1,0:T(8,128)(2,1)}, bf16[4,3,128,128]{3,2,1,0:T(8,128)(2,1)}, u32[]{:S(2)}, u32[]{:S(2)}) collective-permute-start(bf16[4,3,128,128]{3,2,1,0:T(8,128)(2,1)} %bitcast.36), channel_id=1, source_target_pairs={{20,0},{24,4},{28,8},{0,12},{4,16},{8,20},{12,24},{16,28},{21,1},{... | collective-permute-start | bytes 1179656 | tf_op jit(solution)/shard_map/ppermute | solution.py:12
  33.8 3.0 %collective-permute-start.7 = (bf16[4,3,128,128]{3,2,1,0:T(8,128)(2,1)}, bf16[4,3,128,128]{3,2,1,0:T(8,128)(2,1)S(1)}, u32[]{:S(2)}, u32[]{:S(2)}) collective-permute-start(bf16[4,3,128,128]{3,2,1,0:T(8,128)(2,1)} %bitcast.37), channel_id=1, source_target_pairs={{16,0},{20,4},{24,8},{28,12},{0,16},{4,20},{8,24},{12,28},{17,1},{... | collective-permute-start | bytes 1179656 | tf_op jit(solution)/shard_map/ppermute | solution.py:12
  36.9 0.6 gather_fusion
  37.6 0.1 copy.58
  37.7 1.0 sort.15
  38.8 0.1 copy.72
  38.9 0.1 copy.61
  39.0 0.2 reduce_window_sum.18
  39.3 0.6 convert_reduce_fusion
  39.9 1.4 dynamic-update-slice
  41.4 1.3 select_reduce_fusion
  42.7 39.4 %all-reduce.1 = s32[8]{0:T(128)S(1)} all-reduce(s32[8]{0:T(128)S(1)} %dynamic-update-slice), channel_id=1, replica_groups=mesh['rows'=8,'cols'=4] {'rows'}, use_global_device_ids=true, to_apply=%add.1 | all-reduce | flops 8 | bytes 64
  82.1 0.6 fusion.5
  82.8 0.2 reduce-window.4
  82.9 1.2 add_subtract_fusion
  84.1 0.7 copy.68
  84.8 0.1 copy.62
  84.8 0.7 copy-done.1
  85.6 2.3 %collective-permute-start.12 = (bf16[4,3,128,128]{3,2,1,0:T(8,128)(2,1)}, bf16[4,3,128,128]{3,2,1,0:T(8,128)(2,1)S(1)}, u32[]{:S(2)}, u32[]{:S(2)}) collective-permute-start(bf16[4,3,128,128]{3,2,1,0:T(8,128)(2,1)} %bitcast.38), channel_id=1, source_target_pairs={{8,0},{12,4},{16,8},{20,12},{24,16},{28,20},{0,24},{4,28},{9,1},{1... | collective-permute-start | bytes 1179656 | tf_op jit(solution)/shard_map/ppermute | solution.py:12
  87.8 1.0 constant_dynamic-update-slice_fusion.7
  88.9 9.9 %collective-permute-start.11 = (bf16[4,3,128,128]{3,2,1,0:T(8,128)(2,1)}, bf16[4,3,128,128]{3,2,1,0:T(8,128)(2,1)S(1)}, u32[]{:S(2)}, u32[]{:S(2)}) collective-permute-start(bf16[4,3,128,128]{3,2,1,0:T(8,128)(2,1)} %bitcast.39), channel_id=1, source_target_pairs={{4,0},{8,4},{12,8},{16,12},{20,16},{24,20},{28,24},{0,28},{5,1},{9... | collective-permute-start | bytes 1179656 | tf_op jit(solution)/shard_map/ppermute | solution.py:12
  98.8 1.0 constant_dynamic-update-slice_fusion.6
  99.9 1.0 constant_dynamic-update-slice_fusion.5
  100.9 1.0 constant_dynamic-update-slice_fusion.4
  102.1 6.1 %collective-permute-done.11 = bf16[4,3,128,128]{3,2,1,0:T(8,128)(2,1)S(1)} collective-permute-done((bf16[4,3,128,128]{3,2,1,0:T(8,128)(2,1)}, bf16[4,3,128,128]{3,2,1,0:T(8,128)(2,1)S(1)}, u32[]{:S(2)}, u32[]{:S(2)}) %collective-permute-start.11) | collective-permute-done | bytes 393248 | tf_op jit(solution)/shard_map/ppermute | solution.py:12
  108.3 1.0 constant_dynamic-update-slice_fusion
  109.3 3.5 %gather_fusion.1 = bf16[48,3,128,128]{3,2,1,0:T(8,128)(2,1)} fusion(bf16[32,3,128,128]{3,2,1,0:T(8,128)(2,1)S(1)} %constant_dynamic-update-slice_fusion, s32[1024]{0:T(1024)S(1)} %pad_clamp_fusion), kind=kCustom, calls=%fused_computation.1 | custom fusion | bytes 9437376 | tf_op jit(solution)/shard_map/gather | solution.py:63
  112.8 7.9 %fusion.6 = f32[4,12,3,128,128]{4,3,2,1,0:T(8,128)} fusion(bf16[4,12,3,128,128]{4,3,2,1,0:T(8,128)(2,1)} %bitcast.31, bf16[4,12,128,128,1]{3,2,4,1,0:T(8,128)(2,1)} %bitcast.32), kind=kOutput, calls=%fused_computation.35 | convolution fusion | flops 603979776 | bytes 15728640 | tf_op jit(solution)/shard_map/ptab,ptsbc->ptsac/dot_general | solution.py:65
  120.7 12.0 %copy.64 = f32[4,36,128,128]{3,1,2,0:T(8,128)} copy(f32[4,36,128,128]{2,3,1,0:T(8,128)} %bitcast.30) | data formatting | bytes 18874368 | tf_op jit(solution)/shard_map/reshape | solution.py:73
  132.8 9.6 %convert_bitcast_fusion = bf16[4,1,36,128,128]{4,2,3,0,1:T(8,128)(2,1)S(1)} fusion(f32[4,36,128,128]{3,1,2,0:T(8,128)} %copy.64, s32[4,36]{1,0:T(4,128)S(1)} %copy.62), kind=kOutput, calls=%fused_computation.2 | convolution fusion | flops 1021580352 | bytes 14156352 | tf_op jit(solution)/shard_map/poq,pqac->poac/dot_general | solution.py:70
  142.3 3.4 %copy.67 = bf16[4,1,36,128,128]{4,3,2,1,0:T(8,128)(2,1)} copy(bf16[4,1,36,128,128]{4,2,3,0,1:T(8,128)(2,1)S(1)} %convert_bitcast_fusion) | data formatting | bytes 9437184
  (35 shorter events, 0.6 us)
Async XLA Ops:
  7.2 94.8 %copy-start = (bf16[4,1,3,128,128]{4,3,2,1,0:T(8,128)(2,1)S(1)}, bf16[4,1,3,128,128]{4,3,2,1,0:T(8,128)(2,1)}, u32[]{:S(2)}) copy-start(bf16[4,1,3,128,128]{4,3,2,1,0:T(8,128)(2,1)} %param.2) | copy-start | bytes 1179652
  7.2 105.7 %all-gather.2.cloned.1.call-start = ((), (), s32[]{:S(2)}) async-start(), calls=%async_computation | async-start | bytes 1966080 | tf_op jit(solution)/shard_map/all_gather | solution.py:45
  8.0 16.0 %collective-permute-start.6 = (s32[4,3]{1,0:T(4,128)S(1)}, s32[4,3]{1,0:T(4,128)S(1)}, u32[]{:S(2)}, u32[]{:S(2)}) collective-permute-start(s32[4,3]{1,0:T(4,128)S(1)} %bitcast.40), channel_id=1, source_target_pairs={{12,0},{16,4},{20,8},{24,12},{28,16},{0,20},{4,24},{8,28},{13,1},{... | collective-permute-start | bytes 152 | tf_op jit(solution)/shard_map/ppermute | solution.py:12
  13.1 12.8 %collective-permute-start.5 = (s32[4,3]{1,0:T(4,128)S(1)}, s32[4,3]{1,0:T(4,128)S(1)}, u32[]{:S(2)}, u32[]{:S(2)}) collective-permute-start(s32[4,3]{1,0:T(4,128)S(1)} %bitcast.41), channel_id=1, source_target_pairs={{8,0},{12,4},{16,8},{20,12},{24,16},{28,20},{0,24},{4,28},{9,1},{1... | collective-permute-start | bytes 152 | tf_op jit(solution)/shard_map/ppermute | solution.py:12
  14.4 14.3 %collective-permute-start.4 = (s32[4,3]{1,0:T(4,128)S(1)}, s32[4,3]{1,0:T(4,128)S(1)}, u32[]{:S(2)}, u32[]{:S(2)}) collective-permute-start(s32[4,3]{1,0:T(4,128)S(1)} %bitcast.42), channel_id=1, source_target_pairs={{4,0},{8,4},{12,8},{16,12},{20,16},{24,20},{28,24},{0,28},{5,1},{9... | collective-permute-start | bytes 152 | tf_op jit(solution)/shard_map/ppermute | solution.py:12
  14.9 14.0 %collective-permute-start.3 = (s32[4,3]{1,0:T(4,128)S(1)}, s32[4,3]{1,0:T(4,128)S(1)}, u32[]{:S(2)}, u32[]{:S(2)}) collective-permute-start(s32[4,3]{1,0:T(4,128)S(1)} %bitcast.43), channel_id=1, source_target_pairs={{28,0},{0,4},{4,8},{8,12},{12,16},{16,20},{20,24},{24,28},{29,1},{... | collective-permute-start | bytes 152 | tf_op jit(solution)/shard_map/ppermute | solution.py:12
  16.4 15.1 %collective-permute-start.2 = (s32[4,3]{1,0:T(4,128)S(1)}, s32[4,3]{1,0:T(4,128)S(1)}, u32[]{:S(2)}, u32[]{:S(2)}) collective-permute-start(s32[4,3]{1,0:T(4,128)S(1)} %bitcast.44), channel_id=1, source_target_pairs={{24,0},{28,4},{0,8},{4,12},{8,16},{12,20},{16,24},{20,28},{25,1},{... | collective-permute-start | bytes 152 | tf_op jit(solution)/shard_map/ppermute | solution.py:12
  24.0 8.2 %collective-permute-start.1 = (s32[4,3]{1,0:T(4,128)S(1)}, s32[4,3]{1,0:T(4,128)S(1)}, u32[]{:S(2)}, u32[]{:S(2)}) collective-permute-start(s32[4,3]{1,0:T(4,128)S(1)} %bitcast.45), channel_id=1, source_target_pairs={{20,0},{24,4},{28,8},{0,12},{4,16},{8,20},{12,24},{16,28},{21,1},{... | collective-permute-start | bytes 152 | tf_op jit(solution)/shard_map/ppermute | solution.py:12
  25.9 7.9 %collective-permute-start = (s32[4,3]{1,0:T(4,128)S(1)}, s32[4,3]{1,0:T(4,128)S(1)}, u32[]{:S(2)}, u32[]{:S(2)}) collective-permute-start(s32[4,3]{1,0:T(4,128)S(1)} %bitcast.46), channel_id=1, source_target_pairs={{16,0},{20,4},{24,8},{28,12},{0,16},{4,20},{8,24},{12,28},{17,1},{... | collective-permute-start | bytes 152 | tf_op jit(solution)/shard_map/ppermute | solution.py:12
  28.7 79.6 %collective-permute-start.13 = (bf16[4,3,128,128]{3,2,1,0:T(8,128)(2,1)}, bf16[4,3,128,128]{3,2,1,0:T(8,128)(2,1)}, u32[]{:S(2)}, u32[]{:S(2)}) collective-permute-start(bf16[4,3,128,128]{3,2,1,0:T(8,128)(2,1)} %bitcast.33), channel_id=1, source_target_pairs={{12,0},{16,4},{20,8},{24,12},{28,16},{0,20},{4,24},{8,28},{13,1},{... | collective-permute-start | bytes 1179656 | tf_op jit(solution)/shard_map/ppermute | solution.py:12
  28.9 72.1 %collective-permute-start.10 = (bf16[4,3,128,128]{3,2,1,0:T(8,128)(2,1)}, bf16[4,3,128,128]{3,2,1,0:T(8,128)(2,1)}, u32[]{:S(2)}, u32[]{:S(2)}) collective-permute-start(bf16[4,3,128,128]{3,2,1,0:T(8,128)(2,1)} %bitcast.34), channel_id=1, source_target_pairs={{28,0},{0,4},{4,8},{8,12},{12,16},{16,20},{20,24},{24,28},{29,1},{... | collective-permute-start | bytes 1179656 | tf_op jit(solution)/shard_map/ppermute | solution.py:12
  31.5 68.4 %collective-permute-start.9 = (bf16[4,3,128,128]{3,2,1,0:T(8,128)(2,1)}, bf16[4,3,128,128]{3,2,1,0:T(8,128)(2,1)}, u32[]{:S(2)}, u32[]{:S(2)}) collective-permute-start(bf16[4,3,128,128]{3,2,1,0:T(8,128)(2,1)} %bitcast.35), channel_id=1, source_target_pairs={{24,0},{28,4},{0,8},{4,12},{8,16},{12,20},{16,24},{20,28},{25,1},{... | collective-permute-start | bytes 1179656 | tf_op jit(solution)/shard_map/ppermute | solution.py:12
  32.2 56.7 %collective-permute-start.8 = (bf16[4,3,128,128]{3,2,1,0:T(8,128)(2,1)}, bf16[4,3,128,128]{3,2,1,0:T(8,128)(2,1)}, u32[]{:S(2)}, u32[]{:S(2)}) collective-permute-start(bf16[4,3,128,128]{3,2,1,0:T(8,128)(2,1)} %bitcast.36), channel_id=1, source_target_pairs={{20,0},{24,4},{28,8},{0,12},{4,16},{8,20},{12,24},{16,28},{21,1},{... | collective-permute-start | bytes 1179656 | tf_op jit(solution)/shard_map/ppermute | solution.py:12
  33.8 51.0 %collective-permute-start.7 = (bf16[4,3,128,128]{3,2,1,0:T(8,128)(2,1)}, bf16[4,3,128,128]{3,2,1,0:T(8,128)(2,1)S(1)}, u32[]{:S(2)}, u32[]{:S(2)}) collective-permute-start(bf16[4,3,128,128]{3,2,1,0:T(8,128)(2,1)} %bitcast.37), channel_id=1, source_target_pairs={{16,0},{20,4},{24,8},{28,12},{0,16},{4,20},{8,24},{12,28},{17,1},{... | collective-permute-start | bytes 1179656 | tf_op jit(solution)/shard_map/ppermute | solution.py:12
  84.8 0.7 copy-start.1
  85.6 22.6 %collective-permute-start.12 = (bf16[4,3,128,128]{3,2,1,0:T(8,128)(2,1)}, bf16[4,3,128,128]{3,2,1,0:T(8,128)(2,1)S(1)}, u32[]{:S(2)}, u32[]{:S(2)}) collective-permute-start(bf16[4,3,128,128]{3,2,1,0:T(8,128)(2,1)} %bitcast.38), channel_id=1, source_target_pairs={{8,0},{12,4},{16,8},{20,12},{24,16},{28,20},{0,24},{4,28},{9,1},{1... | collective-permute-start | bytes 1179656 | tf_op jit(solution)/shard_map/ppermute | solution.py:12
  88.9 19.3 %collective-permute-start.11 = (bf16[4,3,128,128]{3,2,1,0:T(8,128)(2,1)}, bf16[4,3,128,128]{3,2,1,0:T(8,128)(2,1)S(1)}, u32[]{:S(2)}, u32[]{:S(2)}) collective-permute-start(bf16[4,3,128,128]{3,2,1,0:T(8,128)(2,1)} %bitcast.39), channel_id=1, source_target_pairs={{4,0},{8,4},{12,8},{16,12},{20,16},{24,20},{28,24},{0,28},{5,1},{9... | collective-permute-start | bytes 1179656 | tf_op jit(solution)/shard_map/ppermute | solution.py:12
Sparse Core Ops, SparseCore 0:
  17.2 20.4 all-gather.1
where the time goes:
time: 153 us
  blocking collectives  44.6 us (29%)
  starting transfers between devices  34.1 us (22%)
  local copies, waits for them, and re-layouts  30.8 us (20%)
  matrix products  17.5 us (11%)
  between operations  14.2 us (9%)
  waiting for transfers between devices  6.14 us (4%)
  other arithmetic  5.23 us (3%)
    unnamed x1, blocking collectives  39.4 us
    ppermute x14, starting transfers between devices, shifted(): return lax.ppermute(block, axis, route)  34.1 us
    unnamed x18, local copies, waits for them, and re-layouts  12.7 us
    reshape x1, local copies, waits for them, and re-layouts, on_device(): products.reshape(panel_rows, row_slots * per_group, block_size, block_size)  12 us
    dot_general x1, matrix products, on_device(): jnp.einsum('poq,pqac->poac', onehot, products.reshape(panel_rows, row_slo...  9.58 us
    dot_general x1, matrix products, on_device(): jnp.einsum('ptab,ptsbc->ptsac', left_vals, right_vals, preferred_element_...  7.9 us
    ppermute x14, waiting for transfers between devices, shifted(): return lax.ppermute(block, axis, route)  6.13 us
    all_gather x1, blocking collectives, on_device(): lax.all_gather(block_cols, 'cols', axis=1, tiled=True)  5.19 us
  transfers between devices with their start and end apart: 15, of which 1 were waited for; matrix products, arithmetic and copies ran while one was open for 12% of the time, Pallas kernels for 0%

commit v1 on v0

v1 whole, which is shorter than its diff:
```python
import functools

import jax
import jax.numpy as jnp
from jax import lax
from jax.experimental import pallas as pl
from jax.experimental.pallas import tpu as pltpu
from jax.sharding import PartitionSpec as P


HP = 4
IDX = 16


VMEM = pl.BlockSpec(memory_space=pltpu.VMEM)
SMEM = pl.BlockSpec(memory_space=pltpu.SMEM)


def mask16(row, lane, value):
    seen = jnp.broadcast_to(row[:, lane : lane + 1], (16, 128))
    return jnp.where(seen == value, 1.0, 0.0).astype(jnp.bfloat16)


def stretch(tile, rows):
    return jnp.concatenate([tile] * (rows // 16), axis=0)


def accumulate(dims, pieces, base_ref, lrel_ref, left, lp_ref, d_ref, emit):
    groups, per_group, bs, bins, cycle = dims
    depth = groups * bs
    lrow = lrel_ref[0:1, :]
    for n, (number, parts) in enumerate(pieces):
        for m in range(groups):
            for j in range(groups):
                total = None
                for t in range(per_group):
                    at = ((m ^ j) * per_group + t) * bs
                    hit = mask16(lrow, (j * groups + m) * per_group + t, float(number))
                    term = left[j][at : at + bs, :] * stretch(hit, bs)
                    total = term if total is None else total + term
                lp_ref[m * bs : (m + 1) * bs, n * depth + j * bs : n * depth + (j + 1) * bs] = total
    rows_of = []
    for number, parts in pieces:
        for ref, held, at in parts:
            if at is not None:
                row = ref[at : at + 16, :].astype(jnp.float32)[0:1, :]
        if base_ref is not None:
            row = row - base_ref[0].astype(jnp.float32)
            row = jnp.where(row < 0, row + float(cycle), row)
        rows_of.append(row)
    for first in range(0, bins, 2):
        chunk = range(first, min(first + 2, bins))
        for n, (number, parts) in enumerate(pieces):
            for ref, held, at in parts:
                for place, j in enumerate(held):
                    for b in chunk:
                        total = None
                        for s in range(per_group):
                            start = (place * per_group + s) * bs
                            hit = mask16(rows_of[n], j * per_group + s, float(b))
                            term = ref[start : start + bs, :] * stretch(hit, bs)
                            total = term if total is None else total + term
                        d_ref[
                            n * depth + j * bs : n * depth + (j + 1) * bs, b * bs : (b + 1) * bs
                        ] = total
        lo, hi = first * bs, (first + len(chunk)) * bs
        emit(lo, hi, jnp.dot(lp_ref[...], d_ref[:, lo:hi], preferred_element_type=jnp.float32))


def unpack_refs(refs, layout, with_base):
    refs = list(refs)
    base_ref = refs.pop(0) if with_base else None
    lrel_ref = refs.pop(0)
    left = [refs.pop(0) for _ in range(4)]
    pieces = []
    for number, parts in layout:
        pieces.append((number, [(refs.pop(0), held, at) for held, at in parts]))
    return base_ref, lrel_ref, left, pieces, refs


def step_kernel(dims, layout, with_base, with_acc, *refs):
    base_ref, lrel_ref, left, pieces, rest = unpack_refs(refs, layout, with_base)
    acc_ref = rest.pop(0) if with_acc else None
    out_ref, lp_ref, d_ref = rest

    def emit(lo, hi, value):
        out_ref[:, lo:hi] = value if acc_ref is None else acc_ref[:, lo:hi] + value

    accumulate(dims, pieces, base_ref, lrel_ref, left, lp_ref, d_ref, emit)


def last_kernel(dims, layout, with_base, *refs):
    base_ref, lrel_ref, left, pieces, rest = unpack_refs(refs, layout, with_base)
    acc_ref, slot_ref, col_ref, _, out_ref, lp_ref, d_ref, stage_ref, sems = rest
    groups, _, bs, bins, _ = dims
    me = col_ref[0]
    copies = []

    def emit(lo, hi, value):
        value = (acc_ref[:, lo:hi] + value).astype(jnp.bfloat16)
        for b in range(lo // bs, hi // bs):
            for m in range(groups):
                k = m * bins + b
                at = b * bs - lo
                stage_ref[k] = value[m * bs : (m + 1) * bs, at : at + bs]
                row = m ^ me
                copy = pltpu.make_async_copy(
                    stage_ref.at[k], out_ref.at[row, slot_ref[row * bins + b]], sems.at[k]
                )
                copy.start()
                copies.append(copy)

    accumulate(dims, pieces, base_ref, lrel_ref, left, lp_ref, d_ref, emit)
    for copy in copies:
        copy.wait()


def call_step(dims, base, lrel, left, panels, acc):
    groups, _, bs, bins, _ = dims
    layout = [(number, [(held, at) for _, held, at in parts]) for number, parts in panels]
    arrays = [array for _, parts in panels for array, _, _ in parts]
    args, specs = [], []
    if base is not None:
        args, specs = [base], [SMEM]
    args += [lrel, *left, *arrays]
    specs += [VMEM] * (1 + len(left) + len(arrays))
    aliases = {}
    if acc is not None:
        aliases = {len(args): 0}
        args.append(acc)
        specs.append(VMEM)
    depth = groups * bs * len(panels)
    rows = groups * bs
    flops = 2 * rows * depth * bins * bs
    return pl.pallas_call(
        functools.partial(step_kernel, dims, layout, base is not None, acc is not None),
        out_shape=jax.ShapeDtypeStruct((rows, bins * bs), jnp.float32),
        in_specs=specs,
        out_specs=VMEM,
        scratch_shapes=[
            pltpu.VMEM((rows, depth), jnp.bfloat16),
            pltpu.VMEM((depth, bins * bs), jnp.bfloat16),
        ],
        input_output_aliases=aliases,
        cost_estimate=pl.CostEstimate(flops=flops, bytes_accessed=6_000_000, transcendentals=0),
    )(*args)


def call_last(dims, base, lrel, left, panels, acc, slots, col, empty):
    groups, _, bs, bins, _ = dims
    layout = [(number, [(held, at) for _, held, at in parts]) for number, parts in panels]
    arrays = [array for _, parts in panels for array, _, _ in parts]
    args, specs = [], []
    if base is not None:
        args, specs = [base], [SMEM]
    args += [lrel, *left, *arrays, acc, slots, col, empty]
    specs += [VMEM] * (2 + len(left) + len(arrays)) + [SMEM, SMEM, pl.BlockSpec(memory_space=pl.ANY)]
    depth = groups * bs * len(panels)
    rows = groups * bs
    flops = 2 * rows * depth * bins * bs
    return pl.pallas_call(
        functools.partial(last_kernel, dims, layout, base is not None),
        out_shape=jax.ShapeDtypeStruct(empty.shape, empty.dtype),
        in_specs=specs,
        out_specs=pl.BlockSpec(memory_space=pl.ANY),
        scratch_shapes=[
            pltpu.VMEM((rows, depth), jnp.bfloat16),
            pltpu.VMEM((depth, bins * bs), jnp.bfloat16),
            pltpu.VMEM((groups * bins, bs, bs), jnp.bfloat16),
            pltpu.SemaphoreType.DMA((groups * bins,)),
        ],
        input_output_aliases={len(args) - 1: 0},
        cost_estimate=pl.CostEstimate(flops=flops, bytes_accessed=6_000_000, transcendentals=0),
        name="last",
    )(*args)


def xor_move(value, axis, bit):
    route = [(i, i ^ bit) for i in range(lax.axis_size(axis))]
    return lax.ppermute(value, axis, route)


def shifted(value, axis, distance):
    size = lax.axis_size(axis)
    route = [((i - distance) % size, i) for i in range(size)]
    return lax.ppermute(value, axis, route)


def one_of(values, wanted):
    return jnp.any(values[..., None] == wanted, axis=-2)


def on_device(blocks, block_cols):
    panel_rows, _, per_group, bs, _ = blocks.shape
    groups = lax.axis_size("cols")
    cycle = lax.axis_size("rows")
    slots_out = groups * per_group * per_group
    if groups != 4 or panel_rows != groups or cycle > 256 or cycle < 2 * HP:
        raise ValueError("unsupported sizes")
    bins = min(cycle, 4 * HP - 1)
    whole = cycle == 2 * HP and bins == cycle
    dims = (groups, per_group, bs, bins, cycle)
    p = lax.axis_index("rows").astype(jnp.int32)
    c = lax.axis_index("cols").astype(jnp.int32)
    lanes = jnp.arange(groups, dtype=jnp.int32)
    body_rows = groups * per_group * bs

    mine = block_cols[:, 0] // groups
    order = lanes ^ c
    numbers = mine[order].astype(jnp.bfloat16).reshape(1, groups * per_group)
    numbers = jnp.pad(numbers, ((0, IDX - 1), (0, bs - groups * per_group)))
    body = jnp.concatenate(
        [lax.dynamic_index_in_dim(blocks[:, 0], c ^ j, 0, keepdims=False) for j in range(groups)], axis=0
    ).reshape(body_rows, bs)
    own = jnp.concatenate([body, numbers], axis=0)
    every = list(range(groups))

    def full(array):
        return [(array, every, body_rows)]

    if whole:
        x1 = xor_move(own, "rows", 2)
        x2 = xor_move(own, "rows", 4)
        y0 = xor_move(own, "rows", 1)
    else:
        window = [own if k == 0 else shifted(own, "rows", -k) for k in range(-HP, HP)]
    left1 = xor_move(own, "cols", 1)
    left2 = xor_move(own, "cols", 2)
    left3 = xor_move(left2, "cols", 1)
    left = [own, left1, left2, left3]

    def numbers_of(array, count=groups * per_group):
        return array[body_rows, :count].astype(jnp.int32)

    held = jnp.stack(
        [numbers_of(left[j]).reshape(groups, per_group)[jnp.array([m ^ j for m in every])] for j in every],
        axis=1,
    )
    if whole:
        lrel = held ^ p
        base = None
        zero = jnp.int32(0)
    else:
        lrel = (held - (p - HP)) % cycle
        zero = (p - 2 * HP) % cycle if bins < cycle else jnp.int32(0)
        base = zero.reshape(1)
    lrel_row = jnp.transpose(lrel, (1, 0, 2)).reshape(1, groups * groups * per_group)
    lrel_row = jnp.pad(lrel_row.astype(jnp.float32), ((0, 7), (0, 128 - lrel_row.shape[1])))
    bin_ids = jnp.arange(bins, dtype=jnp.int32)
    bin_abs = (zero + bin_ids) % cycle

    if whole:
        yx1 = xor_move(x1, "rows", 1)
        x12 = xor_move(x2, "rows", 2)
        yx2 = xor_move(x2, "rows", 1)
        half = groups // 2
        cut = half * per_group * bs
        tail_a = xor_move(x12[:cut], "rows", 1)
        tail_b = xor_move(yx2[cut:], "rows", 2)
        known = held.reshape(1, -1)
        for bit in (4, 2, 1):
            known = jnp.concatenate([known, xor_move(known, "rows", bit)], axis=0)
        places = jnp.array([0, 4, 2, 6, 1, 5, 3, 7], dtype=jnp.int32)
        panel_of = places ^ p
        known = known.reshape(cycle, groups, groups, per_group)
        uses = one_of(known, panel_of)
        has = one_of(known[:, :, 0, :], bin_ids)
        hits = jnp.any(
            uses.transpose(0, 1, 3, 2)[..., None] & has[None, None], axis=(2, 3)
        )
        totals = jnp.sum(hits.astype(jnp.int32), axis=-1)
        earlier = jnp.sum(jnp.where((panel_of < p)[:, None], totals, 0))
        mine_hits = hits[0]
        acc = call_step(dims, base, lrel_row, left, [(0, full(own)), (2, full(x1)), (1, full(y0))], None)
        acc = call_step(dims, base, lrel_row, left, [(3, full(yx1)), (4, full(x2))], acc)
        acc = call_step(dims, base, lrel_row, left, [(5, full(yx2)), (6, full(x12))], acc)
        final = [(7, [(tail_a, every[:half], None), (tail_b, every[half:], cut)])]
    else:
        has = jnp.stack(
            [one_of((numbers_of(w).reshape(groups, per_group) - zero) % cycle, bin_ids) for w in window]
        )
        uses = one_of(lrel, jnp.arange(2 * HP, dtype=jnp.int32))
        mine_hits = jnp.any(uses.transpose(0, 2, 1)[..., None] & has[None], axis=(1, 2))
        panel_total = jnp.sum(mine_hits.astype(jnp.int32))
        all_totals = lax.all_gather(panel_total.reshape(1), "rows", axis=0, tiled=True)
        earlier = jnp.sum(jnp.where(jnp.arange(cycle, dtype=jnp.int32) < p, all_totals, 0))
        acc = None
        for at in (0, 2, 4):
            acc = call_step(dims, base, lrel_row, left, [(e, full(window[e])) for e in (at, at + 1)], acc)
        final = [(e, full(window[e])) for e in (6, 7)]

    pick = (lanes[:, None] ^ c) == lanes[None, :]
    present = jnp.any(pick[:, :, None] & mine_hits[None], axis=1)
    lower = bin_abs[:, None] < bin_abs[None, :]
    counts = jnp.sum(present.astype(jnp.int32), axis=-1)
    rank_in = jnp.sum((present[:, :, None] & lower[None]).astype(jnp.int32), axis=1)
    rank_out = jnp.sum((~present[:, :, None] & lower[None]).astype(jnp.int32), axis=1)
    slots = jnp.where(present, rank_in, counts[:, None] + rank_out)
    at_slot = present[:, None, :] & (slots[:, None, :] == jnp.arange(slots_out, dtype=jnp.int32)[:, None])
    columns = jnp.sum(jnp.where(at_slot, bin_abs * groups + c + 1, 0), axis=-1) - 1
    before = lanes[:, None] > lanes[None, :]
    starts = earlier + jnp.sum(jnp.where(before, counts[None, :], 0), axis=1)

    empty = jnp.zeros((panel_rows, slots_out, bs, bs), jnp.bfloat16)
    out = call_last(dims, base, lrel_row, left, final, acc, slots.reshape(-1), c.reshape(1), empty)
    return out[:, None], columns.astype(jnp.int32)[:, None], starts.astype(jnp.int32)[:, None]


def solution(mesh):
    in_specs = (P("rows", "cols", None, None, None), P("rows", "cols", None))
    out_specs = (P("rows", "cols", None, None, None), P("rows", "cols", None), P("rows", "cols"))

    return jax.shard_map(on_device, mesh=mesh, in_specs=in_specs, out_specs=out_specs, check_vma=False)
```

time: 153 us -> 87.1 us (0.57)
  blocking collectives: 44.6 us -> 0 us
  Pallas kernels: 0 us -> 22.9 us
  matrix products: 17.5 us -> 0 us
  local copies, waits for them, and re-layouts: 30.8 us -> 14.4 us
  waiting for transfers between devices: 6.14 us -> 22.1 us
  between operations: 14.2 us -> 0.99 us
  starting transfers between devices: 34.1 us -> 21.5 us
    unnamed x1 -> x0, blocking collectives: 39.4 us -> none
    pallas_call x0 -> x4, Pallas kernels: none -> 22.9 us  [the longest x3 18.3 us: call_step(): pl.pallas_call(functools.partial(step_kernel, dims, layout, base is not N...]
    dot_general x2 -> x0, matrix products: 17.5 us -> none  [the longest x1 9.58 us: on_device(): jnp.einsum('poq,pqac->poac', onehot, products.reshape(panel_rows, row_slo...]
    ppermute x14, waiting for transfers between devices: 6.13 us -> 22.1 us  [xor_move(): return lax.ppermute(value, axis, route)]
    ppermute x14, starting transfers between devices: 34.1 us -> 21.5 us  [xor_move(): return lax.ppermute(value, axis, route)]
    reshape x3 -> x1, local copies, waits for them, and re-layouts: 12.2 us -> 0.09 us  [on_device(): known = held.reshape(1, -1)]
    unnamed x18 -> x27, local copies, waits for them, and re-layouts: 12.7 us -> 1.79 us
    all_gather x1 -> x0, blocking collectives: 5.19 us -> none  [on_device(): lax.all_gather(block_cols, 'cols', axis=1, tiled=True)]
  transfers between devices with their start and end apart: 15 -> 14, of which waited for: 1 -> 4; matrix products, arithmetic and copies ran while one was open for 12% -> 14% of each run, Pallas kernels for 0% -> 21%
where the time goes in v1:
time: 87.1 us; the launch traced here: 86.8 us
  Pallas kernels  22.9 us (26%)
  waiting for transfers between devices  22.1 us (25%)
  starting transfers between devices  21.5 us (25%)
  local copies, waits for them, and re-layouts  14.4 us (17%)
  other arithmetic  4.94 us (6%)
  between operations  0.99 us (1%)
    ppermute x14, waiting for transfers between devices, xor_move(): return lax.ppermute(value, axis, route)  22.1 us
    ppermute x14, starting transfers between devices, xor_move(): return lax.ppermute(value, axis, route)  21.5 us
    pallas_call x3, Pallas kernels, call_step(): pl.pallas_call(functools.partial(step_kernel, dims, layout, base is not N...  18.3 us
    pallas_call x1, Pallas kernels, call_last(): pl.pallas_call(functools.partial(last_kernel, dims, layout, base is not N...  4.63 us
    broadcast_in_dim x1, local copies, waits for them, and re-layouts, on_device(): empty = jnp.zeros((panel_rows, slots_out, bs, bs), jnp.bfloat16)  3.37 us
    gather x4, local copies, waits for them, and re-layouts, on_device(): numbers_of(left[j]).reshape(groups, per_group)  2.24 us
    concatenate x14, local copies, waits for them, and re-layouts, on_device(): known = jnp.concatenate([known, xor_move(known, 'rows', bit)], axis=0)  2.17 us
    unnamed x27, local copies, waits for them, and re-layouts  1.79 us
  transfers between devices with their start and end apart: 14, of which 4 were waited for; matrix products, arithmetic and copies ran while one was open for 14% of the time, Pallas kernels for 21%

profile of v1, /device:TPU:0, one launch (start us, length us, event | category | flops | bytes accessed | tf_op | source)
XLA Modules:
  0.0 86.8 jit_solution(13252657649418979913)
XLA Ops:
  0.7 0.8 copy.72
  1.5 0.6 gather_fusion
  2.2 1.1 %dynamic-slice_bitcast_fusion.3 = (bf16[3,128,128]{2,1,0:T(8,128)(2,1)S(1)}, bf16[3,128,128]{2,1,0:T(8,128)(2,1)S(1)}, bf16[3,128,128]{2,1,0:T(8,128)(2,1)S(1)}, bf16[3,128,128]{2,1,0:T(8,128)(2,1)S(1)}) fusion(bf16[4,1,3,128,128]{4,3,2,1,0:T(8,128)(2,1)} %param.7, s32[]{:T(128)S(6)} %select_n.86, s32[]{:T(128)S(6)} %select_n.87, s32[]{:T(128)S(6)} %select_n.89, ...), kind=kLoop, calls=%fused_computation.14 | loop fusion | bytes 786448 | tf_op jit(solution)/shard_map/jit(dynamic_index_in_dim)/squeeze | solution.py:213
  3.3 3.1 %collective-permute-start.8 = (bf16[1552,128]{1,0:T(8,128)(2,1)S(1)}, bf16[1552,128]{1,0:T(8,128)(2,1)S(1)}, u32[]{:S(2)}, u32[]{:S(2)}) collective-permute-start(bf16[1552,128]{1,0:T(8,128)(2,1)S(1)} %fusion.1.refs_1_.refs_5_), channel_id=1, source_target_pairs={{0,8},{4,12},{8,0},{12,4},{16,24},{20,28},{24,16},{28,20},{1,9},{5... | collective-permute-start | bytes 1191944 | tf_op jit(solution)/shard_map/ppermute | solution.py:180
  6.4 2.6 %collective-permute-start.3 = (bf16[1552,128]{1,0:T(8,128)(2,1)S(1)}, bf16[1552,128]{1,0:T(8,128)(2,1)S(1)}, u32[]{:S(2)}, u32[]{:S(2)}) collective-permute-start(bf16[1552,128]{1,0:T(8,128)(2,1)S(1)} %fusion.1.refs_1_.refs_5_), channel_id=1, source_target_pairs={{0,16},{4,20},{8,24},{12,28},{16,0},{20,4},{24,8},{28,12},{1,17},{... | collective-permute-start | bytes 1191944 | tf_op jit(solution)/shard_map/ppermute | solution.py:180
  9.0 1.5 %collective-permute-start.1 = (bf16[1552,128]{1,0:T(8,128)(2,1)S(1)}, bf16[1552,128]{1,0:T(8,128)(2,1)S(1)}, u32[]{:S(2)}, u32[]{:S(2)}) collective-permute-start(bf16[1552,128]{1,0:T(8,128)(2,1)S(1)} %fusion.1.refs_1_.refs_5_), channel_id=1, source_target_pairs={{0,2},{1,3},{2,0},{3,1},{4,6},{5,7},{6,4},{7,5},{8,10},{9,11},{10,... | collective-permute-start | bytes 1191944 | tf_op jit(solution)/shard_map/ppermute | solution.py:180
  10.7 0.6 gather_fusion.1
  11.3 15.3 %collective-permute-done.3.refs_6_ = bf16[1552,128]{1,0:T(8,128)(2,1)S(1)} collective-permute-done((bf16[1552,128]{1,0:T(8,128)(2,1)S(1)}, bf16[1552,128]{1,0:T(8,128)(2,1)S(1)}, u32[]{:S(2)}, u32[]{:S(2)}) %collective-permute-start.3) | collective-permute-done | bytes 397344 | tf_op jit(solution)/shard_map/ppermute | solution.py:180
  26.6 1.5 %collective-permute-start.6 = (bf16[1552,128]{1,0:T(8,128)(2,1)S(1)}, bf16[1552,128]{1,0:T(8,128)(2,1)S(1)}, u32[]{:S(2)}, u32[]{:S(2)}) collective-permute-start(bf16[1552,128]{1,0:T(8,128)(2,1)S(1)} %collective-permute-done.3.refs_6_), channel_id=1, source_target_pairs={{0,4},{4,0},{8,12},{12,8},{16,20},{20,16},{24,28},{28,24},{1,5},{5... | collective-permute-start | bytes 1191944 | tf_op jit(solution)/shard_map/ppermute | solution.py:180
  28.1 0.4 collective-permute-start.4
  28.6 0.5 collective-permute-start.10
  29.2 0.2 copy-done.11
  29.4 1.4 %collective-permute-start.9 = (bf16[1552,128]{1,0:T(8,128)(2,1)}, bf16[1552,128]{1,0:T(8,128)(2,1)S(1)}, u32[]{:S(2)}, u32[]{:S(2)}) collective-permute-start(bf16[1552,128]{1,0:T(8,128)(2,1)} %copy-done.11), channel_id=1, source_target_pairs={{0,4},{4,0},{8,12},{12,8},{16,20},{20,16},{24,28},{28,24},{1,5},{5... | collective-permute-start | bytes 1191944 | tf_op jit(solution)/shard_map/ppermute | solution.py:180
  31.0 0.6 gather_fusion.3
  31.6 0.6 gather_fusion.2
  32.1 5.0 %collective-permute-done.6.refs_5_ = bf16[1552,128]{1,0:T(8,128)(2,1)S(1)} collective-permute-done((bf16[1552,128]{1,0:T(8,128)(2,1)S(1)}, bf16[1552,128]{1,0:T(8,128)(2,1)S(1)}, u32[]{:S(2)}, u32[]{:S(2)}) %collective-permute-start.6) | collective-permute-done | bytes 397344 | tf_op jit(solution)/shard_map/ppermute | solution.py:180
  37.1 2.1 %collective-permute-start.7 = (bf16[784,128]{1,0:T(8,128)(2,1)S(1)}, bf16[784,128]{1,0:T(8,128)(2,1)}, u32[]{:S(2)}, u32[]{:S(2)}) collective-permute-start(bf16[784,128]{1,0:T(8,128)(2,1)S(1)} %slice.43), channel_id=1, source_target_pairs={{0,8},{4,12},{8,0},{12,4},{16,24},{20,28},{24,16},{28,20},{1,9},{5... | collective-permute-start | bytes 602120 | tf_op jit(solution)/shard_map/ppermute | solution.py:180
  39.2 0.7 slice.42
  39.9 1.5 %collective-permute-start.5 = (bf16[768,128]{1,0:T(8,128)(2,1)}, bf16[768,128]{1,0:T(8,128)(2,1)}, u32[]{:S(2)}, u32[]{:S(2)}) collective-permute-start(bf16[768,128]{1,0:T(8,128)(2,1)} %slice.42), channel_id=1, source_target_pairs={{0,4},{4,0},{8,12},{12,8},{16,20},{20,16},{24,28},{28,24},{1,5},{5... | collective-permute-start | bytes 589832 | tf_op jit(solution)/shard_map/ppermute | solution.py:180
  41.6 0.6 gather_fusion.4
  42.3 2.6 %collective-permute-start.11 = (s32[1,48]{1,0:T(1,128)S(1)}, s32[1,48]{1,0:T(1,128)S(1)}, u32[]{:S(2)}, u32[]{:S(2)}) collective-permute-start(s32[1,48]{1,0:T(1,128)S(1)} %reshape.215), channel_id=1, source_target_pairs={{0,16},{4,20},{8,24},{12,28},{16,0},{20,4},{24,8},{28,12},{1,17},{... | collective-permute-start | bytes 584 | tf_op jit(solution)/shard_map/ppermute | solution.py:180
  44.9 0.6 pad.9.refs_0_
  45.5 0.2 collective-permute-done.10.refs_7_
  45.7 6.2 %shard_map.94.refs_7_ = f32[512,1024]{1,0:T(8,128)} custom-call(f32[8,128]{1,0:T(8,128)} %pad.9.refs_0_, bf16[1552,128]{1,0:T(8,128)(2,1)} %copy-done, bf16[1552,128]{1,0:T(8,128)(2,1)} %copy-done.2, bf16[1552,128]{1,0:T(8,128)(2,1)} %copy-done.1, bf16[1552,128]{1,0:T(8,128)(2,1)} %copy-done.3, bf16[1552,128]{1,0:T(8,128)(2,1)} %copy-done, ...), custom_call_target="tpu_custom_call" | custom-call | flops 1610612736 | bytes 6000000 | tf_op jit(solution)/shard_map/pallas_call | solution.py:135
  51.9 1.7 %collective-permute-done.9.refs_5_ = bf16[1552,128]{1,0:T(8,128)(2,1)S(1)} collective-permute-done((bf16[1552,128]{1,0:T(8,128)(2,1)}, bf16[1552,128]{1,0:T(8,128)(2,1)S(1)}, u32[]{:S(2)}, u32[]{:S(2)}) %collective-permute-start.9) | collective-permute-done | bytes 397344 | tf_op jit(solution)/shard_map/ppermute | solution.py:180
  53.5 0.7 copy-done.7
  54.3 6.0 %shard_map.95.refs_7_ = f32[512,1024]{1,0:T(8,128)} custom-call(f32[8,128]{1,0:T(8,128)} %pad.9.refs_0_, bf16[1552,128]{1,0:T(8,128)(2,1)} %copy-done, bf16[1552,128]{1,0:T(8,128)(2,1)} %copy-done.2, bf16[1552,128]{1,0:T(8,128)(2,1)} %copy-done.1, bf16[1552,128]{1,0:T(8,128)(2,1)} %copy-done.3, ...), custom_call_target="tpu_custom_call", output_to_operand_aliasing={{}: (7, {})} | custom-call | flops 1073741824 | bytes 6000000 | tf_op jit(solution)/shard_map/pallas_call | solution.py:135
  60.3 2.7 %collective-permute-start.12 = (s32[2,48]{1,0:T(2,128)S(1)}, s32[2,48]{1,0:T(2,128)S(1)}, u32[]{:S(2)}, u32[]{:S(2)}) collective-permute-start(s32[2,48]{1,0:T(2,128)S(1)} %pad_add_fusion.5), channel_id=1, source_target_pairs={{0,8},{4,12},{8,0},{12,4},{16,24},{20,28},{24,16},{28,20},{1,9},{5... | collective-permute-start | bytes 1160 | tf_op jit(solution)/shard_map/ppermute | solution.py:180
  63.0 6.0 %shard_map.96.refs_7_ = f32[512,1024]{1,0:T(8,128)} custom-call(f32[8,128]{1,0:T(8,128)} %pad.9.refs_0_, bf16[1552,128]{1,0:T(8,128)(2,1)} %copy-done, bf16[1552,128]{1,0:T(8,128)(2,1)} %copy-done.2, bf16[1552,128]{1,0:T(8,128)(2,1)} %copy-done.1, bf16[1552,128]{1,0:T(8,128)(2,1)} %copy-done.3, ...), custom_call_target="tpu_custom_call", output_to_operand_aliasing={{}: (7, {})} | custom-call | flops 1073741824 | bytes 6000000 | tf_op jit(solution)/shard_map/pallas_call | solution.py:135
  69.2 1.6 %collective-permute-start.13 = (s32[4,48]{1,0:T(4,128)S(1)}, s32[4,48]{1,0:T(4,128)S(1)}, u32[]{:S(2)}, u32[]{:S(2)}) collective-permute-start(s32[4,48]{1,0:T(4,128)S(1)} %pad_add_fusion.4), channel_id=1, source_target_pairs={{0,4},{4,0},{8,12},{12,8},{16,20},{20,16},{24,28},{28,24},{1,5},{5... | collective-permute-start | bytes 2312 | tf_op jit(solution)/shard_map/ppermute | solution.py:180
  70.8 0.2 copy.82
  71.0 0.2 copy.75
  71.1 0.5 broadcast.224
  71.6 0.7 reduce.17
  72.5 0.2 copy.83
  72.7 0.2 copy.76
  73.0 0.2 copy.84
  73.3 0.2 copy.77
  73.6 0.2 copy.85
  74.2 0.2 copy.78
  74.6 0.2 and_reduce_fusion
  74.9 0.2 convert_reduce_fusion
  75.6 0.7 select_n.95.refs_8_
  76.4 0.6 broadcast_add_fusion
  77.0 0.7 select_reduce_fusion.1
  77.7 1.2 %add_bitcast_fusion.1 = s32[4,1]{0,1:T(1,128)} fusion(s32[4]{0:T(128)S(1)} %select_reduce_fusion.2, s32[]{:T(128)} %select_reduce_fusion.1), kind=kLoop, calls=%fused_computation.65 | loop fusion | flops 4 | bytes 36 | tf_op jit(solution)/shard_map/add | solution.py:302
  78.8 3.4 %broadcast_in_dim.48.refs_10_ = bf16[4,36,128,128]{3,2,1,0:T(8,128)(2,1)} broadcast(bf16[]{:T(256)} %constant.81.clone.1), dimensions={} | broadcast | bytes 4718594 | tf_op jit(solution)/shard_map/broadcast_in_dim | solution.py:304
  82.2 4.6 %last.1 = bf16[4,36,128,128]{3,2,1,0:T(8,128)(2,1)} custom-call(f32[8,128]{1,0:T(8,128)} %pad.9.refs_0_, bf16[1552,128]{1,0:T(8,128)(2,1)} %copy-done, bf16[1552,128]{1,0:T(8,128)(2,1)} %copy-done.2, bf16[1552,128]{1,0:T(8,128)(2,1)} %copy-done.1, bf16[1552,128]{1,0:T(8,128)(2,1)} %copy-done.3, ...), custom_call_target="tpu_custom_call", output_to_operand_aliasing={{}: (10, {})} | custom-call | flops 536870912 | bytes 6000000 | tf_op jit(solution)/shard_map/last/pallas_call | solution.py:161
  (89 shorter events, 2.8 us)
Async XLA Ops:
  0.6 10.0 %copy-start.10 = (s32[4]{0:T(128)S(1)}, s32[4]{0:T(128)}, u32[]{:S(2)}) copy-start(s32[4]{0:T(128)} %constant.111) | copy-start | bytes 52
  0.6 10.0 %copy-start.9 = (s32[4]{0:T(128)S(1)}, s32[4]{0:T(128)}, u32[]{:S(2)}) copy-start(s32[4]{0:T(128)} %constant.112) | copy-start | bytes 52
  0.7 10.0 %copy-start.12 = (s32[8]{0:T(128)S(1)}, s32[8]{0:T(128)}, u32[]{:S(2)}) copy-start(s32[8]{0:T(128)} %constant.91.clone) | copy-start | bytes 100
  0.7 10.6 %copy-start.8 = (s32[4]{0:T(128)S(1)}, s32[4]{0:T(128)}, u32[]{:S(2)}) copy-start(s32[4]{0:T(128)} %constant.113) | copy-start | bytes 52
  3.3 42.3 %copy-start = (bf16[1552,128]{1,0:T(8,128)(2,1)}, bf16[1552,128]{1,0:T(8,128)(2,1)S(1)}, u32[]{:S(2)}) copy-start(bf16[1552,128]{1,0:T(8,128)(2,1)S(1)} %fusion.1.refs_1_.refs_5_) | copy-start | bytes 1191940
  3.3 25.3 %collective-permute-start.8 = (bf16[1552,128]{1,0:T(8,128)(2,1)S(1)}, bf16[1552,128]{1,0:T(8,128)(2,1)S(1)}, u32[]{:S(2)}, u32[]{:S(2)}) collective-permute-start(bf16[1552,128]{1,0:T(8,128)(2,1)S(1)} %fusion.1.refs_1_.refs_5_), channel_id=1, source_target_pairs={{0,8},{4,12},{8,0},{12,4},{16,24},{20,28},{24,16},{28,20},{1,9},{5... | collective-permute-start | bytes 1191944 | tf_op jit(solution)/shard_map/ppermute | solution.py:180
  6.4 20.1 %collective-permute-start.3 = (bf16[1552,128]{1,0:T(8,128)(2,1)S(1)}, bf16[1552,128]{1,0:T(8,128)(2,1)S(1)}, u32[]{:S(2)}, u32[]{:S(2)}) collective-permute-start(bf16[1552,128]{1,0:T(8,128)(2,1)S(1)} %fusion.1.refs_1_.refs_5_), channel_id=1, source_target_pairs={{0,16},{4,20},{8,24},{12,28},{16,0},{20,4},{24,8},{28,12},{1,17},{... | collective-permute-start | bytes 1191944 | tf_op jit(solution)/shard_map/ppermute | solution.py:180
  9.0 19.5 %collective-permute-start.1 = (bf16[1552,128]{1,0:T(8,128)(2,1)S(1)}, bf16[1552,128]{1,0:T(8,128)(2,1)S(1)}, u32[]{:S(2)}, u32[]{:S(2)}) collective-permute-start(bf16[1552,128]{1,0:T(8,128)(2,1)S(1)} %fusion.1.refs_1_.refs_5_), channel_id=1, source_target_pairs={{0,2},{1,3},{2,0},{3,1},{4,6},{5,7},{6,4},{7,5},{8,10},{9,11},{10,... | collective-permute-start | bytes 1191944 | tf_op jit(solution)/shard_map/ppermute | solution.py:180
  10.5 18.9 %collective-permute-start = (bf16[1552,128]{1,0:T(8,128)(2,1)S(1)}, bf16[1552,128]{1,0:T(8,128)(2,1)S(1)}, u32[]{:S(2)}, u32[]{:S(2)}) collective-permute-start(bf16[1552,128]{1,0:T(8,128)(2,1)S(1)} %fusion.1.refs_1_.refs_5_), channel_id=1, source_target_pairs={{0,1},{1,0},{2,3},{3,2},{4,5},{5,4},{6,7},{7,6},{8,9},{9,8},{10,11... | collective-permute-start | bytes 1191944 | tf_op jit(solution)/shard_map/ppermute | solution.py:180
  26.6 27.0 %copy-start.6 = (bf16[1552,128]{1,0:T(8,128)(2,1)}, bf16[1552,128]{1,0:T(8,128)(2,1)S(1)}, u32[]{:S(2)}) copy-start(bf16[1552,128]{1,0:T(8,128)(2,1)S(1)} %collective-permute-done.3.refs_6_) | copy-start | bytes 1191940
  26.6 10.5 %collective-permute-start.6 = (bf16[1552,128]{1,0:T(8,128)(2,1)S(1)}, bf16[1552,128]{1,0:T(8,128)(2,1)S(1)}, u32[]{:S(2)}, u32[]{:S(2)}) collective-permute-start(bf16[1552,128]{1,0:T(8,128)(2,1)S(1)} %collective-permute-done.3.refs_6_), channel_id=1, source_target_pairs={{0,4},{4,0},{8,12},{12,8},{16,20},{20,16},{24,28},{28,24},{1,5},{5... | collective-permute-start | bytes 1191944 | tf_op jit(solution)/shard_map/ppermute | solution.py:180
  28.1 11.1 %collective-permute-start.4 = (bf16[1552,128]{1,0:T(8,128)(2,1)S(1)}, bf16[1552,128]{1,0:T(8,128)(2,1)S(1)}, u32[]{:S(2)}, u32[]{:S(2)}) collective-permute-start(bf16[1552,128]{1,0:T(8,128)(2,1)S(1)} %collective-permute-done.3.refs_6_), channel_id=1, source_target_pairs={{0,8},{4,12},{8,0},{12,4},{16,24},{20,28},{24,16},{28,20},{1,9},{5... | collective-permute-start | bytes 1191944 | tf_op jit(solution)/shard_map/ppermute | solution.py:180
  28.5 17.1 %copy-start.1 = (bf16[1552,128]{1,0:T(8,128)(2,1)}, bf16[1552,128]{1,0:T(8,128)(2,1)S(1)}, u32[]{:S(2)}) copy-start(bf16[1552,128]{1,0:T(8,128)(2,1)S(1)} %collective-permute-done.1.refs_3_) | copy-start | bytes 1191940
  28.5 12.9 %collective-permute-start.2 = (bf16[1552,128]{1,0:T(8,128)(2,1)S(1)}, bf16[1552,128]{1,0:T(8,128)(2,1)S(1)}, u32[]{:S(2)}, u32[]{:S(2)}) collective-permute-start(bf16[1552,128]{1,0:T(8,128)(2,1)S(1)} %collective-permute-done.1.refs_3_), channel_id=1, source_target_pairs={{0,1},{1,0},{2,3},{3,2},{4,5},{5,4},{6,7},{7,6},{8,9},{9,8},{10,11... | collective-permute-start | bytes 1191944 | tf_op jit(solution)/shard_map/ppermute | solution.py:180
  28.6 0.8 copy-start.11
  28.6 17.0 %collective-permute-start.10 = (bf16[1552,128]{1,0:T(8,128)(2,1)S(1)}, bf16[1552,128]{1,0:T(8,128)(2,1)}, u32[]{:S(2)}, u32[]{:S(2)}) collective-permute-start(bf16[1552,128]{1,0:T(8,128)(2,1)S(1)} %fusion.1.refs_1_.refs_5_), channel_id=1, source_target_pairs={{0,4},{4,0},{8,12},{12,8},{16,20},{20,16},{24,28},{28,24},{1,5},{5... | collective-permute-start | bytes 1191944 | tf_op jit(solution)/shard_map/ppermute | solution.py:180
  29.4 16.2 %copy-start.2 = (bf16[1552,128]{1,0:T(8,128)(2,1)}, bf16[1552,128]{1,0:T(8,128)(2,1)S(1)}, u32[]{:S(2)}) copy-start(bf16[1552,128]{1,0:T(8,128)(2,1)S(1)} %collective-permute-done.refs_2_) | copy-start | bytes 1191940
  29.4 24.1 %collective-permute-start.9 = (bf16[1552,128]{1,0:T(8,128)(2,1)}, bf16[1552,128]{1,0:T(8,128)(2,1)S(1)}, u32[]{:S(2)}, u32[]{:S(2)}) collective-permute-start(bf16[1552,128]{1,0:T(8,128)(2,1)} %copy-done.11), channel_id=1, source_target_pairs={{0,4},{4,0},{8,12},{12,8},{16,20},{20,16},{24,28},{28,24},{1,5},{5... | collective-permute-start | bytes 1191944 | tf_op jit(solution)/shard_map/ppermute | solution.py:180
  37.1 23.2 %copy-start.4 = (bf16[1552,128]{1,0:T(8,128)(2,1)}, bf16[1552,128]{1,0:T(8,128)(2,1)S(1)}, u32[]{:S(2)}) copy-start(bf16[1552,128]{1,0:T(8,128)(2,1)S(1)} %collective-permute-done.6.refs_5_) | copy-start | bytes 1191940
  37.1 41.7 %collective-permute-start.7 = (bf16[784,128]{1,0:T(8,128)(2,1)S(1)}, bf16[784,128]{1,0:T(8,128)(2,1)}, u32[]{:S(2)}, u32[]{:S(2)}) collective-permute-start(bf16[784,128]{1,0:T(8,128)(2,1)S(1)} %slice.43), channel_id=1, source_target_pairs={{0,8},{4,12},{8,0},{12,4},{16,24},{20,28},{24,16},{28,20},{1,9},{5... | collective-permute-start | bytes 602120 | tf_op jit(solution)/shard_map/ppermute | solution.py:180
  39.2 21.1 %copy-start.5 = (bf16[1552,128]{1,0:T(8,128)(2,1)}, bf16[1552,128]{1,0:T(8,128)(2,1)S(1)}, u32[]{:S(2)}) copy-start(bf16[1552,128]{1,0:T(8,128)(2,1)S(1)} %collective-permute-done.4.refs_6_) | copy-start | bytes 1191940
  39.9 38.9 %collective-permute-start.5 = (bf16[768,128]{1,0:T(8,128)(2,1)}, bf16[768,128]{1,0:T(8,128)(2,1)}, u32[]{:S(2)}, u32[]{:S(2)}) collective-permute-start(bf16[768,128]{1,0:T(8,128)(2,1)} %slice.42), channel_id=1, source_target_pairs={{0,4},{4,0},{8,12},{12,8},{16,20},{20,16},{24,28},{28,24},{1,5},{5... | collective-permute-start | bytes 589832 | tf_op jit(solution)/shard_map/ppermute | solution.py:180
  41.5 4.2 %copy-start.3 = (bf16[1552,128]{1,0:T(8,128)(2,1)}, bf16[1552,128]{1,0:T(8,128)(2,1)S(1)}, u32[]{:S(2)}) copy-start(bf16[1552,128]{1,0:T(8,128)(2,1)S(1)} %collective-permute-done.2.refs_4_) | copy-start | bytes 1191940
  42.3 18.0 %collective-permute-start.11 = (s32[1,48]{1,0:T(1,128)S(1)}, s32[1,48]{1,0:T(1,128)S(1)}, u32[]{:S(2)}, u32[]{:S(2)}) collective-permute-start(s32[1,48]{1,0:T(1,128)S(1)} %reshape.215), channel_id=1, source_target_pairs={{0,16},{4,20},{8,24},{12,28},{16,0},{20,4},{24,8},{28,12},{1,17},{... | collective-permute-start | bytes 584 | tf_op jit(solution)/shard_map/ppermute | solution.py:180
  53.5 0.7 copy-start.7
  60.3 8.8 %collective-permute-start.12 = (s32[2,48]{1,0:T(2,128)S(1)}, s32[2,48]{1,0:T(2,128)S(1)}, u32[]{:S(2)}, u32[]{:S(2)}) collective-permute-start(s32[2,48]{1,0:T(2,128)S(1)} %pad_add_fusion.5), channel_id=1, source_target_pairs={{0,8},{4,12},{8,0},{12,4},{16,24},{20,28},{24,16},{28,20},{1,9},{5... | collective-permute-start | bytes 1160 | tf_op jit(solution)/shard_map/ppermute | solution.py:180
  69.2 4.3 %collective-permute-start.13 = (s32[4,48]{1,0:T(4,128)S(1)}, s32[4,48]{1,0:T(4,128)S(1)}, u32[]{:S(2)}, u32[]{:S(2)}) collective-permute-start(s32[4,48]{1,0:T(4,128)S(1)} %pad_add_fusion.4), channel_id=1, source_target_pairs={{0,4},{4,0},{8,12},{12,8},{16,20},{20,16},{24,28},{28,24},{1,5},{5... | collective-permute-start | bytes 2312 | tf_op jit(solution)/shard_map/ppermute | solution.py:180

commit v2 on v0

v2 whole, which is shorter than its diff:
```python
import functools

import jax
import jax.numpy as jnp
from jax import lax
from jax.experimental import pallas as pl
from jax.experimental.pallas import tpu as pltpu
from jax.sharding import PartitionSpec as P


HP = 4
IDX = 16


VMEM = pl.BlockSpec(memory_space=pltpu.VMEM)
SMEM = pl.BlockSpec(memory_space=pltpu.SMEM)
ANY = pl.BlockSpec(memory_space=pl.ANY)
GRANT = 20 * 1024 * 1024


class Dims:
    def __init__(self, groups, per_group, bs, bins, cycle):
        self.groups, self.per_group, self.bs = groups, per_group, bs
        self.bins, self.cycle = bins, cycle
        self.half = groups // 2 * per_group * bs
        self.rows = groups * bs
        self.slots = groups * per_group * per_group
        self.whole = cycle == 2 * HP and bins == cycle

    def at(self, j, s):
        return (j * self.per_group + s) * self.bs + (IDX if j >= self.groups // 2 else 0)


def ring_place(panel, cycle):
    return jnp.where(panel % 2 == 0, panel // 2, cycle - 1 - panel // 2)


def panel_number(dims, distance):
    me = lax.axis_index("rows").astype(jnp.int32)
    if not dims.whole:
        return (me + distance + dims.cycle) % dims.cycle
    place = (ring_place(me, dims.cycle) + distance + dims.cycle) % dims.cycle
    return jnp.where(place < dims.cycle // 2, 2 * place, 2 * (dims.cycle - 1 - place) + 1)


def first_bin(dims):
    me = lax.axis_index("rows").astype(jnp.int32)
    return (me - 2 * HP + 2 * dims.cycle) % dims.cycle


def stretch(tile, rows):
    return jnp.concatenate([tile] * (rows // 16), axis=0)


def prep_kernel(dims, blocks_ref, cols_ref, full_ref, a_ref, b_ref):
    me = lax.axis_index("cols").astype(jnp.int32)
    bs = dims.bs
    lane = lax.broadcasted_iota(jnp.int32, (IDX, 128), 1)
    row = jnp.zeros((IDX, 128), jnp.int32)
    for j in range(dims.groups):
        for s in range(dims.per_group):
            value = blocks_ref[me ^ j, 0, s]
            at = dims.at(j, s)
            full_ref[at : at + bs, :] = value
            if at < dims.half:
                a_ref[at : at + bs, :] = value
            else:
                at -= dims.half + IDX
                b_ref[at : at + bs, :] = value
            row = jnp.where(lane == j * dims.per_group + s, cols_ref[me ^ j, 0, s] // dims.groups, row)
    numbers = row.astype(jnp.float32).astype(jnp.bfloat16)
    full_ref[dims.half : dims.half + IDX, :] = numbers
    a_ref[dims.half : dims.half + IDX, :] = numbers


def accumulate(dims, pieces, left, lp_ref, d_ref, emit):
    groups, per_group, bs, bins = dims.groups, dims.per_group, dims.bs, dims.bins
    depth = dims.rows
    lrows = [ref[dims.half : dims.half + 16, :].astype(jnp.float32)[0:1, :] for ref in left]
    for n, (distance, _, _) in enumerate(pieces):
        number = panel_number(dims, distance).astype(jnp.float32)
        for j in range(groups):
            hits = jnp.where(lrows[j] == number, 1.0, 0.0)
            for m in range(groups):
                total = None
                for t in range(per_group):
                    at = dims.at(m ^ j, t)
                    lane = (m ^ j) * per_group + t
                    hit = jnp.broadcast_to(hits[:, lane : lane + 1], (16, 128)).astype(jnp.bfloat16)
                    term = left[j][at : at + bs, :] * stretch(hit, bs)
                    total = term if total is None else total + term
                lp_ref[m * bs : (m + 1) * bs, n * depth + j * bs : n * depth + (j + 1) * bs] = total
    rows_of = []
    for _, ref, _ in pieces:
        row = ref[dims.half : dims.half + 16, :].astype(jnp.float32)[0:1, :]
        if dims.bins < dims.cycle:
            row = row - first_bin(dims).astype(jnp.float32)
            row = jnp.where(row < 0, row + float(dims.cycle), row)
        rows_of.append(row)
    for first in range(0, bins, 2):
        chunk = range(first, min(first + 2, bins))
        for n, (_, a_ref, b_ref) in enumerate(pieces):
            for b in chunk:
                hits = jnp.where(rows_of[n] == float(b), 1.0, 0.0)
                for j in range(groups):
                    total = None
                    for s in range(per_group):
                        ref, start = a_ref, dims.at(j, s)
                        if b_ref is not None and j >= groups // 2:
                            ref, start = b_ref, start - dims.half - IDX
                        lane = j * per_group + s
                        hit = jnp.broadcast_to(hits[:, lane : lane + 1], (16, 128)).astype(jnp.bfloat16)
                        term = ref[start : start + bs, :] * stretch(hit, bs)
                        total = term if total is None else total + term
                    d_ref[
                        n * depth + j * bs : n * depth + (j + 1) * bs, b * bs : (b + 1) * bs
                    ] = total
        lo, hi = first * bs, (first + len(chunk)) * bs
        emit(lo, hi, jnp.dot(lp_ref[...], d_ref[:, lo:hi], preferred_element_type=jnp.float32))


def take(refs, count):
    return [refs.pop(0) for _ in range(count)]


def take_pieces(refs, layout):
    pieces = []
    for distance, two in layout:
        pieces.append((distance, refs.pop(0), refs.pop(0) if two else None))
    return pieces


def step_kernel(dims, layout, with_acc, with_zero, *refs):
    refs = list(refs)
    left = take(refs, dims.groups)
    pieces = take_pieces(refs, layout)
    acc_ref = refs.pop(0) if with_acc else None
    out_ref = refs.pop(0)
    zero_ref = refs.pop(0) if with_zero else None
    lp_ref, d_ref = take(refs, 2)
    copies = []
    if with_zero:
        blank_ref, sems = refs
        blank_ref[...] = jnp.zeros_like(blank_ref)
        for i in range(zero_ref.shape[0]):
            copy = pltpu.make_async_copy(
                blank_ref, zero_ref.at[i, dims.bins : dims.slots], sems.at[i]
            )
            copy.start()
            copies.append(copy)

    def emit(lo, hi, value):
        out_ref[:, lo:hi] = value if acc_ref is None else acc_ref[:, lo:hi] + value

    accumulate(dims, pieces, left, lp_ref, d_ref, emit)
    for copy in copies:
        copy.wait()


def last_kernel(dims, layout, *refs):
    refs = list(refs)
    left = take(refs, dims.groups)
    pieces = take_pieces(refs, layout)
    acc_ref, slot_ref, _, out_ref, lp_ref, d_ref, stage_ref, sems = refs
    groups, bs, bins = dims.groups, dims.bs, dims.bins
    me = lax.axis_index("cols").astype(jnp.int32)
    copies = []

    def emit(lo, hi, value):
        value = (acc_ref[:, lo:hi] + value).astype(jnp.bfloat16)
        for b in range(lo // bs, hi // bs):
            for m in range(groups):
                k = m * bins + b
                at = b * bs - lo
                stage_ref[k] = value[m * bs : (m + 1) * bs, at : at + bs]
                copy = pltpu.make_async_copy(
                    stage_ref.at[k], out_ref.at[m ^ me, slot_ref[k]], sems.at[k]
                )
                copy.start()
                copies.append(copy)

    accumulate(dims, pieces, left, lp_ref, d_ref, emit)
    for copy in copies:
        copy.wait()


def index_kernel(dims, known_ref, slot_ref, cols_ref, start_ref, mask_ref, count_ref):
    groups, per_group, bins, cycle = dims.groups, dims.per_group, dims.bins, dims.cycle
    p = lax.axis_index("rows").astype(jnp.int32)
    c = lax.axis_index("cols").astype(jnp.int32)
    places = hyper_places(cycle)
    for n in range(cycle):
        for r in range(groups):
            bits = jnp.int32(0)
            for s in range(per_group):
                bits = bits | (jnp.int32(1) << known_ref[n * groups, r * per_group + s])
            mask_ref[(p ^ places[n]) * groups + r] = bits
    earlier = jnp.int32(0)
    for n in range(cycle):
        total = jnp.int32(0)
        for m in range(groups):
            bits = jnp.int32(0)
            for j in range(groups):
                for t in range(per_group):
                    k = known_ref[n * groups + j, (m ^ j) * per_group + t]
                    bits = bits | mask_ref[k * groups + j]
            count = jnp.int32(0)
            for b in range(bins):
                count = count + ((bits >> b) & 1)
            total = total + count
            if n == 0:
                count_ref[m ^ c] = count
                used = jnp.int32(0)
                for b in range(bins):
                    one = (bits >> b) & 1
                    slot = jnp.where(one == 1, used, count + b - used)
                    slot_ref[m * bins + b] = slot
                    cols_ref[m ^ c, 0, slot] = jnp.where(one == 1, b * groups + c, -1)
                    used = used + one
        if n > 0:
            earlier = earlier + jnp.where((p ^ places[n]) < p, total, 0)
    for i in range(groups):
        start_ref[i, 0] = earlier
        earlier = earlier + count_ref[i]
        for o in range(bins, dims.slots):
            cols_ref[i, 0, o] = -1


def hyper_bits(cycle):
    bits, bit = [], cycle // 2
    while bit:
        bits.append(bit)
        bit //= 2
    return bits


def hyper_places(cycle):
    places = [0]
    for bit in hyper_bits(cycle):
        places = places + [v ^ bit for v in places]
    return places


def flat(panels):
    layout = [(distance, second is not None) for distance, _, second in panels]
    arrays = [x for _, first, second in panels for x in (first, second) if x is not None]
    return layout, arrays


def scratch_of(dims, panels):
    depth = dims.rows * len(panels)
    return [
        pltpu.VMEM((dims.rows, depth), jnp.bfloat16),
        pltpu.VMEM((depth, dims.bins * dims.bs), jnp.bfloat16),
    ]


def cost_of(dims, panels):
    flops = 2 * dims.rows * dims.rows * len(panels) * dims.bins * dims.bs
    return pl.CostEstimate(flops=flops, bytes_accessed=4_000_000, transcendentals=0)


def call_step(dims, left, panels, acc, zero=False):
    layout, arrays = flat(panels)
    args = [*left, *arrays]
    aliases = {}
    if acc is not None:
        aliases = {len(args): 0}
        args.append(acc)
    shapes = [jax.ShapeDtypeStruct((dims.rows, dims.bins * dims.bs), jnp.float32)]
    specs = [VMEM]
    scratch = scratch_of(dims, panels)
    if zero:
        shapes.append(
            jax.ShapeDtypeStruct((dims.groups, dims.slots, dims.bs, dims.bs), jnp.bfloat16)
        )
        specs.append(ANY)
        scratch += [
            pltpu.VMEM((dims.slots - dims.bins, dims.bs, dims.bs), jnp.bfloat16),
            pltpu.SemaphoreType.DMA((dims.groups,)),
        ]
    return pl.pallas_call(
        functools.partial(step_kernel, dims, layout, acc is not None, zero),
        out_shape=shapes,
        in_specs=[VMEM] * len(args),
        out_specs=specs,
        scratch_shapes=scratch,
        input_output_aliases=aliases,
        compiler_params=pltpu.CompilerParams(vmem_limit_bytes=GRANT),
        cost_estimate=cost_of(dims, panels),
    )(*args)


def call_last(dims, left, panels, acc, slots, empty):
    layout, arrays = flat(panels)
    args = [*left, *arrays, acc, slots, empty]
    return pl.pallas_call(
        functools.partial(last_kernel, dims, layout),
        out_shape=jax.ShapeDtypeStruct(empty.shape, empty.dtype),
        in_specs=[VMEM] * (len(args) - 2) + [SMEM, ANY],
        out_specs=ANY,
        scratch_shapes=scratch_of(dims, panels)
        + [
            pltpu.VMEM((dims.groups * dims.bins, dims.bs, dims.bs), jnp.bfloat16),
            pltpu.SemaphoreType.DMA((dims.groups * dims.bins,)),
        ],
        input_output_aliases={len(args) - 1: 0},
        compiler_params=pltpu.CompilerParams(vmem_limit_bytes=GRANT),
        cost_estimate=cost_of(dims, panels),
    )(*args)


def xor_move(value, axis, bit):
    return lax.ppermute(value, axis, [(i, i ^ bit) for i in range(lax.axis_size(axis))])


def shifted(value, axis, distance):
    size = lax.axis_size(axis)
    return lax.ppermute(value, axis, [((i - distance) % size, i) for i in range(size)])


def ring_moves(cycle):
    ring = [2 * k for k in range(cycle // 2)] + [2 * k + 1 for k in reversed(range(cycle // 2))]
    up = [(ring[k], ring[(k + 1) % cycle]) for k in range(cycle)]
    return up, [(b, a) for a, b in up]


def one_of(values, wanted):
    return jnp.any(values[..., None] == wanted, axis=-2)


def window_index(dims, left, window):
    groups, per_group, bins, cycle = dims.groups, dims.per_group, dims.bins, dims.cycle
    p = lax.axis_index("rows").astype(jnp.int32)
    c = lax.axis_index("cols").astype(jnp.int32)
    lanes = jnp.arange(groups, dtype=jnp.int32)

    def numbers_of(array):
        numbers = array[dims.half, : groups * per_group].astype(jnp.int32)
        return numbers.reshape(groups, per_group)

    held = jnp.stack(
        [numbers_of(left[j])[jnp.array([m ^ j for m in range(groups)])] for j in range(groups)], axis=1
    )
    lrel = (held - (p - HP)) % cycle
    zero = (p - 2 * HP) % cycle if bins < cycle else jnp.int32(0)
    bin_ids = jnp.arange(bins, dtype=jnp.int32)
    bin_abs = (zero + bin_ids) % cycle
    has = jnp.stack([one_of((numbers_of(w) - zero) % cycle, bin_ids) for w in window])
    uses = one_of(lrel, jnp.arange(2 * HP, dtype=jnp.int32))
    hits = jnp.any(uses.transpose(0, 2, 1)[..., None] & has[None], axis=(1, 2))
    counts = jnp.sum(hits.astype(jnp.int32), axis=-1)
    all_totals = lax.all_gather(jnp.sum(counts).reshape(1), "rows", axis=0, tiled=True)
    earlier = jnp.sum(jnp.where(jnp.arange(cycle, dtype=jnp.int32) < p, all_totals, 0))
    lower = bin_abs[:, None] < bin_abs[None, :]
    rank_in = jnp.sum((hits[:, :, None] & lower[None]).astype(jnp.int32), axis=1)
    rank_out = jnp.sum((~hits[:, :, None] & lower[None]).astype(jnp.int32), axis=1)
    slots = jnp.where(hits, rank_in, counts[:, None] + rank_out)
    at_slot = hits[:, None, :] & (slots[:, None, :] == jnp.arange(dims.slots, dtype=jnp.int32)[:, None])
    columns = jnp.sum(jnp.where(at_slot, bin_abs * groups + c + 1, 0), axis=-1) - 1
    pick = (lanes[:, None] ^ c) == lanes[None, :]
    columns = jnp.sum(jnp.where(pick[:, :, None], columns[None], 0), axis=1)
    before = (lanes[None, :] ^ c) < lanes[:, None]
    starts = earlier + jnp.sum(jnp.where(before, counts[None, :], 0), axis=1)
    return slots.reshape(-1), columns[:, None].astype(jnp.int32), starts[:, None].astype(jnp.int32)


def on_device(blocks, block_cols):
    panel_rows, _, per_group, bs, _ = blocks.shape
    groups = lax.axis_size("cols")
    cycle = lax.axis_size("rows")
    if groups != 4 or panel_rows != groups or cycle > 256 or cycle < 2 * HP:
        raise ValueError("unsupported sizes")
    dims = Dims(groups, per_group, bs, min(cycle, 4 * HP - 1), cycle)

    def payload(rows):
        return jax.ShapeDtypeStruct((rows, bs), jnp.bfloat16)

    own, own_a, own_b = pl.pallas_call(
        functools.partial(prep_kernel, dims),
        out_shape=[payload(2 * dims.half + IDX), payload(dims.half + IDX), payload(dims.half)],
        in_specs=[VMEM, SMEM],
        out_specs=[VMEM] * 3,
        compiler_params=pltpu.CompilerParams(vmem_limit_bytes=GRANT),
        name="prep",
    )(blocks, block_cols)

    if dims.whole:
        up, down = ring_moves(cycle)
        pa, pb, qa, qb = [own_a], [own_b], [own_a], [own_b]
        for k in range(1, HP + 1):
            pa.append(lax.ppermute(pa[-1], "rows", up))
            qb.append(lax.ppermute(qb[-1], "rows", down))
            if k < HP:
                pb.append(lax.ppermute(pb[-1], "rows", up))
                qa.append(lax.ppermute(qa[-1], "rows", down))
    else:
        window = [own if k == 0 else shifted(own, "rows", -k) for k in range(-HP, HP)]
    left1 = xor_move(own, "cols", 1)
    left2 = xor_move(own, "cols", 2)
    left3 = xor_move(left2, "cols", 1)
    left = [own, left1, left2, left3]

    if dims.whole:
        known = jnp.concatenate([x[dims.half : dims.half + 1] for x in left], axis=0)
        for bit in hyper_bits(cycle):
            known = jnp.concatenate([known, xor_move(known, "rows", bit)], axis=0)
        known = known[:, : groups * per_group].astype(jnp.int32)
        slots, columns, starts = pl.pallas_call(
            functools.partial(index_kernel, dims),
            out_shape=[
                jax.ShapeDtypeStruct((groups * dims.bins,), jnp.int32),
                jax.ShapeDtypeStruct((groups, 1, dims.slots), jnp.int32),
                jax.ShapeDtypeStruct((groups, 1), jnp.int32),
            ],
            in_specs=[SMEM],
            out_specs=[SMEM] * 3,
            scratch_shapes=[
                pltpu.SMEM((cycle * groups,), jnp.int32),
                pltpu.SMEM((groups,), jnp.int32),
            ],
            compiler_params=pltpu.CompilerParams(vmem_limit_bytes=GRANT),
            name="index",
        )(known)
        acc, empty = call_step(dims, left, [(0, own, None)], None, zero=True)
        for k in range(1, HP):
            panels = [(-k, pa[k], pb[k]), (k, qa[k], qb[k])]
            acc = call_step(dims, left, panels, acc)[0]
        final = [(HP, pa[HP], qb[HP])]
    else:
        slots, columns, starts = window_index(dims, left, window)
        acc, empty = call_step(dims, left, [(0, own, None)], None, zero=True)
        pairs = [(k, window[k + HP], None) for k in range(-HP, HP) if k]
        for k in range(0, len(pairs) - 1, 2):
            acc = call_step(dims, left, pairs[k : k + 2], acc)[0]
        final = pairs[-1:]
    out = call_last(dims, left, final, acc, slots, empty)
    return out[:, None], columns, starts


def solution(mesh):
    in_specs = (P("rows", "cols", None, None, None), P("rows", "cols", None))
    out_specs = (P("rows", "cols", None, None, None), P("rows", "cols", None), P("rows", "cols"))

    return jax.shard_map(on_device, mesh=mesh, in_specs=in_specs, out_specs=out_specs, check_vma=False)
```

time: 153 us -> 71.1 us (0.46)
  blocking collectives: 44.6 us -> 0 us
  local copies, waits for them, and re-layouts: 30.8 us -> 8.04 us
  Pallas kernels: 0 us -> 19.9 us
  matrix products: 17.5 us -> 0 us
  between operations: 14.2 us -> 0.75 us
  waiting for transfers between devices: 6.14 us -> 17.5 us
  starting transfers between devices: 34.1 us -> 24.4 us
  other arithmetic: 5.23 us -> 0.02 us
    unnamed x1 -> x0, blocking collectives: 39.4 us -> none
    pallas_call x0 -> x7, Pallas kernels: none -> 19.9 us  [the longest x4 13.4 us: call_step(): pl.pallas_call(functools.partial(step_kernel, dims, layout, acc is not No...]
    dot_general x2 -> x0, matrix products: 17.5 us -> none  [the longest x1 9.58 us: on_device(): jnp.einsum('poq,pqac->poac', onehot, products.reshape(panel_rows, row_slo...]
    reshape x3 -> x0, local copies, waits for them, and re-layouts: 12.2 us -> none  [the longest x1 12 us: on_device(): products.reshape(panel_rows, row_slots * per_group, block_size, block_size)]
    ppermute x14 -> x20, waiting for transfers between devices: 6.13 us -> 17.5 us  [the longest x3 7.8 us: on_device(): pb.append(lax.ppermute(pb[-1], 'rows', up))]
    ppermute x14 -> x20, starting transfers between devices: 34.1 us -> 24.4 us  [the longest x6 9.12 us: xor_move(): lax.ppermute(value, axis, [(i, i ^ bit) for i in range(lax.axis_size(axis...]
    all_gather x1 -> x0, blocking collectives: 5.19 us -> none  [on_device(): lax.all_gather(block_cols, 'cols', axis=1, tiled=True)]
    unnamed x18 -> x20, local copies, waits for them, and re-layouts: 12.7 us -> 7.9 us
  transfers between devices with their start and end apart: 15 -> 20, of which waited for: 1 -> 5; matrix products, arithmetic and copies ran while one was open for 12% -> 1% of each run, Pallas kernels for 0% -> 22%
where the time goes in v2:
time: 71.1 us; the launch traced here: 70.7 us
  starting transfers between devices  24.4 us (34%)
  Pallas kernels  19.9 us (28%)
  waiting for transfers between devices  17.5 us (25%)
  local copies, waits for them, and re-layouts  8.04 us (11%)
  between operations  0.75 us (1%)
    pallas_call x4, Pallas kernels, call_step(): pl.pallas_call(functools.partial(step_kernel, dims, layout, acc is not No...  13.4 us
    ppermute x6, starting transfers between devices, xor_move(): lax.ppermute(value, axis, [(i, i ^ bit) for i in range(lax.axis_size(axis...  9.12 us
    unnamed x20, local copies, waits for them, and re-layouts  7.9 us
    ppermute x3, waiting for transfers between devices, on_device(): pb.append(lax.ppermute(pb[-1], 'rows', up))  7.8 us
    ppermute x4, starting transfers between devices, on_device(): pa.append(lax.ppermute(pa[-1], 'rows', up))  4.17 us
    ppermute x4, starting transfers between devices, on_device(): qb.append(lax.ppermute(qb[-1], 'rows', down))  3.94 us
    ppermute x4, waiting for transfers between devices, on_device(): pa.append(lax.ppermute(pa[-1], 'rows', up))  3.81 us
    ppermute x3, starting transfers between devices, on_device(): pb.append(lax.ppermute(pb[-1], 'rows', up))  3.66 us
  transfers between devices with their start and end apart: 20, of which 5 were waited for; matrix products, arithmetic and copies ran while one was open for 1% of the time, Pallas kernels for 22%

profile of v2, /device:TPU:0, one launch (start us, length us, event | category | flops | bytes accessed | tf_op | source)
XLA Modules:
  0.0 70.7 jit_solution(10561081714613149664)
XLA Ops:
  0.6 0.8 %copy.9.cols_ref = s32[4,1,3]{2,1,0:T(1,128)S(1)} copy(s32[4,1,3]{0,1,2:T(1,128)} %param.3) | data formatting | bytes 96 | tf_op args[1]
  1.4 1.0 %copy-done.4 = bf16[4,1,3,128,128]{4,3,2,1,0:T(8,128)(2,1)S(1)} copy-done((bf16[4,1,3,128,128]{4,3,2,1,0:T(8,128)(2,1)S(1)}, bf16[4,1,3,128,128]{4,3,2,1,0:T(8,128)(2,1)}, u32[]{:S(2)}) %copy-start.4) | copy-done | bytes 393240
  2.4 0.7 %prep.1 = (bf16[1552,128]{1,0:T(8,128)(2,1)S(1)}, bf16[784,128]{1,0:T(8,128)(2,1)S(1)}, bf16[768,128]{1,0:T(8,128)(2,1)S(1)}) custom-call(bf16[4,1,3,128,128]{4,3,2,1,0:T(8,128)(2,1)S(1)} %copy-done.4, s32[4,1,3]{2,1,0:T(1,128)S(1)} %copy.9.cols_ref), custom_call_target="tpu_custom_call" | custom-call | tf_op jit(solution)/shard_map/prep/pallas_call | solution.py:379
  3.1 3.0 %collective-permute-start.1 = (bf16[1552,128]{1,0:T(8,128)(2,1)S(1)}, bf16[1552,128]{1,0:T(8,128)(2,1)S(1)}, u32[]{:S(2)}, u32[]{:S(2)}) collective-permute-start(bf16[1552,128]{1,0:T(8,128)(2,1)S(1)} %get-tuple-element.11.refs_0_.refs_4_), channel_id=1, source_target_pairs={{0,2},{1,3},{2,0},{3,1},{4,6},{5,7},{6,4},{7,5},{8,10},{9,11},{10,... | collective-permute-start | bytes 1191944 | tf_op jit(solution)/shard_map/ppermute | solution.py:314
  6.2 1.6 %collective-permute-start.3 = (bf16[784,128]{1,0:T(8,128)(2,1)S(1)}, bf16[784,128]{1,0:T(8,128)(2,1)S(1)}, u32[]{:S(2)}, u32[]{:S(2)}) collective-permute-start(bf16[784,128]{1,0:T(8,128)(2,1)S(1)} %get-tuple-element.12), channel_id=1, source_target_pairs={{0,8},{8,16},{16,24},{24,28},{28,20},{20,12},{12,4},{4,0},{1,9},{9... | collective-permute-start | bytes 602120 | tf_op jit(solution)/shard_map/ppermute | solution.py:392
  7.7 1.6 %collective-permute-start.11 = (bf16[768,128]{1,0:T(8,128)(2,1)S(1)}, bf16[768,128]{1,0:T(8,128)(2,1)S(1)}, u32[]{:S(2)}, u32[]{:S(2)}) collective-permute-start(bf16[768,128]{1,0:T(8,128)(2,1)S(1)} %get-tuple-element.13), channel_id=1, source_target_pairs={{0,8},{8,16},{16,24},{24,28},{28,20},{20,12},{12,4},{4,0},{1,9},{9... | collective-permute-start | bytes 589832 | tf_op jit(solution)/shard_map/ppermute | solution.py:395
  9.3 0.4 collective-permute-start.7
  9.8 0.4 collective-permute-start.14
  10.2 3.8 %collective-permute-done.3.refs_4_ = bf16[784,128]{1,0:T(8,128)(2,1)S(1)} collective-permute-done((bf16[784,128]{1,0:T(8,128)(2,1)S(1)}, bf16[784,128]{1,0:T(8,128)(2,1)S(1)}, u32[]{:S(2)}, u32[]{:S(2)}) %collective-permute-start.3) | collective-permute-done | bytes 200736 | tf_op jit(solution)/shard_map/ppermute | solution.py:392
  14.0 1.6 %collective-permute-start.4 = (bf16[784,128]{1,0:T(8,128)(2,1)S(1)}, bf16[784,128]{1,0:T(8,128)(2,1)S(1)}, u32[]{:S(2)}, u32[]{:S(2)}) collective-permute-start(bf16[784,128]{1,0:T(8,128)(2,1)S(1)} %collective-permute-done.3.refs_4_), channel_id=1, source_target_pairs={{0,8},{8,16},{16,24},{24,28},{28,20},{20,12},{12,4},{4,0},{1,9},{9... | collective-permute-start | bytes 602120 | tf_op jit(solution)/shard_map/ppermute | solution.py:392
  15.6 2.6 %collective-permute-done.11.refs_5_ = bf16[768,128]{1,0:T(8,128)(2,1)S(1)} collective-permute-done((bf16[768,128]{1,0:T(8,128)(2,1)S(1)}, bf16[768,128]{1,0:T(8,128)(2,1)S(1)}, u32[]{:S(2)}, u32[]{:S(2)}) %collective-permute-start.11) | collective-permute-done | bytes 196640 | tf_op jit(solution)/shard_map/ppermute | solution.py:395
  18.2 1.6 %collective-permute-start.12 = (bf16[768,128]{1,0:T(8,128)(2,1)S(1)}, bf16[768,128]{1,0:T(8,128)(2,1)}, u32[]{:S(2)}, u32[]{:S(2)}) collective-permute-start(bf16[768,128]{1,0:T(8,128)(2,1)S(1)} %collective-permute-done.11.refs_5_), channel_id=1, source_target_pairs={{0,8},{8,16},{16,24},{24,28},{28,20},{20,12},{12,4},{4,0},{1,9},{9... | collective-permute-start | bytes 589832 | tf_op jit(solution)/shard_map/ppermute | solution.py:395
  19.8 0.2 collective-permute-start.2
  20.1 0.5 collective-permute-start.8
  20.5 5.2 %collective-permute-done.12.refs_5_ = bf16[768,128]{1,0:T(8,128)(2,1)} collective-permute-done((bf16[768,128]{1,0:T(8,128)(2,1)S(1)}, bf16[768,128]{1,0:T(8,128)(2,1)}, u32[]{:S(2)}, u32[]{:S(2)}) %collective-permute-start.12) | collective-permute-done | bytes 196640 | tf_op jit(solution)/shard_map/ppermute | solution.py:395
  25.7 1.5 %collective-permute-start.15 = (bf16[784,128]{1,0:T(8,128)(2,1)S(1)}, bf16[784,128]{1,0:T(8,128)(2,1)}, u32[]{:S(2)}, u32[]{:S(2)}) collective-permute-start(bf16[784,128]{1,0:T(8,128)(2,1)S(1)} %collective-permute-done.14.refs_6_), channel_id=1, source_target_pairs={{8,0},{16,8},{24,16},{28,24},{20,28},{12,20},{4,12},{0,4},{9,1},{1... | collective-permute-start | bytes 602120 | tf_op jit(solution)/shard_map/ppermute | solution.py:396
  27.2 0.5 collective-permute-start.5
  27.7 0.7 copy-done.5
  28.4 0.0 collective-permute-done.8.refs_7_
  28.4 1.5 %collective-permute-start.9 = (bf16[768,128]{1,0:T(8,128)(2,1)S(1)}, bf16[768,128]{1,0:T(8,128)(2,1)}, u32[]{:S(2)}, u32[]{:S(2)}) collective-permute-start(bf16[768,128]{1,0:T(8,128)(2,1)S(1)} %collective-permute-done.8.refs_7_), channel_id=1, source_target_pairs={{8,0},{16,8},{24,16},{28,24},{20,28},{12,20},{4,12},{0,4},{9,1},{1... | collective-permute-start | bytes 589832 | tf_op jit(solution)/shard_map/ppermute | solution.py:393
  29.9 0.0 collective-permute-done.refs_1_
  29.9 0.5 collective-permute-start.13
  30.4 3.2 %collective-permute-done.15.refs_6_ = bf16[784,128]{1,0:T(8,128)(2,1)} collective-permute-done((bf16[784,128]{1,0:T(8,128)(2,1)S(1)}, bf16[784,128]{1,0:T(8,128)(2,1)}, u32[]{:S(2)}, u32[]{:S(2)}) %collective-permute-start.15) | collective-permute-done | bytes 200736 | tf_op jit(solution)/shard_map/ppermute | solution.py:396
  33.6 1.5 %collective-permute-start.16 = (bf16[784,128]{1,0:T(8,128)(2,1)}, bf16[784,128]{1,0:T(8,128)(2,1)}, u32[]{:S(2)}, u32[]{:S(2)}) collective-permute-start(bf16[784,128]{1,0:T(8,128)(2,1)} %collective-permute-done.15.refs_6_), channel_id=1, source_target_pairs={{8,0},{16,8},{24,16},{28,24},{20,28},{12,20},{4,12},{0,4},{9,1},{1... | collective-permute-start | bytes 602120 | tf_op jit(solution)/shard_map/ppermute | solution.py:396
  35.2 2.7 %collective-permute-done.9.refs_7_ = bf16[768,128]{1,0:T(8,128)(2,1)} collective-permute-done((bf16[768,128]{1,0:T(8,128)(2,1)S(1)}, bf16[768,128]{1,0:T(8,128)(2,1)}, u32[]{:S(2)}, u32[]{:S(2)}) %collective-permute-start.9) | collective-permute-done | bytes 196640 | tf_op jit(solution)/shard_map/ppermute | solution.py:393
  37.8 1.5 %collective-permute-start.10 = (bf16[768,128]{1,0:T(8,128)(2,1)}, bf16[768,128]{1,0:T(8,128)(2,1)}, u32[]{:S(2)}, u32[]{:S(2)}) collective-permute-start(bf16[768,128]{1,0:T(8,128)(2,1)} %collective-permute-done.9.refs_7_), channel_id=1, source_target_pairs={{8,0},{16,8},{24,16},{28,24},{20,28},{12,20},{4,12},{0,4},{9,1},{1... | collective-permute-start | bytes 589832 | tf_op jit(solution)/shard_map/ppermute | solution.py:393
  39.4 0.0 collective-permute-done.5.refs_4_
  39.4 0.5 collective-permute-start.6
  39.9 2.7 %collective-permute-start.17 = (bf16[4,128]{1,0:T(4,128)(2,1)S(1)}, bf16[4,128]{1,0:T(4,128)(2,1)S(1)}, u32[]{:S(2)}, u32[]{:S(2)}) collective-permute-start(bf16[4,128]{1,0:T(4,128)(2,1)S(1)} %pad_maximum_fusion), channel_id=1, source_target_pairs={{0,16},{4,20},{8,24},{12,28},{16,0},{20,4},{24,8},{28,12},{1,17},{... | collective-permute-start | bytes 3080 | tf_op jit(solution)/shard_map/ppermute | solution.py:314
  42.6 3.2 %shard_map.49 = (f32[512,1024]{1,0:T(8,128)S(1)}, bf16[4,36,128,128]{3,2,1,0:T(8,128)(2,1)}) custom-call(bf16[1552,128]{1,0:T(8,128)(2,1)S(1)} %get-tuple-element.11.refs_0_.refs_4_, bf16[1552,128]{1,0:T(8,128)(2,1)S(1)} %collective-permute-done.refs_1_, bf16[1552,128]{1,0:T(8,128)(2,1)S(1)} %collective-permute-done.1.refs_2_, ...), custom_call_target="tpu_custom_call" | custom-call | flops 536870912 | bytes 4000000 | tf_op jit(solution)/shard_map/pallas_call | solution.py:282
  45.8 2.7 %shard_map.50.refs_8_ = f32[512,1024]{1,0:T(8,128)S(1)} custom-call(bf16[1552,128]{1,0:T(8,128)(2,1)S(1)} %get-tuple-element.11.refs_0_.refs_4_, bf16[1552,128]{1,0:T(8,128)(2,1)S(1)} %collective-permute-done.refs_1_, bf16[1552,128]{1,0:T(8,128)(2,1)S(1)} %collective-permute-done.1.refs_2_, ...), custom_call_target="tpu_custom_call", output_to_operand_aliasing={{}: (8, {})} | custom-call | flops 1073741824 | bytes 4000000 | tf_op jit(solution)/shard_map/pallas_call | solution.py:282
  48.5 0.0 collective-permute-done.17
  48.5 1.6 %collective-permute-start.18 = (bf16[8,128]{1,0:T(8,128)(2,1)S(1)}, bf16[8,128]{1,0:T(8,128)(2,1)S(1)}, u32[]{:S(2)}, u32[]{:S(2)}) collective-permute-start(bf16[8,128]{1,0:T(8,128)(2,1)S(1)} %concatenate.16), channel_id=1, source_target_pairs={{0,8},{4,12},{8,0},{12,4},{16,24},{20,28},{24,16},{28,20},{1,9},{5... | collective-permute-start | bytes 6152 | tf_op jit(solution)/shard_map/ppermute | solution.py:314
  50.2 1.0 %copy-done.1 = bf16[1552,128]{1,0:T(8,128)(2,1)S(1)} copy-done((bf16[1552,128]{1,0:T(8,128)(2,1)S(1)}, bf16[1552,128]{1,0:T(8,128)(2,1)}, u32[]{:S(2)}) %copy-start.1) | copy-done | bytes 397336
  51.2 0.9 %copy-done.6 = bf16[784,128]{1,0:T(8,128)(2,1)S(1)} copy-done((bf16[784,128]{1,0:T(8,128)(2,1)S(1)}, bf16[784,128]{1,0:T(8,128)(2,1)}, u32[]{:S(2)}) %copy-start.6) | copy-done | bytes 200728
  52.1 0.9 %copy-done.8 = bf16[768,128]{1,0:T(8,128)(2,1)S(1)} copy-done((bf16[768,128]{1,0:T(8,128)(2,1)S(1)}, bf16[768,128]{1,0:T(8,128)(2,1)}, u32[]{:S(2)}) %copy-start.8) | copy-done | bytes 196632
  53.0 3.7 %shard_map.51.refs_8_ = f32[512,1024]{1,0:T(8,128)S(1)} custom-call(bf16[1552,128]{1,0:T(8,128)(2,1)S(1)} %get-tuple-element.11.refs_0_.refs_4_, bf16[1552,128]{1,0:T(8,128)(2,1)S(1)} %collective-permute-done.refs_1_, bf16[1552,128]{1,0:T(8,128)(2,1)S(1)} %collective-permute-done.1.refs_2_, ...), custom_call_target="tpu_custom_call", output_to_operand_aliasing={{}: (8, {})} | custom-call | flops 1073741824 | bytes 4000000 | tf_op jit(solution)/shard_map/pallas_call | solution.py:282
  56.8 1.6 %collective-permute-start.19 = (bf16[16,128]{1,0:T(8,128)(2,1)S(1)}, bf16[16,128]{1,0:T(8,128)(2,1)S(1)}, u32[]{:S(2)}, u32[]{:S(2)}) collective-permute-start(bf16[16,128]{1,0:T(8,128)(2,1)S(1)} %concatenate.17), channel_id=1, source_target_pairs={{0,4},{4,0},{8,12},{12,8},{16,20},{20,16},{24,28},{28,24},{1,5},{5... | collective-permute-start | bytes 12296 | tf_op jit(solution)/shard_map/ppermute | solution.py:314
  58.3 0.0 collective-permute-done.13.refs_5_
  58.4 0.0 collective-permute-done.16.refs_6_
  58.4 1.0 %copy-done.2 = bf16[1552,128]{1,0:T(8,128)(2,1)S(1)} copy-done((bf16[1552,128]{1,0:T(8,128)(2,1)S(1)}, bf16[1552,128]{1,0:T(8,128)(2,1)}, u32[]{:S(2)}) %copy-start.2) | copy-done | bytes 397336
  59.4 3.8 %shard_map.52.refs_6_ = f32[512,1024]{1,0:T(8,128)S(1)} custom-call(bf16[1552,128]{1,0:T(8,128)(2,1)S(1)} %get-tuple-element.11.refs_0_.refs_4_, bf16[1552,128]{1,0:T(8,128)(2,1)S(1)} %collective-permute-done.refs_1_, bf16[1552,128]{1,0:T(8,128)(2,1)S(1)} %collective-permute-done.1.refs_2_, ...), custom_call_target="tpu_custom_call", output_to_operand_aliasing={{}: (8, {})} | custom-call | flops 1073741824 | bytes 4000000 | tf_op jit(solution)/shard_map/pallas_call | solution.py:282
  63.1 0.0 collective-permute-done.19
  63.1 0.1 concatenate.18
  63.2 2.4 %index.1 = (s32[32]{0:T(128)S(1)}, s32[4,1,36]{2,1,0:T(1,128)}, s32[4,1]{1,0:T(4,128)S(1)}) custom-call(s32[32,12]{1,0:T(8,128)S(1)} %slice_convert_fusion.known_ref), custom_call_target="tpu_custom_call" | custom-call | tf_op jit(solution)/shard_map/index/pallas_call | solution.py:409
  65.6 0.6 copy.11
  66.2 1.0 %copy-done.3 = bf16[1552,128]{1,0:T(8,128)(2,1)S(1)} copy-done((bf16[1552,128]{1,0:T(8,128)(2,1)S(1)}, bf16[1552,128]{1,0:T(8,128)(2,1)}, u32[]{:S(2)}) %copy-start.3) | copy-done | bytes 397336
  67.2 3.4 %shard_map.53 = bf16[4,36,128,128]{3,2,1,0:T(8,128)(2,1)} custom-call(bf16[1552,128]{1,0:T(8,128)(2,1)S(1)} %get-tuple-element.11.refs_0_.refs_4_, bf16[1552,128]{1,0:T(8,128)(2,1)S(1)} %collective-permute-done.refs_1_, bf16[1552,128]{1,0:T(8,128)(2,1)S(1)} %collective-permute-done.1.refs_2_, ...), custom_call_target="tpu_custom_call", output_to_operand_aliasing={{}: (8, {})} | custom-call | flops 536870912 | bytes 4000000 | tf_op jit(solution)/shard_map/pallas_call | solution.py:297
  (28 shorter events, 0.1 us)
Async XLA Ops:
  1.4 1.0 %copy-start.4 = (bf16[4,1,3,128,128]{4,3,2,1,0:T(8,128)(2,1)S(1)}, bf16[4,1,3,128,128]{4,3,2,1,0:T(8,128)(2,1)}, u32[]{:S(2)}) copy-start(bf16[4,1,3,128,128]{4,3,2,1,0:T(8,128)(2,1)} %blocks_ref.1) | copy-start | bytes 1179652
  3.1 16.7 %collective-permute-start.1 = (bf16[1552,128]{1,0:T(8,128)(2,1)S(1)}, bf16[1552,128]{1,0:T(8,128)(2,1)S(1)}, u32[]{:S(2)}, u32[]{:S(2)}) collective-permute-start(bf16[1552,128]{1,0:T(8,128)(2,1)S(1)} %get-tuple-element.11.refs_0_.refs_4_), channel_id=1, source_target_pairs={{0,2},{1,3},{2,0},{3,1},{4,6},{5,7},{6,4},{7,5},{8,10},{9,11},{10,... | collective-permute-start | bytes 1191944 | tf_op jit(solution)/shard_map/ppermute | solution.py:314
  6.2 7.9 %collective-permute-start.3 = (bf16[784,128]{1,0:T(8,128)(2,1)S(1)}, bf16[784,128]{1,0:T(8,128)(2,1)S(1)}, u32[]{:S(2)}, u32[]{:S(2)}) collective-permute-start(bf16[784,128]{1,0:T(8,128)(2,1)S(1)} %get-tuple-element.12), channel_id=1, source_target_pairs={{0,8},{8,16},{16,24},{24,28},{28,20},{20,12},{12,4},{4,0},{1,9},{9... | collective-permute-start | bytes 602120 | tf_op jit(solution)/shard_map/ppermute | solution.py:392
  7.7 10.5 %collective-permute-start.11 = (bf16[768,128]{1,0:T(8,128)(2,1)S(1)}, bf16[768,128]{1,0:T(8,128)(2,1)S(1)}, u32[]{:S(2)}, u32[]{:S(2)}) collective-permute-start(bf16[768,128]{1,0:T(8,128)(2,1)S(1)} %get-tuple-element.13), channel_id=1, source_target_pairs={{0,8},{8,16},{16,24},{24,28},{28,20},{20,12},{12,4},{4,0},{1,9},{9... | collective-permute-start | bytes 589832 | tf_op jit(solution)/shard_map/ppermute | solution.py:395
  9.3 8.9 %collective-permute-start.7 = (bf16[768,128]{1,0:T(8,128)(2,1)S(1)}, bf16[768,128]{1,0:T(8,128)(2,1)S(1)}, u32[]{:S(2)}, u32[]{:S(2)}) collective-permute-start(bf16[768,128]{1,0:T(8,128)(2,1)S(1)} %get-tuple-element.13), channel_id=1, source_target_pairs={{8,0},{16,8},{24,16},{28,24},{20,28},{12,20},{4,12},{0,4},{9,1},{1... | collective-permute-start | bytes 589832 | tf_op jit(solution)/shard_map/ppermute | solution.py:393
  9.8 10.3 %collective-permute-start.14 = (bf16[784,128]{1,0:T(8,128)(2,1)S(1)}, bf16[784,128]{1,0:T(8,128)(2,1)S(1)}, u32[]{:S(2)}, u32[]{:S(2)}) collective-permute-start(bf16[784,128]{1,0:T(8,128)(2,1)S(1)} %get-tuple-element.12), channel_id=1, source_target_pairs={{8,0},{16,8},{24,16},{28,24},{20,28},{12,20},{4,12},{0,4},{9,1},{1... | collective-permute-start | bytes 602120 | tf_op jit(solution)/shard_map/ppermute | solution.py:396
  14.0 13.2 %collective-permute-start.4 = (bf16[784,128]{1,0:T(8,128)(2,1)S(1)}, bf16[784,128]{1,0:T(8,128)(2,1)S(1)}, u32[]{:S(2)}, u32[]{:S(2)}) collective-permute-start(bf16[784,128]{1,0:T(8,128)(2,1)S(1)} %collective-permute-done.3.refs_4_), channel_id=1, source_target_pairs={{0,8},{8,16},{16,24},{24,28},{28,20},{20,12},{12,4},{4,0},{1,9},{9... | collective-permute-start | bytes 602120 | tf_op jit(solution)/shard_map/ppermute | solution.py:392
  18.2 11.7 %collective-permute-start = (bf16[1552,128]{1,0:T(8,128)(2,1)S(1)}, bf16[1552,128]{1,0:T(8,128)(2,1)S(1)}, u32[]{:S(2)}, u32[]{:S(2)}) collective-permute-start(bf16[1552,128]{1,0:T(8,128)(2,1)S(1)} %get-tuple-element.11.refs_0_.refs_4_), channel_id=1, source_target_pairs={{0,1},{1,0},{2,3},{3,2},{4,5},{5,4},{6,7},{7,6},{8,9},{9,8},{10,11... | collective-permute-start | bytes 1191944 | tf_op jit(solution)/shard_map/ppermute | solution.py:314
  18.2 7.4 %collective-permute-start.12 = (bf16[768,128]{1,0:T(8,128)(2,1)S(1)}, bf16[768,128]{1,0:T(8,128)(2,1)}, u32[]{:S(2)}, u32[]{:S(2)}) collective-permute-start(bf16[768,128]{1,0:T(8,128)(2,1)S(1)} %collective-permute-done.11.refs_5_), channel_id=1, source_target_pairs={{0,8},{8,16},{16,24},{24,28},{28,20},{20,12},{12,4},{4,0},{1,9},{9... | collective-permute-start | bytes 589832 | tf_op jit(solution)/shard_map/ppermute | solution.py:395
  19.8 20.1 %collective-permute-start.2 = (bf16[1552,128]{1,0:T(8,128)(2,1)S(1)}, bf16[1552,128]{1,0:T(8,128)(2,1)S(1)}, u32[]{:S(2)}, u32[]{:S(2)}) collective-permute-start(bf16[1552,128]{1,0:T(8,128)(2,1)S(1)} %collective-permute-done.1.refs_2_), channel_id=1, source_target_pairs={{0,1},{1,0},{2,3},{3,2},{4,5},{5,4},{6,7},{7,6},{8,9},{9,8},{10,11... | collective-permute-start | bytes 1191944 | tf_op jit(solution)/shard_map/ppermute | solution.py:314
  20.1 8.3 %collective-permute-start.8 = (bf16[768,128]{1,0:T(8,128)(2,1)S(1)}, bf16[768,128]{1,0:T(8,128)(2,1)S(1)}, u32[]{:S(2)}, u32[]{:S(2)}) collective-permute-start(bf16[768,128]{1,0:T(8,128)(2,1)S(1)} %collective-permute-done.7.refs_7_), channel_id=1, source_target_pairs={{8,0},{16,8},{24,16},{28,24},{20,28},{12,20},{4,12},{0,4},{9,1},{1... | collective-permute-start | bytes 589832 | tf_op jit(solution)/shard_map/ppermute | solution.py:393
  25.7 8.0 %collective-permute-start.15 = (bf16[784,128]{1,0:T(8,128)(2,1)S(1)}, bf16[784,128]{1,0:T(8,128)(2,1)}, u32[]{:S(2)}, u32[]{:S(2)}) collective-permute-start(bf16[784,128]{1,0:T(8,128)(2,1)S(1)} %collective-permute-done.14.refs_6_), channel_id=1, source_target_pairs={{8,0},{16,8},{24,16},{28,24},{20,28},{12,20},{4,12},{0,4},{9,1},{1... | collective-permute-start | bytes 602120 | tf_op jit(solution)/shard_map/ppermute | solution.py:396
  27.2 12.2 %collective-permute-start.5 = (bf16[784,128]{1,0:T(8,128)(2,1)S(1)}, bf16[784,128]{1,0:T(8,128)(2,1)S(1)}, u32[]{:S(2)}, u32[]{:S(2)}) collective-permute-start(bf16[784,128]{1,0:T(8,128)(2,1)S(1)} %collective-permute-done.4.refs_4_), channel_id=1, source_target_pairs={{0,8},{8,16},{16,24},{24,28},{28,20},{20,12},{12,4},{4,0},{1,9},{9... | collective-permute-start | bytes 602120 | tf_op jit(solution)/shard_map/ppermute | solution.py:392
  27.7 0.7 copy-start.5
  28.4 20.1 %copy-start.7 = (bf16[768,128]{1,0:T(8,128)(2,1)}, bf16[768,128]{1,0:T(8,128)(2,1)S(1)}, u32[]{:S(2)}) copy-start(bf16[768,128]{1,0:T(8,128)(2,1)S(1)} %collective-permute-done.8.refs_7_) | copy-start | bytes 589828
  28.4 9.5 %collective-permute-start.9 = (bf16[768,128]{1,0:T(8,128)(2,1)S(1)}, bf16[768,128]{1,0:T(8,128)(2,1)}, u32[]{:S(2)}, u32[]{:S(2)}) collective-permute-start(bf16[768,128]{1,0:T(8,128)(2,1)S(1)} %collective-permute-done.8.refs_7_), channel_id=1, source_target_pairs={{8,0},{16,8},{24,16},{28,24},{20,28},{12,20},{4,12},{0,4},{9,1},{1... | collective-permute-start | bytes 589832 | tf_op jit(solution)/shard_map/ppermute | solution.py:393
  29.9 28.4 %collective-permute-start.13 = (bf16[768,128]{1,0:T(8,128)(2,1)}, bf16[768,128]{1,0:T(8,128)(2,1)}, u32[]{:S(2)}, u32[]{:S(2)}) collective-permute-start(bf16[768,128]{1,0:T(8,128)(2,1)} %collective-permute-done.12.refs_5_), channel_id=1, source_target_pairs={{0,8},{8,16},{16,24},{24,28},{28,20},{20,12},{12,4},{4,0},{1,9},{9... | collective-permute-start | bytes 589832 | tf_op jit(solution)/shard_map/ppermute | solution.py:395
  33.6 24.7 %collective-permute-start.16 = (bf16[784,128]{1,0:T(8,128)(2,1)}, bf16[784,128]{1,0:T(8,128)(2,1)}, u32[]{:S(2)}, u32[]{:S(2)}) collective-permute-start(bf16[784,128]{1,0:T(8,128)(2,1)} %collective-permute-done.15.refs_6_), channel_id=1, source_target_pairs={{8,0},{16,8},{24,16},{28,24},{20,28},{12,20},{4,12},{0,4},{9,1},{1... | collective-permute-start | bytes 602120 | tf_op jit(solution)/shard_map/ppermute | solution.py:396
  37.8 28.4 %collective-permute-start.10 = (bf16[768,128]{1,0:T(8,128)(2,1)}, bf16[768,128]{1,0:T(8,128)(2,1)}, u32[]{:S(2)}, u32[]{:S(2)}) collective-permute-start(bf16[768,128]{1,0:T(8,128)(2,1)} %collective-permute-done.9.refs_7_), channel_id=1, source_target_pairs={{8,0},{16,8},{24,16},{28,24},{20,28},{12,20},{4,12},{0,4},{9,1},{1... | collective-permute-start | bytes 589832 | tf_op jit(solution)/shard_map/ppermute | solution.py:393
  39.4 26.9 %collective-permute-start.6 = (bf16[784,128]{1,0:T(8,128)(2,1)S(1)}, bf16[784,128]{1,0:T(8,128)(2,1)}, u32[]{:S(2)}, u32[]{:S(2)}) collective-permute-start(bf16[784,128]{1,0:T(8,128)(2,1)S(1)} %collective-permute-done.5.refs_4_), channel_id=1, source_target_pairs={{0,8},{8,16},{16,24},{24,28},{28,20},{20,12},{12,4},{4,0},{1,9},{9... | collective-permute-start | bytes 602120 | tf_op jit(solution)/shard_map/ppermute | solution.py:392
  39.9 8.6 %copy-start = (bf16[1552,128]{1,0:T(8,128)(2,1)}, bf16[1552,128]{1,0:T(8,128)(2,1)S(1)}, u32[]{:S(2)}) copy-start(bf16[1552,128]{1,0:T(8,128)(2,1)S(1)} %collective-permute-done.2.refs_3_) | copy-start | bytes 1191940
  39.9 8.6 %collective-permute-start.17 = (bf16[4,128]{1,0:T(4,128)(2,1)S(1)}, bf16[4,128]{1,0:T(4,128)(2,1)S(1)}, u32[]{:S(2)}, u32[]{:S(2)}) collective-permute-start(bf16[4,128]{1,0:T(4,128)(2,1)S(1)} %pad_maximum_fusion), channel_id=1, source_target_pairs={{0,16},{4,20},{8,24},{12,28},{16,0},{20,4},{24,8},{28,12},{1,17},{... | collective-permute-start | bytes 3080 | tf_op jit(solution)/shard_map/ppermute | solution.py:314
  48.5 8.2 %collective-permute-start.18 = (bf16[8,128]{1,0:T(8,128)(2,1)S(1)}, bf16[8,128]{1,0:T(8,128)(2,1)S(1)}, u32[]{:S(2)}, u32[]{:S(2)}) collective-permute-start(bf16[8,128]{1,0:T(8,128)(2,1)S(1)} %concatenate.16), channel_id=1, source_target_pairs={{0,8},{4,12},{8,0},{12,4},{16,24},{20,28},{24,16},{28,20},{1,9},{5... | collective-permute-start | bytes 6152 | tf_op jit(solution)/shard_map/ppermute | solution.py:314
  50.2 1.0 %copy-start.1 = (bf16[1552,128]{1,0:T(8,128)(2,1)S(1)}, bf16[1552,128]{1,0:T(8,128)(2,1)}, u32[]{:S(2)}) copy-start(bf16[1552,128]{1,0:T(8,128)(2,1)} %copy-done) | copy-start | bytes 1191940
  51.2 0.9 %copy-start.6 = (bf16[784,128]{1,0:T(8,128)(2,1)S(1)}, bf16[784,128]{1,0:T(8,128)(2,1)}, u32[]{:S(2)}) copy-start(bf16[784,128]{1,0:T(8,128)(2,1)} %copy-done.5) | copy-start | bytes 602116
  52.1 0.9 %copy-start.8 = (bf16[768,128]{1,0:T(8,128)(2,1)S(1)}, bf16[768,128]{1,0:T(8,128)(2,1)}, u32[]{:S(2)}) copy-start(bf16[768,128]{1,0:T(8,128)(2,1)} %copy-done.7) | copy-start | bytes 589828
  56.8 6.4 %collective-permute-start.19 = (bf16[16,128]{1,0:T(8,128)(2,1)S(1)}, bf16[16,128]{1,0:T(8,128)(2,1)S(1)}, u32[]{:S(2)}, u32[]{:S(2)}) collective-permute-start(bf16[16,128]{1,0:T(8,128)(2,1)S(1)} %concatenate.17), channel_id=1, source_target_pairs={{0,4},{4,0},{8,12},{12,8},{16,20},{20,16},{24,28},{28,24},{1,5},{5... | collective-permute-start | bytes 12296 | tf_op jit(solution)/shard_map/ppermute | solution.py:314
  58.4 1.0 %copy-start.2 = (bf16[1552,128]{1,0:T(8,128)(2,1)S(1)}, bf16[1552,128]{1,0:T(8,128)(2,1)}, u32[]{:S(2)}) copy-start(bf16[1552,128]{1,0:T(8,128)(2,1)} %copy-done) | copy-start | bytes 1191940
  66.2 1.0 %copy-start.3 = (bf16[1552,128]{1,0:T(8,128)(2,1)S(1)}, bf16[1552,128]{1,0:T(8,128)(2,1)}, u32[]{:S(2)}) copy-start(bf16[1552,128]{1,0:T(8,128)(2,1)} %copy-done) | copy-start | bytes 1191940

commit v3 on v2

--- a/solution.py
+++ b/solution.py
@@ -15,7 +15,8 @@
 VMEM = pl.BlockSpec(memory_space=pltpu.VMEM)
 SMEM = pl.BlockSpec(memory_space=pltpu.SMEM)
 ANY = pl.BlockSpec(memory_space=pl.ANY)
-GRANT = 20 * 1024 * 1024
+HBM = pl.BlockSpec(memory_space=pltpu.HBM)
+GRANT = 12 * 1024 * 1024
 
 
 class Dims:
@@ -52,25 +53,29 @@
     return jnp.concatenate([tile] * (rows // 16), axis=0)
 
 
-def prep_kernel(dims, blocks_ref, cols_ref, full_ref, a_ref, b_ref):
+def prep_kernel(dims, blocks_ref, cols_ref, full_ref, a_ref, b_ref, sems):
     me = lax.axis_index("cols").astype(jnp.int32)
-    bs = dims.bs
+    span = dims.per_group * dims.bs
+    copies = []
+    for j in range(dims.groups):
+        at = dims.at(j, 0)
+        ref, start = (a_ref, at) if at < dims.half else (b_ref, at - dims.half - IDX)
+        for k, (out_ref, first) in enumerate(((ref, start), (full_ref, at))):
+            copy = pltpu.make_async_copy(
+                blocks_ref.at[pl.ds((me ^ j) * span, span)], out_ref.at[first : first + span], sems.at[j, k]
+            )
+            copy.start()
+            copies.append(copy)
     lane = lax.broadcasted_iota(jnp.int32, (IDX, 128), 1)
     row = jnp.zeros((IDX, 128), jnp.int32)
     for j in range(dims.groups):
         for s in range(dims.per_group):
-            value = blocks_ref[me ^ j, 0, s]
-            at = dims.at(j, s)
-            full_ref[at : at + bs, :] = value
-            if at < dims.half:
-                a_ref[at : at + bs, :] = value
-            else:
-                at -= dims.half + IDX
-                b_ref[at : at + bs, :] = value
-            row = jnp.where(lane == j * dims.per_group + s, cols_ref[me ^ j, 0, s] // dims.groups, row)
+            row = jnp.where(lane == j * dims.per_group + s, cols_ref[s, 0, me ^ j] // dims.groups, row)
     numbers = row.astype(jnp.float32).astype(jnp.bfloat16)
     full_ref[dims.half : dims.half + IDX, :] = numbers
     a_ref[dims.half : dims.half + IDX, :] = numbers
+    for copy in copies:
+        copy.wait()
 
 
 def accumulate(dims, pieces, left, lp_ref, d_ref, emit):
@@ -188,13 +193,13 @@
     groups, per_group, bins, cycle = dims.groups, dims.per_group, dims.bins, dims.cycle
     p = lax.axis_index("rows").astype(jnp.int32)
     c = lax.axis_index("cols").astype(jnp.int32)
-    places = hyper_places(cycle)
+    number = [panel_number(dims, n if n <= HP else n - cycle) for n in range(cycle)]
     for n in range(cycle):
         for r in range(groups):
             bits = jnp.int32(0)
             for s in range(per_group):
                 bits = bits | (jnp.int32(1) << known_ref[n * groups, r * per_group + s])
-            mask_ref[(p ^ places[n]) * groups + r] = bits
+            mask_ref[number[n] * groups + r] = bits
     earlier = jnp.int32(0)
     for n in range(cycle):
         total = jnp.int32(0)
@@ -218,27 +223,12 @@
                     cols_ref[m ^ c, 0, slot] = jnp.where(one == 1, b * groups + c, -1)
                     used = used + one
         if n > 0:
-            earlier = earlier + jnp.where((p ^ places[n]) < p, total, 0)
+            earlier = earlier + jnp.where(number[n] < p, total, 0)
     for i in range(groups):
-        start_ref[i, 0] = earlier
+        start_ref[0, i] = earlier
         earlier = earlier + count_ref[i]
         for o in range(bins, dims.slots):
             cols_ref[i, 0, o] = -1
-
-
-def hyper_bits(cycle):
-    bits, bit = [], cycle // 2
-    while bit:
-        bits.append(bit)
-        bit //= 2
-    return bits
-
-
-def hyper_places(cycle):
-    places = [0]
-    for bit in hyper_bits(cycle):
-        places = places + [v ^ bit for v in places]
-    return places
 
 
 def flat(panels):
@@ -379,11 +369,14 @@
     own, own_a, own_b = pl.pallas_call(
         functools.partial(prep_kernel, dims),
         out_shape=[payload(2 * dims.half + IDX), payload(dims.half + IDX), payload(dims.half)],
-        in_specs=[VMEM, SMEM],
+        in_specs=[HBM, SMEM],
         out_specs=[VMEM] * 3,
+        scratch_shapes=[
+            pltpu.SemaphoreType.DMA((groups, 2)),
+        ],
         compiler_params=pltpu.CompilerParams(vmem_limit_bytes=GRANT),
         name="prep",
-    )(blocks, block_cols)
+    )(blocks.reshape(-1, bs), jnp.transpose(block_cols, (2, 1, 0)))
 
     if dims.whole:
         up, down = ring_moves(cycle)
@@ -402,16 +395,20 @@
     left = [own, left1, left2, left3]
 
     if dims.whole:
-        known = jnp.concatenate([x[dims.half : dims.half + 1] for x in left], axis=0)
-        for bit in hyper_bits(cycle):
-            known = jnp.concatenate([known, xor_move(known, "rows", bit)], axis=0)
+        heard = {0: jnp.concatenate([x[dims.half : dims.half + 1] for x in left], axis=0)}
+        for k in range(1, HP + 1):
+            heard[-k] = lax.ppermute(heard[1 - k], "rows", up)
+            if k < HP:
+                heard[k] = lax.ppermute(heard[k - 1], "rows", down)
+        order = [0, 1, 2, 3, -4, -3, -2, -1]
+        known = jnp.concatenate([heard[k] for k in order], axis=0)
         known = known[:, : groups * per_group].astype(jnp.int32)
         slots, columns, starts = pl.pallas_call(
             functools.partial(index_kernel, dims),
             out_shape=[
                 jax.ShapeDtypeStruct((groups * dims.bins,), jnp.int32),
                 jax.ShapeDtypeStruct((groups, 1, dims.slots), jnp.int32),
-                jax.ShapeDtypeStruct((groups, 1), jnp.int32),
+                jax.ShapeDtypeStruct((1, groups), jnp.int32),
             ],
             in_specs=[SMEM],
             out_specs=[SMEM] * 3,
@@ -422,10 +419,11 @@
             compiler_params=pltpu.CompilerParams(vmem_limit_bytes=GRANT),
             name="index",
         )(known)
-        acc, empty = call_step(dims, left, [(0, own, None)], None, zero=True)
-        for k in range(1, HP):
-            panels = [(-k, pa[k], pb[k]), (k, qa[k], qb[k])]
-            acc = call_step(dims, left, panels, acc)[0]
+        starts = starts.reshape(groups, 1)
+        pairs = [[(-k, pa[k], pb[k]), (k, qa[k], qb[k])] for k in range(1, HP)]
+        acc, empty = call_step(dims, left, [(0, own, None)] + pairs[0], None, zero=True)
+        for k in range(2, HP):
+            acc = call_step(dims, left, pairs[k - 1], acc)[0]
         final = [(HP, pa[HP], qb[HP])]
     else:
         slots, columns, starts = window_index(dims, left, window)

time: 71.1 us -> 66.4 us (0.934)
  local copies, waits for them, and re-layouts: 8.04 us -> 2.79 us
  Pallas kernels: 19.9 us -> 18.8 us
  waiting for transfers between devices: 17.5 us -> 18.5 us
    ppermute x6 -> x3, waiting for transfers between devices: 0.02 us -> 7.18 us  [xor_move(): lax.ppermute(value, axis, [(i, i ^ bit) for i in range(lax.axis_size(axis...]
    ppermute x0 -> x7, starting transfers between devices: none -> 6.44 us  [the longest x3 4.78 us: on_device(): heard[k] = lax.ppermute(heard[k - 1], 'rows', down)]
    ppermute x6 -> x3, starting transfers between devices: 9.12 us -> 3.04 us  [xor_move(): lax.ppermute(value, axis, [(i, i ^ bit) for i in range(lax.axis_size(axis...]
    unnamed x20 -> x8, local copies, waits for them, and re-layouts: 7.9 us -> 2.66 us
    ppermute x3, waiting for transfers between devices: 7.8 us -> 3.96 us  [on_device(): pb.append(lax.ppermute(pb[-1], 'rows', up))]
    ppermute x4, waiting for transfers between devices: 3.81 us -> 0.47 us  [on_device(): pa.append(lax.ppermute(pa[-1], 'rows', up))]
    ppermute x4, starting transfers between devices: 4.17 us -> 1.42 us  [on_device(): pa.append(lax.ppermute(pa[-1], 'rows', up))]
    pallas_call x4 -> x3, Pallas kernels: 13.4 us -> 11.3 us  [call_step(): pl.pallas_call(functools.partial(step_kernel, dims, layout, acc is not No...]
  transfers between devices with their start and end apart: 20 -> 24, of which waited for: 5 -> 5; matrix products, arithmetic and copies ran while one was open for 1% -> 0% of each run, Pallas kernels for 22% -> 21%
where the time goes in v3:
time: 66.4 us; the launch traced here: 66.1 us
  starting transfers between devices  25 us (38%)
  Pallas kernels  18.8 us (28%)
  waiting for transfers between devices  18.5 us (28%)
  local copies, waits for them, and re-layouts  2.79 us (4%)
  between operations  0.94 us (1%)
    pallas_call x3, Pallas kernels, call_step(): pl.pallas_call(functools.partial(step_kernel, dims, layout, acc is not No...  11.3 us
    ppermute x3, waiting for transfers between devices, xor_move(): lax.ppermute(value, axis, [(i, i ^ bit) for i in range(lax.axis_size(axis...  7.18 us
    ppermute x4, starting transfers between devices, on_device(): qb.append(lax.ppermute(qb[-1], 'rows', down))  5.23 us
    ppermute x3, starting transfers between devices, on_device(): qa.append(lax.ppermute(qa[-1], 'rows', down))  5.03 us
    ppermute x3, starting transfers between devices, on_device(): heard[k] = lax.ppermute(heard[k - 1], 'rows', down)  4.78 us
    ppermute x3, waiting for transfers between devices, on_device(): pb.append(lax.ppermute(pb[-1], 'rows', up))  3.96 us
    ppermute x3, starting transfers between devices, on_device(): pb.append(lax.ppermute(pb[-1], 'rows', up))  3.85 us
    ppermute x3, waiting for transfers between devices, on_device(): qa.append(lax.ppermute(qa[-1], 'rows', down))  3.63 us
  transfers between devices with their start and end apart: 24, of which 5 were waited for; matrix products, arithmetic and copies ran while one was open for 0% of the time, Pallas kernels for 21%

profile of v3, /device:TPU:0, one launch (start us, length us, event | category | flops | bytes accessed | tf_op | source)
XLA Modules:
  0.0 66.1 jit_solution(13757751575049681191)
XLA Ops:
  0.6 1.0 %copy-done.2 = bf16[4,1,3,128,128]{4,3,2,1,0:T(8,128)(2,1)S(1)} copy-done((bf16[4,1,3,128,128]{4,3,2,1,0:T(8,128)(2,1)S(1)}, bf16[4,1,3,128,128]{4,3,2,1,0:T(8,128)(2,1)}, u32[]{:S(2)}) %copy-start.2) | copy-done | bytes 393240
  1.6 0.7 %copy-done.3 = s32[4,1,3]{0,1,2:T(1,128)S(1)} copy-done((s32[4,1,3]{0,1,2:T(1,128)S(1)}, s32[4,1,3]{0,1,2:T(1,128)}, u32[]{:S(2)}) %copy-start.3) | copy-done | bytes 72
  2.3 1.7 %prep.1 = (bf16[1552,128]{1,0:T(8,128)(2,1)S(1)}, bf16[784,128]{1,0:T(8,128)(2,1)S(1)}, bf16[768,128]{1,0:T(8,128)(2,1)S(1)}) custom-call(bf16[1536,128]{1,0:T(8,128)(2,1)S(1)} %bitcast.6, s32[3,1,4]{2,1,0:T(1,128)S(1)} %bitcast.7), custom_call_target="tpu_custom_call" | custom-call | tf_op jit(solution)/shard_map/prep/pallas_call | solution.py:369
  4.1 3.0 %collective-permute-start.1 = (bf16[1552,128]{1,0:T(8,128)(2,1)S(1)}, bf16[1552,128]{1,0:T(8,128)(2,1)S(1)}, u32[]{:S(2)}, u32[]{:S(2)}) collective-permute-start(bf16[1552,128]{1,0:T(8,128)(2,1)S(1)} %get-tuple-element.11.refs_0_.refs_4_), channel_id=1, source_target_pairs={{0,2},{1,3},{2,0},{3,1},{4,6},{5,7},{6,4},{7,5},{8,10},{9,11},{10,... | collective-permute-start | bytes 1191944 | tf_op jit(solution)/shard_map/ppermute | solution.py:304
  7.1 1.6 %collective-permute-start.11 = (bf16[768,128]{1,0:T(8,128)(2,1)S(1)}, bf16[768,128]{1,0:T(8,128)(2,1)S(1)}, u32[]{:S(2)}, u32[]{:S(2)}) collective-permute-start(bf16[768,128]{1,0:T(8,128)(2,1)S(1)} %get-tuple-element.13), channel_id=1, source_target_pairs={{0,8},{8,16},{16,24},{24,28},{28,20},{20,12},{12,4},{4,0},{1,9},{9... | collective-permute-start | bytes 589832 | tf_op jit(solution)/shard_map/ppermute | solution.py:388
  8.7 0.4 collective-permute-start.7
  9.1 7.2 %collective-permute-done.1.refs_2_ = bf16[1552,128]{1,0:T(8,128)(2,1)S(1)} collective-permute-done((bf16[1552,128]{1,0:T(8,128)(2,1)S(1)}, bf16[1552,128]{1,0:T(8,128)(2,1)S(1)}, u32[]{:S(2)}, u32[]{:S(2)}) %collective-permute-start.1) | collective-permute-done | bytes 397344 | tf_op jit(solution)/shard_map/ppermute | solution.py:304
  16.3 0.0 collective-permute-start.2
  16.3 1.8 %collective-permute-start.14 = (bf16[784,128]{1,0:T(8,128)(2,1)S(1)}, bf16[784,128]{1,0:T(8,128)(2,1)S(1)}, u32[]{:S(2)}, u32[]{:S(2)}) collective-permute-start(bf16[784,128]{1,0:T(8,128)(2,1)S(1)} %get-tuple-element.12), channel_id=1, source_target_pairs={{8,0},{16,8},{24,16},{28,24},{20,28},{12,20},{4,12},{0,4},{9,1},{1... | collective-permute-start | bytes 602120 | tf_op jit(solution)/shard_map/ppermute | solution.py:389
  18.1 0.3 collective-permute-start.3
  18.3 1.8 %collective-permute-start.12 = (bf16[768,128]{1,0:T(8,128)(2,1)S(1)}, bf16[768,128]{1,0:T(8,128)(2,1)S(1)}, u32[]{:S(2)}, u32[]{:S(2)}) collective-permute-start(bf16[768,128]{1,0:T(8,128)(2,1)S(1)} %collective-permute-done.11.refs_6_), channel_id=1, source_target_pairs={{0,8},{8,16},{16,24},{24,28},{28,20},{20,12},{12,4},{4,0},{1,9},{9... | collective-permute-start | bytes 589832 | tf_op jit(solution)/shard_map/ppermute | solution.py:388
  20.2 3.6 %collective-permute-done.14.refs_7_ = bf16[784,128]{1,0:T(8,128)(2,1)S(1)} collective-permute-done((bf16[784,128]{1,0:T(8,128)(2,1)S(1)}, bf16[784,128]{1,0:T(8,128)(2,1)S(1)}, u32[]{:S(2)}, u32[]{:S(2)}) %collective-permute-start.14) | collective-permute-done | bytes 200736 | tf_op jit(solution)/shard_map/ppermute | solution.py:389
  23.8 1.7 %collective-permute-start.15 = (bf16[784,128]{1,0:T(8,128)(2,1)S(1)}, bf16[784,128]{1,0:T(8,128)(2,1)S(1)}, u32[]{:S(2)}, u32[]{:S(2)}) collective-permute-start(bf16[784,128]{1,0:T(8,128)(2,1)S(1)} %collective-permute-done.14.refs_7_), channel_id=1, source_target_pairs={{8,0},{16,8},{24,16},{28,24},{20,28},{12,20},{4,12},{0,4},{9,1},{1... | collective-permute-start | bytes 602120 | tf_op jit(solution)/shard_map/ppermute | solution.py:389
  25.5 0.5 collective-permute-done.3.refs_5_
  25.9 0.3 collective-permute-start.4
  26.2 4.0 %collective-permute-done.12.refs_5_ = bf16[768,128]{1,0:T(8,128)(2,1)S(1)} collective-permute-done((bf16[768,128]{1,0:T(8,128)(2,1)S(1)}, bf16[768,128]{1,0:T(8,128)(2,1)S(1)}, u32[]{:S(2)}, u32[]{:S(2)}) %collective-permute-start.12) | collective-permute-done | bytes 196640 | tf_op jit(solution)/shard_map/ppermute | solution.py:388
  30.1 1.6 %collective-permute-start.8 = (bf16[768,128]{1,0:T(8,128)(2,1)S(1)}, bf16[768,128]{1,0:T(8,128)(2,1)S(1)}, u32[]{:S(2)}, u32[]{:S(2)}) collective-permute-start(bf16[768,128]{1,0:T(8,128)(2,1)S(1)} %collective-permute-done.7.refs_8_), channel_id=1, source_target_pairs={{8,0},{16,8},{24,16},{28,24},{20,28},{12,20},{4,12},{0,4},{9,1},{1... | collective-permute-start | bytes 589832 | tf_op jit(solution)/shard_map/ppermute | solution.py:386
  31.7 0.5 collective-permute-start.13
  32.2 0.3 collective-permute-start.20
  32.5 3.3 %collective-permute-done.8.refs_7_ = bf16[768,128]{1,0:T(8,128)(2,1)S(1)} collective-permute-done((bf16[768,128]{1,0:T(8,128)(2,1)S(1)}, bf16[768,128]{1,0:T(8,128)(2,1)S(1)}, u32[]{:S(2)}, u32[]{:S(2)}) %collective-permute-start.8) | collective-permute-done | bytes 196640 | tf_op jit(solution)/shard_map/ppermute | solution.py:386
  35.8 1.6 %collective-permute-start.9 = (bf16[768,128]{1,0:T(8,128)(2,1)S(1)}, bf16[768,128]{1,0:T(8,128)(2,1)}, u32[]{:S(2)}, u32[]{:S(2)}) collective-permute-start(bf16[768,128]{1,0:T(8,128)(2,1)S(1)} %collective-permute-done.8.refs_7_), channel_id=1, source_target_pairs={{8,0},{16,8},{24,16},{28,24},{20,28},{12,20},{4,12},{0,4},{9,1},{1... | collective-permute-start | bytes 589832 | tf_op jit(solution)/shard_map/ppermute | solution.py:386
  37.4 1.6 %collective-permute-start.16 = (bf16[784,128]{1,0:T(8,128)(2,1)S(1)}, bf16[784,128]{1,0:T(8,128)(2,1)S(1)}, u32[]{:S(2)}, u32[]{:S(2)}) collective-permute-start(bf16[784,128]{1,0:T(8,128)(2,1)S(1)} %collective-permute-done.15.refs_6_), channel_id=1, source_target_pairs={{8,0},{16,8},{24,16},{28,24},{20,28},{12,20},{4,12},{0,4},{9,1},{1... | collective-permute-start | bytes 602120 | tf_op jit(solution)/shard_map/ppermute | solution.py:389
  39.0 0.0 collective-permute-done.4.refs_4_
  39.0 0.5 collective-permute-start.5
  39.4 0.0 collective-permute-done.13.refs_5_
  39.4 1.6 %collective-permute-start.17 = (bf16[4,128]{1,0:T(4,128)(2,1)S(1)}, bf16[4,128]{1,0:T(4,128)(2,1)S(1)}, u32[]{:S(2)}, u32[]{:S(2)}) collective-permute-start(bf16[4,128]{1,0:T(4,128)(2,1)S(1)} %pad_maximum_fusion), channel_id=1, source_target_pairs={{8,0},{16,8},{24,16},{28,24},{20,28},{12,20},{4,12},{0,4},{9,1},{1... | collective-permute-start | bytes 3080 | tf_op jit(solution)/shard_map/ppermute | solution.py:402
  41.0 0.5 collective-permute-start.21
  41.5 5.0 %shard_map.49 = (f32[512,1024]{1,0:T(8,128)S(1)}, bf16[4,36,128,128]{3,2,1,0:T(8,128)(2,1)}) custom-call(bf16[1552,128]{1,0:T(8,128)(2,1)S(1)} %get-tuple-element.11.refs_0_.refs_4_, bf16[1552,128]{1,0:T(8,128)(2,1)S(1)} %collective-permute-done.refs_1_, bf16[1552,128]{1,0:T(8,128)(2,1)S(1)} %collective-permute-done.1.refs_2_, ...), custom_call_target="tpu_custom_call" | custom-call | flops 1610612736 | bytes 4000000 | tf_op jit(solution)/shard_map/pallas_call | solution.py:272
  46.5 0.0 collective-permute-done.17
  46.5 1.6 %collective-permute-start.18 = (bf16[4,128]{1,0:T(4,128)(2,1)S(1)}, bf16[4,128]{1,0:T(4,128)(2,1)S(1)}, u32[]{:S(2)}, u32[]{:S(2)}) collective-permute-start(bf16[4,128]{1,0:T(4,128)(2,1)S(1)} %collective-permute-done.17), channel_id=1, source_target_pairs={{8,0},{16,8},{24,16},{28,24},{20,28},{12,20},{4,12},{0,4},{9,1},{1... | collective-permute-start | bytes 3080 | tf_op jit(solution)/shard_map/ppermute | solution.py:402
  48.1 0.0 collective-permute-done.21
  48.1 0.4 collective-permute-start.22
  48.5 2.7 %shard_map.50.refs_8_ = f32[512,1024]{1,0:T(8,128)S(1)} custom-call(bf16[1552,128]{1,0:T(8,128)(2,1)S(1)} %get-tuple-element.11.refs_0_.refs_4_, bf16[1552,128]{1,0:T(8,128)(2,1)S(1)} %collective-permute-done.refs_1_, bf16[1552,128]{1,0:T(8,128)(2,1)S(1)} %collective-permute-done.1.refs_2_, ...), custom_call_target="tpu_custom_call", output_to_operand_aliasing={{}: (8, {})} | custom-call | flops 1073741824 | bytes 4000000 | tf_op jit(solution)/shard_map/pallas_call | solution.py:272
  51.2 0.0 collective-permute-done.9.refs_7_
  51.2 1.6 %collective-permute-start.10 = (bf16[768,128]{1,0:T(8,128)(2,1)}, bf16[768,128]{1,0:T(8,128)(2,1)}, u32[]{:S(2)}, u32[]{:S(2)}) collective-permute-start(bf16[768,128]{1,0:T(8,128)(2,1)} %collective-permute-done.9.refs_7_), channel_id=1, source_target_pairs={{8,0},{16,8},{24,16},{28,24},{20,28},{12,20},{4,12},{0,4},{9,1},{1... | collective-permute-start | bytes 589832 | tf_op jit(solution)/shard_map/ppermute | solution.py:386
  52.9 0.5 collective-permute-start.6
  53.3 0.0 collective-permute-done.18
  53.3 1.6 %collective-permute-start.19 = (bf16[4,128]{1,0:T(4,128)(2,1)S(1)}, bf16[4,128]{1,0:T(4,128)(2,1)S(1)}, u32[]{:S(2)}, u32[]{:S(2)}) collective-permute-start(bf16[4,128]{1,0:T(4,128)(2,1)S(1)} %collective-permute-done.18), channel_id=1, source_target_pairs={{8,0},{16,8},{24,16},{28,24},{20,28},{12,20},{4,12},{0,4},{9,1},{1... | collective-permute-start | bytes 3080 | tf_op jit(solution)/shard_map/ppermute | solution.py:402
  54.9 0.0 collective-permute-done.22
  54.9 0.5 collective-permute-start.23
  55.4 0.0 collective-permute-done.16.refs_6_
  55.4 3.6 %shard_map.51.refs_6_ = f32[512,1024]{1,0:T(8,128)S(1)} custom-call(bf16[1552,128]{1,0:T(8,128)(2,1)S(1)} %get-tuple-element.11.refs_0_.refs_4_, bf16[1552,128]{1,0:T(8,128)(2,1)S(1)} %collective-permute-done.refs_1_, bf16[1552,128]{1,0:T(8,128)(2,1)S(1)} %collective-permute-done.1.refs_2_, ...), custom_call_target="tpu_custom_call", output_to_operand_aliasing={{}: (8, {})} | custom-call | flops 1073741824 | bytes 4000000 | tf_op jit(solution)/shard_map/pallas_call | solution.py:272
  59.0 0.0 collective-permute-done.23
  59.0 0.1 concatenate.8
  59.1 2.3 %index.1 = (s32[32]{0:T(128)S(1)}, s32[4,1,36]{2,1,0:T(1,128)}, s32[1,4]{1,0:T(1,128)}) custom-call(s32[32,12]{1,0:T(8,128)S(1)} %slice_convert_fusion.known_ref), custom_call_target="tpu_custom_call" | custom-call | tf_op jit(solution)/shard_map/index/pallas_call | solution.py:406
  61.5 0.0 collective-permute-done.6.refs_4_
  61.5 1.0 %copy-done.1 = bf16[1552,128]{1,0:T(8,128)(2,1)S(1)} copy-done((bf16[1552,128]{1,0:T(8,128)(2,1)S(1)}, bf16[1552,128]{1,0:T(8,128)(2,1)}, u32[]{:S(2)}) %copy-start.1) | copy-done | bytes 397336
  62.5 3.4 %shard_map.52 = bf16[4,36,128,128]{3,2,1,0:T(8,128)(2,1)} custom-call(bf16[1552,128]{1,0:T(8,128)(2,1)S(1)} %get-tuple-element.11.refs_0_.refs_4_, bf16[1552,128]{1,0:T(8,128)(2,1)S(1)} %collective-permute-done.refs_1_, bf16[1552,128]{1,0:T(8,128)(2,1)S(1)} %collective-permute-done.1.refs_2_, ...), custom_call_target="tpu_custom_call", output_to_operand_aliasing={{}: (8, {})} | custom-call | flops 536870912 | bytes 4000000 | tf_op jit(solution)/shard_map/pallas_call | solution.py:287
  (21 shorter events, 0.1 us)
Async XLA Ops:
  0.6 1.0 %copy-start.2 = (bf16[4,1,3,128,128]{4,3,2,1,0:T(8,128)(2,1)S(1)}, bf16[4,1,3,128,128]{4,3,2,1,0:T(8,128)(2,1)}, u32[]{:S(2)}) copy-start(bf16[4,1,3,128,128]{4,3,2,1,0:T(8,128)(2,1)} %param.2) | copy-start | bytes 1179652
  1.6 0.7 %copy-start.3 = (s32[4,1,3]{0,1,2:T(1,128)S(1)}, s32[4,1,3]{0,1,2:T(1,128)}, u32[]{:S(2)}) copy-start(s32[4,1,3]{0,1,2:T(1,128)} %param.3) | copy-start | bytes 148
  4.1 12.2 %collective-permute-start.1 = (bf16[1552,128]{1,0:T(8,128)(2,1)S(1)}, bf16[1552,128]{1,0:T(8,128)(2,1)S(1)}, u32[]{:S(2)}, u32[]{:S(2)}) collective-permute-start(bf16[1552,128]{1,0:T(8,128)(2,1)S(1)} %get-tuple-element.11.refs_0_.refs_4_), channel_id=1, source_target_pairs={{0,2},{1,3},{2,0},{3,1},{4,6},{5,7},{6,4},{7,5},{8,10},{9,11},{10,... | collective-permute-start | bytes 1191944 | tf_op jit(solution)/shard_map/ppermute | solution.py:304
  7.1 11.0 %collective-permute-start.11 = (bf16[768,128]{1,0:T(8,128)(2,1)S(1)}, bf16[768,128]{1,0:T(8,128)(2,1)S(1)}, u32[]{:S(2)}, u32[]{:S(2)}) collective-permute-start(bf16[768,128]{1,0:T(8,128)(2,1)S(1)} %get-tuple-element.13), channel_id=1, source_target_pairs={{0,8},{8,16},{16,24},{24,28},{28,20},{20,12},{12,4},{4,0},{1,9},{9... | collective-permute-start | bytes 589832 | tf_op jit(solution)/shard_map/ppermute | solution.py:388
  8.7 23.1 %collective-permute-start = (bf16[1552,128]{1,0:T(8,128)(2,1)S(1)}, bf16[1552,128]{1,0:T(8,128)(2,1)S(1)}, u32[]{:S(2)}, u32[]{:S(2)}) collective-permute-start(bf16[1552,128]{1,0:T(8,128)(2,1)S(1)} %get-tuple-element.11.refs_0_.refs_4_), channel_id=1, source_target_pairs={{0,1},{1,0},{2,3},{3,2},{4,5},{5,4},{6,7},{7,6},{8,9},{9,8},{10,11... | collective-permute-start | bytes 1191944 | tf_op jit(solution)/shard_map/ppermute | solution.py:304
  8.7 9.7 %collective-permute-start.7 = (bf16[768,128]{1,0:T(8,128)(2,1)S(1)}, bf16[768,128]{1,0:T(8,128)(2,1)S(1)}, u32[]{:S(2)}, u32[]{:S(2)}) collective-permute-start(bf16[768,128]{1,0:T(8,128)(2,1)S(1)} %get-tuple-element.13), channel_id=1, source_target_pairs={{8,0},{16,8},{24,16},{28,24},{20,28},{12,20},{4,12},{0,4},{9,1},{1... | collective-permute-start | bytes 589832 | tf_op jit(solution)/shard_map/ppermute | solution.py:386
  16.3 15.9 %collective-permute-start.2 = (bf16[1552,128]{1,0:T(8,128)(2,1)S(1)}, bf16[1552,128]{1,0:T(8,128)(2,1)S(1)}, u32[]{:S(2)}, u32[]{:S(2)}) collective-permute-start(bf16[1552,128]{1,0:T(8,128)(2,1)S(1)} %collective-permute-done.1.refs_2_), channel_id=1, source_target_pairs={{0,1},{1,0},{2,3},{3,2},{4,5},{5,4},{6,7},{7,6},{8,9},{9,8},{10,11... | collective-permute-start | bytes 1191944 | tf_op jit(solution)/shard_map/ppermute | solution.py:304
  16.3 7.5 %collective-permute-start.14 = (bf16[784,128]{1,0:T(8,128)(2,1)S(1)}, bf16[784,128]{1,0:T(8,128)(2,1)S(1)}, u32[]{:S(2)}, u32[]{:S(2)}) collective-permute-start(bf16[784,128]{1,0:T(8,128)(2,1)S(1)} %get-tuple-element.12), channel_id=1, source_target_pairs={{8,0},{16,8},{24,16},{28,24},{20,28},{12,20},{4,12},{0,4},{9,1},{1... | collective-permute-start | bytes 602120 | tf_op jit(solution)/shard_map/ppermute | solution.py:389
  18.1 7.9 %collective-permute-start.3 = (bf16[784,128]{1,0:T(8,128)(2,1)S(1)}, bf16[784,128]{1,0:T(8,128)(2,1)S(1)}, u32[]{:S(2)}, u32[]{:S(2)}) collective-permute-start(bf16[784,128]{1,0:T(8,128)(2,1)S(1)} %get-tuple-element.12), channel_id=1, source_target_pairs={{0,8},{8,16},{16,24},{24,28},{28,20},{20,12},{12,4},{4,0},{1,9},{9... | collective-permute-start | bytes 602120 | tf_op jit(solution)/shard_map/ppermute | solution.py:385
  18.3 11.8 %collective-permute-start.12 = (bf16[768,128]{1,0:T(8,128)(2,1)S(1)}, bf16[768,128]{1,0:T(8,128)(2,1)S(1)}, u32[]{:S(2)}, u32[]{:S(2)}) collective-permute-start(bf16[768,128]{1,0:T(8,128)(2,1)S(1)} %collective-permute-done.11.refs_6_), channel_id=1, source_target_pairs={{0,8},{8,16},{16,24},{24,28},{28,20},{20,12},{12,4},{4,0},{1,9},{9... | collective-permute-start | bytes 589832 | tf_op jit(solution)/shard_map/ppermute | solution.py:388
  23.8 13.6 %collective-permute-start.15 = (bf16[784,128]{1,0:T(8,128)(2,1)S(1)}, bf16[784,128]{1,0:T(8,128)(2,1)S(1)}, u32[]{:S(2)}, u32[]{:S(2)}) collective-permute-start(bf16[784,128]{1,0:T(8,128)(2,1)S(1)} %collective-permute-done.14.refs_7_), channel_id=1, source_target_pairs={{8,0},{16,8},{24,16},{28,24},{20,28},{12,20},{4,12},{0,4},{9,1},{1... | collective-permute-start | bytes 602120 | tf_op jit(solution)/shard_map/ppermute | solution.py:389
  25.9 13.0 %collective-permute-start.4 = (bf16[784,128]{1,0:T(8,128)(2,1)S(1)}, bf16[784,128]{1,0:T(8,128)(2,1)S(1)}, u32[]{:S(2)}, u32[]{:S(2)}) collective-permute-start(bf16[784,128]{1,0:T(8,128)(2,1)S(1)} %collective-permute-done.3.refs_5_), channel_id=1, source_target_pairs={{0,8},{8,16},{16,24},{24,28},{28,20},{20,12},{12,4},{4,0},{1,9},{9... | collective-permute-start | bytes 602120 | tf_op jit(solution)/shard_map/ppermute | solution.py:385
  30.1 5.7 %collective-permute-start.8 = (bf16[768,128]{1,0:T(8,128)(2,1)S(1)}, bf16[768,128]{1,0:T(8,128)(2,1)S(1)}, u32[]{:S(2)}, u32[]{:S(2)}) collective-permute-start(bf16[768,128]{1,0:T(8,128)(2,1)S(1)} %collective-permute-done.7.refs_8_), channel_id=1, source_target_pairs={{8,0},{16,8},{24,16},{28,24},{20,28},{12,20},{4,12},{0,4},{9,1},{1... | collective-permute-start | bytes 589832 | tf_op jit(solution)/shard_map/ppermute | solution.py:386
  31.7 7.7 %collective-permute-start.13 = (bf16[768,128]{1,0:T(8,128)(2,1)S(1)}, bf16[768,128]{1,0:T(8,128)(2,1)S(1)}, u32[]{:S(2)}, u32[]{:S(2)}) collective-permute-start(bf16[768,128]{1,0:T(8,128)(2,1)S(1)} %collective-permute-done.12.refs_5_), channel_id=1, source_target_pairs={{0,8},{8,16},{16,24},{24,28},{28,20},{20,12},{12,4},{4,0},{1,9},{9... | collective-permute-start | bytes 589832 | tf_op jit(solution)/shard_map/ppermute | solution.py:388
  32.2 23.2 %copy-start = (bf16[1552,128]{1,0:T(8,128)(2,1)}, bf16[1552,128]{1,0:T(8,128)(2,1)S(1)}, u32[]{:S(2)}) copy-start(bf16[1552,128]{1,0:T(8,128)(2,1)S(1)} %collective-permute-done.2.refs_3_) | copy-start | bytes 1191940
  32.2 8.8 %collective-permute-start.20 = (bf16[4,128]{1,0:T(4,128)(2,1)S(1)}, bf16[4,128]{1,0:T(4,128)(2,1)S(1)}, u32[]{:S(2)}, u32[]{:S(2)}) collective-permute-start(bf16[4,128]{1,0:T(4,128)(2,1)S(1)} %pad_maximum_fusion), channel_id=1, source_target_pairs={{0,8},{8,16},{16,24},{24,28},{28,20},{20,12},{12,4},{4,0},{1,9},{9... | collective-permute-start | bytes 3080 | tf_op jit(solution)/shard_map/ppermute | solution.py:400
  35.8 15.4 %collective-permute-start.9 = (bf16[768,128]{1,0:T(8,128)(2,1)S(1)}, bf16[768,128]{1,0:T(8,128)(2,1)}, u32[]{:S(2)}, u32[]{:S(2)}) collective-permute-start(bf16[768,128]{1,0:T(8,128)(2,1)S(1)} %collective-permute-done.8.refs_7_), channel_id=1, source_target_pairs={{8,0},{16,8},{24,16},{28,24},{20,28},{12,20},{4,12},{0,4},{9,1},{1... | collective-permute-start | bytes 589832 | tf_op jit(solution)/shard_map/ppermute | solution.py:386
  37.4 18.0 %collective-permute-start.16 = (bf16[784,128]{1,0:T(8,128)(2,1)S(1)}, bf16[784,128]{1,0:T(8,128)(2,1)S(1)}, u32[]{:S(2)}, u32[]{:S(2)}) collective-permute-start(bf16[784,128]{1,0:T(8,128)(2,1)S(1)} %collective-permute-done.15.refs_6_), channel_id=1, source_target_pairs={{8,0},{16,8},{24,16},{28,24},{20,28},{12,20},{4,12},{0,4},{9,1},{1... | collective-permute-start | bytes 602120 | tf_op jit(solution)/shard_map/ppermute | solution.py:389
  39.0 13.9 %collective-permute-start.5 = (bf16[784,128]{1,0:T(8,128)(2,1)S(1)}, bf16[784,128]{1,0:T(8,128)(2,1)S(1)}, u32[]{:S(2)}, u32[]{:S(2)}) collective-permute-start(bf16[784,128]{1,0:T(8,128)(2,1)S(1)} %collective-permute-done.4.refs_4_), channel_id=1, source_target_pairs={{0,8},{8,16},{16,24},{24,28},{28,20},{20,12},{12,4},{4,0},{1,9},{9... | collective-permute-start | bytes 602120 | tf_op jit(solution)/shard_map/ppermute | solution.py:385
  39.4 7.0 %collective-permute-start.17 = (bf16[4,128]{1,0:T(4,128)(2,1)S(1)}, bf16[4,128]{1,0:T(4,128)(2,1)S(1)}, u32[]{:S(2)}, u32[]{:S(2)}) collective-permute-start(bf16[4,128]{1,0:T(4,128)(2,1)S(1)} %pad_maximum_fusion), channel_id=1, source_target_pairs={{8,0},{16,8},{24,16},{28,24},{20,28},{12,20},{4,12},{0,4},{9,1},{1... | collective-permute-start | bytes 3080 | tf_op jit(solution)/shard_map/ppermute | solution.py:402
  41.0 7.1 %collective-permute-start.21 = (bf16[4,128]{1,0:T(4,128)(2,1)S(1)}, bf16[4,128]{1,0:T(4,128)(2,1)S(1)}, u32[]{:S(2)}, u32[]{:S(2)}) collective-permute-start(bf16[4,128]{1,0:T(4,128)(2,1)S(1)} %collective-permute-done.20), channel_id=1, source_target_pairs={{0,8},{8,16},{16,24},{24,28},{28,20},{20,12},{12,4},{4,0},{1,9},{9... | collective-permute-start | bytes 3080 | tf_op jit(solution)/shard_map/ppermute | solution.py:400
  46.5 6.9 %collective-permute-start.18 = (bf16[4,128]{1,0:T(4,128)(2,1)S(1)}, bf16[4,128]{1,0:T(4,128)(2,1)S(1)}, u32[]{:S(2)}, u32[]{:S(2)}) collective-permute-start(bf16[4,128]{1,0:T(4,128)(2,1)S(1)} %collective-permute-done.17), channel_id=1, source_target_pairs={{8,0},{16,8},{24,16},{28,24},{20,28},{12,20},{4,12},{0,4},{9,1},{1... | collective-permute-start | bytes 3080 | tf_op jit(solution)/shard_map/ppermute | solution.py:402
  48.1 6.8 %collective-permute-start.22 = (bf16[4,128]{1,0:T(4,128)(2,1)S(1)}, bf16[4,128]{1,0:T(4,128)(2,1)S(1)}, u32[]{:S(2)}, u32[]{:S(2)}) collective-permute-start(bf16[4,128]{1,0:T(4,128)(2,1)S(1)} %collective-permute-done.21), channel_id=1, source_target_pairs={{0,8},{8,16},{16,24},{24,28},{28,20},{20,12},{12,4},{4,0},{1,9},{9... | collective-permute-start | bytes 3080 | tf_op jit(solution)/shard_map/ppermute | solution.py:400
  51.2 10.2 %collective-permute-start.10 = (bf16[768,128]{1,0:T(8,128)(2,1)}, bf16[768,128]{1,0:T(8,128)(2,1)}, u32[]{:S(2)}, u32[]{:S(2)}) collective-permute-start(bf16[768,128]{1,0:T(8,128)(2,1)} %collective-permute-done.9.refs_7_), channel_id=1, source_target_pairs={{8,0},{16,8},{24,16},{28,24},{20,28},{12,20},{4,12},{0,4},{9,1},{1... | collective-permute-start | bytes 589832 | tf_op jit(solution)/shard_map/ppermute | solution.py:386
  52.9 8.6 %collective-permute-start.6 = (bf16[784,128]{1,0:T(8,128)(2,1)S(1)}, bf16[784,128]{1,0:T(8,128)(2,1)}, u32[]{:S(2)}, u32[]{:S(2)}) collective-permute-start(bf16[784,128]{1,0:T(8,128)(2,1)S(1)} %collective-permute-done.5.refs_4_), channel_id=1, source_target_pairs={{0,8},{8,16},{16,24},{24,28},{28,20},{20,12},{12,4},{4,0},{1,9},{9... | collective-permute-start | bytes 602120 | tf_op jit(solution)/shard_map/ppermute | solution.py:385
  53.3 5.6 %collective-permute-start.19 = (bf16[4,128]{1,0:T(4,128)(2,1)S(1)}, bf16[4,128]{1,0:T(4,128)(2,1)S(1)}, u32[]{:S(2)}, u32[]{:S(2)}) collective-permute-start(bf16[4,128]{1,0:T(4,128)(2,1)S(1)} %collective-permute-done.18), channel_id=1, source_target_pairs={{8,0},{16,8},{24,16},{28,24},{20,28},{12,20},{4,12},{0,4},{9,1},{1... | collective-permute-start | bytes 3080 | tf_op jit(solution)/shard_map/ppermute | solution.py:402
  54.9 4.1 %collective-permute-start.23 = (bf16[4,128]{1,0:T(4,128)(2,1)S(1)}, bf16[4,128]{1,0:T(4,128)(2,1)S(1)}, u32[]{:S(2)}, u32[]{:S(2)}) collective-permute-start(bf16[4,128]{1,0:T(4,128)(2,1)S(1)} %collective-permute-done.22), channel_id=1, source_target_pairs={{0,8},{8,16},{16,24},{24,28},{28,20},{20,12},{12,4},{4,0},{1,9},{9... | collective-permute-start | bytes 3080 | tf_op jit(solution)/shard_map/ppermute | solution.py:400
  61.5 1.0 %copy-start.1 = (bf16[1552,128]{1,0:T(8,128)(2,1)S(1)}, bf16[1552,128]{1,0:T(8,128)(2,1)}, u32[]{:S(2)}) copy-start(bf16[1552,128]{1,0:T(8,128)(2,1)} %copy-done) | copy-start | bytes 1191940

commit v4 on v3

--- a/solution.py
+++ b/solution.py
@@ -53,7 +53,10 @@
     return jnp.concatenate([tile] * (rows // 16), axis=0)
 
 
-def prep_kernel(dims, blocks_ref, cols_ref, full_ref, a_ref, b_ref, sems):
+def prep_kernel(dims, *refs):
+    refs = list(refs)
+    cols = take(refs, dims.groups)
+    blocks_ref, full_ref, a_ref, b_ref, tile_ref, sems = refs
     me = lax.axis_index("cols").astype(jnp.int32)
     span = dims.per_group * dims.bs
     copies = []
@@ -66,14 +69,22 @@
             )
             copy.start()
             copies.append(copy)
+    line = lax.broadcasted_iota(jnp.int32, (IDX, 128), 0)
     lane = lax.broadcasted_iota(jnp.int32, (IDX, 128), 1)
-    row = jnp.zeros((IDX, 128), jnp.int32)
+    tile = jnp.zeros((IDX, 128), jnp.int32)
     for j in range(dims.groups):
-        for s in range(dims.per_group):
-            row = jnp.where(lane == j * dims.per_group + s, cols_ref[s, 0, me ^ j] // dims.groups, row)
-    numbers = row.astype(jnp.float32).astype(jnp.bfloat16)
-    full_ref[dims.half : dims.half + IDX, :] = numbers
-    a_ref[dims.half : dims.half + IDX, :] = numbers
+        row = jnp.zeros((IDX, 128), jnp.int32)
+        for r in range(dims.groups):
+            for s in range(dims.per_group):
+                number = cols[j][s, 0, me ^ j ^ r] // dims.groups
+                row = jnp.where(lane == r * dims.per_group + s, number, row)
+        tile = jnp.where(line == j, row, tile)
+    numbers = tile.astype(jnp.float32).astype(jnp.bfloat16)
+    tile_ref[...] = numbers
+    for ref in (a_ref, b_ref):
+        ref[dims.half : dims.half + IDX, :] = numbers
+    for at in (dims.half, 2 * dims.half + IDX):
+        full_ref[at : at + IDX, :] = numbers
     for copy in copies:
         copy.wait()
 
@@ -135,13 +146,15 @@
     return pieces
 
 
-def step_kernel(dims, layout, with_acc, with_zero, *refs):
+def step_kernel(dims, layout, with_acc, with_zero, tiles, *refs):
     refs = list(refs)
     left = take(refs, dims.groups)
     pieces = take_pieces(refs, layout)
+    tile_refs = take(refs, len(tiles))
     acc_ref = refs.pop(0) if with_acc else None
     out_ref = refs.pop(0)
     zero_ref = refs.pop(0) if with_zero else None
+    index_refs = take(refs, 3) if tiles else None
     lp_ref, d_ref = take(refs, 2)
     copies = []
     if with_zero:
@@ -153,9 +166,19 @@
             )
             copy.start()
             copies.append(copy)
+    if tiles:
+        wide_ref, known_ref, mask_ref, count_ref, sem = refs
+        for k, (n, at) in enumerate(tiles):
+            tile = tile_refs[k][at : at + IDX, :].astype(jnp.float32).astype(jnp.int32)
+            wide_ref[n * 8 : (n + 1) * 8, :] = tile[:8]
+        known = pltpu.make_async_copy(wide_ref, known_ref, sem)
+        known.start()
 
     def emit(lo, hi, value):
         out_ref[:, lo:hi] = value if acc_ref is None else acc_ref[:, lo:hi] + value
+        if tiles and lo == 0:
+            known.wait()
+            index_work(dims, known_ref, *index_refs, mask_ref, count_ref)
 
     accumulate(dims, pieces, left, lp_ref, d_ref, emit)
     for copy in copies:
@@ -189,7 +212,7 @@
         copy.wait()
 
 
-def index_kernel(dims, known_ref, slot_ref, cols_ref, start_ref, mask_ref, count_ref):
+def index_work(dims, known_ref, slot_ref, cols_ref, start_ref, mask_ref, count_ref):
     groups, per_group, bins, cycle = dims.groups, dims.per_group, dims.bins, dims.cycle
     p = lax.axis_index("rows").astype(jnp.int32)
     c = lax.axis_index("cols").astype(jnp.int32)
@@ -198,7 +221,7 @@
         for r in range(groups):
             bits = jnp.int32(0)
             for s in range(per_group):
-                bits = bits | (jnp.int32(1) << known_ref[n * groups, r * per_group + s])
+                bits = bits | (jnp.int32(1) << known_ref[n * 8, r * per_group + s])
             mask_ref[number[n] * groups + r] = bits
     earlier = jnp.int32(0)
     for n in range(cycle):
@@ -207,7 +230,7 @@
             bits = jnp.int32(0)
             for j in range(groups):
                 for t in range(per_group):
-                    k = known_ref[n * groups + j, (m ^ j) * per_group + t]
+                    k = known_ref[n * 8 + j, (m ^ j) * per_group + t]
                     bits = bits | mask_ref[k * groups + j]
             count = jnp.int32(0)
             for b in range(bins):
@@ -250,9 +273,9 @@
     return pl.CostEstimate(flops=flops, bytes_accessed=4_000_000, transcendentals=0)
 
 
-def call_step(dims, left, panels, acc, zero=False):
+def call_step(dims, left, panels, acc, zero=False, tiles=()):
     layout, arrays = flat(panels)
-    args = [*left, *arrays]
+    args = [*left, *arrays, *(array for _, array, _ in tiles)]
     aliases = {}
     if acc is not None:
         aliases = {len(args): 0}
@@ -269,8 +292,23 @@
             pltpu.VMEM((dims.slots - dims.bins, dims.bs, dims.bs), jnp.bfloat16),
             pltpu.SemaphoreType.DMA((dims.groups,)),
         ]
+    if tiles:
+        shapes += [
+            jax.ShapeDtypeStruct((dims.groups * dims.bins,), jnp.int32),
+            jax.ShapeDtypeStruct((dims.groups, 1, dims.slots), jnp.int32),
+            jax.ShapeDtypeStruct((1, dims.groups), jnp.int32),
+        ]
+        specs += [SMEM] * 3
+        scratch += [
+            pltpu.VMEM((dims.cycle * 8, 128), jnp.int32),
+            pltpu.SMEM((dims.cycle * 8, 128), jnp.int32),
+            pltpu.SMEM((dims.cycle * dims.groups,), jnp.int32),
+            pltpu.SMEM((dims.groups,), jnp.int32),
+            pltpu.SemaphoreType.DMA,
+        ]
+    marks = tuple((n, at) for n, _, at in tiles)
     return pl.pallas_call(
-        functools.partial(step_kernel, dims, layout, acc is not None, zero),
+        functools.partial(step_kernel, dims, layout, acc is not None, zero, marks),
         out_shape=shapes,
         in_specs=[VMEM] * len(args),
         out_specs=specs,
@@ -366,17 +404,16 @@
     def payload(rows):
         return jax.ShapeDtypeStruct((rows, bs), jnp.bfloat16)
 
-    own, own_a, own_b = pl.pallas_call(
+    cols = [block_cols] + [xor_move(block_cols, "cols", j) for j in range(1, groups)]
+    own, own_a, own_b, tile = pl.pallas_call(
         functools.partial(prep_kernel, dims),
-        out_shape=[payload(2 * dims.half + IDX), payload(dims.half + IDX), payload(dims.half)],
-        in_specs=[HBM, SMEM],
-        out_specs=[VMEM] * 3,
-        scratch_shapes=[
-            pltpu.SemaphoreType.DMA((groups, 2)),
-        ],
+        out_shape=[payload(2 * dims.half + 2 * IDX)] + [payload(dims.half + IDX)] * 2 + [payload(IDX)],
+        in_specs=[SMEM] * groups + [ANY],
+        out_specs=[VMEM] * 4,
+        scratch_shapes=[pltpu.SemaphoreType.DMA((groups, 2))],
         compiler_params=pltpu.CompilerParams(vmem_limit_bytes=GRANT),
         name="prep",
-    )(blocks.reshape(-1, bs), jnp.transpose(block_cols, (2, 1, 0)))
+    )(*(jnp.transpose(x, (2, 1, 0)) for x in cols), blocks.reshape(-1, bs))
 
     if dims.whole:
         up, down = ring_moves(cycle)
@@ -395,35 +432,16 @@
     left = [own, left1, left2, left3]
 
     if dims.whole:
-        heard = {0: jnp.concatenate([x[dims.half : dims.half + 1] for x in left], axis=0)}
-        for k in range(1, HP + 1):
-            heard[-k] = lax.ppermute(heard[1 - k], "rows", up)
-            if k < HP:
-                heard[k] = lax.ppermute(heard[k - 1], "rows", down)
-        order = [0, 1, 2, 3, -4, -3, -2, -1]
-        known = jnp.concatenate([heard[k] for k in order], axis=0)
-        known = known[:, : groups * per_group].astype(jnp.int32)
-        slots, columns, starts = pl.pallas_call(
-            functools.partial(index_kernel, dims),
-            out_shape=[
-                jax.ShapeDtypeStruct((groups * dims.bins,), jnp.int32),
-                jax.ShapeDtypeStruct((groups, 1, dims.slots), jnp.int32),
-                jax.ShapeDtypeStruct((1, groups), jnp.int32),
-            ],
-            in_specs=[SMEM],
-            out_specs=[SMEM] * 3,
-            scratch_shapes=[
-                pltpu.SMEM((cycle * groups,), jnp.int32),
-                pltpu.SMEM((groups,), jnp.int32),
-            ],
-            compiler_params=pltpu.CompilerParams(vmem_limit_bytes=GRANT),
-            name="index",
-        )(known)
-        starts = starts.reshape(groups, 1)
+        far = lax.ppermute(tile, "rows", [(a, dict(up)[dict(up)[dict(up)[b]]]) for a, b in up])
         pairs = [[(-k, pa[k], pb[k]), (k, qa[k], qb[k])] for k in range(1, HP)]
         acc, empty = call_step(dims, left, [(0, own, None)] + pairs[0], None, zero=True)
-        for k in range(2, HP):
+        for k in range(2, HP - 1):
             acc = call_step(dims, left, pairs[k - 1], acc)[0]
+        tiles = [(0, tile, 0), (HP, far, 0)]
+        for k in range(1, HP):
+            tiles += [(cycle - k, pa[k], dims.half), (k, qb[k], dims.half)]
+        acc, slots, columns, starts = call_step(dims, left, pairs[-1], acc, tiles=tiles)
+        starts = starts.reshape(groups, 1)
         final = [(HP, pa[HP], qb[HP])]
     else:
         slots, columns, starts = window_index(dims, left, window)

time: 66.4 us -> 59.3 us (0.89)
  waiting for transfers between devices: 18.5 us -> 15.3 us
  starting transfers between devices: 25 us -> 23.5 us
  local copies, waits for them, and re-layouts: 2.79 us -> 1.68 us
  Pallas kernels: 18.8 us -> 17.9 us
    ppermute x3 -> x6, waiting for transfers between devices: 7.18 us -> 3.76 us  [xor_move(): lax.ppermute(value, axis, [(i, i ^ bit) for i in range(lax.axis_size(axis...]
    ppermute x4, waiting for transfers between devices: 3.29 us -> 0.01 us  [on_device(): qb.append(lax.ppermute(qb[-1], 'rows', down))]
    ppermute x7 -> x1, starting transfers between devices: 6.44 us -> 3.54 us  [on_device(): lax.ppermute(tile, 'rows', [(a, dict(up)[dict(up)[dict(up)[b]]]) for a, b...]
    ppermute x3, waiting for transfers between devices: 3.63 us -> 6.13 us  [on_device(): qa.append(lax.ppermute(qa[-1], 'rows', down))]
    pallas_call x1 -> x0, Pallas kernels: 2.34 us -> none  [on_device(): pl.pallas_call(functools.partial(index_kernel, dims), out_shape=[jax.Shap...]
    pallas_call x3, Pallas kernels: 11.3 us -> 13 us  [call_step(): pl.pallas_call(functools.partial(step_kernel, dims, layout, acc is not No...]
    ppermute x4, starting transfers between devices: 1.42 us -> 2.81 us  [on_device(): pa.append(lax.ppermute(pa[-1], 'rows', up))]
    ppermute x3, waiting for transfers between devices: 3.96 us -> 5.34 us  [on_device(): pb.append(lax.ppermute(pb[-1], 'rows', up))]
  transfers between devices with their start and end apart: 24 -> 21, of which waited for: 5 -> 6; matrix products, arithmetic and copies ran while one was open for 0% -> 0% of each run, Pallas kernels for 21% -> 22%
where the time goes in v4:
time: 59.3 us; the launch traced here: 59.1 us
  starting transfers between devices  23.5 us (40%)
  Pallas kernels  17.9 us (30%)
  waiting for transfers between devices  15.3 us (26%)
  local copies, waits for them, and re-layouts  1.68 us (3%)
  between operations  0.72 us (1%)
    pallas_call x3, Pallas kernels, call_step(): pl.pallas_call(functools.partial(step_kernel, dims, layout, acc is not No...  13 us
    ppermute x3, waiting for transfers between devices, on_device(): qa.append(lax.ppermute(qa[-1], 'rows', down))  6.13 us
    ppermute x3, waiting for transfers between devices, on_device(): pb.append(lax.ppermute(pb[-1], 'rows', up))  5.34 us
    ppermute x3, starting transfers between devices, on_device(): pb.append(lax.ppermute(pb[-1], 'rows', up))  5.2 us
    ppermute x3, starting transfers between devices, on_device(): qa.append(lax.ppermute(qa[-1], 'rows', down))  4.4 us
    ppermute x4, starting transfers between devices, on_device(): qb.append(lax.ppermute(qb[-1], 'rows', down))  4.22 us
    ppermute x6, waiting for transfers between devices, xor_move(): lax.ppermute(value, axis, [(i, i ^ bit) for i in range(lax.axis_size(axis...  3.76 us
    ppermute x1, starting transfers between devices, on_device(): lax.ppermute(tile, 'rows', [(a, dict(up)[dict(up)[dict(up)[b]]]) for a, b...  3.54 us
  transfers between devices with their start and end apart: 21, of which 6 were waited for; matrix products, arithmetic and copies ran while one was open for 0% of the time, Pallas kernels for 22%

profile of v4, /device:TPU:0, one launch (start us, length us, event | category | flops | bytes accessed | tf_op | source)
XLA Modules:
  0.0 59.1 jit_solution(5783109999141854123)
XLA Ops:
  0.6 0.6 collective-permute-start
  1.2 2.6 %collective-permute-start.2 = (s32[4,1,3]{0,1,2:T(1,128)}, s32[4,1,3]{0,1,2:T(1,128)S(1)}, u32[]{:S(2)}, u32[]{:S(2)}) collective-permute-start(s32[4,1,3]{0,1,2:T(1,128)} %param.3), channel_id=1, source_target_pairs={{0,3},{1,2},{2,1},{3,0},{4,7},{5,6},{6,5},{7,4},{8,11},{9,10},{10,... | collective-permute-start | bytes 152 | tf_op jit(solution)/shard_map/ppermute | solution.py:342
  3.8 0.0 collective-permute-start.1
  3.8 0.0 collective-permute-done
  3.8 1.5 %collective-permute-done.2 = s32[4,1,3]{0,1,2:T(1,128)S(1)} collective-permute-done((s32[4,1,3]{0,1,2:T(1,128)}, s32[4,1,3]{0,1,2:T(1,128)S(1)}, u32[]{:S(2)}, u32[]{:S(2)}) %collective-permute-start.2) | collective-permute-done | bytes 80 | tf_op jit(solution)/shard_map/ppermute | solution.py:342
  5.3 2.3 %collective-permute-done.1 = s32[4,1,3]{0,1,2:T(1,128)S(1)} collective-permute-done((s32[4,1,3]{0,1,2:T(1,128)}, s32[4,1,3]{0,1,2:T(1,128)S(1)}, u32[]{:S(2)}, u32[]{:S(2)}) %collective-permute-start.1) | collective-permute-done | bytes 80 | tf_op jit(solution)/shard_map/ppermute | solution.py:342
  7.6 1.0 %copy-done = bf16[4,1,3,128,128]{4,3,2,1,0:T(8,128)(2,1)S(1)} copy-done((bf16[4,1,3,128,128]{4,3,2,1,0:T(8,128)(2,1)S(1)}, bf16[4,1,3,128,128]{4,3,2,1,0:T(8,128)(2,1)}, u32[]{:S(2)}) %copy-start) | copy-done | bytes 393240
  8.6 0.7 %copy-done.1 = s32[4,1,3]{0,1,2:T(1,128)S(1)} copy-done((s32[4,1,3]{0,1,2:T(1,128)S(1)}, s32[4,1,3]{0,1,2:T(1,128)}, u32[]{:S(2)}) %copy-start.1) | copy-done | bytes 72
  9.2 2.0 %prep.1 = (bf16[1568,128]{1,0:T(8,128)(2,1)S(1)}, bf16[784,128]{1,0:T(8,128)(2,1)S(1)}, bf16[784,128]{1,0:T(8,128)(2,1)S(1)}, bf16[16,128]{1,0:T(8,128)(2,1)S(1)}) custom-call(s32[3,1,4]{2,1,0:T(1,128)S(1)} %bitcast.10, s32[3,1,4]{2,1,0:T(1,128)S(1)} %bitcast.11, s32[3,1,4]{2,1,0:T(1,128)S(1)} %bitcast.13, s32[3,1,4]{2,1,0:T(1,128)S(1)} %bitcast.12, ...), custom_call_target="tpu_custom_call" | custom-call | tf_op jit(solution)/shard_map/prep/pallas_call | solution.py:408
  11.2 0.1 collective-permute-start.4
  11.4 2.0 %collective-permute-start.17 = (bf16[784,128]{1,0:T(8,128)(2,1)S(1)}, bf16[784,128]{1,0:T(8,128)(2,1)S(1)}, u32[]{:S(2)}, u32[]{:S(2)}) collective-permute-start(bf16[784,128]{1,0:T(8,128)(2,1)S(1)} %get-tuple-element.14), channel_id=1, source_target_pairs={{8,0},{16,8},{24,16},{28,24},{20,28},{12,20},{4,12},{0,4},{9,1},{1... | collective-permute-start | bytes 602120 | tf_op jit(solution)/shard_map/ppermute | solution.py:426
  13.4 0.1 collective-permute-start.6
  13.4 2.0 %collective-permute-start.14 = (bf16[784,128]{1,0:T(8,128)(2,1)S(1)}, bf16[784,128]{1,0:T(8,128)(2,1)S(1)}, u32[]{:S(2)}, u32[]{:S(2)}) collective-permute-start(bf16[784,128]{1,0:T(8,128)(2,1)S(1)} %get-tuple-element.15), channel_id=1, source_target_pairs={{0,8},{8,16},{16,24},{24,28},{28,20},{20,12},{12,4},{4,0},{1,9},{9... | collective-permute-start | bytes 602120 | tf_op jit(solution)/shard_map/ppermute | solution.py:425
  15.4 0.0 collective-permute-start.10
  15.4 3.8 %collective-permute-done.17.refs_7_ = bf16[784,128]{1,0:T(8,128)(2,1)S(1)} collective-permute-done((bf16[784,128]{1,0:T(8,128)(2,1)S(1)}, bf16[784,128]{1,0:T(8,128)(2,1)S(1)}, u32[]{:S(2)}, u32[]{:S(2)}) %collective-permute-start.17) | collective-permute-done | bytes 200736 | tf_op jit(solution)/shard_map/ppermute | solution.py:426
  19.3 2.0 %collective-permute-start.18 = (bf16[784,128]{1,0:T(8,128)(2,1)S(1)}, bf16[784,128]{1,0:T(8,128)(2,1)S(1)}, u32[]{:S(2)}, u32[]{:S(2)}) collective-permute-start(bf16[784,128]{1,0:T(8,128)(2,1)S(1)} %collective-permute-done.17.refs_7_), channel_id=1, source_target_pairs={{8,0},{16,8},{24,16},{28,24},{20,28},{12,20},{4,12},{0,4},{9,1},{1... | collective-permute-start | bytes 602120 | tf_op jit(solution)/shard_map/ppermute | solution.py:426
  21.2 0.0 collective-permute-done.6.refs_5_.refs_10_
  21.2 0.0 collective-permute-start.3
  21.2 2.1 %collective-permute-done.14.refs_6_ = bf16[784,128]{1,0:T(8,128)(2,1)S(1)} collective-permute-done((bf16[784,128]{1,0:T(8,128)(2,1)S(1)}, bf16[784,128]{1,0:T(8,128)(2,1)S(1)}, u32[]{:S(2)}, u32[]{:S(2)}) %collective-permute-start.14) | collective-permute-done | bytes 200736 | tf_op jit(solution)/shard_map/ppermute | solution.py:425
  23.3 0.5 collective-permute-start.7
  23.8 0.0 collective-permute-done.10.refs_8_.refs_11_
  23.8 1.7 %collective-permute-start.11 = (bf16[784,128]{1,0:T(8,128)(2,1)S(1)}, bf16[784,128]{1,0:T(8,128)(2,1)S(1)}, u32[]{:S(2)}, u32[]{:S(2)}) collective-permute-start(bf16[784,128]{1,0:T(8,128)(2,1)S(1)} %collective-permute-done.10.refs_8_.refs_11_), channel_id=1, source_target_pairs={{8,0},{16,8},{24,16},{28,24},{20,28},{12,20},{4,12},{0,4},{9,1},{1... | collective-permute-start | bytes 602120 | tf_op jit(solution)/shard_map/ppermute | solution.py:423
  25.5 0.0 collective-permute-done.4.refs_2_
  25.5 0.0 collective-permute-start.5
  25.5 2.3 %collective-permute-done.18.refs_6_ = bf16[784,128]{1,0:T(8,128)(2,1)S(1)} collective-permute-done((bf16[784,128]{1,0:T(8,128)(2,1)S(1)}, bf16[784,128]{1,0:T(8,128)(2,1)S(1)}, u32[]{:S(2)}, u32[]{:S(2)}) %collective-permute-start.18) | collective-permute-done | bytes 200736 | tf_op jit(solution)/shard_map/ppermute | solution.py:426
  27.9 1.6 %collective-permute-start.15 = (bf16[784,128]{1,0:T(8,128)(2,1)S(1)}, bf16[784,128]{1,0:T(8,128)(2,1)S(1)}, u32[]{:S(2)}, u32[]{:S(2)}) collective-permute-start(bf16[784,128]{1,0:T(8,128)(2,1)S(1)} %collective-permute-done.14.refs_6_), channel_id=1, source_target_pairs={{0,8},{8,16},{16,24},{24,28},{28,20},{20,12},{12,4},{4,0},{1,9},{9... | collective-permute-start | bytes 602120 | tf_op jit(solution)/shard_map/ppermute | solution.py:425
  29.5 0.0 collective-permute-done.7.refs_4_.refs_12_
  29.5 1.6 %collective-permute-start.8 = (bf16[784,128]{1,0:T(8,128)(2,1)S(1)}, bf16[784,128]{1,0:T(8,128)(2,1)S(1)}, u32[]{:S(2)}, u32[]{:S(2)}) collective-permute-start(bf16[784,128]{1,0:T(8,128)(2,1)S(1)} %collective-permute-done.7.refs_4_.refs_12_), channel_id=1, source_target_pairs={{0,8},{8,16},{16,24},{24,28},{28,20},{20,12},{12,4},{4,0},{1,9},{9... | collective-permute-start | bytes 602120 | tf_op jit(solution)/shard_map/ppermute | solution.py:422
  31.0 0.0 collective-permute-done.11.refs_7_.refs_13_
  31.0 1.1 %collective-permute-start.12 = (bf16[784,128]{1,0:T(8,128)(2,1)S(1)}, bf16[784,128]{1,0:T(8,128)(2,1)S(1)}, u32[]{:S(2)}, u32[]{:S(2)}) collective-permute-start(bf16[784,128]{1,0:T(8,128)(2,1)S(1)} %collective-permute-done.11.refs_7_.refs_13_), channel_id=1, source_target_pairs={{8,0},{16,8},{24,16},{28,24},{20,28},{12,20},{4,12},{0,4},{9,1},{1... | collective-permute-start | bytes 602120 | tf_op jit(solution)/shard_map/ppermute | solution.py:423
  32.2 3.3 %collective-permute-done.15.refs_5_ = bf16[784,128]{1,0:T(8,128)(2,1)S(1)} collective-permute-done((bf16[784,128]{1,0:T(8,128)(2,1)S(1)}, bf16[784,128]{1,0:T(8,128)(2,1)S(1)}, u32[]{:S(2)}, u32[]{:S(2)}) %collective-permute-start.15) | collective-permute-done | bytes 200736 | tf_op jit(solution)/shard_map/ppermute | solution.py:425
  35.5 3.5 %collective-permute-start.20 = (bf16[16,128]{1,0:T(8,128)(2,1)S(1)}, bf16[16,128]{1,0:T(8,128)(2,1)S(1)}, u32[]{:S(2)}, u32[]{:S(2)}) collective-permute-start(bf16[16,128]{1,0:T(8,128)(2,1)S(1)} %get-tuple-element.16.refs_8_), channel_id=1, source_target_pairs={{0,28},{8,20},{16,12},{24,4},{28,0},{20,8},{12,16},{4,24},{1,29},{... | collective-permute-start | bytes 12296 | tf_op jit(solution)/shard_map/ppermute | solution.py:435
  39.0 0.0 collective-permute-done.3.refs_1_
  39.0 0.5 collective-permute-start.19
  39.5 0.0 collective-permute-done.8.refs_4_.refs_14_
  39.5 1.6 %collective-permute-start.16 = (bf16[784,128]{1,0:T(8,128)(2,1)S(1)}, bf16[784,128]{1,0:T(8,128)(2,1)S(1)}, u32[]{:S(2)}, u32[]{:S(2)}) collective-permute-start(bf16[784,128]{1,0:T(8,128)(2,1)S(1)} %collective-permute-done.15.refs_5_), channel_id=1, source_target_pairs={{0,8},{8,16},{16,24},{24,28},{28,20},{20,12},{12,4},{4,0},{1,9},{9... | collective-permute-start | bytes 602120 | tf_op jit(solution)/shard_map/ppermute | solution.py:425
  41.0 0.0 collective-permute-done.12.refs_7_.refs_15_
  41.0 0.7 %collective-permute-start.9 = (bf16[784,128]{1,0:T(8,128)(2,1)S(1)}, bf16[784,128]{1,0:T(8,128)(2,1)S(1)}, u32[]{:S(2)}, u32[]{:S(2)}) collective-permute-start(bf16[784,128]{1,0:T(8,128)(2,1)S(1)} %collective-permute-done.8.refs_4_.refs_14_), channel_id=1, source_target_pairs={{0,8},{8,16},{16,24},{24,28},{28,20},{20,12},{12,4},{4,0},{1,9},{9... | collective-permute-start | bytes 602120 | tf_op jit(solution)/shard_map/ppermute | solution.py:422
  41.7 0.0 collective-permute-done.5.refs_3_
  41.7 1.4 %collective-permute-start.13 = (bf16[784,128]{1,0:T(8,128)(2,1)S(1)}, bf16[784,128]{1,0:T(8,128)(2,1)S(1)}, u32[]{:S(2)}, u32[]{:S(2)}) collective-permute-start(bf16[784,128]{1,0:T(8,128)(2,1)S(1)} %collective-permute-done.12.refs_7_.refs_15_), channel_id=1, source_target_pairs={{8,0},{16,8},{24,16},{28,24},{20,28},{12,20},{4,12},{0,4},{9,1},{1... | collective-permute-start | bytes 602120 | tf_op jit(solution)/shard_map/ppermute | solution.py:423
  43.1 5.0 %shard_map.49 = (f32[512,1024]{1,0:T(8,128)S(1)}, bf16[4,36,128,128]{3,2,1,0:T(8,128)(2,1)}) custom-call(bf16[1568,128]{1,0:T(8,128)(2,1)S(1)} %get-tuple-element.13.refs_0_.refs_4_, bf16[1568,128]{1,0:T(8,128)(2,1)S(1)} %collective-permute-done.3.refs_1_, bf16[1568,128]{1,0:T(8,128)(2,1)S(1)} %collective-permute-done.4.refs_2_, ...), custom_call_target="tpu_custom_call" | custom-call | flops 1610612736 | bytes 4000000 | tf_op jit(solution)/shard_map/pallas_call | solution.py:310
  48.0 2.7 %shard_map.50.refs_16_ = f32[512,1024]{1,0:T(8,128)S(1)} custom-call(bf16[1568,128]{1,0:T(8,128)(2,1)S(1)} %get-tuple-element.13.refs_0_.refs_4_, bf16[1568,128]{1,0:T(8,128)(2,1)S(1)} %collective-permute-done.3.refs_1_, bf16[1568,128]{1,0:T(8,128)(2,1)S(1)} %collective-permute-done.4.refs_2_, ...), custom_call_target="tpu_custom_call", output_to_operand_aliasing={{}: (8, {})} | custom-call | flops 1073741824 | bytes 4000000 | tf_op jit(solution)/shard_map/pallas_call | solution.py:310
  50.7 0.0 collective-permute-done.19.refs_6_
  50.7 0.0 collective-permute-done.16.refs_5_
  50.8 5.3 %shard_map.51 = (f32[512,1024]{1,0:T(8,128)S(1)}, s32[32]{0:T(128)S(1)}, s32[4,1,36]{2,1,0:T(1,128)}, s32[1,4]{1,0:T(1,128)}) custom-call(bf16[1568,128]{1,0:T(8,128)(2,1)S(1)} %get-tuple-element.13.refs_0_.refs_4_, bf16[1568,128]{1,0:T(8,128)(2,1)S(1)} %collective-permute-done.3.refs_1_, ...), custom_call_target="tpu_custom_call", output_to_operand_aliasing={{0}: (16, {})} | custom-call | flops 1073741824 | bytes 4000000 | tf_op jit(solution)/shard_map/pallas_call | solution.py:310
  56.1 0.0 collective-permute-done.9.refs_4_
  56.1 0.0 collective-permute-done.13.refs_5_
  56.1 3.0 %shard_map.52 = bf16[4,36,128,128]{3,2,1,0:T(8,128)(2,1)} custom-call(bf16[1568,128]{1,0:T(8,128)(2,1)S(1)} %get-tuple-element.13.refs_0_.refs_4_, bf16[1568,128]{1,0:T(8,128)(2,1)S(1)} %collective-permute-done.3.refs_1_, bf16[1568,128]{1,0:T(8,128)(2,1)S(1)} %collective-permute-done.4.refs_2_, ...), custom_call_target="tpu_custom_call", output_to_operand_aliasing={{}: (8, {})} | custom-call | flops 536870912 | bytes 4000000 | tf_op jit(solution)/shard_map/pallas_call | solution.py:325
  (3 shorter events, 0.0 us)
Async XLA Ops:
  0.6 3.2 %collective-permute-start = (s32[4,1,3]{0,1,2:T(1,128)}, s32[4,1,3]{0,1,2:T(1,128)S(1)}, u32[]{:S(2)}, u32[]{:S(2)}) collective-permute-start(s32[4,1,3]{0,1,2:T(1,128)} %param.3), channel_id=1, source_target_pairs={{0,1},{1,0},{2,3},{3,2},{4,5},{5,4},{6,7},{7,6},{8,9},{9,8},{10,11... | collective-permute-start | bytes 152 | tf_op jit(solution)/shard_map/ppermute | solution.py:342
  1.2 4.1 %collective-permute-start.2 = (s32[4,1,3]{0,1,2:T(1,128)}, s32[4,1,3]{0,1,2:T(1,128)S(1)}, u32[]{:S(2)}, u32[]{:S(2)}) collective-permute-start(s32[4,1,3]{0,1,2:T(1,128)} %param.3), channel_id=1, source_target_pairs={{0,3},{1,2},{2,1},{3,0},{4,7},{5,6},{6,5},{7,4},{8,11},{9,10},{10,... | collective-permute-start | bytes 152 | tf_op jit(solution)/shard_map/ppermute | solution.py:342
  3.8 3.8 %collective-permute-start.1 = (s32[4,1,3]{0,1,2:T(1,128)}, s32[4,1,3]{0,1,2:T(1,128)S(1)}, u32[]{:S(2)}, u32[]{:S(2)}) collective-permute-start(s32[4,1,3]{0,1,2:T(1,128)} %param.3), channel_id=1, source_target_pairs={{0,2},{1,3},{2,0},{3,1},{4,6},{5,7},{6,4},{7,5},{8,10},{9,11},{10,... | collective-permute-start | bytes 152 | tf_op jit(solution)/shard_map/ppermute | solution.py:342
  7.6 1.0 %copy-start = (bf16[4,1,3,128,128]{4,3,2,1,0:T(8,128)(2,1)S(1)}, bf16[4,1,3,128,128]{4,3,2,1,0:T(8,128)(2,1)}, u32[]{:S(2)}) copy-start(bf16[4,1,3,128,128]{4,3,2,1,0:T(8,128)(2,1)} %param.2) | copy-start | bytes 1179652
  8.6 0.7 %copy-start.1 = (s32[4,1,3]{0,1,2:T(1,128)S(1)}, s32[4,1,3]{0,1,2:T(1,128)}, u32[]{:S(2)}) copy-start(s32[4,1,3]{0,1,2:T(1,128)} %param.3) | copy-start | bytes 148
  11.2 14.3 %collective-permute-start.4 = (bf16[1568,128]{1,0:T(8,128)(2,1)S(1)}, bf16[1568,128]{1,0:T(8,128)(2,1)S(1)}, u32[]{:S(2)}, u32[]{:S(2)}) collective-permute-start(bf16[1568,128]{1,0:T(8,128)(2,1)S(1)} %get-tuple-element.13.refs_0_.refs_4_), channel_id=1, source_target_pairs={{0,2},{1,3},{2,0},{3,1},{4,6},{5,7},{6,4},{7,5},{8,10},{9,11},{10,... | collective-permute-start | bytes 1204232 | tf_op jit(solution)/shard_map/ppermute | solution.py:342
  11.4 7.9 %collective-permute-start.17 = (bf16[784,128]{1,0:T(8,128)(2,1)S(1)}, bf16[784,128]{1,0:T(8,128)(2,1)S(1)}, u32[]{:S(2)}, u32[]{:S(2)}) collective-permute-start(bf16[784,128]{1,0:T(8,128)(2,1)S(1)} %get-tuple-element.14), channel_id=1, source_target_pairs={{8,0},{16,8},{24,16},{28,24},{20,28},{12,20},{4,12},{0,4},{9,1},{1... | collective-permute-start | bytes 602120 | tf_op jit(solution)/shard_map/ppermute | solution.py:426
  13.4 7.9 %collective-permute-start.6 = (bf16[784,128]{1,0:T(8,128)(2,1)S(1)}, bf16[784,128]{1,0:T(8,128)(2,1)S(1)}, u32[]{:S(2)}, u32[]{:S(2)}) collective-permute-start(bf16[784,128]{1,0:T(8,128)(2,1)S(1)} %get-tuple-element.14), channel_id=1, source_target_pairs={{0,8},{8,16},{16,24},{24,28},{28,20},{20,12},{12,4},{4,0},{1,9},{9... | collective-permute-start | bytes 602120 | tf_op jit(solution)/shard_map/ppermute | solution.py:422
  13.4 9.9 %collective-permute-start.14 = (bf16[784,128]{1,0:T(8,128)(2,1)S(1)}, bf16[784,128]{1,0:T(8,128)(2,1)S(1)}, u32[]{:S(2)}, u32[]{:S(2)}) collective-permute-start(bf16[784,128]{1,0:T(8,128)(2,1)S(1)} %get-tuple-element.15), channel_id=1, source_target_pairs={{0,8},{8,16},{16,24},{24,28},{28,20},{20,12},{12,4},{4,0},{1,9},{9... | collective-permute-start | bytes 602120 | tf_op jit(solution)/shard_map/ppermute | solution.py:425
  15.4 8.4 %collective-permute-start.10 = (bf16[784,128]{1,0:T(8,128)(2,1)S(1)}, bf16[784,128]{1,0:T(8,128)(2,1)S(1)}, u32[]{:S(2)}, u32[]{:S(2)}) collective-permute-start(bf16[784,128]{1,0:T(8,128)(2,1)S(1)} %get-tuple-element.15), channel_id=1, source_target_pairs={{8,0},{16,8},{24,16},{28,24},{20,28},{12,20},{4,12},{0,4},{9,1},{1... | collective-permute-start | bytes 602120 | tf_op jit(solution)/shard_map/ppermute | solution.py:423
  19.3 8.6 %collective-permute-start.18 = (bf16[784,128]{1,0:T(8,128)(2,1)S(1)}, bf16[784,128]{1,0:T(8,128)(2,1)S(1)}, u32[]{:S(2)}, u32[]{:S(2)}) collective-permute-start(bf16[784,128]{1,0:T(8,128)(2,1)S(1)} %collective-permute-done.17.refs_7_), channel_id=1, source_target_pairs={{8,0},{16,8},{24,16},{28,24},{20,28},{12,20},{4,12},{0,4},{9,1},{1... | collective-permute-start | bytes 602120 | tf_op jit(solution)/shard_map/ppermute | solution.py:426
  21.2 17.8 %collective-permute-start.3 = (bf16[1568,128]{1,0:T(8,128)(2,1)S(1)}, bf16[1568,128]{1,0:T(8,128)(2,1)S(1)}, u32[]{:S(2)}, u32[]{:S(2)}) collective-permute-start(bf16[1568,128]{1,0:T(8,128)(2,1)S(1)} %get-tuple-element.13.refs_0_.refs_4_), channel_id=1, source_target_pairs={{0,1},{1,0},{2,3},{3,2},{4,5},{5,4},{6,7},{7,6},{8,9},{9,8},{10,11... | collective-permute-start | bytes 1204232 | tf_op jit(solution)/shard_map/ppermute | solution.py:342
  23.3 6.2 %collective-permute-start.7 = (bf16[784,128]{1,0:T(8,128)(2,1)S(1)}, bf16[784,128]{1,0:T(8,128)(2,1)S(1)}, u32[]{:S(2)}, u32[]{:S(2)}) collective-permute-start(bf16[784,128]{1,0:T(8,128)(2,1)S(1)} %collective-permute-done.6.refs_5_.refs_10_), channel_id=1, source_target_pairs={{0,8},{8,16},{16,24},{24,28},{28,20},{20,12},{12,4},{4,0},{1,9},{9... | collective-permute-start | bytes 602120 | tf_op jit(solution)/shard_map/ppermute | solution.py:422
  23.8 7.2 %collective-permute-start.11 = (bf16[784,128]{1,0:T(8,128)(2,1)S(1)}, bf16[784,128]{1,0:T(8,128)(2,1)S(1)}, u32[]{:S(2)}, u32[]{:S(2)}) collective-permute-start(bf16[784,128]{1,0:T(8,128)(2,1)S(1)} %collective-permute-done.10.refs_8_.refs_11_), channel_id=1, source_target_pairs={{8,0},{16,8},{24,16},{28,24},{20,28},{12,20},{4,12},{0,4},{9,1},{1... | collective-permute-start | bytes 602120 | tf_op jit(solution)/shard_map/ppermute | solution.py:423
  25.5 16.2 %collective-permute-start.5 = (bf16[1568,128]{1,0:T(8,128)(2,1)S(1)}, bf16[1568,128]{1,0:T(8,128)(2,1)S(1)}, u32[]{:S(2)}, u32[]{:S(2)}) collective-permute-start(bf16[1568,128]{1,0:T(8,128)(2,1)S(1)} %collective-permute-done.4.refs_2_), channel_id=1, source_target_pairs={{0,1},{1,0},{2,3},{3,2},{4,5},{5,4},{6,7},{7,6},{8,9},{9,8},{10,11... | collective-permute-start | bytes 1204232 | tf_op jit(solution)/shard_map/ppermute | solution.py:342
  27.9 7.6 %collective-permute-start.15 = (bf16[784,128]{1,0:T(8,128)(2,1)S(1)}, bf16[784,128]{1,0:T(8,128)(2,1)S(1)}, u32[]{:S(2)}, u32[]{:S(2)}) collective-permute-start(bf16[784,128]{1,0:T(8,128)(2,1)S(1)} %collective-permute-done.14.refs_6_), channel_id=1, source_target_pairs={{0,8},{8,16},{16,24},{24,28},{28,20},{20,12},{12,4},{4,0},{1,9},{9... | collective-permute-start | bytes 602120 | tf_op jit(solution)/shard_map/ppermute | solution.py:425
  29.5 10.0 %collective-permute-start.8 = (bf16[784,128]{1,0:T(8,128)(2,1)S(1)}, bf16[784,128]{1,0:T(8,128)(2,1)S(1)}, u32[]{:S(2)}, u32[]{:S(2)}) collective-permute-start(bf16[784,128]{1,0:T(8,128)(2,1)S(1)} %collective-permute-done.7.refs_4_.refs_12_), channel_id=1, source_target_pairs={{0,8},{8,16},{16,24},{24,28},{28,20},{20,12},{12,4},{4,0},{1,9},{9... | collective-permute-start | bytes 602120 | tf_op jit(solution)/shard_map/ppermute | solution.py:422
  31.0 10.0 %collective-permute-start.12 = (bf16[784,128]{1,0:T(8,128)(2,1)S(1)}, bf16[784,128]{1,0:T(8,128)(2,1)S(1)}, u32[]{:S(2)}, u32[]{:S(2)}) collective-permute-start(bf16[784,128]{1,0:T(8,128)(2,1)S(1)} %collective-permute-done.11.refs_7_.refs_13_), channel_id=1, source_target_pairs={{8,0},{16,8},{24,16},{28,24},{20,28},{12,20},{4,12},{0,4},{9,1},{1... | collective-permute-start | bytes 602120 | tf_op jit(solution)/shard_map/ppermute | solution.py:423
  35.5 15.3 %collective-permute-start.20 = (bf16[16,128]{1,0:T(8,128)(2,1)S(1)}, bf16[16,128]{1,0:T(8,128)(2,1)S(1)}, u32[]{:S(2)}, u32[]{:S(2)}) collective-permute-start(bf16[16,128]{1,0:T(8,128)(2,1)S(1)} %get-tuple-element.16.refs_8_), channel_id=1, source_target_pairs={{0,28},{8,20},{16,12},{24,4},{28,0},{20,8},{12,16},{4,24},{1,29},{... | collective-permute-start | bytes 12296 | tf_op jit(solution)/shard_map/ppermute | solution.py:435
  39.0 11.7 %collective-permute-start.19 = (bf16[784,128]{1,0:T(8,128)(2,1)S(1)}, bf16[784,128]{1,0:T(8,128)(2,1)S(1)}, u32[]{:S(2)}, u32[]{:S(2)}) collective-permute-start(bf16[784,128]{1,0:T(8,128)(2,1)S(1)} %collective-permute-done.18.refs_6_), channel_id=1, source_target_pairs={{8,0},{16,8},{24,16},{28,24},{20,28},{12,20},{4,12},{0,4},{9,1},{1... | collective-permute-start | bytes 602120 | tf_op jit(solution)/shard_map/ppermute | solution.py:426
  39.5 11.3 %collective-permute-start.16 = (bf16[784,128]{1,0:T(8,128)(2,1)S(1)}, bf16[784,128]{1,0:T(8,128)(2,1)S(1)}, u32[]{:S(2)}, u32[]{:S(2)}) collective-permute-start(bf16[784,128]{1,0:T(8,128)(2,1)S(1)} %collective-permute-done.15.refs_5_), channel_id=1, source_target_pairs={{0,8},{8,16},{16,24},{24,28},{28,20},{20,12},{12,4},{4,0},{1,9},{9... | collective-permute-start | bytes 602120 | tf_op jit(solution)/shard_map/ppermute | solution.py:425
  41.0 15.1 %collective-permute-start.9 = (bf16[784,128]{1,0:T(8,128)(2,1)S(1)}, bf16[784,128]{1,0:T(8,128)(2,1)S(1)}, u32[]{:S(2)}, u32[]{:S(2)}) collective-permute-start(bf16[784,128]{1,0:T(8,128)(2,1)S(1)} %collective-permute-done.8.refs_4_.refs_14_), channel_id=1, source_target_pairs={{0,8},{8,16},{16,24},{24,28},{28,20},{20,12},{12,4},{4,0},{1,9},{9... | collective-permute-start | bytes 602120 | tf_op jit(solution)/shard_map/ppermute | solution.py:422
  41.7 14.4 %collective-permute-start.13 = (bf16[784,128]{1,0:T(8,128)(2,1)S(1)}, bf16[784,128]{1,0:T(8,128)(2,1)S(1)}, u32[]{:S(2)}, u32[]{:S(2)}) collective-permute-start(bf16[784,128]{1,0:T(8,128)(2,1)S(1)} %collective-permute-done.12.refs_7_.refs_15_), channel_id=1, source_target_pairs={{8,0},{16,8},{24,16},{28,24},{20,28},{12,20},{4,12},{0,4},{9,1},{1... | collective-permute-start | bytes 602120 | tf_op jit(solution)/shard_map/ppermute | solution.py:423

commit v5 on v4

--- a/solution.py
+++ b/solution.py
@@ -15,7 +15,6 @@
 VMEM = pl.BlockSpec(memory_space=pltpu.VMEM)
 SMEM = pl.BlockSpec(memory_space=pltpu.SMEM)
 ANY = pl.BlockSpec(memory_space=pl.ANY)
-HBM = pl.BlockSpec(memory_space=pltpu.HBM)
 GRANT = 12 * 1024 * 1024
 
 
@@ -53,47 +52,60 @@
     return jnp.concatenate([tile] * (rows // 16), axis=0)
 
 
-def prep_kernel(dims, *refs):
-    refs = list(refs)
-    cols = take(refs, dims.groups)
-    blocks_ref, full_ref, a_ref, b_ref, tile_ref, sems = refs
+def prep_kernel(dims, blocks_ref, a_ref, b_ref, sems):
     me = lax.axis_index("cols").astype(jnp.int32)
     span = dims.per_group * dims.bs
     copies = []
     for j in range(dims.groups):
-        at = dims.at(j, 0)
-        ref, start = (a_ref, at) if at < dims.half else (b_ref, at - dims.half - IDX)
-        for k, (out_ref, first) in enumerate(((ref, start), (full_ref, at))):
-            copy = pltpu.make_async_copy(
-                blocks_ref.at[pl.ds((me ^ j) * span, span)], out_ref.at[first : first + span], sems.at[j, k]
-            )
-            copy.start()
-            copies.append(copy)
+        at = j * span
+        ref, start = (a_ref, at) if at < dims.half else (b_ref, at - dims.half)
+        copy = pltpu.make_async_copy(
+            blocks_ref.at[pl.ds((me ^ j) * span, span)], ref.at[start : start + span], sems.at[j]
+        )
+        copy.start()
+        copies.append(copy)
+    for copy in copies:
+        copy.wait()
+
+
+def number_kernel(dims, *refs):
+    refs = list(refs)
+    names = take(refs, dims.groups)
+    a_ref, b_ref, full_ref, a_out, b_out, tile_ref, cols_ref, sems = refs
+    copies = []
+    for j in range(dims.groups):
+        copies.append(pltpu.make_async_copy(names[j], cols_ref.at[j], sems.at[j]))
+        copies[-1].start()
+    half = dims.half
+    for ref, out_ref, at in ((a_ref, a_out, 0), (b_ref, b_out, half + IDX)):
+        value = ref[...]
+        out_ref[0:half, :] = value
+        full_ref[at : at + half, :] = value
+    me = lax.axis_index("cols").astype(jnp.int32)
     line = lax.broadcasted_iota(jnp.int32, (IDX, 128), 0)
     lane = lax.broadcasted_iota(jnp.int32, (IDX, 128), 1)
     tile = jnp.zeros((IDX, 128), jnp.int32)
+    for copy in copies:
+        copy.wait()
     for j in range(dims.groups):
         row = jnp.zeros((IDX, 128), jnp.int32)
         for r in range(dims.groups):
             for s in range(dims.per_group):
-                number = cols[j][s, 0, me ^ j ^ r] // dims.groups
-                row = jnp.where(lane == r * dims.per_group + s, number, row)
+                row = jnp.where(lane == r * dims.per_group + s, cols_ref[j, s, 0, me ^ j ^ r], row)
         tile = jnp.where(line == j, row, tile)
-    numbers = tile.astype(jnp.float32).astype(jnp.bfloat16)
+    numbers = (tile // dims.groups).astype(jnp.float32).astype(jnp.bfloat16)
     tile_ref[...] = numbers
-    for ref in (a_ref, b_ref):
-        ref[dims.half : dims.half + IDX, :] = numbers
-    for at in (dims.half, 2 * dims.half + IDX):
+    for ref in (a_out, b_out):
+        ref[half : half + IDX, :] = numbers
+    for at in (half, 2 * half + IDX):
         full_ref[at : at + IDX, :] = numbers
-    for copy in copies:
-        copy.wait()
 
 
 def accumulate(dims, pieces, left, lp_ref, d_ref, emit):
     groups, per_group, bs, bins = dims.groups, dims.per_group, dims.bs, dims.bins
     depth = dims.rows
     lrows = [ref[dims.half : dims.half + 16, :].astype(jnp.float32)[0:1, :] for ref in left]
-    for n, (distance, _, _) in enumerate(pieces):
+    for n, (distance, *_) in enumerate(pieces):
         number = panel_number(dims, distance).astype(jnp.float32)
         for j in range(groups):
             hits = jnp.where(lrows[j] == number, 1.0, 0.0)
@@ -107,15 +119,15 @@
                     total = term if total is None else total + term
                 lp_ref[m * bs : (m + 1) * bs, n * depth + j * bs : n * depth + (j + 1) * bs] = total
     rows_of = []
-    for _, ref, _ in pieces:
-        row = ref[dims.half : dims.half + 16, :].astype(jnp.float32)[0:1, :]
+    for *_, ref, at in pieces:
+        row = ref[at : at + 16, :].astype(jnp.float32)[0:1, :]
         if dims.bins < dims.cycle:
             row = row - first_bin(dims).astype(jnp.float32)
             row = jnp.where(row < 0, row + float(dims.cycle), row)
         rows_of.append(row)
     for first in range(0, bins, 2):
         chunk = range(first, min(first + 2, bins))
-        for n, (_, a_ref, b_ref) in enumerate(pieces):
+        for n, (_, a_ref, b_ref, _, _) in enumerate(pieces):
             for b in chunk:
                 hits = jnp.where(rows_of[n] == float(b), 1.0, 0.0)
                 for j in range(groups):
@@ -139,46 +151,42 @@
     return [refs.pop(0) for _ in range(count)]
 
 
-def take_pieces(refs, layout):
+def take_pieces(dims, refs, layout):
     pieces = []
-    for distance, two in layout:
-        pieces.append((distance, refs.pop(0), refs.pop(0) if two else None))
+    for distance, two, where in layout:
+        a_ref = refs.pop(0)
+        b_ref = refs.pop(0) if two else None
+        if where == "far":
+            source, at = refs.pop(0), 0
+        else:
+            source, at = (b_ref if where == "b" else a_ref), dims.half
+        pieces.append((distance, a_ref, b_ref, source, at))
     return pieces
 
 
-def step_kernel(dims, layout, with_acc, with_zero, tiles, *refs):
+def step_kernel(dims, layout, with_acc, blank_rows, tiles, *refs):
     refs = list(refs)
     left = take(refs, dims.groups)
-    pieces = take_pieces(refs, layout)
+    pieces = take_pieces(dims, refs, layout)
     tile_refs = take(refs, len(tiles))
-    acc_ref = refs.pop(0) if with_acc else None
-    out_ref = refs.pop(0)
-    zero_ref = refs.pop(0) if with_zero else None
+    acc_ref = None
+    if with_acc:
+        acc_ref, _ = take(refs, 2)
+    out_ref, zero_ref = take(refs, 2)
     index_refs = take(refs, 3) if tiles else None
-    lp_ref, d_ref = take(refs, 2)
+    lp_ref, d_ref, blank_ref, sems = take(refs, 4)
+    blank_ref[...] = jnp.zeros_like(blank_ref)
     copies = []
-    if with_zero:
-        blank_ref, sems = refs
-        blank_ref[...] = jnp.zeros_like(blank_ref)
-        for i in range(zero_ref.shape[0]):
-            copy = pltpu.make_async_copy(
-                blank_ref, zero_ref.at[i, dims.bins : dims.slots], sems.at[i]
-            )
-            copy.start()
-            copies.append(copy)
+    for i in blank_rows:
+        copy = pltpu.make_async_copy(blank_ref, zero_ref.at[i, dims.bins : dims.slots], sems.at[i])
+        copy.start()
+        copies.append(copy)
     if tiles:
-        wide_ref, known_ref, mask_ref, count_ref, sem = refs
-        for k, (n, at) in enumerate(tiles):
-            tile = tile_refs[k][at : at + IDX, :].astype(jnp.float32).astype(jnp.int32)
-            wide_ref[n * 8 : (n + 1) * 8, :] = tile[:8]
-        known = pltpu.make_async_copy(wide_ref, known_ref, sem)
-        known.start()
+        wide_ref, count_ref = refs
+        index_work(dims, tiles, tile_refs, wide_ref, *index_refs, count_ref)
 
     def emit(lo, hi, value):
         out_ref[:, lo:hi] = value if acc_ref is None else acc_ref[:, lo:hi] + value
-        if tiles and lo == 0:
-            known.wait()
-            index_work(dims, known_ref, *index_refs, mask_ref, count_ref)
 
     accumulate(dims, pieces, left, lp_ref, d_ref, emit)
     for copy in copies:
@@ -188,7 +196,7 @@
 def last_kernel(dims, layout, *refs):
     refs = list(refs)
     left = take(refs, dims.groups)
-    pieces = take_pieces(refs, layout)
+    pieces = take_pieces(dims, refs, layout)
     acc_ref, slot_ref, _, out_ref, lp_ref, d_ref, stage_ref, sems = refs
     groups, bs, bins = dims.groups, dims.bs, dims.bins
     me = lax.axis_index("cols").astype(jnp.int32)
@@ -212,41 +220,50 @@
         copy.wait()
 
 
-def index_work(dims, known_ref, slot_ref, cols_ref, start_ref, mask_ref, count_ref):
+def index_work(dims, tiles, tile_refs, wide_ref, slot_ref, cols_ref, start_ref, count_ref):
     groups, per_group, bins, cycle = dims.groups, dims.per_group, dims.bins, dims.cycle
     p = lax.axis_index("rows").astype(jnp.int32)
     c = lax.axis_index("cols").astype(jnp.int32)
-    number = [panel_number(dims, n if n <= HP else n - cycle) for n in range(cycle)]
-    for n in range(cycle):
-        for r in range(groups):
-            bits = jnp.int32(0)
-            for s in range(per_group):
-                bits = bits | (jnp.int32(1) << known_ref[n * 8, r * per_group + s])
-            mask_ref[number[n] * groups + r] = bits
-    earlier = jnp.int32(0)
-    for n in range(cycle):
-        total = jnp.int32(0)
-        for m in range(groups):
-            bits = jnp.int32(0)
-            for j in range(groups):
-                for t in range(per_group):
-                    k = known_ref[n * 8 + j, (m ^ j) * per_group + t]
-                    bits = bits | mask_ref[k * groups + j]
-            count = jnp.int32(0)
-            for b in range(bins):
-                count = count + ((bits >> b) & 1)
-            total = total + count
-            if n == 0:
-                count_ref[m ^ c] = count
-                used = jnp.int32(0)
-                for b in range(bins):
-                    one = (bits >> b) & 1
-                    slot = jnp.where(one == 1, used, count + b - used)
-                    slot_ref[m * bins + b] = slot
-                    cols_ref[m ^ c, 0, slot] = jnp.where(one == 1, b * groups + c, -1)
-                    used = used + one
-        if n > 0:
-            earlier = earlier + jnp.where(number[n] < p, total, 0)
+    for (n, at), ref in zip(tiles, tile_refs):
+        tile = ref[at : at + IDX, :].astype(jnp.float32).astype(jnp.int32)
+        for j in range(groups):
+            wide_ref[j * cycle + n : j * cycle + n + 1, :] = tile[j : j + 1]
+    held = [wide_ref[j * cycle : (j + 1) * cycle, :] for j in range(groups)]
+    bit = jnp.int32(1) << held[0]
+    found = []
+    for j in range(groups):
+        lanes = range(j * per_group, (j + 1) * per_group)
+        union = functools.reduce(jnp.bitwise_or, [bit[:, k : k + 1] for k in lanes])
+        union = jnp.broadcast_to(union, (cycle, 128))
+        look = jnp.zeros((cycle, 128), jnp.int32)
+        for n in range(cycle):
+            row = jnp.broadcast_to(union[n : n + 1, :], (cycle, 128))
+            look = jnp.where(held[j] == panel_number(dims, n), row, look)
+        found.append(look)
+    panels = panel_number(dims, lax.broadcasted_iota(jnp.int32, (cycle, 1), 0))
+    total = jnp.zeros((cycle, 1), jnp.int32)
+    for m in range(groups):
+        picks = []
+        for j in range(groups):
+            for t in range(per_group):
+                lane = (m ^ j) * per_group + t
+                picks.append(found[j][:, lane : lane + 1])
+        bits = functools.reduce(jnp.bitwise_or, picks)
+        for b in range(bins):
+            total = total + ((bits >> b) & 1)
+        mine = bits[0, 0]
+        count = jnp.int32(0)
+        for b in range(bins):
+            count = count + ((mine >> b) & 1)
+        count_ref[m ^ c] = count
+        used = jnp.int32(0)
+        for b in range(bins):
+            one = (mine >> b) & 1
+            slot = jnp.where(one == 1, used, count + b - used)
+            slot_ref[m * bins + b] = slot
+            cols_ref[m ^ c, 0, slot] = jnp.where(one == 1, b * groups + c, -1)
+            used = used + one
+    earlier = jnp.sum(jnp.where(panels < p, total, 0))
     for i in range(groups):
         start_ref[0, i] = earlier
         earlier = earlier + count_ref[i]
@@ -255,8 +272,11 @@
 
 
 def flat(panels):
-    layout = [(distance, second is not None) for distance, _, second in panels]
-    arrays = [x for _, first, second in panels for x in (first, second) if x is not None]
+    layout, arrays = [], []
+    for distance, first, second, where in panels:
+        two = second is not None
+        layout.append((distance, two, where if isinstance(where, str) else "far"))
+        arrays += [first] + [second] * two + [where] * (not isinstance(where, str))
     return layout, arrays
 
 
@@ -273,45 +293,41 @@
     return pl.CostEstimate(flops=flops, bytes_accessed=4_000_000, transcendentals=0)
 
 
-def call_step(dims, left, panels, acc, zero=False, tiles=()):
+def call_step(dims, left, panels, carry, blank_rows, tiles=()):
     layout, arrays = flat(panels)
     args = [*left, *arrays, *(array for _, array, _ in tiles)]
+    specs = [VMEM] * len(args)
     aliases = {}
-    if acc is not None:
-        aliases = {len(args): 0}
-        args.append(acc)
-    shapes = [jax.ShapeDtypeStruct((dims.rows, dims.bins * dims.bs), jnp.float32)]
-    specs = [VMEM]
-    scratch = scratch_of(dims, panels)
-    if zero:
-        shapes.append(
-            jax.ShapeDtypeStruct((dims.groups, dims.slots, dims.bs, dims.bs), jnp.bfloat16)
-        )
-        specs.append(ANY)
-        scratch += [
-            pltpu.VMEM((dims.slots - dims.bins, dims.bs, dims.bs), jnp.bfloat16),
-            pltpu.SemaphoreType.DMA((dims.groups,)),
-        ]
+    if carry is not None:
+        aliases = {len(args): 0, len(args) + 1: 1}
+        args += carry
+        specs += [VMEM, ANY]
+    shapes = [
+        jax.ShapeDtypeStruct((dims.rows, dims.bins * dims.bs), jnp.float32),
+        jax.ShapeDtypeStruct((dims.groups, dims.slots, dims.bs, dims.bs), jnp.bfloat16),
+    ]
+    out_specs = [VMEM, ANY]
+    scratch = scratch_of(dims, panels) + [
+        pltpu.VMEM((dims.slots - dims.bins, dims.bs, dims.bs), jnp.bfloat16),
+        pltpu.SemaphoreType.DMA((dims.groups,)),
+    ]
     if tiles:
         shapes += [
             jax.ShapeDtypeStruct((dims.groups * dims.bins,), jnp.int32),
             jax.ShapeDtypeStruct((dims.groups, 1, dims.slots), jnp.int32),
             jax.ShapeDtypeStruct((1, dims.groups), jnp.int32),
         ]
-        specs += [SMEM] * 3
+        out_specs += [SMEM] * 3
         scratch += [
-            pltpu.VMEM((dims.cycle * 8, 128), jnp.int32),
-            pltpu.SMEM((dims.cycle * 8, 128), jnp.int32),
-            pltpu.SMEM((dims.cycle * dims.groups,), jnp.int32),
+            pltpu.VMEM((dims.groups * dims.cycle, 128), jnp.int32),
             pltpu.SMEM((dims.groups,), jnp.int32),
-            pltpu.SemaphoreType.DMA,
         ]
     marks = tuple((n, at) for n, _, at in tiles)
     return pl.pallas_call(
-        functools.partial(step_kernel, dims, layout, acc is not None, zero, marks),
+        functools.partial(step_kernel, dims, layout, carry is not None, tuple(blank_rows), marks),
         out_shape=shapes,
-        in_specs=[VMEM] * len(args),
-        out_specs=specs,
+        in_specs=specs,
+        out_specs=out_specs,
         scratch_shapes=scratch,
         input_output_aliases=aliases,
         compiler_params=pltpu.CompilerParams(vmem_limit_bytes=GRANT),
@@ -404,20 +420,36 @@
     def payload(rows):
         return jax.ShapeDtypeStruct((rows, bs), jnp.bfloat16)
 
+    params = pltpu.CompilerParams(vmem_limit_bytes=GRANT)
     cols = [block_cols] + [xor_move(block_cols, "cols", j) for j in range(1, groups)]
+    cols = [jnp.transpose(x, (2, 1, 0)) for x in cols]
+    cols[0] = pltpu.with_memory_space_constraint(cols[0], pltpu.HBM)
+    flat_blocks = pltpu.with_memory_space_constraint(blocks.reshape(-1, bs), pltpu.HBM)
+    bare_a, bare_b = pl.pallas_call(
+        functools.partial(prep_kernel, dims),
+        out_shape=[payload(dims.half)] * 2,
+        in_specs=[ANY],
+        out_specs=[VMEM] * 2,
+        scratch_shapes=[pltpu.SemaphoreType.DMA((groups,))],
+        compiler_params=params,
+        name="prep",
+    )(flat_blocks)
     own, own_a, own_b, tile = pl.pallas_call(
-        functools.partial(prep_kernel, dims),
+        functools.partial(number_kernel, dims),
         out_shape=[payload(2 * dims.half + 2 * IDX)] + [payload(dims.half + IDX)] * 2 + [payload(IDX)],
-        in_specs=[SMEM] * groups + [ANY],
+        in_specs=[ANY] * groups + [VMEM] * 2,
         out_specs=[VMEM] * 4,
-        scratch_shapes=[pltpu.SemaphoreType.DMA((groups, 2))],
-        compiler_params=pltpu.CompilerParams(vmem_limit_bytes=GRANT),
-        name="prep",
-    )(*(jnp.transpose(x, (2, 1, 0)) for x in cols), blocks.reshape(-1, bs))
+        scratch_shapes=[
+            pltpu.SMEM((groups, per_group, 1, groups), jnp.int32),
+            pltpu.SemaphoreType.DMA((groups,)),
+        ],
+        compiler_params=params,
+        name="numbers",
+    )(*cols, bare_a, bare_b)
 
     if dims.whole:
         up, down = ring_moves(cycle)
-        pa, pb, qa, qb = [own_a], [own_b], [own_a], [own_b]
+        pa, pb, qa, qb = [bare_a], [own_b], [own_a], [bare_b]
         for k in range(1, HP + 1):
             pa.append(lax.ppermute(pa[-1], "rows", up))
             qb.append(lax.ppermute(qb[-1], "rows", down))
@@ -433,23 +465,23 @@
 
     if dims.whole:
         far = lax.ppermute(tile, "rows", [(a, dict(up)[dict(up)[dict(up)[b]]]) for a, b in up])
-        pairs = [[(-k, pa[k], pb[k]), (k, qa[k], qb[k])] for k in range(1, HP)]
-        acc, empty = call_step(dims, left, [(0, own, None)] + pairs[0], None, zero=True)
-        for k in range(2, HP - 1):
-            acc = call_step(dims, left, pairs[k - 1], acc)[0]
+        pairs = [[(-k, pa[k], pb[k], "b"), (k, qa[k], qb[k], "a")] for k in range(1, HP)]
+        carry = call_step(dims, left, [(0, own, None, "a")] + pairs[0], None, [0, 1])
+        carry = call_step(dims, left, pairs[1], carry, [2])
         tiles = [(0, tile, 0), (HP, far, 0)]
         for k in range(1, HP):
-            tiles += [(cycle - k, pa[k], dims.half), (k, qb[k], dims.half)]
-        acc, slots, columns, starts = call_step(dims, left, pairs[-1], acc, tiles=tiles)
+            tiles += [(cycle - k, pb[k], dims.half), (k, qa[k], dims.half)]
+        acc, empty, slots, columns, starts = call_step(dims, left, pairs[2], carry, [3], tiles)
         starts = starts.reshape(groups, 1)
-        final = [(HP, pa[HP], qb[HP])]
+        final = [(HP, pa[HP], qb[HP], far)]
     else:
         slots, columns, starts = window_index(dims, left, window)
-        acc, empty = call_step(dims, left, [(0, own, None)], None, zero=True)
-        pairs = [(k, window[k + HP], None) for k in range(-HP, HP) if k]
+        carry = call_step(dims, left, [(0, own, None, "a")], None, range(groups))
+        pairs = [(k, window[k + HP], None, "a") for k in range(-HP, HP) if k]
         for k in range(0, len(pairs) - 1, 2):
-            acc = call_step(dims, left, pairs[k : k + 2], acc)[0]
+            carry = call_step(dims, left, pairs[k : k + 2], carry, [])
         final = pairs[-1:]
+        acc, empty = carry
     out = call_last(dims, left, final, acc, slots, empty)
     return out[:, None], columns, starts
 

time: 59.3 us -> 58.8 us (level)
  waiting for transfers between devices: 15.3 us -> 18.2 us
  local copies, waits for them, and re-layouts: 1.68 us -> 0 us
  starting transfers between devices: 23.5 us -> 22.2 us
    ppermute x4, waiting for transfers between devices: 0.01 us -> 7.09 us  [on_device(): qb.append(lax.ppermute(qb[-1], 'rows', down))]
    ppermute x3, waiting for transfers between devices: 6.13 us -> 0.01 us  [on_device(): qa.append(lax.ppermute(qa[-1], 'rows', down))]
    ppermute x4, waiting for transfers between devices: 0.01 us -> 6 us  [on_device(): pa.append(lax.ppermute(pa[-1], 'rows', up))]
    ppermute x3, waiting for transfers between devices: 5.34 us -> 0.01 us  [on_device(): pb.append(lax.ppermute(pb[-1], 'rows', up))]
    ppermute x3, starting transfers between devices: 5.2 us -> 1.58 us  [on_device(): pb.append(lax.ppermute(pb[-1], 'rows', up))]
    ppermute x4, starting transfers between devices: 4.22 us -> 7.37 us  [on_device(): qb.append(lax.ppermute(qb[-1], 'rows', down))]
    unnamed x4 -> x0, local copies, waits for them, and re-layouts: 1.68 us -> none
    ppermute x6, waiting for transfers between devices: 3.76 us -> 5.09 us  [xor_move(): lax.ppermute(value, axis, [(i, i ^ bit) for i in range(lax.axis_size(axis...]
  transfers between devices with their start and end apart: 21 -> 21, of which waited for: 6 -> 8; matrix products, arithmetic and copies ran while one was open for 0% -> 0% of each run, Pallas kernels for 22% -> 23%
where the time goes in v5:
time: 58.8 us; the launch traced here: 58.7 us
  starting transfers between devices  22.2 us (38%)
  waiting for transfers between devices  18.2 us (31%)
  Pallas kernels  17.5 us (30%)
  between operations  0.74 us (1%)
    pallas_call x3, Pallas kernels, call_step(): pl.pallas_call(functools.partial(step_kernel, dims, layout, carry is not...  12.7 us
    ppermute x4, starting transfers between devices, on_device(): qb.append(lax.ppermute(qb[-1], 'rows', down))  7.37 us
    ppermute x4, waiting for transfers between devices, on_device(): qb.append(lax.ppermute(qb[-1], 'rows', down))  7.09 us
    ppermute x4, waiting for transfers between devices, on_device(): pa.append(lax.ppermute(pa[-1], 'rows', up))  6 us
    ppermute x6, waiting for transfers between devices, xor_move(): lax.ppermute(value, axis, [(i, i ^ bit) for i in range(lax.axis_size(axis...  5.09 us
    ppermute x6, starting transfers between devices, xor_move(): lax.ppermute(value, axis, [(i, i ^ bit) for i in range(lax.axis_size(axis...  3.8 us
    ppermute x1, starting transfers between devices, on_device(): lax.ppermute(tile, 'rows', [(a, dict(up)[dict(up)[dict(up)[b]]]) for a, b...  3.54 us
    ppermute x3, starting transfers between devices, on_device(): qa.append(lax.ppermute(qa[-1], 'rows', down))  3.37 us
  transfers between devices with their start and end apart: 21, of which 8 were waited for; matrix products, arithmetic and copies ran while one was open for 0% of the time, Pallas kernels for 23%

profile of v5, /device:TPU:0, one launch (start us, length us, event | category | flops | bytes accessed | tf_op | source)
XLA Modules:
  0.0 58.7 jit_solution(9473626641345739010)
XLA Ops:
  0.6 0.6 collective-permute-start
  1.2 2.6 %collective-permute-start.1 = (s32[4,1,3]{0,1,2:T(1,128)}, s32[4,1,3]{0,1,2:T(1,128)S(1)}, u32[]{:S(2)}, u32[]{:S(2)}) collective-permute-start(s32[4,1,3]{0,1,2:T(1,128)} %param.3), channel_id=1, source_target_pairs={{0,2},{1,3},{2,0},{3,1},{4,6},{5,7},{6,4},{7,5},{8,10},{9,11},{10,... | collective-permute-start | bytes 152 | tf_op jit(solution)/shard_map/ppermute | solution.py:358
  3.7 0.0 collective-permute-start.2
  3.8 1.1 %prep.1 = (bf16[768,128]{1,0:T(8,128)(2,1)S(1)}, bf16[768,128]{1,0:T(8,128)(2,1)S(1)}) custom-call(bf16[1536,128]{1,0:T(8,128)(2,1)} %bitcast.13), custom_call_target="tpu_custom_call" | custom-call | tf_op jit(solution)/shard_map/prep/pallas_call | solution.py:428
  4.9 0.0 collective-permute-done
  4.9 0.6 %collective-permute-done.1 = s32[4,1,3]{0,1,2:T(1,128)S(1)} collective-permute-done((s32[4,1,3]{0,1,2:T(1,128)}, s32[4,1,3]{0,1,2:T(1,128)S(1)}, u32[]{:S(2)}, u32[]{:S(2)}) %collective-permute-start.1) | collective-permute-done | bytes 80 | tf_op jit(solution)/shard_map/ppermute | solution.py:358
  5.5 1.4 %collective-permute-done.2 = s32[4,1,3]{0,1,2:T(1,128)S(1)} collective-permute-done((s32[4,1,3]{0,1,2:T(1,128)}, s32[4,1,3]{0,1,2:T(1,128)S(1)}, u32[]{:S(2)}, u32[]{:S(2)}) %collective-permute-start.2) | collective-permute-done | bytes 80 | tf_op jit(solution)/shard_map/ppermute | solution.py:358
  7.0 0.8 %numbers.1 = (bf16[1568,128]{1,0:T(8,128)(2,1)S(1)}, bf16[784,128]{1,0:T(8,128)(2,1)S(1)}, bf16[784,128]{1,0:T(8,128)(2,1)S(1)}, bf16[16,128]{1,0:T(8,128)(2,1)S(1)}) custom-call(s32[3,1,4]{2,1,0:T(1,128)} %bitcast.14, s32[3,1,4]{2,1,0:T(1,128)S(1)} %bitcast.9, s32[3,1,4]{2,1,0:T(1,128)S(1)} %bitcast.10, s32[3,1,4]{2,1,0:T(1,128)S(1)} %bitcast.11, ...), custom_call_target="tpu_custom_call" | custom-call | tf_op jit(solution)/shard_map/numbers/pallas_call | solution.py:437
  7.8 0.6 %collective-permute-start.4 = (bf16[1568,128]{1,0:T(8,128)(2,1)S(1)}, bf16[1568,128]{1,0:T(8,128)(2,1)S(1)}, u32[]{:S(2)}, u32[]{:S(2)}) collective-permute-start(bf16[1568,128]{1,0:T(8,128)(2,1)S(1)} %get-tuple-element.20.refs_0_.refs_4_), channel_id=1, source_target_pairs={{0,2},{1,3},{2,0},{3,1},{4,6},{5,7},{6,4},{7,5},{8,10},{9,11},{10,... | collective-permute-start | bytes 1204232 | tf_op jit(solution)/shard_map/ppermute | solution.py:358
  8.4 1.5 %collective-permute-start.10 = (bf16[768,128]{1,0:T(8,128)(2,1)S(1)}, bf16[768,128]{1,0:T(8,128)(2,1)S(1)}, u32[]{:S(2)}, u32[]{:S(2)}) collective-permute-start(bf16[768,128]{1,0:T(8,128)(2,1)S(1)} %get-tuple-element.19.refs_5_), channel_id=1, source_target_pairs={{8,0},{16,8},{24,16},{28,24},{20,28},{12,20},{4,12},{0,4},{9,1},{1... | collective-permute-start | bytes 589832 | tf_op jit(solution)/shard_map/ppermute | solution.py:455
  9.9 0.5 collective-permute-start.15
  10.5 1.6 %collective-permute-start.6 = (bf16[768,128]{1,0:T(8,128)(2,1)S(1)}, bf16[768,128]{1,0:T(8,128)(2,1)S(1)}, u32[]{:S(2)}, u32[]{:S(2)}) collective-permute-start(bf16[768,128]{1,0:T(8,128)(2,1)S(1)} %get-tuple-element.18.refs_4_), channel_id=1, source_target_pairs={{0,8},{8,16},{16,24},{24,28},{28,20},{20,12},{12,4},{4,0},{1,9},{9... | collective-permute-start | bytes 589832 | tf_op jit(solution)/shard_map/ppermute | solution.py:454
  12.0 0.4 collective-permute-start.18
  12.5 3.7 %collective-permute-done.10.refs_8_ = bf16[768,128]{1,0:T(8,128)(2,1)S(1)} collective-permute-done((bf16[768,128]{1,0:T(8,128)(2,1)S(1)}, bf16[768,128]{1,0:T(8,128)(2,1)S(1)}, u32[]{:S(2)}, u32[]{:S(2)}) %collective-permute-start.10) | collective-permute-done | bytes 196640 | tf_op jit(solution)/shard_map/ppermute | solution.py:455
  16.2 0.0 collective-permute-start.3
  16.2 3.0 %collective-permute-done.4.refs_2_ = bf16[1568,128]{1,0:T(8,128)(2,1)S(1)} collective-permute-done((bf16[1568,128]{1,0:T(8,128)(2,1)S(1)}, bf16[1568,128]{1,0:T(8,128)(2,1)S(1)}, u32[]{:S(2)}, u32[]{:S(2)}) %collective-permute-start.4) | collective-permute-done | bytes 401440 | tf_op jit(solution)/shard_map/ppermute | solution.py:358
  19.2 0.0 collective-permute-start.5
  19.2 1.4 %collective-permute-done.6.refs_5_ = bf16[768,128]{1,0:T(8,128)(2,1)S(1)} collective-permute-done((bf16[768,128]{1,0:T(8,128)(2,1)S(1)}, bf16[768,128]{1,0:T(8,128)(2,1)S(1)}, u32[]{:S(2)}, u32[]{:S(2)}) %collective-permute-start.6) | collective-permute-done | bytes 196640 | tf_op jit(solution)/shard_map/ppermute | solution.py:454
  20.6 1.6 %collective-permute-start.11 = (bf16[768,128]{1,0:T(8,128)(2,1)S(1)}, bf16[768,128]{1,0:T(8,128)(2,1)S(1)}, u32[]{:S(2)}, u32[]{:S(2)}) collective-permute-start(bf16[768,128]{1,0:T(8,128)(2,1)S(1)} %collective-permute-done.10.refs_8_), channel_id=1, source_target_pairs={{8,0},{16,8},{24,16},{28,24},{20,28},{12,20},{4,12},{0,4},{9,1},{1... | collective-permute-start | bytes 589832 | tf_op jit(solution)/shard_map/ppermute | solution.py:455
  22.2 0.0 collective-permute-done.15.refs_6_.refs_10_
  22.2 0.5 collective-permute-start.16
  22.6 0.0 collective-permute-done.18.refs_7_.refs_11_
  22.6 0.5 collective-permute-start.7
  23.1 3.4 %collective-permute-done.11.refs_7_ = bf16[768,128]{1,0:T(8,128)(2,1)S(1)} collective-permute-done((bf16[768,128]{1,0:T(8,128)(2,1)S(1)}, bf16[768,128]{1,0:T(8,128)(2,1)S(1)}, u32[]{:S(2)}, u32[]{:S(2)}) %collective-permute-start.11) | collective-permute-done | bytes 196640 | tf_op jit(solution)/shard_map/ppermute | solution.py:455
  26.5 1.5 %collective-permute-start.19 = (bf16[784,128]{1,0:T(8,128)(2,1)S(1)}, bf16[784,128]{1,0:T(8,128)(2,1)S(1)}, u32[]{:S(2)}, u32[]{:S(2)}) collective-permute-start(bf16[784,128]{1,0:T(8,128)(2,1)S(1)} %collective-permute-done.18.refs_7_.refs_11_), channel_id=1, source_target_pairs={{8,0},{16,8},{24,16},{28,24},{20,28},{12,20},{4,12},{0,4},{9,1},{1... | collective-permute-start | bytes 602120 | tf_op jit(solution)/shard_map/ppermute | solution.py:458
  28.0 4.0 %collective-permute-done.7.refs_4_ = bf16[768,128]{1,0:T(8,128)(2,1)S(1)} collective-permute-done((bf16[768,128]{1,0:T(8,128)(2,1)S(1)}, bf16[768,128]{1,0:T(8,128)(2,1)S(1)}, u32[]{:S(2)}, u32[]{:S(2)}) %collective-permute-start.7) | collective-permute-done | bytes 196640 | tf_op jit(solution)/shard_map/ppermute | solution.py:454
  32.1 1.6 %collective-permute-start.12 = (bf16[768,128]{1,0:T(8,128)(2,1)S(1)}, bf16[768,128]{1,0:T(8,128)(2,1)S(1)}, u32[]{:S(2)}, u32[]{:S(2)}) collective-permute-start(bf16[768,128]{1,0:T(8,128)(2,1)S(1)} %collective-permute-done.11.refs_7_), channel_id=1, source_target_pairs={{8,0},{16,8},{24,16},{28,24},{20,28},{12,20},{4,12},{0,4},{9,1},{1... | collective-permute-start | bytes 589832 | tf_op jit(solution)/shard_map/ppermute | solution.py:455
  33.6 0.0 collective-permute-done.16.refs_5_.refs_12_
  33.6 0.5 collective-permute-start.8
  34.1 0.0 collective-permute-done.19.refs_6_.refs_13_
  34.1 3.5 %collective-permute-start.14 = (bf16[16,128]{1,0:T(8,128)(2,1)S(1)}, bf16[16,128]{1,0:T(8,128)(2,1)S(1)}, u32[]{:S(2)}, u32[]{:S(2)}) collective-permute-start(bf16[16,128]{1,0:T(8,128)(2,1)S(1)} %get-tuple-element.21.refs_8_), channel_id=1, source_target_pairs={{0,28},{8,20},{16,12},{24,4},{28,0},{20,8},{12,16},{4,24},{1,29},{... | collective-permute-start | bytes 12296 | tf_op jit(solution)/shard_map/ppermute | solution.py:467
  37.6 0.0 collective-permute-done.3.refs_1_
  37.6 0.6 %collective-permute-start.17 = (bf16[784,128]{1,0:T(8,128)(2,1)S(1)}, bf16[784,128]{1,0:T(8,128)(2,1)S(1)}, u32[]{:S(2)}, u32[]{:S(2)}) collective-permute-start(bf16[784,128]{1,0:T(8,128)(2,1)S(1)} %collective-permute-done.16.refs_5_.refs_12_), channel_id=1, source_target_pairs={{0,8},{8,16},{16,24},{24,28},{28,20},{20,12},{12,4},{4,0},{1,9},{9... | collective-permute-start | bytes 602120 | tf_op jit(solution)/shard_map/ppermute | solution.py:457
  38.3 0.0 collective-permute-done.12.refs_7_
  38.3 1.4 %collective-permute-start.20 = (bf16[784,128]{1,0:T(8,128)(2,1)S(1)}, bf16[784,128]{1,0:T(8,128)(2,1)S(1)}, u32[]{:S(2)}, u32[]{:S(2)}) collective-permute-start(bf16[784,128]{1,0:T(8,128)(2,1)S(1)} %collective-permute-done.19.refs_6_.refs_13_), channel_id=1, source_target_pairs={{8,0},{16,8},{24,16},{28,24},{20,28},{12,20},{4,12},{0,4},{9,1},{1... | collective-permute-start | bytes 602120 | tf_op jit(solution)/shard_map/ppermute | solution.py:458
  39.7 0.6 collective-permute-done.8.refs_4_
  40.2 2.7 %collective-permute-start.13 = (bf16[768,128]{1,0:T(8,128)(2,1)S(1)}, bf16[768,128]{1,0:T(8,128)(2,1)S(1)}, u32[]{:S(2)}, u32[]{:S(2)}) collective-permute-start(bf16[768,128]{1,0:T(8,128)(2,1)S(1)} %collective-permute-done.12.refs_7_), channel_id=1, source_target_pairs={{8,0},{16,8},{24,16},{28,24},{20,28},{12,20},{4,12},{0,4},{9,1},{1... | collective-permute-start | bytes 589832 | tf_op jit(solution)/shard_map/ppermute | solution.py:455
  42.9 0.0 collective-permute-done.5.refs_3_
  42.9 0.0 collective-permute-start.9
  42.9 4.4 %shard_map.49 = (f32[512,1024]{1,0:T(8,128)S(1)}, bf16[4,36,128,128]{3,2,1,0:T(8,128)(2,1)}) custom-call(bf16[1568,128]{1,0:T(8,128)(2,1)S(1)} %get-tuple-element.20.refs_0_.refs_4_, bf16[1568,128]{1,0:T(8,128)(2,1)S(1)} %collective-permute-done.3.refs_1_, bf16[1568,128]{1,0:T(8,128)(2,1)S(1)} %collective-permute-done.4.refs_2_, ...), custom_call_target="tpu_custom_call" | custom-call | flops 1610612736 | bytes 4000000 | tf_op jit(solution)/shard_map/pallas_call | solution.py:326
  47.3 3.7 %shard_map.50 = (f32[512,1024]{1,0:T(8,128)S(1)}, bf16[4,36,128,128]{3,2,1,0:T(8,128)(2,1)}) custom-call(bf16[1568,128]{1,0:T(8,128)(2,1)S(1)} %get-tuple-element.20.refs_0_.refs_4_, bf16[1568,128]{1,0:T(8,128)(2,1)S(1)} %collective-permute-done.3.refs_1_, ...), custom_call_target="tpu_custom_call", output_to_operand_aliasing={{0}: (8, {}), {1}: (9, {})} | custom-call | flops 1073741824 | bytes 4000000 | tf_op jit(solution)/shard_map/pallas_call | solution.py:326
  51.0 0.0 collective-permute-done.14.refs_9_.refs_6_
  51.0 0.0 collective-permute-done.17.refs_5_.refs_14_
  51.0 0.0 collective-permute-done.20.refs_6_.refs_15_
  51.0 4.6 %shard_map.51 = (f32[512,1024]{1,0:T(8,128)S(1)}, bf16[4,36,128,128]{3,2,1,0:T(8,128)(2,1)}, s32[32]{0:T(128)S(1)}, s32[4,1,36]{2,1,0:T(1,128)}, s32[1,4]{1,0:T(1,128)}) custom-call(bf16[1568,128]{1,0:T(8,128)(2,1)S(1)} %get-tuple-element.20.refs_0_.refs_4_, ...), custom_call_target="tpu_custom_call", output_to_operand_aliasing={{0}: (16, {}), {1}: (17, {})} | custom-call | flops 1073741824 | bytes 4000000 | tf_op jit(solution)/shard_map/pallas_call | solution.py:326
  55.7 0.0 collective-permute-done.13.refs_5_
  55.7 0.0 collective-permute-done.9.refs_4_
  55.7 3.0 %shard_map.52 = bf16[4,36,128,128]{3,2,1,0:T(8,128)(2,1)} custom-call(bf16[1568,128]{1,0:T(8,128)(2,1)S(1)} %get-tuple-element.20.refs_0_.refs_4_, bf16[1568,128]{1,0:T(8,128)(2,1)S(1)} %collective-permute-done.3.refs_1_, bf16[1568,128]{1,0:T(8,128)(2,1)S(1)} %collective-permute-done.4.refs_2_, ...), custom_call_target="tpu_custom_call", output_to_operand_aliasing={{}: (9, {})} | custom-call | flops 536870912 | bytes 4000000 | tf_op jit(solution)/shard_map/pallas_call | solution.py:341
Async XLA Ops:
  0.6 4.2 %collective-permute-start = (s32[4,1,3]{0,1,2:T(1,128)}, s32[4,1,3]{0,1,2:T(1,128)S(1)}, u32[]{:S(2)}, u32[]{:S(2)}) collective-permute-start(s32[4,1,3]{0,1,2:T(1,128)} %param.3), channel_id=1, source_target_pairs={{0,1},{1,0},{2,3},{3,2},{4,5},{5,4},{6,7},{7,6},{8,9},{9,8},{10,11... | collective-permute-start | bytes 152 | tf_op jit(solution)/shard_map/ppermute | solution.py:358
  1.2 4.3 %collective-permute-start.1 = (s32[4,1,3]{0,1,2:T(1,128)}, s32[4,1,3]{0,1,2:T(1,128)S(1)}, u32[]{:S(2)}, u32[]{:S(2)}) collective-permute-start(s32[4,1,3]{0,1,2:T(1,128)} %param.3), channel_id=1, source_target_pairs={{0,2},{1,3},{2,0},{3,1},{4,6},{5,7},{6,4},{7,5},{8,10},{9,11},{10,... | collective-permute-start | bytes 152 | tf_op jit(solution)/shard_map/ppermute | solution.py:358
  3.7 3.2 %collective-permute-start.2 = (s32[4,1,3]{0,1,2:T(1,128)}, s32[4,1,3]{0,1,2:T(1,128)S(1)}, u32[]{:S(2)}, u32[]{:S(2)}) collective-permute-start(s32[4,1,3]{0,1,2:T(1,128)} %param.3), channel_id=1, source_target_pairs={{0,3},{1,2},{2,1},{3,0},{4,7},{5,6},{6,5},{7,4},{8,11},{9,10},{10,... | collective-permute-start | bytes 152 | tf_op jit(solution)/shard_map/ppermute | solution.py:358
  7.8 11.4 %collective-permute-start.4 = (bf16[1568,128]{1,0:T(8,128)(2,1)S(1)}, bf16[1568,128]{1,0:T(8,128)(2,1)S(1)}, u32[]{:S(2)}, u32[]{:S(2)}) collective-permute-start(bf16[1568,128]{1,0:T(8,128)(2,1)S(1)} %get-tuple-element.20.refs_0_.refs_4_), channel_id=1, source_target_pairs={{0,2},{1,3},{2,0},{3,1},{4,6},{5,7},{6,4},{7,5},{8,10},{9,11},{10,... | collective-permute-start | bytes 1204232 | tf_op jit(solution)/shard_map/ppermute | solution.py:358
  8.4 7.8 %collective-permute-start.10 = (bf16[768,128]{1,0:T(8,128)(2,1)S(1)}, bf16[768,128]{1,0:T(8,128)(2,1)S(1)}, u32[]{:S(2)}, u32[]{:S(2)}) collective-permute-start(bf16[768,128]{1,0:T(8,128)(2,1)S(1)} %get-tuple-element.19.refs_5_), channel_id=1, source_target_pairs={{8,0},{16,8},{24,16},{28,24},{20,28},{12,20},{4,12},{0,4},{9,1},{1... | collective-permute-start | bytes 589832 | tf_op jit(solution)/shard_map/ppermute | solution.py:455
  9.9 12.2 %collective-permute-start.15 = (bf16[784,128]{1,0:T(8,128)(2,1)S(1)}, bf16[784,128]{1,0:T(8,128)(2,1)S(1)}, u32[]{:S(2)}, u32[]{:S(2)}) collective-permute-start(bf16[784,128]{1,0:T(8,128)(2,1)S(1)} %get-tuple-element.22), channel_id=1, source_target_pairs={{0,8},{8,16},{16,24},{24,28},{28,20},{20,12},{12,4},{4,0},{1,9},{9... | collective-permute-start | bytes 602120 | tf_op jit(solution)/shard_map/ppermute | solution.py:457
  10.5 10.2 %collective-permute-start.6 = (bf16[768,128]{1,0:T(8,128)(2,1)S(1)}, bf16[768,128]{1,0:T(8,128)(2,1)S(1)}, u32[]{:S(2)}, u32[]{:S(2)}) collective-permute-start(bf16[768,128]{1,0:T(8,128)(2,1)S(1)} %get-tuple-element.18.refs_4_), channel_id=1, source_target_pairs={{0,8},{8,16},{16,24},{24,28},{28,20},{20,12},{12,4},{4,0},{1,9},{9... | collective-permute-start | bytes 589832 | tf_op jit(solution)/shard_map/ppermute | solution.py:454
  12.0 10.6 %collective-permute-start.18 = (bf16[784,128]{1,0:T(8,128)(2,1)S(1)}, bf16[784,128]{1,0:T(8,128)(2,1)S(1)}, u32[]{:S(2)}, u32[]{:S(2)}) collective-permute-start(bf16[784,128]{1,0:T(8,128)(2,1)S(1)} %get-tuple-element.23), channel_id=1, source_target_pairs={{8,0},{16,8},{24,16},{28,24},{20,28},{12,20},{4,12},{0,4},{9,1},{1... | collective-permute-start | bytes 602120 | tf_op jit(solution)/shard_map/ppermute | solution.py:458
  16.2 21.4 %collective-permute-start.3 = (bf16[1568,128]{1,0:T(8,128)(2,1)S(1)}, bf16[1568,128]{1,0:T(8,128)(2,1)S(1)}, u32[]{:S(2)}, u32[]{:S(2)}) collective-permute-start(bf16[1568,128]{1,0:T(8,128)(2,1)S(1)} %get-tuple-element.20.refs_0_.refs_4_), channel_id=1, source_target_pairs={{0,1},{1,0},{2,3},{3,2},{4,5},{5,4},{6,7},{7,6},{8,9},{9,8},{10,11... | collective-permute-start | bytes 1204232 | tf_op jit(solution)/shard_map/ppermute | solution.py:358
  19.2 23.7 %collective-permute-start.5 = (bf16[1568,128]{1,0:T(8,128)(2,1)S(1)}, bf16[1568,128]{1,0:T(8,128)(2,1)S(1)}, u32[]{:S(2)}, u32[]{:S(2)}) collective-permute-start(bf16[1568,128]{1,0:T(8,128)(2,1)S(1)} %collective-permute-done.4.refs_2_), channel_id=1, source_target_pairs={{0,1},{1,0},{2,3},{3,2},{4,5},{5,4},{6,7},{7,6},{8,9},{9,8},{10,11... | collective-permute-start | bytes 1204232 | tf_op jit(solution)/shard_map/ppermute | solution.py:358
  20.6 5.9 %collective-permute-start.11 = (bf16[768,128]{1,0:T(8,128)(2,1)S(1)}, bf16[768,128]{1,0:T(8,128)(2,1)S(1)}, u32[]{:S(2)}, u32[]{:S(2)}) collective-permute-start(bf16[768,128]{1,0:T(8,128)(2,1)S(1)} %collective-permute-done.10.refs_8_), channel_id=1, source_target_pairs={{8,0},{16,8},{24,16},{28,24},{20,28},{12,20},{4,12},{0,4},{9,1},{1... | collective-permute-start | bytes 589832 | tf_op jit(solution)/shard_map/ppermute | solution.py:455
  22.2 11.5 %collective-permute-start.16 = (bf16[784,128]{1,0:T(8,128)(2,1)S(1)}, bf16[784,128]{1,0:T(8,128)(2,1)S(1)}, u32[]{:S(2)}, u32[]{:S(2)}) collective-permute-start(bf16[784,128]{1,0:T(8,128)(2,1)S(1)} %collective-permute-done.15.refs_6_.refs_10_), channel_id=1, source_target_pairs={{0,8},{8,16},{16,24},{24,28},{28,20},{20,12},{12,4},{4,0},{1,9},{9... | collective-permute-start | bytes 602120 | tf_op jit(solution)/shard_map/ppermute | solution.py:457
  22.6 9.4 %collective-permute-start.7 = (bf16[768,128]{1,0:T(8,128)(2,1)S(1)}, bf16[768,128]{1,0:T(8,128)(2,1)S(1)}, u32[]{:S(2)}, u32[]{:S(2)}) collective-permute-start(bf16[768,128]{1,0:T(8,128)(2,1)S(1)} %collective-permute-done.6.refs_5_), channel_id=1, source_target_pairs={{0,8},{8,16},{16,24},{24,28},{28,20},{20,12},{12,4},{4,0},{1,9},{9... | collective-permute-start | bytes 589832 | tf_op jit(solution)/shard_map/ppermute | solution.py:454
  26.5 7.6 %collective-permute-start.19 = (bf16[784,128]{1,0:T(8,128)(2,1)S(1)}, bf16[784,128]{1,0:T(8,128)(2,1)S(1)}, u32[]{:S(2)}, u32[]{:S(2)}) collective-permute-start(bf16[784,128]{1,0:T(8,128)(2,1)S(1)} %collective-permute-done.18.refs_7_.refs_11_), channel_id=1, source_target_pairs={{8,0},{16,8},{24,16},{28,24},{20,28},{12,20},{4,12},{0,4},{9,1},{1... | collective-permute-start | bytes 602120 | tf_op jit(solution)/shard_map/ppermute | solution.py:458
  32.1 6.2 %collective-permute-start.12 = (bf16[768,128]{1,0:T(8,128)(2,1)S(1)}, bf16[768,128]{1,0:T(8,128)(2,1)S(1)}, u32[]{:S(2)}, u32[]{:S(2)}) collective-permute-start(bf16[768,128]{1,0:T(8,128)(2,1)S(1)} %collective-permute-done.11.refs_7_), channel_id=1, source_target_pairs={{8,0},{16,8},{24,16},{28,24},{20,28},{12,20},{4,12},{0,4},{9,1},{1... | collective-permute-start | bytes 589832 | tf_op jit(solution)/shard_map/ppermute | solution.py:455
  33.6 6.6 %collective-permute-start.8 = (bf16[768,128]{1,0:T(8,128)(2,1)S(1)}, bf16[768,128]{1,0:T(8,128)(2,1)S(1)}, u32[]{:S(2)}, u32[]{:S(2)}) collective-permute-start(bf16[768,128]{1,0:T(8,128)(2,1)S(1)} %collective-permute-done.7.refs_4_), channel_id=1, source_target_pairs={{0,8},{8,16},{16,24},{24,28},{28,20},{20,12},{12,4},{4,0},{1,9},{9... | collective-permute-start | bytes 589832 | tf_op jit(solution)/shard_map/ppermute | solution.py:454
  34.1 16.9 %collective-permute-start.14 = (bf16[16,128]{1,0:T(8,128)(2,1)S(1)}, bf16[16,128]{1,0:T(8,128)(2,1)S(1)}, u32[]{:S(2)}, u32[]{:S(2)}) collective-permute-start(bf16[16,128]{1,0:T(8,128)(2,1)S(1)} %get-tuple-element.21.refs_8_), channel_id=1, source_target_pairs={{0,28},{8,20},{16,12},{24,4},{28,0},{20,8},{12,16},{4,24},{1,29},{... | collective-permute-start | bytes 12296 | tf_op jit(solution)/shard_map/ppermute | solution.py:467
  37.6 13.4 %collective-permute-start.17 = (bf16[784,128]{1,0:T(8,128)(2,1)S(1)}, bf16[784,128]{1,0:T(8,128)(2,1)S(1)}, u32[]{:S(2)}, u32[]{:S(2)}) collective-permute-start(bf16[784,128]{1,0:T(8,128)(2,1)S(1)} %collective-permute-done.16.refs_5_.refs_12_), channel_id=1, source_target_pairs={{0,8},{8,16},{16,24},{24,28},{28,20},{20,12},{12,4},{4,0},{1,9},{9... | collective-permute-start | bytes 602120 | tf_op jit(solution)/shard_map/ppermute | solution.py:457
  38.3 12.7 %collective-permute-start.20 = (bf16[784,128]{1,0:T(8,128)(2,1)S(1)}, bf16[784,128]{1,0:T(8,128)(2,1)S(1)}, u32[]{:S(2)}, u32[]{:S(2)}) collective-permute-start(bf16[784,128]{1,0:T(8,128)(2,1)S(1)} %collective-permute-done.19.refs_6_.refs_13_), channel_id=1, source_target_pairs={{8,0},{16,8},{24,16},{28,24},{20,28},{12,20},{4,12},{0,4},{9,1},{1... | collective-permute-start | bytes 602120 | tf_op jit(solution)/shard_map/ppermute | solution.py:458
  40.2 15.4 %collective-permute-start.13 = (bf16[768,128]{1,0:T(8,128)(2,1)S(1)}, bf16[768,128]{1,0:T(8,128)(2,1)S(1)}, u32[]{:S(2)}, u32[]{:S(2)}) collective-permute-start(bf16[768,128]{1,0:T(8,128)(2,1)S(1)} %collective-permute-done.12.refs_7_), channel_id=1, source_target_pairs={{8,0},{16,8},{24,16},{28,24},{20,28},{12,20},{4,12},{0,4},{9,1},{1... | collective-permute-start | bytes 589832 | tf_op jit(solution)/shard_map/ppermute | solution.py:455
  42.9 12.7 %collective-permute-start.9 = (bf16[768,128]{1,0:T(8,128)(2,1)S(1)}, bf16[768,128]{1,0:T(8,128)(2,1)S(1)}, u32[]{:S(2)}, u32[]{:S(2)}) collective-permute-start(bf16[768,128]{1,0:T(8,128)(2,1)S(1)} %collective-permute-done.8.refs_4_), channel_id=1, source_target_pairs={{0,8},{8,16},{16,24},{24,28},{28,20},{20,12},{12,4},{4,0},{1,9},{9... | collective-permute-start | bytes 589832 | tf_op jit(solution)/shard_map/ppermute | solution.py:454

commit v6 on v5

--- a/solution.py
+++ b/solution.py
@@ -164,23 +164,29 @@
     return pieces
 
 
-def step_kernel(dims, layout, with_acc, blank_rows, tiles, *refs):
+def zero_kernel(dims, out_ref, blank_ref, sems):
+    per = blank_ref.shape[0]
+    blank_ref[...] = jnp.zeros_like(blank_ref)
+    copies = []
+    for i in range(dims.groups):
+        for first in range(dims.bins, dims.slots, per):
+            copies.append(
+                pltpu.make_async_copy(blank_ref, out_ref.at[i, first : first + per], sems.at[len(copies)])
+            )
+            copies[-1].start()
+    for copy in copies:
+        copy.wait()
+
+
+def step_kernel(dims, layout, with_acc, tiles, *refs):
     refs = list(refs)
     left = take(refs, dims.groups)
     pieces = take_pieces(dims, refs, layout)
     tile_refs = take(refs, len(tiles))
-    acc_ref = None
-    if with_acc:
-        acc_ref, _ = take(refs, 2)
-    out_ref, zero_ref = take(refs, 2)
+    acc_ref = refs.pop(0) if with_acc else None
+    out_ref = refs.pop(0)
     index_refs = take(refs, 3) if tiles else None
-    lp_ref, d_ref, blank_ref, sems = take(refs, 4)
-    blank_ref[...] = jnp.zeros_like(blank_ref)
-    copies = []
-    for i in blank_rows:
-        copy = pltpu.make_async_copy(blank_ref, zero_ref.at[i, dims.bins : dims.slots], sems.at[i])
-        copy.start()
-        copies.append(copy)
+    lp_ref, d_ref = take(refs, 2)
     if tiles:
         wide_ref, count_ref = refs
         index_work(dims, tiles, tile_refs, wide_ref, *index_refs, count_ref)
@@ -189,8 +195,6 @@
         out_ref[:, lo:hi] = value if acc_ref is None else acc_ref[:, lo:hi] + value
 
     accumulate(dims, pieces, left, lp_ref, d_ref, emit)
-    for copy in copies:
-        copy.wait()
 
 
 def last_kernel(dims, layout, *refs):
@@ -293,24 +297,32 @@
     return pl.CostEstimate(flops=flops, bytes_accessed=4_000_000, transcendentals=0)
 
 
-def call_step(dims, left, panels, carry, blank_rows, tiles=()):
+def call_zero(dims):
+    count = dims.slots - dims.bins
+    per = max(n for n in range(1, 5) if count % n == 0)
+    return pl.pallas_call(
+        functools.partial(zero_kernel, dims),
+        out_shape=jax.ShapeDtypeStruct((dims.groups, dims.slots, dims.bs, dims.bs), jnp.bfloat16),
+        out_specs=ANY,
+        scratch_shapes=[
+            pltpu.VMEM((per, dims.bs, dims.bs), jnp.bfloat16),
+            pltpu.SemaphoreType.DMA((dims.groups * count // per,)),
+        ],
+        compiler_params=pltpu.CompilerParams(vmem_limit_bytes=GRANT),
+        name="zero",
+    )()
+
+
+def call_step(dims, left, panels, acc, tiles=()):
     layout, arrays = flat(panels)
     args = [*left, *arrays, *(array for _, array, _ in tiles)]
-    specs = [VMEM] * len(args)
     aliases = {}
-    if carry is not None:
-        aliases = {len(args): 0, len(args) + 1: 1}
-        args += carry
-        specs += [VMEM, ANY]
-    shapes = [
-        jax.ShapeDtypeStruct((dims.rows, dims.bins * dims.bs), jnp.float32),
-        jax.ShapeDtypeStruct((dims.groups, dims.slots, dims.bs, dims.bs), jnp.bfloat16),
-    ]
-    out_specs = [VMEM, ANY]
-    scratch = scratch_of(dims, panels) + [
-        pltpu.VMEM((dims.slots - dims.bins, dims.bs, dims.bs), jnp.bfloat16),
-        pltpu.SemaphoreType.DMA((dims.groups,)),
-    ]
+    if acc is not None:
+        aliases = {len(args): 0}
+        args.append(acc)
+    shapes = [jax.ShapeDtypeStruct((dims.rows, dims.bins * dims.bs), jnp.float32)]
+    out_specs = [VMEM]
+    scratch = scratch_of(dims, panels)
     if tiles:
         shapes += [
             jax.ShapeDtypeStruct((dims.groups * dims.bins,), jnp.int32),
@@ -324,9 +336,9 @@
         ]
     marks = tuple((n, at) for n, _, at in tiles)
     return pl.pallas_call(
-        functools.partial(step_kernel, dims, layout, carry is not None, tuple(blank_rows), marks),
+        functools.partial(step_kernel, dims, layout, acc is not None, marks),
         out_shape=shapes,
-        in_specs=specs,
+        in_specs=[VMEM] * len(args),
         out_specs=out_specs,
         scratch_shapes=scratch,
         input_output_aliases=aliases,
@@ -466,22 +478,22 @@
     if dims.whole:
         far = lax.ppermute(tile, "rows", [(a, dict(up)[dict(up)[dict(up)[b]]]) for a, b in up])
         pairs = [[(-k, pa[k], pb[k], "b"), (k, qa[k], qb[k], "a")] for k in range(1, HP)]
-        carry = call_step(dims, left, [(0, own, None, "a")] + pairs[0], None, [0, 1])
-        carry = call_step(dims, left, pairs[1], carry, [2])
+        acc = call_step(dims, left, [(0, own, None, "a")] + pairs[0], None)[0]
+        acc = call_step(dims, left, pairs[1], acc)[0]
         tiles = [(0, tile, 0), (HP, far, 0)]
         for k in range(1, HP):
             tiles += [(cycle - k, pb[k], dims.half), (k, qa[k], dims.half)]
-        acc, empty, slots, columns, starts = call_step(dims, left, pairs[2], carry, [3], tiles)
+        acc, slots, columns, starts = call_step(dims, left, pairs[2], acc, tiles)
         starts = starts.reshape(groups, 1)
         final = [(HP, pa[HP], qb[HP], far)]
     else:
         slots, columns, starts = window_index(dims, left, window)
-        carry = call_step(dims, left, [(0, own, None, "a")], None, range(groups))
+        acc = call_step(dims, left, [(0, own, None, "a")], None)[0]
         pairs = [(k, window[k + HP], None, "a") for k in range(-HP, HP) if k]
         for k in range(0, len(pairs) - 1, 2):
-            carry = call_step(dims, left, pairs[k : k + 2], carry, [])
+            acc = call_step(dims, left, pairs[k : k + 2], acc)[0]
         final = pairs[-1:]
-        acc, empty = carry
+    empty = call_zero(dims)
     out = call_last(dims, left, final, acc, slots, empty)
     return out[:, None], columns, starts
 

time: 58.8 us -> 54.1 us (0.920)
  waiting for transfers between devices: 18.2 us -> 16 us
  Pallas kernels: 17.5 us -> 15.9 us
  starting transfers between devices: 22.2 us -> 21.3 us
    ppermute x4, waiting for transfers between devices: 7.09 us -> 2.91 us  [on_device(): qb.append(lax.ppermute(qb[-1], 'rows', down))]
    ppermute x4, starting transfers between devices: 7.37 us -> 3.44 us  [on_device(): qb.append(lax.ppermute(qb[-1], 'rows', down))]
    ppermute x4, starting transfers between devices: 2.54 us -> 5.52 us  [on_device(): pa.append(lax.ppermute(pa[-1], 'rows', up))]
    ppermute x3, starting transfers between devices: 1.58 us -> 3.72 us  [on_device(): pb.append(lax.ppermute(pb[-1], 'rows', up))]
    ppermute x4, waiting for transfers between devices: 6 us -> 7.85 us  [on_device(): pa.append(lax.ppermute(pa[-1], 'rows', up))]
    pallas_call x3 -> x4, Pallas kernels: 12.7 us -> 11 us  [the longest x3 8.93 us: call_step(): pl.pallas_call(functools.partial(step_kernel, dims, layout, acc is not No...]
    ppermute x3, starting transfers between devices: 3.37 us -> 1.99 us  [on_device(): qa.append(lax.ppermute(qa[-1], 'rows', down))]
  transfers between devices with their start and end apart: 21 -> 21, of which waited for: 8 -> 8; matrix products, arithmetic and copies ran while one was open for 0% -> 0% of each run, Pallas kernels for 23% -> 22%
where the time goes in v6:
time: 54.1 us; the launch traced here: 53.9 us
  starting transfers between devices  21.3 us (39%)
  waiting for transfers between devices  16 us (30%)
  Pallas kernels  15.9 us (29%)
  between operations  0.74 us (1%)
    pallas_call x3, Pallas kernels, call_step(): pl.pallas_call(functools.partial(step_kernel, dims, layout, acc is not No...  8.93 us
    ppermute x4, waiting for transfers between devices, on_device(): pa.append(lax.ppermute(pa[-1], 'rows', up))  7.85 us
    ppermute x4, starting transfers between devices, on_device(): pa.append(lax.ppermute(pa[-1], 'rows', up))  5.52 us
    ppermute x6, waiting for transfers between devices, xor_move(): lax.ppermute(value, axis, [(i, i ^ bit) for i in range(lax.axis_size(axis...  4.94 us
    ppermute x3, starting transfers between devices, on_device(): pb.append(lax.ppermute(pb[-1], 'rows', up))  3.72 us
    ppermute x4, starting transfers between devices, on_device(): qb.append(lax.ppermute(qb[-1], 'rows', down))  3.44 us
    ppermute x6, starting transfers between devices, xor_move(): lax.ppermute(value, axis, [(i, i ^ bit) for i in range(lax.axis_size(axis...  3.34 us
    ppermute x1, starting transfers between devices, on_device(): lax.ppermute(tile, 'rows', [(a, dict(up)[dict(up)[dict(up)[b]]]) for a, b...  3.3 us
  transfers between devices with their start and end apart: 21, of which 8 were waited for; matrix products, arithmetic and copies ran while one was open for 0% of the time, Pallas kernels for 22%

profile of v6, /device:TPU:0, one launch (start us, length us, event | category | flops | bytes accessed | tf_op | source)
XLA Modules:
  0.0 53.9 jit_solution(323565004038383974)
XLA Ops:
  0.6 0.6 %collective-permute-start = (s32[4,1,3]{0,1,2:T(1,128)}, s32[4,1,3]{0,1,2:T(1,128)S(1)}, u32[]{:S(2)}, u32[]{:S(2)}) collective-permute-start(s32[4,1,3]{0,1,2:T(1,128)} %param.3), channel_id=1, source_target_pairs={{0,1},{1,0},{2,3},{3,2},{4,5},{5,4},{6,7},{7,6},{8,9},{9,8},{10,11... | collective-permute-start | bytes 152 | tf_op jit(solution)/shard_map/ppermute | solution.py:370
  1.2 2.6 %collective-permute-start.2 = (s32[4,1,3]{0,1,2:T(1,128)}, s32[4,1,3]{0,1,2:T(1,128)S(1)}, u32[]{:S(2)}, u32[]{:S(2)}) collective-permute-start(s32[4,1,3]{0,1,2:T(1,128)} %param.3), channel_id=1, source_target_pairs={{0,3},{1,2},{2,1},{3,0},{4,7},{5,6},{6,5},{7,4},{8,11},{9,10},{10,... | collective-permute-start | bytes 152 | tf_op jit(solution)/shard_map/ppermute | solution.py:370
  3.8 0.0 collective-permute-start.1
  3.8 1.1 %prep.1 = (bf16[768,128]{1,0:T(8,128)(2,1)S(1)}, bf16[768,128]{1,0:T(8,128)(2,1)S(1)}) custom-call(bf16[1536,128]{1,0:T(8,128)(2,1)} %bitcast.13), custom_call_target="tpu_custom_call" | custom-call | tf_op jit(solution)/shard_map/prep/pallas_call | solution.py:440
  4.9 0.0 collective-permute-done
  4.9 0.4 collective-permute-done.2
  5.3 2.3 %collective-permute-done.1 = s32[4,1,3]{0,1,2:T(1,128)S(1)} collective-permute-done((s32[4,1,3]{0,1,2:T(1,128)}, s32[4,1,3]{0,1,2:T(1,128)S(1)}, u32[]{:S(2)}, u32[]{:S(2)}) %collective-permute-start.1) | collective-permute-done | bytes 80 | tf_op jit(solution)/shard_map/ppermute | solution.py:370
  7.6 0.8 %numbers.1 = (bf16[1568,128]{1,0:T(8,128)(2,1)S(1)}, bf16[784,128]{1,0:T(8,128)(2,1)S(1)}, bf16[784,128]{1,0:T(8,128)(2,1)S(1)}, bf16[16,128]{1,0:T(8,128)(2,1)S(1)}) custom-call(s32[3,1,4]{2,1,0:T(1,128)} %bitcast.14, s32[3,1,4]{2,1,0:T(1,128)S(1)} %bitcast.9, s32[3,1,4]{2,1,0:T(1,128)S(1)} %bitcast.11, s32[3,1,4]{2,1,0:T(1,128)S(1)} %bitcast.10, ...), custom_call_target="tpu_custom_call" | custom-call | tf_op jit(solution)/shard_map/numbers/pallas_call | solution.py:449
  8.4 0.1 collective-permute-start.4
  8.5 2.0 %collective-permute-start.6 = (bf16[768,128]{1,0:T(8,128)(2,1)S(1)}, bf16[768,128]{1,0:T(8,128)(2,1)S(1)}, u32[]{:S(2)}, u32[]{:S(2)}) collective-permute-start(bf16[768,128]{1,0:T(8,128)(2,1)S(1)} %get-tuple-element.13.refs_4_), channel_id=1, source_target_pairs={{0,8},{8,16},{16,24},{24,28},{28,20},{20,12},{12,4},{4,0},{1,9},{9... | collective-permute-start | bytes 589832 | tf_op jit(solution)/shard_map/ppermute | solution.py:466
  10.6 1.6 %collective-permute-start.15 = (bf16[784,128]{1,0:T(8,128)(2,1)S(1)}, bf16[784,128]{1,0:T(8,128)(2,1)S(1)}, u32[]{:S(2)}, u32[]{:S(2)}) collective-permute-start(bf16[784,128]{1,0:T(8,128)(2,1)S(1)} %get-tuple-element.17), channel_id=1, source_target_pairs={{0,8},{8,16},{16,24},{24,28},{28,20},{20,12},{12,4},{4,0},{1,9},{9... | collective-permute-start | bytes 602120 | tf_op jit(solution)/shard_map/ppermute | solution.py:469
  12.1 0.4 collective-permute-start.10
  12.6 0.0 collective-permute-start.18
  12.6 3.7 %collective-permute-done.6.refs_5_ = bf16[768,128]{1,0:T(8,128)(2,1)S(1)} collective-permute-done((bf16[768,128]{1,0:T(8,128)(2,1)S(1)}, bf16[768,128]{1,0:T(8,128)(2,1)S(1)}, u32[]{:S(2)}, u32[]{:S(2)}) %collective-permute-start.6) | collective-permute-done | bytes 196640 | tf_op jit(solution)/shard_map/ppermute | solution.py:466
  16.3 0.0 collective-permute-start.3
  16.3 2.3 %collective-permute-done.4.refs_2_ = bf16[1568,128]{1,0:T(8,128)(2,1)S(1)} collective-permute-done((bf16[1568,128]{1,0:T(8,128)(2,1)S(1)}, bf16[1568,128]{1,0:T(8,128)(2,1)S(1)}, u32[]{:S(2)}, u32[]{:S(2)}) %collective-permute-start.4) | collective-permute-done | bytes 401440 | tf_op jit(solution)/shard_map/ppermute | solution.py:370
  18.6 0.0 collective-permute-start.5
  18.6 1.0 %collective-permute-done.10.refs_8_ = bf16[768,128]{1,0:T(8,128)(2,1)S(1)} collective-permute-done((bf16[768,128]{1,0:T(8,128)(2,1)S(1)}, bf16[768,128]{1,0:T(8,128)(2,1)S(1)}, u32[]{:S(2)}, u32[]{:S(2)}) %collective-permute-start.10) | collective-permute-done | bytes 196640 | tf_op jit(solution)/shard_map/ppermute | solution.py:467
  19.6 1.6 %collective-permute-start.7 = (bf16[768,128]{1,0:T(8,128)(2,1)S(1)}, bf16[768,128]{1,0:T(8,128)(2,1)S(1)}, u32[]{:S(2)}, u32[]{:S(2)}) collective-permute-start(bf16[768,128]{1,0:T(8,128)(2,1)S(1)} %collective-permute-done.6.refs_5_), channel_id=1, source_target_pairs={{0,8},{8,16},{16,24},{24,28},{28,20},{20,12},{12,4},{4,0},{1,9},{9... | collective-permute-start | bytes 589832 | tf_op jit(solution)/shard_map/ppermute | solution.py:466
  21.1 0.0 collective-permute-done.15.refs_6_.refs_10_
  21.1 1.5 %collective-permute-start.16 = (bf16[784,128]{1,0:T(8,128)(2,1)S(1)}, bf16[784,128]{1,0:T(8,128)(2,1)S(1)}, u32[]{:S(2)}, u32[]{:S(2)}) collective-permute-start(bf16[784,128]{1,0:T(8,128)(2,1)S(1)} %collective-permute-done.15.refs_6_.refs_10_), channel_id=1, source_target_pairs={{0,8},{8,16},{16,24},{24,28},{28,20},{20,12},{12,4},{4,0},{1,9},{9... | collective-permute-start | bytes 602120 | tf_op jit(solution)/shard_map/ppermute | solution.py:469
  22.7 0.0 collective-permute-done.18.refs_7_.refs_11_
  22.7 0.5 collective-permute-start.11
  23.2 4.2 %collective-permute-done.7.refs_4_ = bf16[768,128]{1,0:T(8,128)(2,1)S(1)} collective-permute-done((bf16[768,128]{1,0:T(8,128)(2,1)S(1)}, bf16[768,128]{1,0:T(8,128)(2,1)S(1)}, u32[]{:S(2)}, u32[]{:S(2)}) %collective-permute-start.7) | collective-permute-done | bytes 196640 | tf_op jit(solution)/shard_map/ppermute | solution.py:466
  27.3 0.6 %collective-permute-start.19 = (bf16[784,128]{1,0:T(8,128)(2,1)S(1)}, bf16[784,128]{1,0:T(8,128)(2,1)S(1)}, u32[]{:S(2)}, u32[]{:S(2)}) collective-permute-start(bf16[784,128]{1,0:T(8,128)(2,1)S(1)} %collective-permute-done.18.refs_7_.refs_11_), channel_id=1, source_target_pairs={{8,0},{16,8},{24,16},{28,24},{20,28},{12,20},{4,12},{0,4},{9,1},{1... | collective-permute-start | bytes 602120 | tf_op jit(solution)/shard_map/ppermute | solution.py:470
  27.9 1.9 %collective-permute-done.11.refs_7_ = bf16[768,128]{1,0:T(8,128)(2,1)S(1)} collective-permute-done((bf16[768,128]{1,0:T(8,128)(2,1)S(1)}, bf16[768,128]{1,0:T(8,128)(2,1)S(1)}, u32[]{:S(2)}, u32[]{:S(2)}) %collective-permute-start.11) | collective-permute-done | bytes 196640 | tf_op jit(solution)/shard_map/ppermute | solution.py:467
  29.8 1.3 %collective-permute-start.8 = (bf16[768,128]{1,0:T(8,128)(2,1)S(1)}, bf16[768,128]{1,0:T(8,128)(2,1)S(1)}, u32[]{:S(2)}, u32[]{:S(2)}) collective-permute-start(bf16[768,128]{1,0:T(8,128)(2,1)S(1)} %collective-permute-done.7.refs_4_), channel_id=1, source_target_pairs={{0,8},{8,16},{16,24},{24,28},{28,20},{20,12},{12,4},{4,0},{1,9},{9... | collective-permute-start | bytes 589832 | tf_op jit(solution)/shard_map/ppermute | solution.py:466
  31.1 0.0 collective-permute-done.16.refs_5_.refs_12_
  31.1 1.1 %collective-permute-start.12 = (bf16[768,128]{1,0:T(8,128)(2,1)S(1)}, bf16[768,128]{1,0:T(8,128)(2,1)S(1)}, u32[]{:S(2)}, u32[]{:S(2)}) collective-permute-start(bf16[768,128]{1,0:T(8,128)(2,1)S(1)} %collective-permute-done.11.refs_7_), channel_id=1, source_target_pairs={{8,0},{16,8},{24,16},{28,24},{20,28},{12,20},{4,12},{0,4},{9,1},{1... | collective-permute-start | bytes 589832 | tf_op jit(solution)/shard_map/ppermute | solution.py:467
  32.2 2.1 %zero.1.refs_9_ = bf16[4,36,128,128]{3,2,1,0:T(8,128)(2,1)} custom-call(), custom_call_target="tpu_custom_call" | custom-call | tf_op jit(solution)/shard_map/zero/pallas_call | solution.py:303
  34.3 0.3 collective-permute-done.19.refs_6_.refs_13_
  34.6 3.3 %collective-permute-start.14 = (bf16[16,128]{1,0:T(8,128)(2,1)S(1)}, bf16[16,128]{1,0:T(8,128)(2,1)S(1)}, u32[]{:S(2)}, u32[]{:S(2)}) collective-permute-start(bf16[16,128]{1,0:T(8,128)(2,1)S(1)} %get-tuple-element.16.refs_8_), channel_id=1, source_target_pairs={{0,28},{8,20},{16,12},{24,4},{28,0},{20,8},{12,16},{4,24},{1,29},{... | collective-permute-start | bytes 12296 | tf_op jit(solution)/shard_map/ppermute | solution.py:479
  37.9 0.0 collective-permute-done.3.refs_1_
  37.9 0.6 %collective-permute-start.17 = (bf16[784,128]{1,0:T(8,128)(2,1)S(1)}, bf16[784,128]{1,0:T(8,128)(2,1)S(1)}, u32[]{:S(2)}, u32[]{:S(2)}) collective-permute-start(bf16[784,128]{1,0:T(8,128)(2,1)S(1)} %collective-permute-done.16.refs_5_.refs_12_), channel_id=1, source_target_pairs={{0,8},{8,16},{16,24},{24,28},{28,20},{20,12},{12,4},{4,0},{1,9},{9... | collective-permute-start | bytes 602120 | tf_op jit(solution)/shard_map/ppermute | solution.py:469
  38.5 0.0 collective-permute-done.8.refs_4_
  38.5 1.4 %collective-permute-start.20 = (bf16[784,128]{1,0:T(8,128)(2,1)S(1)}, bf16[784,128]{1,0:T(8,128)(2,1)S(1)}, u32[]{:S(2)}, u32[]{:S(2)}) collective-permute-start(bf16[784,128]{1,0:T(8,128)(2,1)S(1)} %collective-permute-done.19.refs_6_.refs_13_), channel_id=1, source_target_pairs={{8,0},{16,8},{24,16},{28,24},{20,28},{12,20},{4,12},{0,4},{9,1},{1... | collective-permute-start | bytes 602120 | tf_op jit(solution)/shard_map/ppermute | solution.py:470
  39.9 0.0 collective-permute-done.12.refs_7_
  39.9 0.6 %collective-permute-start.9 = (bf16[768,128]{1,0:T(8,128)(2,1)S(1)}, bf16[768,128]{1,0:T(8,128)(2,1)S(1)}, u32[]{:S(2)}, u32[]{:S(2)}) collective-permute-start(bf16[768,128]{1,0:T(8,128)(2,1)S(1)} %collective-permute-done.8.refs_4_), channel_id=1, source_target_pairs={{0,8},{8,16},{16,24},{24,28},{28,20},{20,12},{12,4},{4,0},{1,9},{9... | collective-permute-start | bytes 589832 | tf_op jit(solution)/shard_map/ppermute | solution.py:466
  40.5 0.0 collective-permute-done.5.refs_3_
  40.6 1.4 %collective-permute-start.13 = (bf16[768,128]{1,0:T(8,128)(2,1)S(1)}, bf16[768,128]{1,0:T(8,128)(2,1)S(1)}, u32[]{:S(2)}, u32[]{:S(2)}) collective-permute-start(bf16[768,128]{1,0:T(8,128)(2,1)S(1)} %collective-permute-done.12.refs_7_), channel_id=1, source_target_pairs={{8,0},{16,8},{24,16},{28,24},{20,28},{12,20},{4,12},{0,4},{9,1},{1... | collective-permute-start | bytes 589832 | tf_op jit(solution)/shard_map/ppermute | solution.py:467
  42.0 3.1 %shard_map.49.refs_8_ = f32[512,1024]{1,0:T(8,128)S(1)} custom-call(bf16[1568,128]{1,0:T(8,128)(2,1)S(1)} %get-tuple-element.15.refs_0_.refs_4_, bf16[1568,128]{1,0:T(8,128)(2,1)S(1)} %collective-permute-done.3.refs_1_, bf16[1568,128]{1,0:T(8,128)(2,1)S(1)} %collective-permute-done.4.refs_2_, bf16[1568,128]{1,0:T(8,128)(2,1)S(1)} %collective-permute-done.5.refs_3_, ...), custom_call_target="tpu_custom_call" | custom-call | flops 1610612736 | bytes 4000000 | tf_op jit(solution)/shard_map/pallas_call | solution.py:338
  45.0 2.7 %shard_map.50.refs_16_ = f32[512,1024]{1,0:T(8,128)S(1)} custom-call(bf16[1568,128]{1,0:T(8,128)(2,1)S(1)} %get-tuple-element.15.refs_0_.refs_4_, bf16[1568,128]{1,0:T(8,128)(2,1)S(1)} %collective-permute-done.3.refs_1_, bf16[1568,128]{1,0:T(8,128)(2,1)S(1)} %collective-permute-done.4.refs_2_, ...), custom_call_target="tpu_custom_call", output_to_operand_aliasing={{}: (8, {})} | custom-call | flops 1073741824 | bytes 4000000 | tf_op jit(solution)/shard_map/pallas_call | solution.py:338
  47.7 0.0 collective-permute-done.14.refs_9_.refs_6_
  47.7 0.0 collective-permute-done.17.refs_5_.refs_14_
  47.7 0.0 collective-permute-done.20.refs_6_.refs_15_
  47.7 3.2 %shard_map.51 = (f32[512,1024]{1,0:T(8,128)S(1)}, s32[32]{0:T(128)S(1)}, s32[4,1,36]{2,1,0:T(1,128)}, s32[1,4]{1,0:T(1,128)}) custom-call(bf16[1568,128]{1,0:T(8,128)(2,1)S(1)} %get-tuple-element.15.refs_0_.refs_4_, bf16[1568,128]{1,0:T(8,128)(2,1)S(1)} %collective-permute-done.3.refs_1_, ...), custom_call_target="tpu_custom_call", output_to_operand_aliasing={{0}: (16, {})} | custom-call | flops 1073741824 | bytes 4000000 | tf_op jit(solution)/shard_map/pallas_call | solution.py:338
  50.9 0.0 collective-permute-done.13.refs_5_
  51.0 3.0 %shard_map.52 = bf16[4,36,128,128]{3,2,1,0:T(8,128)(2,1)} custom-call(bf16[1568,128]{1,0:T(8,128)(2,1)S(1)} %get-tuple-element.15.refs_0_.refs_4_, bf16[1568,128]{1,0:T(8,128)(2,1)S(1)} %collective-permute-done.3.refs_1_, bf16[1568,128]{1,0:T(8,128)(2,1)S(1)} %collective-permute-done.4.refs_2_, ...), custom_call_target="tpu_custom_call", output_to_operand_aliasing={{}: (9, {})} | custom-call | flops 536870912 | bytes 4000000 | tf_op jit(solution)/shard_map/pallas_call | solution.py:353
  (1 shorter events, 0.0 us)
Async XLA Ops:
  0.6 4.3 %collective-permute-start = (s32[4,1,3]{0,1,2:T(1,128)}, s32[4,1,3]{0,1,2:T(1,128)S(1)}, u32[]{:S(2)}, u32[]{:S(2)}) collective-permute-start(s32[4,1,3]{0,1,2:T(1,128)} %param.3), channel_id=1, source_target_pairs={{0,1},{1,0},{2,3},{3,2},{4,5},{5,4},{6,7},{7,6},{8,9},{9,8},{10,11... | collective-permute-start | bytes 152 | tf_op jit(solution)/shard_map/ppermute | solution.py:370
  1.2 4.1 %collective-permute-start.2 = (s32[4,1,3]{0,1,2:T(1,128)}, s32[4,1,3]{0,1,2:T(1,128)S(1)}, u32[]{:S(2)}, u32[]{:S(2)}) collective-permute-start(s32[4,1,3]{0,1,2:T(1,128)} %param.3), channel_id=1, source_target_pairs={{0,3},{1,2},{2,1},{3,0},{4,7},{5,6},{6,5},{7,4},{8,11},{9,10},{10,... | collective-permute-start | bytes 152 | tf_op jit(solution)/shard_map/ppermute | solution.py:370
  3.8 3.8 %collective-permute-start.1 = (s32[4,1,3]{0,1,2:T(1,128)}, s32[4,1,3]{0,1,2:T(1,128)S(1)}, u32[]{:S(2)}, u32[]{:S(2)}) collective-permute-start(s32[4,1,3]{0,1,2:T(1,128)} %param.3), channel_id=1, source_target_pairs={{0,2},{1,3},{2,0},{3,1},{4,6},{5,7},{6,4},{7,5},{8,10},{9,11},{10,... | collective-permute-start | bytes 152 | tf_op jit(solution)/shard_map/ppermute | solution.py:370
  8.4 10.2 %collective-permute-start.4 = (bf16[1568,128]{1,0:T(8,128)(2,1)S(1)}, bf16[1568,128]{1,0:T(8,128)(2,1)S(1)}, u32[]{:S(2)}, u32[]{:S(2)}) collective-permute-start(bf16[1568,128]{1,0:T(8,128)(2,1)S(1)} %get-tuple-element.15.refs_0_.refs_4_), channel_id=1, source_target_pairs={{0,2},{1,3},{2,0},{3,1},{4,6},{5,7},{6,4},{7,5},{8,10},{9,11},{10,... | collective-permute-start | bytes 1204232 | tf_op jit(solution)/shard_map/ppermute | solution.py:370
  8.5 7.8 %collective-permute-start.6 = (bf16[768,128]{1,0:T(8,128)(2,1)S(1)}, bf16[768,128]{1,0:T(8,128)(2,1)S(1)}, u32[]{:S(2)}, u32[]{:S(2)}) collective-permute-start(bf16[768,128]{1,0:T(8,128)(2,1)S(1)} %get-tuple-element.13.refs_4_), channel_id=1, source_target_pairs={{0,8},{8,16},{16,24},{24,28},{28,20},{20,12},{12,4},{4,0},{1,9},{9... | collective-permute-start | bytes 589832 | tf_op jit(solution)/shard_map/ppermute | solution.py:466
  10.6 10.6 %collective-permute-start.15 = (bf16[784,128]{1,0:T(8,128)(2,1)S(1)}, bf16[784,128]{1,0:T(8,128)(2,1)S(1)}, u32[]{:S(2)}, u32[]{:S(2)}) collective-permute-start(bf16[784,128]{1,0:T(8,128)(2,1)S(1)} %get-tuple-element.17), channel_id=1, source_target_pairs={{0,8},{8,16},{16,24},{24,28},{28,20},{20,12},{12,4},{4,0},{1,9},{9... | collective-permute-start | bytes 602120 | tf_op jit(solution)/shard_map/ppermute | solution.py:469
  12.1 7.4 %collective-permute-start.10 = (bf16[768,128]{1,0:T(8,128)(2,1)S(1)}, bf16[768,128]{1,0:T(8,128)(2,1)S(1)}, u32[]{:S(2)}, u32[]{:S(2)}) collective-permute-start(bf16[768,128]{1,0:T(8,128)(2,1)S(1)} %get-tuple-element.14.refs_5_), channel_id=1, source_target_pairs={{8,0},{16,8},{24,16},{28,24},{20,28},{12,20},{4,12},{0,4},{9,1},{1... | collective-permute-start | bytes 589832 | tf_op jit(solution)/shard_map/ppermute | solution.py:467
  12.6 10.1 %collective-permute-start.18 = (bf16[784,128]{1,0:T(8,128)(2,1)S(1)}, bf16[784,128]{1,0:T(8,128)(2,1)S(1)}, u32[]{:S(2)}, u32[]{:S(2)}) collective-permute-start(bf16[784,128]{1,0:T(8,128)(2,1)S(1)} %get-tuple-element.18), channel_id=1, source_target_pairs={{8,0},{16,8},{24,16},{28,24},{20,28},{12,20},{4,12},{0,4},{9,1},{1... | collective-permute-start | bytes 602120 | tf_op jit(solution)/shard_map/ppermute | solution.py:470
  16.3 21.6 %collective-permute-start.3 = (bf16[1568,128]{1,0:T(8,128)(2,1)S(1)}, bf16[1568,128]{1,0:T(8,128)(2,1)S(1)}, u32[]{:S(2)}, u32[]{:S(2)}) collective-permute-start(bf16[1568,128]{1,0:T(8,128)(2,1)S(1)} %get-tuple-element.15.refs_0_.refs_4_), channel_id=1, source_target_pairs={{0,1},{1,0},{2,3},{3,2},{4,5},{5,4},{6,7},{7,6},{8,9},{9,8},{10,11... | collective-permute-start | bytes 1204232 | tf_op jit(solution)/shard_map/ppermute | solution.py:370
  18.6 22.0 %collective-permute-start.5 = (bf16[1568,128]{1,0:T(8,128)(2,1)S(1)}, bf16[1568,128]{1,0:T(8,128)(2,1)S(1)}, u32[]{:S(2)}, u32[]{:S(2)}) collective-permute-start(bf16[1568,128]{1,0:T(8,128)(2,1)S(1)} %collective-permute-done.4.refs_2_), channel_id=1, source_target_pairs={{0,1},{1,0},{2,3},{3,2},{4,5},{5,4},{6,7},{7,6},{8,9},{9,8},{10,11... | collective-permute-start | bytes 1204232 | tf_op jit(solution)/shard_map/ppermute | solution.py:370
  19.6 7.8 %collective-permute-start.7 = (bf16[768,128]{1,0:T(8,128)(2,1)S(1)}, bf16[768,128]{1,0:T(8,128)(2,1)S(1)}, u32[]{:S(2)}, u32[]{:S(2)}) collective-permute-start(bf16[768,128]{1,0:T(8,128)(2,1)S(1)} %collective-permute-done.6.refs_5_), channel_id=1, source_target_pairs={{0,8},{8,16},{16,24},{24,28},{28,20},{20,12},{12,4},{4,0},{1,9},{9... | collective-permute-start | bytes 589832 | tf_op jit(solution)/shard_map/ppermute | solution.py:466
  21.1 10.0 %collective-permute-start.16 = (bf16[784,128]{1,0:T(8,128)(2,1)S(1)}, bf16[784,128]{1,0:T(8,128)(2,1)S(1)}, u32[]{:S(2)}, u32[]{:S(2)}) collective-permute-start(bf16[784,128]{1,0:T(8,128)(2,1)S(1)} %collective-permute-done.15.refs_6_.refs_10_), channel_id=1, source_target_pairs={{0,8},{8,16},{16,24},{24,28},{28,20},{20,12},{12,4},{4,0},{1,9},{9... | collective-permute-start | bytes 602120 | tf_op jit(solution)/shard_map/ppermute | solution.py:469
  22.7 7.2 %collective-permute-start.11 = (bf16[768,128]{1,0:T(8,128)(2,1)S(1)}, bf16[768,128]{1,0:T(8,128)(2,1)S(1)}, u32[]{:S(2)}, u32[]{:S(2)}) collective-permute-start(bf16[768,128]{1,0:T(8,128)(2,1)S(1)} %collective-permute-done.10.refs_8_), channel_id=1, source_target_pairs={{8,0},{16,8},{24,16},{28,24},{20,28},{12,20},{4,12},{0,4},{9,1},{1... | collective-permute-start | bytes 589832 | tf_op jit(solution)/shard_map/ppermute | solution.py:467
  27.3 7.3 %collective-permute-start.19 = (bf16[784,128]{1,0:T(8,128)(2,1)S(1)}, bf16[784,128]{1,0:T(8,128)(2,1)S(1)}, u32[]{:S(2)}, u32[]{:S(2)}) collective-permute-start(bf16[784,128]{1,0:T(8,128)(2,1)S(1)} %collective-permute-done.18.refs_7_.refs_11_), channel_id=1, source_target_pairs={{8,0},{16,8},{24,16},{28,24},{20,28},{12,20},{4,12},{0,4},{9,1},{1... | collective-permute-start | bytes 602120 | tf_op jit(solution)/shard_map/ppermute | solution.py:470
  29.8 8.7 %collective-permute-start.8 = (bf16[768,128]{1,0:T(8,128)(2,1)S(1)}, bf16[768,128]{1,0:T(8,128)(2,1)S(1)}, u32[]{:S(2)}, u32[]{:S(2)}) collective-permute-start(bf16[768,128]{1,0:T(8,128)(2,1)S(1)} %collective-permute-done.7.refs_4_), channel_id=1, source_target_pairs={{0,8},{8,16},{16,24},{24,28},{28,20},{20,12},{12,4},{4,0},{1,9},{9... | collective-permute-start | bytes 589832 | tf_op jit(solution)/shard_map/ppermute | solution.py:466
  31.1 8.8 %collective-permute-start.12 = (bf16[768,128]{1,0:T(8,128)(2,1)S(1)}, bf16[768,128]{1,0:T(8,128)(2,1)S(1)}, u32[]{:S(2)}, u32[]{:S(2)}) collective-permute-start(bf16[768,128]{1,0:T(8,128)(2,1)S(1)} %collective-permute-done.11.refs_7_), channel_id=1, source_target_pairs={{8,0},{16,8},{24,16},{28,24},{20,28},{12,20},{4,12},{0,4},{9,1},{1... | collective-permute-start | bytes 589832 | tf_op jit(solution)/shard_map/ppermute | solution.py:467
  34.6 13.1 %collective-permute-start.14 = (bf16[16,128]{1,0:T(8,128)(2,1)S(1)}, bf16[16,128]{1,0:T(8,128)(2,1)S(1)}, u32[]{:S(2)}, u32[]{:S(2)}) collective-permute-start(bf16[16,128]{1,0:T(8,128)(2,1)S(1)} %get-tuple-element.16.refs_8_), channel_id=1, source_target_pairs={{0,28},{8,20},{16,12},{24,4},{28,0},{20,8},{12,16},{4,24},{1,29},{... | collective-permute-start | bytes 12296 | tf_op jit(solution)/shard_map/ppermute | solution.py:479
  37.9 9.8 %collective-permute-start.17 = (bf16[784,128]{1,0:T(8,128)(2,1)S(1)}, bf16[784,128]{1,0:T(8,128)(2,1)S(1)}, u32[]{:S(2)}, u32[]{:S(2)}) collective-permute-start(bf16[784,128]{1,0:T(8,128)(2,1)S(1)} %collective-permute-done.16.refs_5_.refs_12_), channel_id=1, source_target_pairs={{0,8},{8,16},{16,24},{24,28},{28,20},{20,12},{12,4},{4,0},{1,9},{9... | collective-permute-start | bytes 602120 | tf_op jit(solution)/shard_map/ppermute | solution.py:469
  38.5 9.2 %collective-permute-start.20 = (bf16[784,128]{1,0:T(8,128)(2,1)S(1)}, bf16[784,128]{1,0:T(8,128)(2,1)S(1)}, u32[]{:S(2)}, u32[]{:S(2)}) collective-permute-start(bf16[784,128]{1,0:T(8,128)(2,1)S(1)} %collective-permute-done.19.refs_6_.refs_13_), channel_id=1, source_target_pairs={{8,0},{16,8},{24,16},{28,24},{20,28},{12,20},{4,12},{0,4},{9,1},{1... | collective-permute-start | bytes 602120 | tf_op jit(solution)/shard_map/ppermute | solution.py:470
  39.9 11.0 %collective-permute-start.9 = (bf16[768,128]{1,0:T(8,128)(2,1)S(1)}, bf16[768,128]{1,0:T(8,128)(2,1)S(1)}, u32[]{:S(2)}, u32[]{:S(2)}) collective-permute-start(bf16[768,128]{1,0:T(8,128)(2,1)S(1)} %collective-permute-done.8.refs_4_), channel_id=1, source_target_pairs={{0,8},{8,16},{16,24},{24,28},{28,20},{20,12},{12,4},{4,0},{1,9},{9... | collective-permute-start | bytes 589832 | tf_op jit(solution)/shard_map/ppermute | solution.py:466
  40.6 10.4 %collective-permute-start.13 = (bf16[768,128]{1,0:T(8,128)(2,1)S(1)}, bf16[768,128]{1,0:T(8,128)(2,1)S(1)}, u32[]{:S(2)}, u32[]{:S(2)}) collective-permute-start(bf16[768,128]{1,0:T(8,128)(2,1)S(1)} %collective-permute-done.12.refs_7_), channel_id=1, source_target_pairs={{8,0},{16,8},{24,16},{28,24},{20,28},{12,20},{4,12},{0,4},{9,1},{1... | collective-permute-start | bytes 589832 | tf_op jit(solution)/shard_map/ppermute | solution.py:467

commit v7 on v6

--- a/solution.py
+++ b/solution.py
@@ -28,7 +28,7 @@
         self.whole = cycle == 2 * HP and bins == cycle
 
     def at(self, j, s):
-        return (j * self.per_group + s) * self.bs + (IDX if j >= self.groups // 2 else 0)
+        return (j * self.per_group + s) * self.bs
 
 
 def ring_place(panel, cycle):
@@ -52,18 +52,19 @@
     return jnp.concatenate([tile] * (rows // 16), axis=0)
 
 
-def prep_kernel(dims, blocks_ref, a_ref, b_ref, sems):
+def prep_kernel(dims, blocks_ref, full_ref, a_ref, b_ref, sems):
     me = lax.axis_index("cols").astype(jnp.int32)
     span = dims.per_group * dims.bs
     copies = []
     for j in range(dims.groups):
         at = j * span
         ref, start = (a_ref, at) if at < dims.half else (b_ref, at - dims.half)
-        copy = pltpu.make_async_copy(
-            blocks_ref.at[pl.ds((me ^ j) * span, span)], ref.at[start : start + span], sems.at[j]
-        )
-        copy.start()
-        copies.append(copy)
+        for k, (out_ref, first) in enumerate(((ref, start), (full_ref, at))):
+            copy = pltpu.make_async_copy(
+                blocks_ref.at[pl.ds((me ^ j) * span, span)], out_ref.at[first : first + span], sems.at[j, k]
+            )
+            copy.start()
+            copies.append(copy)
     for copy in copies:
         copy.wait()
 
@@ -71,16 +72,14 @@
 def number_kernel(dims, *refs):
     refs = list(refs)
     names = take(refs, dims.groups)
-    a_ref, b_ref, full_ref, a_out, b_out, tile_ref, cols_ref, sems = refs
+    a_ref, b_ref, a_out, b_out, tile_ref, cols_ref, sems = refs
     copies = []
     for j in range(dims.groups):
         copies.append(pltpu.make_async_copy(names[j], cols_ref.at[j], sems.at[j]))
         copies[-1].start()
     half = dims.half
-    for ref, out_ref, at in ((a_ref, a_out, 0), (b_ref, b_out, half + IDX)):
-        value = ref[...]
-        out_ref[0:half, :] = value
-        full_ref[at : at + half, :] = value
+    for ref, out_ref in ((a_ref, a_out), (b_ref, b_out)):
+        out_ref[0:half, :] = ref[...]
     me = lax.axis_index("cols").astype(jnp.int32)
     line = lax.broadcasted_iota(jnp.int32, (IDX, 128), 0)
     lane = lax.broadcasted_iota(jnp.int32, (IDX, 128), 1)
@@ -97,27 +96,27 @@
     tile_ref[...] = numbers
     for ref in (a_out, b_out):
         ref[half : half + IDX, :] = numbers
-    for at in (half, 2 * half + IDX):
-        full_ref[at : at + IDX, :] = numbers
-
-
-def accumulate(dims, pieces, left, lp_ref, d_ref, emit):
+
+
+def left_matrix(dims, distance, left, tile_ref, lp_ref, first):
+    per_group, bs = dims.per_group, dims.bs
+    numbers = tile_ref[...].astype(jnp.float32)
+    hits = jnp.where(numbers == panel_number(dims, distance).astype(jnp.float32), 1.0, 0.0)
+    for j in range(dims.groups):
+        for m in range(dims.groups):
+            total = None
+            for t in range(per_group):
+                at = dims.at(m ^ j, t)
+                lane = (m ^ j) * per_group + t
+                hit = jnp.broadcast_to(hits[j : j + 1, lane : lane + 1], (16, 128)).astype(jnp.bfloat16)
+                term = left[j][at : at + bs, :] * stretch(hit, bs)
+                total = term if total is None else total + term
+            lp_ref[m * bs : (m + 1) * bs, first + j * bs : first + (j + 1) * bs] = total
+
+
+def accumulate(dims, pieces, lp_ref, d_ref, emit):
     groups, per_group, bs, bins = dims.groups, dims.per_group, dims.bs, dims.bins
     depth = dims.rows
-    lrows = [ref[dims.half : dims.half + 16, :].astype(jnp.float32)[0:1, :] for ref in left]
-    for n, (distance, *_) in enumerate(pieces):
-        number = panel_number(dims, distance).astype(jnp.float32)
-        for j in range(groups):
-            hits = jnp.where(lrows[j] == number, 1.0, 0.0)
-            for m in range(groups):
-                total = None
-                for t in range(per_group):
-                    at = dims.at(m ^ j, t)
-                    lane = (m ^ j) * per_group + t
-                    hit = jnp.broadcast_to(hits[:, lane : lane + 1], (16, 128)).astype(jnp.bfloat16)
-                    term = left[j][at : at + bs, :] * stretch(hit, bs)
-                    total = term if total is None else total + term
-                lp_ref[m * bs : (m + 1) * bs, n * depth + j * bs : n * depth + (j + 1) * bs] = total
     rows_of = []
     for *_, ref, at in pieces:
         row = ref[at : at + 16, :].astype(jnp.float32)[0:1, :]
@@ -135,7 +134,7 @@
                     for s in range(per_group):
                         ref, start = a_ref, dims.at(j, s)
                         if b_ref is not None and j >= groups // 2:
-                            ref, start = b_ref, start - dims.half - IDX
+                            ref, start = b_ref, start - dims.half
                         lane = j * per_group + s
                         hit = jnp.broadcast_to(hits[:, lane : lane + 1], (16, 128)).astype(jnp.bfloat16)
                         term = ref[start : start + bs, :] * stretch(hit, bs)
@@ -159,7 +158,7 @@
         if where == "far":
             source, at = refs.pop(0), 0
         else:
-            source, at = (b_ref if where == "b" else a_ref), dims.half
+            source, at = (b_ref if where == "b" else a_ref), dims.half if two else 2 * dims.half
         pieces.append((distance, a_ref, b_ref, source, at))
     return pieces
 
@@ -178,36 +177,51 @@
         copy.wait()
 
 
-def step_kernel(dims, layout, with_acc, tiles, *refs):
+def step_kernel(dims, layout, with_acc, ahead, tiles, *refs):
     refs = list(refs)
     left = take(refs, dims.groups)
+    tile_ref = refs.pop(0)
     pieces = take_pieces(dims, refs, layout)
     tile_refs = take(refs, len(tiles))
     acc_ref = refs.pop(0) if with_acc else None
     out_ref = refs.pop(0)
+    ahead_ref = refs.pop(0) if ahead is not None else None
     index_refs = take(refs, 3) if tiles else None
     lp_ref, d_ref = take(refs, 2)
+    copies = []
     if tiles:
-        wide_ref, count_ref = refs
-        index_work(dims, tiles, tile_refs, wide_ref, *index_refs, count_ref)
+        wide_ref, count_ref, slot_ref, cols_ref, start_ref, sems = refs
+        index_work(dims, tiles, tile_refs, wide_ref, slot_ref, cols_ref, start_ref, count_ref)
+        for k, (ref, out) in enumerate(zip((slot_ref, cols_ref, start_ref), index_refs)):
+            copies.append(pltpu.make_async_copy(ref, out, sems.at[k]))
+            copies[-1].start()
 
     def emit(lo, hi, value):
         out_ref[:, lo:hi] = value if acc_ref is None else acc_ref[:, lo:hi] + value
 
-    accumulate(dims, pieces, left, lp_ref, d_ref, emit)
+    for n, (distance, *_) in enumerate(pieces):
+        left_matrix(dims, distance, left, tile_ref, lp_ref, n * dims.rows)
+    accumulate(dims, pieces, lp_ref, d_ref, emit)
+    if ahead is not None:
+        left_matrix(dims, ahead, left, tile_ref, ahead_ref, 0)
+    for copy in copies:
+        copy.wait()
 
 
 def last_kernel(dims, layout, *refs):
     refs = list(refs)
-    left = take(refs, dims.groups)
     pieces = take_pieces(dims, refs, layout)
-    acc_ref, slot_ref, _, out_ref, lp_ref, d_ref, stage_ref, sems = refs
+    lp_ref, acc_ref, slots_ref, _, out_ref, d_ref, stage_ref, slot_ref, sems, sem = refs
     groups, bs, bins = dims.groups, dims.bs, dims.bins
     me = lax.axis_index("cols").astype(jnp.int32)
+    slots = pltpu.make_async_copy(slots_ref, slot_ref, sem)
+    slots.start()
     copies = []
 
     def emit(lo, hi, value):
         value = (acc_ref[:, lo:hi] + value).astype(jnp.bfloat16)
+        if lo == 0:
+            slots.wait()
         for b in range(lo // bs, hi // bs):
             for m in range(groups):
                 k = m * bins + b
@@ -219,7 +233,7 @@
                 copy.start()
                 copies.append(copy)
 
-    accumulate(dims, pieces, left, lp_ref, d_ref, emit)
+    accumulate(dims, pieces, lp_ref, d_ref, emit)
     for copy in copies:
         copy.wait()
 
@@ -313,9 +327,9 @@
     )()
 
 
-def call_step(dims, left, panels, acc, tiles=()):
+def call_step(dims, left, tile, panels, acc, ahead=None, tiles=()):
     layout, arrays = flat(panels)
-    args = [*left, *arrays, *(array for _, array, _ in tiles)]
+    args = [*left, tile, *arrays, *(array for _, array, _ in tiles)]
     aliases = {}
     if acc is not None:
         aliases = {len(args): 0}
@@ -323,20 +337,22 @@
     shapes = [jax.ShapeDtypeStruct((dims.rows, dims.bins * dims.bs), jnp.float32)]
     out_specs = [VMEM]
     scratch = scratch_of(dims, panels)
+    if ahead is not None:
+        shapes.append(jax.ShapeDtypeStruct((dims.rows, dims.rows), jnp.bfloat16))
+        out_specs.append(VMEM)
     if tiles:
-        shapes += [
-            jax.ShapeDtypeStruct((dims.groups * dims.bins,), jnp.int32),
-            jax.ShapeDtypeStruct((dims.groups, 1, dims.slots), jnp.int32),
-            jax.ShapeDtypeStruct((1, dims.groups), jnp.int32),
-        ]
-        out_specs += [SMEM] * 3
+        small = [(dims.groups * dims.bins,), (dims.groups, 1, dims.slots), (1, dims.groups)]
+        shapes += [jax.ShapeDtypeStruct(shape, jnp.int32) for shape in small]
+        out_specs += [ANY] * 3
         scratch += [
             pltpu.VMEM((dims.groups * dims.cycle, 128), jnp.int32),
             pltpu.SMEM((dims.groups,), jnp.int32),
+            *(pltpu.SMEM(shape, jnp.int32) for shape in small),
+            pltpu.SemaphoreType.DMA((3,)),
         ]
     marks = tuple((n, at) for n, _, at in tiles)
     return pl.pallas_call(
-        functools.partial(step_kernel, dims, layout, acc is not None, marks),
+        functools.partial(step_kernel, dims, layout, acc is not None, ahead, marks),
         out_shape=shapes,
         in_specs=[VMEM] * len(args),
         out_specs=out_specs,
@@ -347,18 +363,20 @@
     )(*args)
 
 
-def call_last(dims, left, panels, acc, slots, empty):
+def call_last(dims, panels, lp, acc, slots, empty):
     layout, arrays = flat(panels)
-    args = [*left, *arrays, acc, slots, empty]
+    args = [*arrays, lp, acc, slots, empty]
     return pl.pallas_call(
         functools.partial(last_kernel, dims, layout),
         out_shape=jax.ShapeDtypeStruct(empty.shape, empty.dtype),
-        in_specs=[VMEM] * (len(args) - 2) + [SMEM, ANY],
+        in_specs=[VMEM] * (len(args) - 2) + [ANY, ANY],
         out_specs=ANY,
-        scratch_shapes=scratch_of(dims, panels)
+        scratch_shapes=scratch_of(dims, panels)[1:]
         + [
             pltpu.VMEM((dims.groups * dims.bins, dims.bs, dims.bs), jnp.bfloat16),
+            pltpu.SMEM((dims.groups * dims.bins,), jnp.int32),
             pltpu.SemaphoreType.DMA((dims.groups * dims.bins,)),
+            pltpu.SemaphoreType.DMA,
         ],
         input_output_aliases={len(args) - 1: 0},
         compiler_params=pltpu.CompilerParams(vmem_limit_bytes=GRANT),
@@ -385,24 +403,24 @@
     return jnp.any(values[..., None] == wanted, axis=-2)
 
 
-def window_index(dims, left, window):
+def window_index(dims, tile, window):
     groups, per_group, bins, cycle = dims.groups, dims.per_group, dims.bins, dims.cycle
     p = lax.axis_index("rows").astype(jnp.int32)
     c = lax.axis_index("cols").astype(jnp.int32)
     lanes = jnp.arange(groups, dtype=jnp.int32)
 
     def numbers_of(array):
-        numbers = array[dims.half, : groups * per_group].astype(jnp.int32)
+        numbers = array[: groups * per_group].astype(jnp.int32)
         return numbers.reshape(groups, per_group)
 
     held = jnp.stack(
-        [numbers_of(left[j])[jnp.array([m ^ j for m in range(groups)])] for j in range(groups)], axis=1
+        [numbers_of(tile[j])[jnp.array([m ^ j for m in range(groups)])] for j in range(groups)], axis=1
     )
     lrel = (held - (p - HP)) % cycle
     zero = (p - 2 * HP) % cycle if bins < cycle else jnp.int32(0)
     bin_ids = jnp.arange(bins, dtype=jnp.int32)
     bin_abs = (zero + bin_ids) % cycle
-    has = jnp.stack([one_of((numbers_of(w) - zero) % cycle, bin_ids) for w in window])
+    has = jnp.stack([one_of((numbers_of(w[2 * dims.half]) - zero) % cycle, bin_ids) for w in window])
     uses = one_of(lrel, jnp.arange(2 * HP, dtype=jnp.int32))
     hits = jnp.any(uses.transpose(0, 2, 1)[..., None] & has[None], axis=(1, 2))
     counts = jnp.sum(hits.astype(jnp.int32), axis=-1)
@@ -437,20 +455,20 @@
     cols = [jnp.transpose(x, (2, 1, 0)) for x in cols]
     cols[0] = pltpu.with_memory_space_constraint(cols[0], pltpu.HBM)
     flat_blocks = pltpu.with_memory_space_constraint(blocks.reshape(-1, bs), pltpu.HBM)
-    bare_a, bare_b = pl.pallas_call(
+    own, bare_a, bare_b = pl.pallas_call(
         functools.partial(prep_kernel, dims),
-        out_shape=[payload(dims.half)] * 2,
+        out_shape=[payload(2 * dims.half)] + [payload(dims.half)] * 2,
         in_specs=[ANY],
-        out_specs=[VMEM] * 2,
-        scratch_shapes=[pltpu.SemaphoreType.DMA((groups,))],
+        out_specs=[VMEM] * 3,
+        scratch_shapes=[pltpu.SemaphoreType.DMA((groups, 2))],
         compiler_params=params,
         name="prep",
     )(flat_blocks)
-    own, own_a, own_b, tile = pl.pallas_call(
+    own_a, own_b, tile = pl.pallas_call(
         functools.partial(number_kernel, dims),
-        out_shape=[payload(2 * dims.half + 2 * IDX)] + [payload(dims.half + IDX)] * 2 + [payload(IDX)],
+        out_shape=[payload(dims.half + IDX)] * 2 + [payload(IDX)],
         in_specs=[ANY] * groups + [VMEM] * 2,
-        out_specs=[VMEM] * 4,
+        out_specs=[VMEM] * 3,
         scratch_shapes=[
             pltpu.SMEM((groups, per_group, 1, groups), jnp.int32),
             pltpu.SemaphoreType.DMA((groups,)),
@@ -469,7 +487,8 @@
                 pb.append(lax.ppermute(pb[-1], "rows", up))
                 qa.append(lax.ppermute(qa[-1], "rows", down))
     else:
-        window = [own if k == 0 else shifted(own, "rows", -k) for k in range(-HP, HP)]
+        sent = jnp.concatenate([bare_a, own_b], axis=0)
+        window = [sent if k == 0 else shifted(sent, "rows", -k) for k in range(-HP, HP)]
     left1 = xor_move(own, "cols", 1)
     left2 = xor_move(own, "cols", 2)
     left3 = xor_move(left2, "cols", 1)
@@ -478,23 +497,24 @@
     if dims.whole:
         far = lax.ppermute(tile, "rows", [(a, dict(up)[dict(up)[dict(up)[b]]]) for a, b in up])
         pairs = [[(-k, pa[k], pb[k], "b"), (k, qa[k], qb[k], "a")] for k in range(1, HP)]
-        acc = call_step(dims, left, [(0, own, None, "a")] + pairs[0], None)[0]
-        acc = call_step(dims, left, pairs[1], acc)[0]
+        first = [(0, bare_a, own_b, "b")] + pairs[0]
+        acc, lp = call_step(dims, left, tile, first, None, ahead=HP)
+        acc = call_step(dims, left, tile, pairs[1], acc)[0]
         tiles = [(0, tile, 0), (HP, far, 0)]
         for k in range(1, HP):
             tiles += [(cycle - k, pb[k], dims.half), (k, qa[k], dims.half)]
-        acc, slots, columns, starts = call_step(dims, left, pairs[2], acc, tiles)
+        acc, slots, columns, starts = call_step(dims, left, tile, pairs[2], acc, tiles=tiles)
         starts = starts.reshape(groups, 1)
         final = [(HP, pa[HP], qb[HP], far)]
     else:
-        slots, columns, starts = window_index(dims, left, window)
-        acc = call_step(dims, left, [(0, own, None, "a")], None)[0]
-        pairs = [(k, window[k + HP], None, "a") for k in range(-HP, HP) if k]
-        for k in range(0, len(pairs) - 1, 2):
-            acc = call_step(dims, left, pairs[k : k + 2], acc)[0]
+        slots, columns, starts = window_index(dims, tile, window)
+        pairs = [(k, window[k + HP], None, "a") for k in range(-HP, HP)]
+        acc, lp = call_step(dims, left, tile, pairs[:1], None, ahead=HP - 1)
+        for k in range(1, len(pairs) - 1, 2):
+            acc = call_step(dims, left, tile, pairs[k : k + 2], acc)[0]
         final = pairs[-1:]
     empty = call_zero(dims)
-    out = call_last(dims, left, final, acc, slots, empty)
+    out = call_last(dims, final, lp, acc, slots, empty)
     return out[:, None], columns, starts
 
 

time: 54.1 us -> 54.1 us (level)
  waiting for transfers between devices: 16 us -> 10.3 us
  starting transfers between devices: 21.3 us -> 26.9 us
    ppermute x4, waiting for transfers between devices: 7.85 us -> 0.86 us  [on_device(): pa.append(lax.ppermute(pa[-1], 'rows', up))]
    ppermute x3, waiting for transfers between devices: 0.33 us -> 4.06 us  [on_device(): qa.append(lax.ppermute(qa[-1], 'rows', down))]
    ppermute x4, waiting for transfers between devices: 2.91 us -> 0.38 us  [on_device(): qb.append(lax.ppermute(qb[-1], 'rows', down))]
    ppermute x4, starting transfers between devices: 3.44 us -> 5.71 us  [on_device(): qb.append(lax.ppermute(qb[-1], 'rows', down))]
    ppermute x6, starting transfers between devices: 3.34 us -> 5.18 us  [xor_move(): lax.ppermute(value, axis, [(i, i ^ bit) for i in range(lax.axis_size(axis...]
    ppermute x1, starting transfers between devices: 3.3 us -> 5.05 us  [on_device(): lax.ppermute(tile, 'rows', [(a, dict(up)[dict(up)[dict(up)[b]]]) for a, b...]
    ppermute x4, starting transfers between devices: 5.52 us -> 3.97 us  [on_device(): pa.append(lax.ppermute(pa[-1], 'rows', up))]
    ppermute x3, starting transfers between devices: 1.99 us -> 3.53 us  [on_device(): qa.append(lax.ppermute(qa[-1], 'rows', down))]
  transfers between devices with their start and end apart: 21 -> 21, of which waited for: 8 -> 5; matrix products, arithmetic and copies ran while one was open for 0% -> 0% of each run, Pallas kernels for 22% -> 22%
where the time goes in v7:
time: 54.1 us; the launch traced here: 53.9 us
  starting transfers between devices  26.9 us (50%)
  Pallas kernels  15.9 us (29%)
  waiting for transfers between devices  10.3 us (19%)
  between operations  0.75 us (1%)
    pallas_call x3, Pallas kernels, call_step(): pl.pallas_call(functools.partial(step_kernel, dims, layout, acc is not No...  9.04 us
    ppermute x4, starting transfers between devices, on_device(): qb.append(lax.ppermute(qb[-1], 'rows', down))  5.71 us
    ppermute x6, starting transfers between devices, xor_move(): lax.ppermute(value, axis, [(i, i ^ bit) for i in range(lax.axis_size(axis...  5.18 us
    ppermute x1, starting transfers between devices, on_device(): lax.ppermute(tile, 'rows', [(a, dict(up)[dict(up)[dict(up)[b]]]) for a, b...  5.05 us
    ppermute x6, waiting for transfers between devices, xor_move(): lax.ppermute(value, axis, [(i, i ^ bit) for i in range(lax.axis_size(axis...  5.02 us
    ppermute x3, waiting for transfers between devices, on_device(): qa.append(lax.ppermute(qa[-1], 'rows', down))  4.06 us
    ppermute x4, starting transfers between devices, on_device(): pa.append(lax.ppermute(pa[-1], 'rows', up))  3.97 us
    ppermute x3, starting transfers between devices, on_device(): qa.append(lax.ppermute(qa[-1], 'rows', down))  3.53 us
  transfers between devices with their start and end apart: 21, of which 5 were waited for; matrix products, arithmetic and copies ran while one was open for 0% of the time, Pallas kernels for 22%

profile of v7, /device:TPU:0, one launch (start us, length us, event | category | flops | bytes accessed | tf_op | source)
XLA Modules:
  0.0 53.9 jit_solution(11747371958503361318)
XLA Ops:
  0.6 1.3 %prep.1 = (bf16[1536,128]{1,0:T(8,128)(2,1)S(1)}, bf16[768,128]{1,0:T(8,128)(2,1)S(1)}, bf16[768,128]{1,0:T(8,128)(2,1)S(1)}) custom-call(bf16[1536,128]{1,0:T(8,128)(2,1)} %bitcast.13), custom_call_target="tpu_custom_call" | custom-call | tf_op jit(solution)/shard_map/prep/pallas_call | solution.py:458
  1.9 3.0 %collective-permute-start.13 = (bf16[1536,128]{1,0:T(8,128)(2,1)S(1)}, bf16[1536,128]{1,0:T(8,128)(2,1)S(1)}, u32[]{:S(2)}, u32[]{:S(2)}) collective-permute-start(bf16[1536,128]{1,0:T(8,128)(2,1)S(1)} %get-tuple-element.18.refs_0_), channel_id=1, source_target_pairs={{0,2},{1,3},{2,0},{3,1},{4,6},{5,7},{6,4},{7,5},{8,10},{9,11},{10,... | collective-permute-start | bytes 1179656 | tf_op jit(solution)/shard_map/ppermute | solution.py:388
  5.0 1.5 %collective-permute-start.4 = (bf16[768,128]{1,0:T(8,128)(2,1)S(1)}, bf16[768,128]{1,0:T(8,128)(2,1)S(1)}, u32[]{:S(2)}, u32[]{:S(2)}) collective-permute-start(bf16[768,128]{1,0:T(8,128)(2,1)S(1)} %get-tuple-element.16.refs_5_), channel_id=1, source_target_pairs={{8,0},{16,8},{24,16},{28,24},{20,28},{12,20},{4,12},{0,4},{9,1},{1... | collective-permute-start | bytes 589832 | tf_op jit(solution)/shard_map/ppermute | solution.py:485
  6.5 0.0 collective-permute-start.8
  6.5 0.6 %collective-permute-start.10 = (s32[4,1,3]{0,1,2:T(1,128)}, s32[4,1,3]{0,1,2:T(1,128)S(1)}, u32[]{:S(2)}, u32[]{:S(2)}) collective-permute-start(s32[4,1,3]{0,1,2:T(1,128)} %param.3), channel_id=1, source_target_pairs={{0,3},{1,2},{2,1},{3,0},{4,7},{5,6},{6,5},{7,4},{8,11},{9,10},{10,... | collective-permute-start | bytes 152 | tf_op jit(solution)/shard_map/ppermute | solution.py:388
  7.1 1.5 %collective-permute-start.9 = (s32[4,1,3]{0,1,2:T(1,128)}, s32[4,1,3]{0,1,2:T(1,128)S(1)}, u32[]{:S(2)}, u32[]{:S(2)}) collective-permute-start(s32[4,1,3]{0,1,2:T(1,128)} %param.3), channel_id=1, source_target_pairs={{0,2},{1,3},{2,0},{3,1},{4,6},{5,7},{6,4},{7,5},{8,10},{9,11},{10,... | collective-permute-start | bytes 152 | tf_op jit(solution)/shard_map/ppermute | solution.py:388
  8.6 0.0 collective-permute-done.8
  8.6 0.5 collective-permute-start
  9.1 4.2 %collective-permute-done.10 = s32[4,1,3]{0,1,2:T(1,128)S(1)} collective-permute-done((s32[4,1,3]{0,1,2:T(1,128)}, s32[4,1,3]{0,1,2:T(1,128)S(1)}, u32[]{:S(2)}, u32[]{:S(2)}) %collective-permute-start.10) | collective-permute-done | bytes 80 | tf_op jit(solution)/shard_map/ppermute | solution.py:388
  13.4 0.8 %collective-permute-done.9 = s32[4,1,3]{0,1,2:T(1,128)S(1)} collective-permute-done((s32[4,1,3]{0,1,2:T(1,128)}, s32[4,1,3]{0,1,2:T(1,128)S(1)}, u32[]{:S(2)}, u32[]{:S(2)}) %collective-permute-start.9) | collective-permute-done | bytes 80 | tf_op jit(solution)/shard_map/ppermute | solution.py:388
  14.1 0.8 %numbers.1 = (bf16[784,128]{1,0:T(8,128)(2,1)S(1)}, bf16[784,128]{1,0:T(8,128)(2,1)S(1)}, bf16[16,128]{1,0:T(8,128)(2,1)S(1)}) custom-call(s32[3,1,4]{2,1,0:T(1,128)} %bitcast.14, s32[3,1,4]{2,1,0:T(1,128)S(1)} %bitcast.9, s32[3,1,4]{2,1,0:T(1,128)S(1)} %bitcast.11, s32[3,1,4]{2,1,0:T(1,128)S(1)} %bitcast.10, ...), custom_call_target="tpu_custom_call" | custom-call | tf_op jit(solution)/shard_map/numbers/pallas_call | solution.py:467
  15.0 1.8 %collective-permute-start.16 = (bf16[784,128]{1,0:T(8,128)(2,1)S(1)}, bf16[784,128]{1,0:T(8,128)(2,1)S(1)}, u32[]{:S(2)}, u32[]{:S(2)}) collective-permute-start(bf16[784,128]{1,0:T(8,128)(2,1)S(1)} %get-tuple-element.20), channel_id=1, source_target_pairs={{8,0},{16,8},{24,16},{28,24},{20,28},{12,20},{4,12},{0,4},{9,1},{1... | collective-permute-start | bytes 602120 | tf_op jit(solution)/shard_map/ppermute | solution.py:488
  16.8 0.0 collective-permute-start.12
  16.8 0.0 collective-permute-done.4.refs_10_
  16.8 0.3 collective-permute-start.15
  17.1 0.0 collective-permute-done.refs_7_
  17.1 1.8 %collective-permute-start.5 = (bf16[768,128]{1,0:T(8,128)(2,1)S(1)}, bf16[768,128]{1,0:T(8,128)(2,1)S(1)}, u32[]{:S(2)}, u32[]{:S(2)}) collective-permute-start(bf16[768,128]{1,0:T(8,128)(2,1)S(1)} %collective-permute-done.4.refs_10_), channel_id=1, source_target_pairs={{8,0},{16,8},{24,16},{28,24},{20,28},{12,20},{4,12},{0,4},{9,1},{1... | collective-permute-start | bytes 589832 | tf_op jit(solution)/shard_map/ppermute | solution.py:485
  18.8 4.1 %collective-permute-done.16.refs_9_.refs_12_ = bf16[784,128]{1,0:T(8,128)(2,1)S(1)} collective-permute-done((bf16[784,128]{1,0:T(8,128)(2,1)S(1)}, bf16[784,128]{1,0:T(8,128)(2,1)S(1)}, u32[]{:S(2)}, u32[]{:S(2)}) %collective-permute-start.16) | collective-permute-done | bytes 200736 | tf_op jit(solution)/shard_map/ppermute | solution.py:488
  22.9 1.8 %collective-permute-start.1 = (bf16[768,128]{1,0:T(8,128)(2,1)S(1)}, bf16[768,128]{1,0:T(8,128)(2,1)S(1)}, u32[]{:S(2)}, u32[]{:S(2)}) collective-permute-start(bf16[768,128]{1,0:T(8,128)(2,1)S(1)} %collective-permute-done.refs_7_), channel_id=1, source_target_pairs={{0,8},{8,16},{16,24},{24,28},{28,20},{20,12},{12,4},{4,0},{1,9},{9... | collective-permute-start | bytes 589832 | tf_op jit(solution)/shard_map/ppermute | solution.py:484
  24.7 0.0 collective-permute-done.13.refs_2_
  24.7 0.0 collective-permute-start.14
  24.7 0.0 collective-permute-done.15.refs_8_.refs_11_
  24.7 1.2 %collective-permute-start.19 = (bf16[784,128]{1,0:T(8,128)(2,1)S(1)}, bf16[784,128]{1,0:T(8,128)(2,1)S(1)}, u32[]{:S(2)}, u32[]{:S(2)}) collective-permute-start(bf16[784,128]{1,0:T(8,128)(2,1)S(1)} %collective-permute-done.16.refs_9_.refs_12_), channel_id=1, source_target_pairs={{8,0},{16,8},{24,16},{28,24},{20,28},{12,20},{4,12},{0,4},{9,1},{1... | collective-permute-start | bytes 602120 | tf_op jit(solution)/shard_map/ppermute | solution.py:488
  25.9 0.4 collective-permute-done.5.refs_8_
  26.3 1.7 %collective-permute-start.17 = (bf16[784,128]{1,0:T(8,128)(2,1)S(1)}, bf16[784,128]{1,0:T(8,128)(2,1)S(1)}, u32[]{:S(2)}, u32[]{:S(2)}) collective-permute-start(bf16[784,128]{1,0:T(8,128)(2,1)S(1)} %collective-permute-done.15.refs_8_.refs_11_), channel_id=1, source_target_pairs={{0,8},{8,16},{16,24},{24,28},{28,20},{20,12},{12,4},{4,0},{1,9},{9... | collective-permute-start | bytes 602120 | tf_op jit(solution)/shard_map/ppermute | solution.py:487
  28.0 0.9 %collective-permute-done.1.refs_5_ = bf16[768,128]{1,0:T(8,128)(2,1)S(1)} collective-permute-done((bf16[768,128]{1,0:T(8,128)(2,1)S(1)}, bf16[768,128]{1,0:T(8,128)(2,1)S(1)}, u32[]{:S(2)}, u32[]{:S(2)}) %collective-permute-start.1) | collective-permute-done | bytes 196640 | tf_op jit(solution)/shard_map/ppermute | solution.py:484
  28.9 1.9 %collective-permute-start.6 = (bf16[768,128]{1,0:T(8,128)(2,1)S(1)}, bf16[768,128]{1,0:T(8,128)(2,1)S(1)}, u32[]{:S(2)}, u32[]{:S(2)}) collective-permute-start(bf16[768,128]{1,0:T(8,128)(2,1)S(1)} %collective-permute-done.5.refs_8_), channel_id=1, source_target_pairs={{8,0},{16,8},{24,16},{28,24},{20,28},{12,20},{4,12},{0,4},{9,1},{1... | collective-permute-start | bytes 589832 | tf_op jit(solution)/shard_map/ppermute | solution.py:485
  30.8 0.0 collective-permute-done.12.refs_1_
  30.8 0.1 collective-permute-start.2
  30.9 2.1 %zero.1.refs_6_ = bf16[4,36,128,128]{3,2,1,0:T(8,128)(2,1)} custom-call(), custom_call_target="tpu_custom_call" | custom-call | tf_op jit(solution)/shard_map/zero/pallas_call | solution.py:317
  33.0 0.0 collective-permute-done.19.refs_7_.refs_14_
  33.0 5.0 %collective-permute-start.11 = (bf16[16,128]{1,0:T(8,128)(2,1)S(1)}, bf16[16,128]{1,0:T(8,128)(2,1)S(1)}, u32[]{:S(2)}, u32[]{:S(2)}) collective-permute-start(bf16[16,128]{1,0:T(8,128)(2,1)S(1)} %get-tuple-element.17.refs_4_.refs_9_), channel_id=1, source_target_pairs={{0,28},{8,20},{16,12},{24,4},{28,0},{20,8},{12,16},{4,24},{1,29},{... | collective-permute-start | bytes 12296 | tf_op jit(solution)/shard_map/ppermute | solution.py:498
  38.1 0.0 collective-permute-done.17.refs_6_.refs_13_
  38.1 0.5 collective-permute-start.20
  38.6 0.0 collective-permute-done.6.refs_8_
  38.6 1.5 %collective-permute-start.18 = (bf16[784,128]{1,0:T(8,128)(2,1)S(1)}, bf16[784,128]{1,0:T(8,128)(2,1)S(1)}, u32[]{:S(2)}, u32[]{:S(2)}) collective-permute-start(bf16[784,128]{1,0:T(8,128)(2,1)S(1)} %collective-permute-done.17.refs_6_.refs_13_), channel_id=1, source_target_pairs={{0,8},{8,16},{16,24},{24,28},{28,20},{20,12},{12,4},{4,0},{1,9},{9... | collective-permute-start | bytes 602120 | tf_op jit(solution)/shard_map/ppermute | solution.py:487
  40.1 0.0 collective-permute-done.2.refs_5_
  40.1 0.5 collective-permute-start.7
  40.6 0.0 collective-permute-done.14.refs_3_
  40.6 1.5 %collective-permute-start.3 = (bf16[768,128]{1,0:T(8,128)(2,1)S(1)}, bf16[768,128]{1,0:T(8,128)(2,1)S(1)}, u32[]{:S(2)}, u32[]{:S(2)}) collective-permute-start(bf16[768,128]{1,0:T(8,128)(2,1)S(1)} %collective-permute-done.2.refs_5_), channel_id=1, source_target_pairs={{0,8},{8,16},{16,24},{24,28},{28,20},{20,12},{12,4},{4,0},{1,9},{9... | collective-permute-start | bytes 589832 | tf_op jit(solution)/shard_map/ppermute | solution.py:484
  42.1 3.2 %shard_map.49 = (f32[512,1024]{1,0:T(8,128)S(1)}, bf16[512,512]{1,0:T(8,128)(2,1)S(1)}) custom-call(bf16[1536,128]{1,0:T(8,128)(2,1)S(1)} %get-tuple-element.18.refs_0_, bf16[1536,128]{1,0:T(8,128)(2,1)S(1)} %collective-permute-done.12.refs_1_, bf16[1536,128]{1,0:T(8,128)(2,1)S(1)} %collective-permute-done.13.refs_2_, ...), custom_call_target="tpu_custom_call" | custom-call | flops 1610612736 | bytes 4000000 | tf_op jit(solution)/shard_map/pallas_call | solution.py:354
  45.4 2.7 %shard_map.50.refs_17_ = f32[512,1024]{1,0:T(8,128)S(1)} custom-call(bf16[1536,128]{1,0:T(8,128)(2,1)S(1)} %get-tuple-element.18.refs_0_, bf16[1536,128]{1,0:T(8,128)(2,1)S(1)} %collective-permute-done.12.refs_1_, bf16[1536,128]{1,0:T(8,128)(2,1)S(1)} %collective-permute-done.13.refs_2_, ...), custom_call_target="tpu_custom_call", output_to_operand_aliasing={{}: (9, {})} | custom-call | flops 1073741824 | bytes 4000000 | tf_op jit(solution)/shard_map/pallas_call | solution.py:354
  48.0 0.0 collective-permute-done.11.refs_10_.refs_2_
  48.1 0.0 collective-permute-done.18.refs_6_.refs_15_
  48.1 3.2 %shard_map.51 = (f32[512,1024]{1,0:T(8,128)S(1)}, s32[32]{0:T(128)S(1)}, s32[4,1,36]{2,1,0:T(1,128)}, s32[1,4]{1,0:T(1,128)}) custom-call(bf16[1536,128]{1,0:T(8,128)(2,1)S(1)} %get-tuple-element.18.refs_0_, bf16[1536,128]{1,0:T(8,128)(2,1)S(1)} %collective-permute-done.12.refs_1_, ...), custom_call_target="tpu_custom_call", output_to_operand_aliasing={{0}: (17, {})} | custom-call | flops 1073741824 | bytes 4000000 | tf_op jit(solution)/shard_map/pallas_call | solution.py:354
  51.2 0.0 collective-permute-done.7.refs_1_
  51.2 0.0 collective-permute-done.3.refs_0_
  51.2 2.6 %shard_map.52 = bf16[4,36,128,128]{3,2,1,0:T(8,128)(2,1)} custom-call(bf16[768,128]{1,0:T(8,128)(2,1)S(1)} %collective-permute-done.3.refs_0_, bf16[768,128]{1,0:T(8,128)(2,1)S(1)} %collective-permute-done.7.refs_1_, bf16[16,128]{1,0:T(8,128)(2,1)S(1)} %collective-permute-done.11.refs_10_.refs_2_, ...), custom_call_target="tpu_custom_call", output_to_operand_aliasing={{}: (6, {})} | custom-call | flops 536870912 | bytes 4000000 | tf_op jit(solution)/shard_map/pallas_call | solution.py:369
  (1 shorter events, 0.0 us)
Async XLA Ops:
  1.9 22.8 %collective-permute-start.13 = (bf16[1536,128]{1,0:T(8,128)(2,1)S(1)}, bf16[1536,128]{1,0:T(8,128)(2,1)S(1)}, u32[]{:S(2)}, u32[]{:S(2)}) collective-permute-start(bf16[1536,128]{1,0:T(8,128)(2,1)S(1)} %get-tuple-element.18.refs_0_), channel_id=1, source_target_pairs={{0,2},{1,3},{2,0},{3,1},{4,6},{5,7},{6,4},{7,5},{8,10},{9,11},{10,... | collective-permute-start | bytes 1179656 | tf_op jit(solution)/shard_map/ppermute | solution.py:388
  5.0 11.8 %collective-permute-start.4 = (bf16[768,128]{1,0:T(8,128)(2,1)S(1)}, bf16[768,128]{1,0:T(8,128)(2,1)S(1)}, u32[]{:S(2)}, u32[]{:S(2)}) collective-permute-start(bf16[768,128]{1,0:T(8,128)(2,1)S(1)} %get-tuple-element.16.refs_5_), channel_id=1, source_target_pairs={{8,0},{16,8},{24,16},{28,24},{20,28},{12,20},{4,12},{0,4},{9,1},{1... | collective-permute-start | bytes 589832 | tf_op jit(solution)/shard_map/ppermute | solution.py:485
  6.5 2.1 %collective-permute-start.8 = (s32[4,1,3]{0,1,2:T(1,128)}, s32[4,1,3]{0,1,2:T(1,128)S(1)}, u32[]{:S(2)}, u32[]{:S(2)}) collective-permute-start(s32[4,1,3]{0,1,2:T(1,128)} %param.3), channel_id=1, source_target_pairs={{0,1},{1,0},{2,3},{3,2},{4,5},{5,4},{6,7},{7,6},{8,9},{9,8},{10,11... | collective-permute-start | bytes 152 | tf_op jit(solution)/shard_map/ppermute | solution.py:388
  6.5 6.9 %collective-permute-start.10 = (s32[4,1,3]{0,1,2:T(1,128)}, s32[4,1,3]{0,1,2:T(1,128)S(1)}, u32[]{:S(2)}, u32[]{:S(2)}) collective-permute-start(s32[4,1,3]{0,1,2:T(1,128)} %param.3), channel_id=1, source_target_pairs={{0,3},{1,2},{2,1},{3,0},{4,7},{5,6},{6,5},{7,4},{8,11},{9,10},{10,... | collective-permute-start | bytes 152 | tf_op jit(solution)/shard_map/ppermute | solution.py:388
  7.1 7.0 %collective-permute-start.9 = (s32[4,1,3]{0,1,2:T(1,128)}, s32[4,1,3]{0,1,2:T(1,128)S(1)}, u32[]{:S(2)}, u32[]{:S(2)}) collective-permute-start(s32[4,1,3]{0,1,2:T(1,128)} %param.3), channel_id=1, source_target_pairs={{0,2},{1,3},{2,0},{3,1},{4,6},{5,7},{6,4},{7,5},{8,10},{9,11},{10,... | collective-permute-start | bytes 152 | tf_op jit(solution)/shard_map/ppermute | solution.py:388
  8.6 8.4 %collective-permute-start = (bf16[768,128]{1,0:T(8,128)(2,1)S(1)}, bf16[768,128]{1,0:T(8,128)(2,1)S(1)}, u32[]{:S(2)}, u32[]{:S(2)}) collective-permute-start(bf16[768,128]{1,0:T(8,128)(2,1)S(1)} %get-tuple-element.15.refs_4_.refs_5_), channel_id=1, source_target_pairs={{0,8},{8,16},{16,24},{24,28},{28,20},{20,12},{12,4},{4,0},{1,9},{9... | collective-permute-start | bytes 589832 | tf_op jit(solution)/shard_map/ppermute | solution.py:484
  15.0 7.9 %collective-permute-start.16 = (bf16[784,128]{1,0:T(8,128)(2,1)S(1)}, bf16[784,128]{1,0:T(8,128)(2,1)S(1)}, u32[]{:S(2)}, u32[]{:S(2)}) collective-permute-start(bf16[784,128]{1,0:T(8,128)(2,1)S(1)} %get-tuple-element.20), channel_id=1, source_target_pairs={{8,0},{16,8},{24,16},{28,24},{20,28},{12,20},{4,12},{0,4},{9,1},{1... | collective-permute-start | bytes 602120 | tf_op jit(solution)/shard_map/ppermute | solution.py:488
  16.8 14.0 %collective-permute-start.12 = (bf16[1536,128]{1,0:T(8,128)(2,1)S(1)}, bf16[1536,128]{1,0:T(8,128)(2,1)S(1)}, u32[]{:S(2)}, u32[]{:S(2)}) collective-permute-start(bf16[1536,128]{1,0:T(8,128)(2,1)S(1)} %get-tuple-element.18.refs_0_), channel_id=1, source_target_pairs={{0,1},{1,0},{2,3},{3,2},{4,5},{5,4},{6,7},{7,6},{8,9},{9,8},{10,11... | collective-permute-start | bytes 1179656 | tf_op jit(solution)/shard_map/ppermute | solution.py:388
  16.8 7.9 %collective-permute-start.15 = (bf16[784,128]{1,0:T(8,128)(2,1)S(1)}, bf16[784,128]{1,0:T(8,128)(2,1)S(1)}, u32[]{:S(2)}, u32[]{:S(2)}) collective-permute-start(bf16[784,128]{1,0:T(8,128)(2,1)S(1)} %get-tuple-element.19.refs_6_), channel_id=1, source_target_pairs={{0,8},{8,16},{16,24},{24,28},{28,20},{20,12},{12,4},{4,0},{1,9},{9... | collective-permute-start | bytes 602120 | tf_op jit(solution)/shard_map/ppermute | solution.py:487
  17.1 9.2 %collective-permute-start.5 = (bf16[768,128]{1,0:T(8,128)(2,1)S(1)}, bf16[768,128]{1,0:T(8,128)(2,1)S(1)}, u32[]{:S(2)}, u32[]{:S(2)}) collective-permute-start(bf16[768,128]{1,0:T(8,128)(2,1)S(1)} %collective-permute-done.4.refs_10_), channel_id=1, source_target_pairs={{8,0},{16,8},{24,16},{28,24},{20,28},{12,20},{4,12},{0,4},{9,1},{1... | collective-permute-start | bytes 589832 | tf_op jit(solution)/shard_map/ppermute | solution.py:485
  22.9 6.0 %collective-permute-start.1 = (bf16[768,128]{1,0:T(8,128)(2,1)S(1)}, bf16[768,128]{1,0:T(8,128)(2,1)S(1)}, u32[]{:S(2)}, u32[]{:S(2)}) collective-permute-start(bf16[768,128]{1,0:T(8,128)(2,1)S(1)} %collective-permute-done.refs_7_), channel_id=1, source_target_pairs={{0,8},{8,16},{16,24},{24,28},{28,20},{20,12},{12,4},{4,0},{1,9},{9... | collective-permute-start | bytes 589832 | tf_op jit(solution)/shard_map/ppermute | solution.py:484
  24.7 15.9 %collective-permute-start.14 = (bf16[1536,128]{1,0:T(8,128)(2,1)S(1)}, bf16[1536,128]{1,0:T(8,128)(2,1)S(1)}, u32[]{:S(2)}, u32[]{:S(2)}) collective-permute-start(bf16[1536,128]{1,0:T(8,128)(2,1)S(1)} %collective-permute-done.13.refs_2_), channel_id=1, source_target_pairs={{0,1},{1,0},{2,3},{3,2},{4,5},{5,4},{6,7},{7,6},{8,9},{9,8},{10,11... | collective-permute-start | bytes 1179656 | tf_op jit(solution)/shard_map/ppermute | solution.py:388
  24.7 8.3 %collective-permute-start.19 = (bf16[784,128]{1,0:T(8,128)(2,1)S(1)}, bf16[784,128]{1,0:T(8,128)(2,1)S(1)}, u32[]{:S(2)}, u32[]{:S(2)}) collective-permute-start(bf16[784,128]{1,0:T(8,128)(2,1)S(1)} %collective-permute-done.16.refs_9_.refs_12_), channel_id=1, source_target_pairs={{8,0},{16,8},{24,16},{28,24},{20,28},{12,20},{4,12},{0,4},{9,1},{1... | collective-permute-start | bytes 602120 | tf_op jit(solution)/shard_map/ppermute | solution.py:488
  26.3 11.8 %collective-permute-start.17 = (bf16[784,128]{1,0:T(8,128)(2,1)S(1)}, bf16[784,128]{1,0:T(8,128)(2,1)S(1)}, u32[]{:S(2)}, u32[]{:S(2)}) collective-permute-start(bf16[784,128]{1,0:T(8,128)(2,1)S(1)} %collective-permute-done.15.refs_8_.refs_11_), channel_id=1, source_target_pairs={{0,8},{8,16},{16,24},{24,28},{28,20},{20,12},{12,4},{4,0},{1,9},{9... | collective-permute-start | bytes 602120 | tf_op jit(solution)/shard_map/ppermute | solution.py:487
  28.9 9.7 %collective-permute-start.6 = (bf16[768,128]{1,0:T(8,128)(2,1)S(1)}, bf16[768,128]{1,0:T(8,128)(2,1)S(1)}, u32[]{:S(2)}, u32[]{:S(2)}) collective-permute-start(bf16[768,128]{1,0:T(8,128)(2,1)S(1)} %collective-permute-done.5.refs_8_), channel_id=1, source_target_pairs={{8,0},{16,8},{24,16},{28,24},{20,28},{12,20},{4,12},{0,4},{9,1},{1... | collective-permute-start | bytes 589832 | tf_op jit(solution)/shard_map/ppermute | solution.py:485
  30.8 9.3 %collective-permute-start.2 = (bf16[768,128]{1,0:T(8,128)(2,1)S(1)}, bf16[768,128]{1,0:T(8,128)(2,1)S(1)}, u32[]{:S(2)}, u32[]{:S(2)}) collective-permute-start(bf16[768,128]{1,0:T(8,128)(2,1)S(1)} %collective-permute-done.1.refs_5_), channel_id=1, source_target_pairs={{0,8},{8,16},{16,24},{24,28},{28,20},{20,12},{12,4},{4,0},{1,9},{9... | collective-permute-start | bytes 589832 | tf_op jit(solution)/shard_map/ppermute | solution.py:484
  33.0 15.0 %collective-permute-start.11 = (bf16[16,128]{1,0:T(8,128)(2,1)S(1)}, bf16[16,128]{1,0:T(8,128)(2,1)S(1)}, u32[]{:S(2)}, u32[]{:S(2)}) collective-permute-start(bf16[16,128]{1,0:T(8,128)(2,1)S(1)} %get-tuple-element.17.refs_4_.refs_9_), channel_id=1, source_target_pairs={{0,28},{8,20},{16,12},{24,4},{28,0},{20,8},{12,16},{4,24},{1,29},{... | collective-permute-start | bytes 12296 | tf_op jit(solution)/shard_map/ppermute | solution.py:498
  38.1 10.0 %collective-permute-start.20 = (bf16[784,128]{1,0:T(8,128)(2,1)S(1)}, bf16[784,128]{1,0:T(8,128)(2,1)S(1)}, u32[]{:S(2)}, u32[]{:S(2)}) collective-permute-start(bf16[784,128]{1,0:T(8,128)(2,1)S(1)} %collective-permute-done.19.refs_7_.refs_14_), channel_id=1, source_target_pairs={{8,0},{16,8},{24,16},{28,24},{20,28},{12,20},{4,12},{0,4},{9,1},{1... | collective-permute-start | bytes 602120 | tf_op jit(solution)/shard_map/ppermute | solution.py:488
  38.6 9.5 %collective-permute-start.18 = (bf16[784,128]{1,0:T(8,128)(2,1)S(1)}, bf16[784,128]{1,0:T(8,128)(2,1)S(1)}, u32[]{:S(2)}, u32[]{:S(2)}) collective-permute-start(bf16[784,128]{1,0:T(8,128)(2,1)S(1)} %collective-permute-done.17.refs_6_.refs_13_), channel_id=1, source_target_pairs={{0,8},{8,16},{16,24},{24,28},{28,20},{20,12},{12,4},{4,0},{1,9},{9... | collective-permute-start | bytes 602120 | tf_op jit(solution)/shard_map/ppermute | solution.py:487
  40.1 11.1 %collective-permute-start.7 = (bf16[768,128]{1,0:T(8,128)(2,1)S(1)}, bf16[768,128]{1,0:T(8,128)(2,1)S(1)}, u32[]{:S(2)}, u32[]{:S(2)}) collective-permute-start(bf16[768,128]{1,0:T(8,128)(2,1)S(1)} %collective-permute-done.6.refs_8_), channel_id=1, source_target_pairs={{8,0},{16,8},{24,16},{28,24},{20,28},{12,20},{4,12},{0,4},{9,1},{1... | collective-permute-start | bytes 589832 | tf_op jit(solution)/shard_map/ppermute | solution.py:485
  40.6 10.6 %collective-permute-start.3 = (bf16[768,128]{1,0:T(8,128)(2,1)S(1)}, bf16[768,128]{1,0:T(8,128)(2,1)S(1)}, u32[]{:S(2)}, u32[]{:S(2)}) collective-permute-start(bf16[768,128]{1,0:T(8,128)(2,1)S(1)} %collective-permute-done.2.refs_5_), channel_id=1, source_target_pairs={{0,8},{8,16},{16,24},{24,28},{28,20},{20,12},{12,4},{4,0},{1,9},{9... | collective-permute-start | bytes 589832 | tf_op jit(solution)/shard_map/ppermute | solution.py:484

commit v8 on v7

--- a/solution.py
+++ b/solution.py
@@ -497,9 +497,8 @@
     if dims.whole:
         far = lax.ppermute(tile, "rows", [(a, dict(up)[dict(up)[dict(up)[b]]]) for a, b in up])
         pairs = [[(-k, pa[k], pb[k], "b"), (k, qa[k], qb[k], "a")] for k in range(1, HP)]
-        first = [(0, bare_a, own_b, "b")] + pairs[0]
-        acc, lp = call_step(dims, left, tile, first, None, ahead=HP)
-        acc = call_step(dims, left, tile, pairs[1], acc)[0]
+        acc, lp = call_step(dims, left, tile, [(0, bare_a, own_b, "b")], None, ahead=HP)
+        acc = call_step(dims, left, tile, pairs[0] + pairs[1], acc)[0]
         tiles = [(0, tile, 0), (HP, far, 0)]
         for k in range(1, HP):
             tiles += [(cycle - k, pb[k], dims.half), (k, qa[k], dims.half)]

time: 54.1 us -> 54.2 us (level)
  no operation moved by 1% of the time
where the time goes in v8:
time: 54.2 us; the launch traced here: 54.1 us
  starting transfers between devices  26.9 us (50%)
  Pallas kernels  16 us (30%)
  waiting for transfers between devices  10.3 us (19%)
  between operations  0.75 us (1%)
    pallas_call x3, Pallas kernels, call_step(): pl.pallas_call(functools.partial(step_kernel, dims, layout, acc is not No...  9.23 us
    ppermute x4, starting transfers between devices, on_device(): qb.append(lax.ppermute(qb[-1], 'rows', down))  5.71 us
    ppermute x6, starting transfers between devices, xor_move(): lax.ppermute(value, axis, [(i, i ^ bit) for i in range(lax.axis_size(axis...  5.18 us
    ppermute x1, starting transfers between devices, on_device(): lax.ppermute(tile, 'rows', [(a, dict(up)[dict(up)[dict(up)[b]]]) for a, b...  5.05 us
    ppermute x6, waiting for transfers between devices, xor_move(): lax.ppermute(value, axis, [(i, i ^ bit) for i in range(lax.axis_size(axis...  5.02 us
    ppermute x3, waiting for transfers between devices, on_device(): qa.append(lax.ppermute(qa[-1], 'rows', down))  4.06 us
    ppermute x4, starting transfers between devices, on_device(): pa.append(lax.ppermute(pa[-1], 'rows', up))  3.97 us
    ppermute x3, starting transfers between devices, on_device(): qa.append(lax.ppermute(qa[-1], 'rows', down))  3.53 us
  transfers between devices with their start and end apart: 21, of which 5 were waited for; matrix products, arithmetic and copies ran while one was open for 0% of the time, Pallas kernels for 22%

profile of v8, /device:TPU:0, one launch (start us, length us, event | category | flops | bytes accessed | tf_op | source)
XLA Modules:
  0.0 54.1 jit_solution(15774983259361034453)
XLA Ops:
  0.6 1.3 %prep.1 = (bf16[1536,128]{1,0:T(8,128)(2,1)S(1)}, bf16[768,128]{1,0:T(8,128)(2,1)S(1)}, bf16[768,128]{1,0:T(8,128)(2,1)S(1)}) custom-call(bf16[1536,128]{1,0:T(8,128)(2,1)} %bitcast.13), custom_call_target="tpu_custom_call" | custom-call | tf_op jit(solution)/shard_map/prep/pallas_call | solution.py:458
  1.9 3.0 %collective-permute-start.13 = (bf16[1536,128]{1,0:T(8,128)(2,1)S(1)}, bf16[1536,128]{1,0:T(8,128)(2,1)S(1)}, u32[]{:S(2)}, u32[]{:S(2)}) collective-permute-start(bf16[1536,128]{1,0:T(8,128)(2,1)S(1)} %get-tuple-element.18.refs_0_), channel_id=1, source_target_pairs={{0,2},{1,3},{2,0},{3,1},{4,6},{5,7},{6,4},{7,5},{8,10},{9,11},{10,... | collective-permute-start | bytes 1179656 | tf_op jit(solution)/shard_map/ppermute | solution.py:388
  5.0 1.5 %collective-permute-start.4 = (bf16[768,128]{1,0:T(8,128)(2,1)S(1)}, bf16[768,128]{1,0:T(8,128)(2,1)S(1)}, u32[]{:S(2)}, u32[]{:S(2)}) collective-permute-start(bf16[768,128]{1,0:T(8,128)(2,1)S(1)} %get-tuple-element.16.refs_5_), channel_id=1, source_target_pairs={{8,0},{16,8},{24,16},{28,24},{20,28},{12,20},{4,12},{0,4},{9,1},{1... | collective-permute-start | bytes 589832 | tf_op jit(solution)/shard_map/ppermute | solution.py:485
  6.5 0.0 collective-permute-start.8
  6.5 0.6 %collective-permute-start.10 = (s32[4,1,3]{0,1,2:T(1,128)}, s32[4,1,3]{0,1,2:T(1,128)S(1)}, u32[]{:S(2)}, u32[]{:S(2)}) collective-permute-start(s32[4,1,3]{0,1,2:T(1,128)} %param.3), channel_id=1, source_target_pairs={{0,3},{1,2},{2,1},{3,0},{4,7},{5,6},{6,5},{7,4},{8,11},{9,10},{10,... | collective-permute-start | bytes 152 | tf_op jit(solution)/shard_map/ppermute | solution.py:388
  7.1 1.5 %collective-permute-start.9 = (s32[4,1,3]{0,1,2:T(1,128)}, s32[4,1,3]{0,1,2:T(1,128)S(1)}, u32[]{:S(2)}, u32[]{:S(2)}) collective-permute-start(s32[4,1,3]{0,1,2:T(1,128)} %param.3), channel_id=1, source_target_pairs={{0,2},{1,3},{2,0},{3,1},{4,6},{5,7},{6,4},{7,5},{8,10},{9,11},{10,... | collective-permute-start | bytes 152 | tf_op jit(solution)/shard_map/ppermute | solution.py:388
  8.6 0.0 collective-permute-done.8
  8.6 0.5 collective-permute-start
  9.1 4.2 %collective-permute-done.10 = s32[4,1,3]{0,1,2:T(1,128)S(1)} collective-permute-done((s32[4,1,3]{0,1,2:T(1,128)}, s32[4,1,3]{0,1,2:T(1,128)S(1)}, u32[]{:S(2)}, u32[]{:S(2)}) %collective-permute-start.10) | collective-permute-done | bytes 80 | tf_op jit(solution)/shard_map/ppermute | solution.py:388
  13.4 0.8 %collective-permute-done.9 = s32[4,1,3]{0,1,2:T(1,128)S(1)} collective-permute-done((s32[4,1,3]{0,1,2:T(1,128)}, s32[4,1,3]{0,1,2:T(1,128)S(1)}, u32[]{:S(2)}, u32[]{:S(2)}) %collective-permute-start.9) | collective-permute-done | bytes 80 | tf_op jit(solution)/shard_map/ppermute | solution.py:388
  14.1 0.8 %numbers.1 = (bf16[784,128]{1,0:T(8,128)(2,1)S(1)}, bf16[784,128]{1,0:T(8,128)(2,1)S(1)}, bf16[16,128]{1,0:T(8,128)(2,1)S(1)}) custom-call(s32[3,1,4]{2,1,0:T(1,128)} %bitcast.14, s32[3,1,4]{2,1,0:T(1,128)S(1)} %bitcast.9, s32[3,1,4]{2,1,0:T(1,128)S(1)} %bitcast.11, s32[3,1,4]{2,1,0:T(1,128)S(1)} %bitcast.10, ...), custom_call_target="tpu_custom_call" | custom-call | tf_op jit(solution)/shard_map/numbers/pallas_call | solution.py:467
  15.0 1.8 %collective-permute-start.18 = (bf16[784,128]{1,0:T(8,128)(2,1)S(1)}, bf16[784,128]{1,0:T(8,128)(2,1)S(1)}, u32[]{:S(2)}, u32[]{:S(2)}) collective-permute-start(bf16[784,128]{1,0:T(8,128)(2,1)S(1)} %get-tuple-element.21), channel_id=1, source_target_pairs={{8,0},{16,8},{24,16},{28,24},{20,28},{12,20},{4,12},{0,4},{9,1},{1... | collective-permute-start | bytes 602120 | tf_op jit(solution)/shard_map/ppermute | solution.py:488
  16.8 0.0 collective-permute-start.12
  16.8 0.0 collective-permute-done.4.refs_8_
  16.8 0.3 collective-permute-start.15
  17.1 0.0 collective-permute-done.refs_5_
  17.1 1.8 %collective-permute-start.5 = (bf16[768,128]{1,0:T(8,128)(2,1)S(1)}, bf16[768,128]{1,0:T(8,128)(2,1)S(1)}, u32[]{:S(2)}, u32[]{:S(2)}) collective-permute-start(bf16[768,128]{1,0:T(8,128)(2,1)S(1)} %collective-permute-done.4.refs_8_), channel_id=1, source_target_pairs={{8,0},{16,8},{24,16},{28,24},{20,28},{12,20},{4,12},{0,4},{9,1},{1... | collective-permute-start | bytes 589832 | tf_op jit(solution)/shard_map/ppermute | solution.py:485
  18.8 4.1 %collective-permute-done.18.refs_7_.refs_12_ = bf16[784,128]{1,0:T(8,128)(2,1)S(1)} collective-permute-done((bf16[784,128]{1,0:T(8,128)(2,1)S(1)}, bf16[784,128]{1,0:T(8,128)(2,1)S(1)}, u32[]{:S(2)}, u32[]{:S(2)}) %collective-permute-start.18) | collective-permute-done | bytes 200736 | tf_op jit(solution)/shard_map/ppermute | solution.py:488
  22.9 1.8 %collective-permute-start.1 = (bf16[768,128]{1,0:T(8,128)(2,1)S(1)}, bf16[768,128]{1,0:T(8,128)(2,1)S(1)}, u32[]{:S(2)}, u32[]{:S(2)}) collective-permute-start(bf16[768,128]{1,0:T(8,128)(2,1)S(1)} %collective-permute-done.refs_5_), channel_id=1, source_target_pairs={{0,8},{8,16},{16,24},{24,28},{28,20},{20,12},{12,4},{4,0},{1,9},{9... | collective-permute-start | bytes 589832 | tf_op jit(solution)/shard_map/ppermute | solution.py:484
  24.7 0.0 collective-permute-done.13.refs_2_
  24.7 0.0 collective-permute-start.14
  24.7 0.0 collective-permute-done.15.refs_6_.refs_11_
  24.7 1.2 %collective-permute-start.19 = (bf16[784,128]{1,0:T(8,128)(2,1)S(1)}, bf16[784,128]{1,0:T(8,128)(2,1)S(1)}, u32[]{:S(2)}, u32[]{:S(2)}) collective-permute-start(bf16[784,128]{1,0:T(8,128)(2,1)S(1)} %collective-permute-done.18.refs_7_.refs_12_), channel_id=1, source_target_pairs={{8,0},{16,8},{24,16},{28,24},{20,28},{12,20},{4,12},{0,4},{9,1},{1... | collective-permute-start | bytes 602120 | tf_op jit(solution)/shard_map/ppermute | solution.py:488
  25.9 0.4 collective-permute-done.5.refs_12_
  26.3 1.7 %collective-permute-start.16 = (bf16[784,128]{1,0:T(8,128)(2,1)S(1)}, bf16[784,128]{1,0:T(8,128)(2,1)S(1)}, u32[]{:S(2)}, u32[]{:S(2)}) collective-permute-start(bf16[784,128]{1,0:T(8,128)(2,1)S(1)} %collective-permute-done.15.refs_6_.refs_11_), channel_id=1, source_target_pairs={{0,8},{8,16},{16,24},{24,28},{28,20},{20,12},{12,4},{4,0},{1,9},{9... | collective-permute-start | bytes 602120 | tf_op jit(solution)/shard_map/ppermute | solution.py:487
  28.0 0.9 %collective-permute-done.1.refs_9_ = bf16[768,128]{1,0:T(8,128)(2,1)S(1)} collective-permute-done((bf16[768,128]{1,0:T(8,128)(2,1)S(1)}, bf16[768,128]{1,0:T(8,128)(2,1)S(1)}, u32[]{:S(2)}, u32[]{:S(2)}) %collective-permute-start.1) | collective-permute-done | bytes 196640 | tf_op jit(solution)/shard_map/ppermute | solution.py:484
  28.9 1.9 %collective-permute-start.6 = (bf16[768,128]{1,0:T(8,128)(2,1)S(1)}, bf16[768,128]{1,0:T(8,128)(2,1)S(1)}, u32[]{:S(2)}, u32[]{:S(2)}) collective-permute-start(bf16[768,128]{1,0:T(8,128)(2,1)S(1)} %collective-permute-done.5.refs_12_), channel_id=1, source_target_pairs={{8,0},{16,8},{24,16},{28,24},{20,28},{12,20},{4,12},{0,4},{9,1},{1... | collective-permute-start | bytes 589832 | tf_op jit(solution)/shard_map/ppermute | solution.py:485
  30.8 0.0 collective-permute-done.12.refs_1_
  30.8 0.1 collective-permute-start.2
  30.9 2.1 %zero.1.refs_6_ = bf16[4,36,128,128]{3,2,1,0:T(8,128)(2,1)} custom-call(), custom_call_target="tpu_custom_call" | custom-call | tf_op jit(solution)/shard_map/zero/pallas_call | solution.py:317
  33.0 0.0 collective-permute-done.19.refs_11_.refs_14_
  33.0 5.0 %collective-permute-start.11 = (bf16[16,128]{1,0:T(8,128)(2,1)S(1)}, bf16[16,128]{1,0:T(8,128)(2,1)S(1)}, u32[]{:S(2)}, u32[]{:S(2)}) collective-permute-start(bf16[16,128]{1,0:T(8,128)(2,1)S(1)} %get-tuple-element.17.refs_4_.refs_9_), channel_id=1, source_target_pairs={{0,28},{8,20},{16,12},{24,4},{28,0},{20,8},{12,16},{4,24},{1,29},{... | collective-permute-start | bytes 12296 | tf_op jit(solution)/shard_map/ppermute | solution.py:498
  38.1 0.0 collective-permute-done.16.refs_10_.refs_13_
  38.1 0.5 collective-permute-start.20
  38.6 0.0 collective-permute-done.6.refs_8_
  38.6 1.5 %collective-permute-start.17 = (bf16[784,128]{1,0:T(8,128)(2,1)S(1)}, bf16[784,128]{1,0:T(8,128)(2,1)S(1)}, u32[]{:S(2)}, u32[]{:S(2)}) collective-permute-start(bf16[784,128]{1,0:T(8,128)(2,1)S(1)} %collective-permute-done.16.refs_10_.refs_13_), channel_id=1, source_target_pairs={{0,8},{8,16},{16,24},{24,28},{28,20},{20,12},{12,4},{4,0},{1,9},{9... | collective-permute-start | bytes 602120 | tf_op jit(solution)/shard_map/ppermute | solution.py:487
  40.1 0.0 collective-permute-done.2.refs_5_
  40.1 0.5 collective-permute-start.7
  40.6 0.0 collective-permute-done.14.refs_3_
  40.6 1.5 %collective-permute-start.3 = (bf16[768,128]{1,0:T(8,128)(2,1)S(1)}, bf16[768,128]{1,0:T(8,128)(2,1)S(1)}, u32[]{:S(2)}, u32[]{:S(2)}) collective-permute-start(bf16[768,128]{1,0:T(8,128)(2,1)S(1)} %collective-permute-done.2.refs_5_), channel_id=1, source_target_pairs={{0,8},{8,16},{16,24},{24,28},{28,20},{20,12},{12,4},{4,0},{1,9},{9... | collective-permute-start | bytes 589832 | tf_op jit(solution)/shard_map/ppermute | solution.py:484
  42.1 1.5 %shard_map.49 = (f32[512,1024]{1,0:T(8,128)S(1)}, bf16[512,512]{1,0:T(8,128)(2,1)S(1)}) custom-call(bf16[1536,128]{1,0:T(8,128)(2,1)S(1)} %get-tuple-element.18.refs_0_, bf16[1536,128]{1,0:T(8,128)(2,1)S(1)} %collective-permute-done.12.refs_1_, bf16[1536,128]{1,0:T(8,128)(2,1)S(1)} %collective-permute-done.13.refs_2_, ...), custom_call_target="tpu_custom_call" | custom-call | flops 536870912 | bytes 4000000 | tf_op jit(solution)/shard_map/pallas_call | solution.py:354
  43.6 4.6 %shard_map.50.refs_17_ = f32[512,1024]{1,0:T(8,128)S(1)} custom-call(bf16[1536,128]{1,0:T(8,128)(2,1)S(1)} %get-tuple-element.18.refs_0_, bf16[1536,128]{1,0:T(8,128)(2,1)S(1)} %collective-permute-done.12.refs_1_, bf16[1536,128]{1,0:T(8,128)(2,1)S(1)} %collective-permute-done.13.refs_2_, ...), custom_call_target="tpu_custom_call", output_to_operand_aliasing={{}: (13, {})} | custom-call | flops 2147483648 | bytes 4000000 | tf_op jit(solution)/shard_map/pallas_call | solution.py:354
  48.2 0.0 collective-permute-done.11.refs_10_.refs_2_
  48.2 0.0 collective-permute-done.17.refs_6_.refs_15_
  48.2 3.2 %shard_map.51 = (f32[512,1024]{1,0:T(8,128)S(1)}, s32[32]{0:T(128)S(1)}, s32[4,1,36]{2,1,0:T(1,128)}, s32[1,4]{1,0:T(1,128)}) custom-call(bf16[1536,128]{1,0:T(8,128)(2,1)S(1)} %get-tuple-element.18.refs_0_, bf16[1536,128]{1,0:T(8,128)(2,1)S(1)} %collective-permute-done.12.refs_1_, ...), custom_call_target="tpu_custom_call", output_to_operand_aliasing={{0}: (17, {})} | custom-call | flops 1073741824 | bytes 4000000 | tf_op jit(solution)/shard_map/pallas_call | solution.py:354
  51.4 0.0 collective-permute-done.7.refs_1_
  51.4 0.0 collective-permute-done.3.refs_0_
  51.4 2.6 %shard_map.52 = bf16[4,36,128,128]{3,2,1,0:T(8,128)(2,1)} custom-call(bf16[768,128]{1,0:T(8,128)(2,1)S(1)} %collective-permute-done.3.refs_0_, bf16[768,128]{1,0:T(8,128)(2,1)S(1)} %collective-permute-done.7.refs_1_, bf16[16,128]{1,0:T(8,128)(2,1)S(1)} %collective-permute-done.11.refs_10_.refs_2_, ...), custom_call_target="tpu_custom_call", output_to_operand_aliasing={{}: (6, {})} | custom-call | flops 536870912 | bytes 4000000 | tf_op jit(solution)/shard_map/pallas_call | solution.py:369
  (1 shorter events, 0.0 us)
Async XLA Ops:
  1.9 22.8 %collective-permute-start.13 = (bf16[1536,128]{1,0:T(8,128)(2,1)S(1)}, bf16[1536,128]{1,0:T(8,128)(2,1)S(1)}, u32[]{:S(2)}, u32[]{:S(2)}) collective-permute-start(bf16[1536,128]{1,0:T(8,128)(2,1)S(1)} %get-tuple-element.18.refs_0_), channel_id=1, source_target_pairs={{0,2},{1,3},{2,0},{3,1},{4,6},{5,7},{6,4},{7,5},{8,10},{9,11},{10,... | collective-permute-start | bytes 1179656 | tf_op jit(solution)/shard_map/ppermute | solution.py:388
  5.0 11.8 %collective-permute-start.4 = (bf16[768,128]{1,0:T(8,128)(2,1)S(1)}, bf16[768,128]{1,0:T(8,128)(2,1)S(1)}, u32[]{:S(2)}, u32[]{:S(2)}) collective-permute-start(bf16[768,128]{1,0:T(8,128)(2,1)S(1)} %get-tuple-element.16.refs_5_), channel_id=1, source_target_pairs={{8,0},{16,8},{24,16},{28,24},{20,28},{12,20},{4,12},{0,4},{9,1},{1... | collective-permute-start | bytes 589832 | tf_op jit(solution)/shard_map/ppermute | solution.py:485
  6.5 2.1 %collective-permute-start.8 = (s32[4,1,3]{0,1,2:T(1,128)}, s32[4,1,3]{0,1,2:T(1,128)S(1)}, u32[]{:S(2)}, u32[]{:S(2)}) collective-permute-start(s32[4,1,3]{0,1,2:T(1,128)} %param.3), channel_id=1, source_target_pairs={{0,1},{1,0},{2,3},{3,2},{4,5},{5,4},{6,7},{7,6},{8,9},{9,8},{10,11... | collective-permute-start | bytes 152 | tf_op jit(solution)/shard_map/ppermute | solution.py:388
  6.5 6.9 %collective-permute-start.10 = (s32[4,1,3]{0,1,2:T(1,128)}, s32[4,1,3]{0,1,2:T(1,128)S(1)}, u32[]{:S(2)}, u32[]{:S(2)}) collective-permute-start(s32[4,1,3]{0,1,2:T(1,128)} %param.3), channel_id=1, source_target_pairs={{0,3},{1,2},{2,1},{3,0},{4,7},{5,6},{6,5},{7,4},{8,11},{9,10},{10,... | collective-permute-start | bytes 152 | tf_op jit(solution)/shard_map/ppermute | solution.py:388
  7.1 7.0 %collective-permute-start.9 = (s32[4,1,3]{0,1,2:T(1,128)}, s32[4,1,3]{0,1,2:T(1,128)S(1)}, u32[]{:S(2)}, u32[]{:S(2)}) collective-permute-start(s32[4,1,3]{0,1,2:T(1,128)} %param.3), channel_id=1, source_target_pairs={{0,2},{1,3},{2,0},{3,1},{4,6},{5,7},{6,4},{7,5},{8,10},{9,11},{10,... | collective-permute-start | bytes 152 | tf_op jit(solution)/shard_map/ppermute | solution.py:388
  8.6 8.4 %collective-permute-start = (bf16[768,128]{1,0:T(8,128)(2,1)S(1)}, bf16[768,128]{1,0:T(8,128)(2,1)S(1)}, u32[]{:S(2)}, u32[]{:S(2)}) collective-permute-start(bf16[768,128]{1,0:T(8,128)(2,1)S(1)} %get-tuple-element.15.refs_4_.refs_5_), channel_id=1, source_target_pairs={{0,8},{8,16},{16,24},{24,28},{28,20},{20,12},{12,4},{4,0},{1,9},{9... | collective-permute-start | bytes 589832 | tf_op jit(solution)/shard_map/ppermute | solution.py:484
  15.0 7.9 %collective-permute-start.18 = (bf16[784,128]{1,0:T(8,128)(2,1)S(1)}, bf16[784,128]{1,0:T(8,128)(2,1)S(1)}, u32[]{:S(2)}, u32[]{:S(2)}) collective-permute-start(bf16[784,128]{1,0:T(8,128)(2,1)S(1)} %get-tuple-element.21), channel_id=1, source_target_pairs={{8,0},{16,8},{24,16},{28,24},{20,28},{12,20},{4,12},{0,4},{9,1},{1... | collective-permute-start | bytes 602120 | tf_op jit(solution)/shard_map/ppermute | solution.py:488
  16.8 14.0 %collective-permute-start.12 = (bf16[1536,128]{1,0:T(8,128)(2,1)S(1)}, bf16[1536,128]{1,0:T(8,128)(2,1)S(1)}, u32[]{:S(2)}, u32[]{:S(2)}) collective-permute-start(bf16[1536,128]{1,0:T(8,128)(2,1)S(1)} %get-tuple-element.18.refs_0_), channel_id=1, source_target_pairs={{0,1},{1,0},{2,3},{3,2},{4,5},{5,4},{6,7},{7,6},{8,9},{9,8},{10,11... | collective-permute-start | bytes 1179656 | tf_op jit(solution)/shard_map/ppermute | solution.py:388
  16.8 7.9 %collective-permute-start.15 = (bf16[784,128]{1,0:T(8,128)(2,1)S(1)}, bf16[784,128]{1,0:T(8,128)(2,1)S(1)}, u32[]{:S(2)}, u32[]{:S(2)}) collective-permute-start(bf16[784,128]{1,0:T(8,128)(2,1)S(1)} %get-tuple-element.19.refs_6_), channel_id=1, source_target_pairs={{0,8},{8,16},{16,24},{24,28},{28,20},{20,12},{12,4},{4,0},{1,9},{9... | collective-permute-start | bytes 602120 | tf_op jit(solution)/shard_map/ppermute | solution.py:487
  17.1 9.2 %collective-permute-start.5 = (bf16[768,128]{1,0:T(8,128)(2,1)S(1)}, bf16[768,128]{1,0:T(8,128)(2,1)S(1)}, u32[]{:S(2)}, u32[]{:S(2)}) collective-permute-start(bf16[768,128]{1,0:T(8,128)(2,1)S(1)} %collective-permute-done.4.refs_8_), channel_id=1, source_target_pairs={{8,0},{16,8},{24,16},{28,24},{20,28},{12,20},{4,12},{0,4},{9,1},{1... | collective-permute-start | bytes 589832 | tf_op jit(solution)/shard_map/ppermute | solution.py:485
  22.9 6.0 %collective-permute-start.1 = (bf16[768,128]{1,0:T(8,128)(2,1)S(1)}, bf16[768,128]{1,0:T(8,128)(2,1)S(1)}, u32[]{:S(2)}, u32[]{:S(2)}) collective-permute-start(bf16[768,128]{1,0:T(8,128)(2,1)S(1)} %collective-permute-done.refs_5_), channel_id=1, source_target_pairs={{0,8},{8,16},{16,24},{24,28},{28,20},{20,12},{12,4},{4,0},{1,9},{9... | collective-permute-start | bytes 589832 | tf_op jit(solution)/shard_map/ppermute | solution.py:484
  24.7 15.9 %collective-permute-start.14 = (bf16[1536,128]{1,0:T(8,128)(2,1)S(1)}, bf16[1536,128]{1,0:T(8,128)(2,1)S(1)}, u32[]{:S(2)}, u32[]{:S(2)}) collective-permute-start(bf16[1536,128]{1,0:T(8,128)(2,1)S(1)} %collective-permute-done.13.refs_2_), channel_id=1, source_target_pairs={{0,1},{1,0},{2,3},{3,2},{4,5},{5,4},{6,7},{7,6},{8,9},{9,8},{10,11... | collective-permute-start | bytes 1179656 | tf_op jit(solution)/shard_map/ppermute | solution.py:388
  24.7 8.3 %collective-permute-start.19 = (bf16[784,128]{1,0:T(8,128)(2,1)S(1)}, bf16[784,128]{1,0:T(8,128)(2,1)S(1)}, u32[]{:S(2)}, u32[]{:S(2)}) collective-permute-start(bf16[784,128]{1,0:T(8,128)(2,1)S(1)} %collective-permute-done.18.refs_7_.refs_12_), channel_id=1, source_target_pairs={{8,0},{16,8},{24,16},{28,24},{20,28},{12,20},{4,12},{0,4},{9,1},{1... | collective-permute-start | bytes 602120 | tf_op jit(solution)/shard_map/ppermute | solution.py:488
  26.3 11.8 %collective-permute-start.16 = (bf16[784,128]{1,0:T(8,128)(2,1)S(1)}, bf16[784,128]{1,0:T(8,128)(2,1)S(1)}, u32[]{:S(2)}, u32[]{:S(2)}) collective-permute-start(bf16[784,128]{1,0:T(8,128)(2,1)S(1)} %collective-permute-done.15.refs_6_.refs_11_), channel_id=1, source_target_pairs={{0,8},{8,16},{16,24},{24,28},{28,20},{20,12},{12,4},{4,0},{1,9},{9... | collective-permute-start | bytes 602120 | tf_op jit(solution)/shard_map/ppermute | solution.py:487
  28.9 9.7 %collective-permute-start.6 = (bf16[768,128]{1,0:T(8,128)(2,1)S(1)}, bf16[768,128]{1,0:T(8,128)(2,1)S(1)}, u32[]{:S(2)}, u32[]{:S(2)}) collective-permute-start(bf16[768,128]{1,0:T(8,128)(2,1)S(1)} %collective-permute-done.5.refs_12_), channel_id=1, source_target_pairs={{8,0},{16,8},{24,16},{28,24},{20,28},{12,20},{4,12},{0,4},{9,1},{1... | collective-permute-start | bytes 589832 | tf_op jit(solution)/shard_map/ppermute | solution.py:485
  30.8 9.3 %collective-permute-start.2 = (bf16[768,128]{1,0:T(8,128)(2,1)S(1)}, bf16[768,128]{1,0:T(8,128)(2,1)S(1)}, u32[]{:S(2)}, u32[]{:S(2)}) collective-permute-start(bf16[768,128]{1,0:T(8,128)(2,1)S(1)} %collective-permute-done.1.refs_9_), channel_id=1, source_target_pairs={{0,8},{8,16},{16,24},{24,28},{28,20},{20,12},{12,4},{4,0},{1,9},{9... | collective-permute-start | bytes 589832 | tf_op jit(solution)/shard_map/ppermute | solution.py:484
  33.0 15.2 %collective-permute-start.11 = (bf16[16,128]{1,0:T(8,128)(2,1)S(1)}, bf16[16,128]{1,0:T(8,128)(2,1)S(1)}, u32[]{:S(2)}, u32[]{:S(2)}) collective-permute-start(bf16[16,128]{1,0:T(8,128)(2,1)S(1)} %get-tuple-element.17.refs_4_.refs_9_), channel_id=1, source_target_pairs={{0,28},{8,20},{16,12},{24,4},{28,0},{20,8},{12,16},{4,24},{1,29},{... | collective-permute-start | bytes 12296 | tf_op jit(solution)/shard_map/ppermute | solution.py:498
  38.1 10.2 %collective-permute-start.20 = (bf16[784,128]{1,0:T(8,128)(2,1)S(1)}, bf16[784,128]{1,0:T(8,128)(2,1)S(1)}, u32[]{:S(2)}, u32[]{:S(2)}) collective-permute-start(bf16[784,128]{1,0:T(8,128)(2,1)S(1)} %collective-permute-done.19.refs_11_.refs_14_), channel_id=1, source_target_pairs={{8,0},{16,8},{24,16},{28,24},{20,28},{12,20},{4,12},{0,4},{9,1},{1... | collective-permute-start | bytes 602120 | tf_op jit(solution)/shard_map/ppermute | solution.py:488
  38.6 9.7 %collective-permute-start.17 = (bf16[784,128]{1,0:T(8,128)(2,1)S(1)}, bf16[784,128]{1,0:T(8,128)(2,1)S(1)}, u32[]{:S(2)}, u32[]{:S(2)}) collective-permute-start(bf16[784,128]{1,0:T(8,128)(2,1)S(1)} %collective-permute-done.16.refs_10_.refs_13_), channel_id=1, source_target_pairs={{0,8},{8,16},{16,24},{24,28},{28,20},{20,12},{12,4},{4,0},{1,9},{9... | collective-permute-start | bytes 602120 | tf_op jit(solution)/shard_map/ppermute | solution.py:487
  40.1 11.3 %collective-permute-start.7 = (bf16[768,128]{1,0:T(8,128)(2,1)S(1)}, bf16[768,128]{1,0:T(8,128)(2,1)S(1)}, u32[]{:S(2)}, u32[]{:S(2)}) collective-permute-start(bf16[768,128]{1,0:T(8,128)(2,1)S(1)} %collective-permute-done.6.refs_8_), channel_id=1, source_target_pairs={{8,0},{16,8},{24,16},{28,24},{20,28},{12,20},{4,12},{0,4},{9,1},{1... | collective-permute-start | bytes 589832 | tf_op jit(solution)/shard_map/ppermute | solution.py:485
  40.6 10.8 %collective-permute-start.3 = (bf16[768,128]{1,0:T(8,128)(2,1)S(1)}, bf16[768,128]{1,0:T(8,128)(2,1)S(1)}, u32[]{:S(2)}, u32[]{:S(2)}) collective-permute-start(bf16[768,128]{1,0:T(8,128)(2,1)S(1)} %collective-permute-done.2.refs_5_), channel_id=1, source_target_pairs={{0,8},{8,16},{16,24},{24,28},{28,20},{20,12},{12,4},{4,0},{1,9},{9... | collective-permute-start | bytes 589832 | tf_op jit(solution)/shard_map/ppermute | solution.py:484

commit v9 on v7

--- a/solution.py
+++ b/solution.py
@@ -52,19 +52,18 @@
     return jnp.concatenate([tile] * (rows // 16), axis=0)
 
 
-def prep_kernel(dims, blocks_ref, full_ref, a_ref, b_ref, sems):
+def prep_kernel(dims, blocks_ref, a_ref, b_ref, sems):
     me = lax.axis_index("cols").astype(jnp.int32)
     span = dims.per_group * dims.bs
     copies = []
     for j in range(dims.groups):
         at = j * span
         ref, start = (a_ref, at) if at < dims.half else (b_ref, at - dims.half)
-        for k, (out_ref, first) in enumerate(((ref, start), (full_ref, at))):
-            copy = pltpu.make_async_copy(
-                blocks_ref.at[pl.ds((me ^ j) * span, span)], out_ref.at[first : first + span], sems.at[j, k]
-            )
-            copy.start()
-            copies.append(copy)
+        copy = pltpu.make_async_copy(
+            blocks_ref.at[pl.ds((me ^ j) * span, span)], ref.at[start : start + span], sems.at[j]
+        )
+        copy.start()
+        copies.append(copy)
     for copy in copies:
         copy.wait()
 
@@ -72,14 +71,16 @@
 def number_kernel(dims, *refs):
     refs = list(refs)
     names = take(refs, dims.groups)
-    a_ref, b_ref, a_out, b_out, tile_ref, cols_ref, sems = refs
+    a_ref, b_ref, full_ref, a_out, b_out, tile_ref, cols_ref, sems = refs
     copies = []
     for j in range(dims.groups):
         copies.append(pltpu.make_async_copy(names[j], cols_ref.at[j], sems.at[j]))
         copies[-1].start()
     half = dims.half
-    for ref, out_ref in ((a_ref, a_out), (b_ref, b_out)):
-        out_ref[0:half, :] = ref[...]
+    for ref, out_ref, at in ((a_ref, a_out, 0), (b_ref, b_out, half)):
+        value = ref[...]
+        out_ref[0:half, :] = value
+        full_ref[at : at + half, :] = value
     me = lax.axis_index("cols").astype(jnp.int32)
     line = lax.broadcasted_iota(jnp.int32, (IDX, 128), 0)
     lane = lax.broadcasted_iota(jnp.int32, (IDX, 128), 1)
@@ -455,20 +456,20 @@
     cols = [jnp.transpose(x, (2, 1, 0)) for x in cols]
     cols[0] = pltpu.with_memory_space_constraint(cols[0], pltpu.HBM)
     flat_blocks = pltpu.with_memory_space_constraint(blocks.reshape(-1, bs), pltpu.HBM)
-    own, bare_a, bare_b = pl.pallas_call(
+    bare_a, bare_b = pl.pallas_call(
         functools.partial(prep_kernel, dims),
-        out_shape=[payload(2 * dims.half)] + [payload(dims.half)] * 2,
+        out_shape=[payload(dims.half)] * 2,
         in_specs=[ANY],
-        out_specs=[VMEM] * 3,
-        scratch_shapes=[pltpu.SemaphoreType.DMA((groups, 2))],
+        out_specs=[VMEM] * 2,
+        scratch_shapes=[pltpu.SemaphoreType.DMA((groups,))],
         compiler_params=params,
         name="prep",
     )(flat_blocks)
-    own_a, own_b, tile = pl.pallas_call(
+    own, own_a, own_b, tile = pl.pallas_call(
         functools.partial(number_kernel, dims),
-        out_shape=[payload(dims.half + IDX)] * 2 + [payload(IDX)],
+        out_shape=[payload(2 * dims.half)] + [payload(dims.half + IDX)] * 2 + [payload(IDX)],
         in_specs=[ANY] * groups + [VMEM] * 2,
-        out_specs=[VMEM] * 3,
+        out_specs=[VMEM] * 4,
         scratch_shapes=[
             pltpu.SMEM((groups, per_group, 1, groups), jnp.int32),
             pltpu.SemaphoreType.DMA((groups,)),

time: 54.1 us -> 52.3 us (0.967)
  starting transfers between devices: 26.9 us -> 24.5 us
  waiting for transfers between devices: 10.3 us -> 11.2 us
    ppermute x4, waiting for transfers between devices: 0.38 us -> 3.78 us  [on_device(): qb.append(lax.ppermute(qb[-1], 'rows', down))]
    ppermute x6, waiting for transfers between devices: 5.02 us -> 2.67 us  [xor_move(): lax.ppermute(value, axis, [(i, i ^ bit) for i in range(lax.axis_size(axis...]
    ppermute x6, starting transfers between devices: 5.18 us -> 3.34 us  [xor_move(): lax.ppermute(value, axis, [(i, i ^ bit) for i in range(lax.axis_size(axis...]
    ppermute x3, waiting for transfers between devices: 4.06 us -> 2.68 us  [on_device(): qa.append(lax.ppermute(qa[-1], 'rows', down))]
    ppermute x3, waiting for transfers between devices: 0.01 us -> 1.11 us  [on_device(): pb.append(lax.ppermute(pb[-1], 'rows', up))]
    ppermute x3, starting transfers between devices: 3.53 us -> 4.6 us  [on_device(): qa.append(lax.ppermute(qa[-1], 'rows', down))]
    ppermute x4, starting transfers between devices: 5.71 us -> 5.05 us  [on_device(): qb.append(lax.ppermute(qb[-1], 'rows', down))]
    ppermute x4, starting transfers between devices: 3.97 us -> 3.42 us  [on_device(): pa.append(lax.ppermute(pa[-1], 'rows', up))]
  transfers between devices with their start and end apart: 21 -> 21, of which waited for: 5 -> 7; matrix products, arithmetic and copies ran while one was open for 0% -> 0% of each run, Pallas kernels for 22% -> 23%
where the time goes in v9:
time: 52.3 us; the launch traced here: 52.1 us
  starting transfers between devices  24.5 us (47%)
  Pallas kernels  15.6 us (30%)
  waiting for transfers between devices  11.2 us (21%)
  between operations  0.74 us (1%)
    pallas_call x3, Pallas kernels, call_step(): pl.pallas_call(functools.partial(step_kernel, dims, layout, acc is not No...  9.02 us
    ppermute x4, starting transfers between devices, on_device(): qb.append(lax.ppermute(qb[-1], 'rows', down))  5.05 us
    ppermute x1, starting transfers between devices, on_device(): lax.ppermute(tile, 'rows', [(a, dict(up)[dict(up)[dict(up)[b]]]) for a, b...  4.67 us
    ppermute x3, starting transfers between devices, on_device(): qa.append(lax.ppermute(qa[-1], 'rows', down))  4.6 us
    ppermute x4, waiting for transfers between devices, on_device(): qb.append(lax.ppermute(qb[-1], 'rows', down))  3.78 us
    ppermute x3, starting transfers between devices, on_device(): pb.append(lax.ppermute(pb[-1], 'rows', up))  3.45 us
    ppermute x4, starting transfers between devices, on_device(): pa.append(lax.ppermute(pa[-1], 'rows', up))  3.42 us
    ppermute x6, starting transfers between devices, xor_move(): lax.ppermute(value, axis, [(i, i ^ bit) for i in range(lax.axis_size(axis...  3.34 us
  transfers between devices with their start and end apart: 21, of which 7 were waited for; matrix products, arithmetic and copies ran while one was open for 0% of the time, Pallas kernels for 23%

profile of v9, /device:TPU:0, one launch (start us, length us, event | category | flops | bytes accessed | tf_op | source)
XLA Modules:
  0.0 52.1 jit_solution(8228471829564905304)
XLA Ops:
  0.6 0.6 %collective-permute-start.8 = (s32[4,1,3]{0,1,2:T(1,128)}, s32[4,1,3]{0,1,2:T(1,128)S(1)}, u32[]{:S(2)}, u32[]{:S(2)}) collective-permute-start(s32[4,1,3]{0,1,2:T(1,128)} %param.3), channel_id=1, source_target_pairs={{0,1},{1,0},{2,3},{3,2},{4,5},{5,4},{6,7},{7,6},{8,9},{9,8},{10,11... | collective-permute-start | bytes 152 | tf_op jit(solution)/shard_map/ppermute | solution.py:389
  1.2 2.6 %collective-permute-start.10 = (s32[4,1,3]{0,1,2:T(1,128)}, s32[4,1,3]{0,1,2:T(1,128)S(1)}, u32[]{:S(2)}, u32[]{:S(2)}) collective-permute-start(s32[4,1,3]{0,1,2:T(1,128)} %param.3), channel_id=1, source_target_pairs={{0,3},{1,2},{2,1},{3,0},{4,7},{5,6},{6,5},{7,4},{8,11},{9,10},{10,... | collective-permute-start | bytes 152 | tf_op jit(solution)/shard_map/ppermute | solution.py:389
  3.8 0.0 collective-permute-start.9
  3.8 1.1 %prep.1 = (bf16[768,128]{1,0:T(8,128)(2,1)S(1)}, bf16[768,128]{1,0:T(8,128)(2,1)S(1)}) custom-call(bf16[1536,128]{1,0:T(8,128)(2,1)} %bitcast.13), custom_call_target="tpu_custom_call" | custom-call | tf_op jit(solution)/shard_map/prep/pallas_call | solution.py:459
  4.9 0.0 collective-permute-done.8
  4.9 0.4 collective-permute-done.10
  5.3 2.3 %collective-permute-done.9 = s32[4,1,3]{0,1,2:T(1,128)S(1)} collective-permute-done((s32[4,1,3]{0,1,2:T(1,128)}, s32[4,1,3]{0,1,2:T(1,128)S(1)}, u32[]{:S(2)}, u32[]{:S(2)}) %collective-permute-start.9) | collective-permute-done | bytes 80 | tf_op jit(solution)/shard_map/ppermute | solution.py:389
  7.6 0.8 %numbers.1 = (bf16[1536,128]{1,0:T(8,128)(2,1)S(1)}, bf16[784,128]{1,0:T(8,128)(2,1)S(1)}, bf16[784,128]{1,0:T(8,128)(2,1)S(1)}, bf16[16,128]{1,0:T(8,128)(2,1)S(1)}) custom-call(s32[3,1,4]{2,1,0:T(1,128)} %bitcast.14, s32[3,1,4]{2,1,0:T(1,128)S(1)} %bitcast.9, s32[3,1,4]{2,1,0:T(1,128)S(1)} %bitcast.11, s32[3,1,4]{2,1,0:T(1,128)S(1)} %bitcast.10, ...), custom_call_target="tpu_custom_call" | custom-call | tf_op jit(solution)/shard_map/numbers/pallas_call | solution.py:468
  8.4 0.1 collective-permute-start.13
  8.5 2.0 %collective-permute-start.4 = (bf16[768,128]{1,0:T(8,128)(2,1)S(1)}, bf16[768,128]{1,0:T(8,128)(2,1)S(1)}, u32[]{:S(2)}, u32[]{:S(2)}) collective-permute-start(bf16[768,128]{1,0:T(8,128)(2,1)S(1)} %get-tuple-element.16.refs_5_), channel_id=1, source_target_pairs={{8,0},{16,8},{24,16},{28,24},{20,28},{12,20},{4,12},{0,4},{9,1},{1... | collective-permute-start | bytes 589832 | tf_op jit(solution)/shard_map/ppermute | solution.py:486
  10.5 0.1 collective-permute-start
  10.6 2.0 %collective-permute-start.16 = (bf16[784,128]{1,0:T(8,128)(2,1)S(1)}, bf16[784,128]{1,0:T(8,128)(2,1)S(1)}, u32[]{:S(2)}, u32[]{:S(2)}) collective-permute-start(bf16[784,128]{1,0:T(8,128)(2,1)S(1)} %get-tuple-element.20), channel_id=1, source_target_pairs={{8,0},{16,8},{24,16},{28,24},{20,28},{12,20},{4,12},{0,4},{9,1},{1... | collective-permute-start | bytes 602120 | tf_op jit(solution)/shard_map/ppermute | solution.py:489
  12.5 0.0 collective-permute-start.12
  12.5 3.8 %collective-permute-done.4.refs_10_ = bf16[768,128]{1,0:T(8,128)(2,1)S(1)} collective-permute-done((bf16[768,128]{1,0:T(8,128)(2,1)S(1)}, bf16[768,128]{1,0:T(8,128)(2,1)S(1)}, u32[]{:S(2)}, u32[]{:S(2)}) %collective-permute-start.4) | collective-permute-done | bytes 196640 | tf_op jit(solution)/shard_map/ppermute | solution.py:486
  16.3 2.0 %collective-permute-start.15 = (bf16[784,128]{1,0:T(8,128)(2,1)S(1)}, bf16[784,128]{1,0:T(8,128)(2,1)S(1)}, u32[]{:S(2)}, u32[]{:S(2)}) collective-permute-start(bf16[784,128]{1,0:T(8,128)(2,1)S(1)} %get-tuple-element.19.refs_6_), channel_id=1, source_target_pairs={{0,8},{8,16},{16,24},{24,28},{28,20},{20,12},{12,4},{4,0},{1,9},{9... | collective-permute-start | bytes 602120 | tf_op jit(solution)/shard_map/ppermute | solution.py:488
  18.3 0.0 collective-permute-done.refs_7_
  18.3 0.0 collective-permute-start.5
  18.4 2.3 %collective-permute-done.16.refs_9_.refs_12_ = bf16[784,128]{1,0:T(8,128)(2,1)S(1)} collective-permute-done((bf16[784,128]{1,0:T(8,128)(2,1)S(1)}, bf16[784,128]{1,0:T(8,128)(2,1)S(1)}, u32[]{:S(2)}, u32[]{:S(2)}) %collective-permute-start.16) | collective-permute-done | bytes 200736 | tf_op jit(solution)/shard_map/ppermute | solution.py:489
  20.6 2.0 %collective-permute-start.1 = (bf16[768,128]{1,0:T(8,128)(2,1)S(1)}, bf16[768,128]{1,0:T(8,128)(2,1)S(1)}, u32[]{:S(2)}, u32[]{:S(2)}) collective-permute-start(bf16[768,128]{1,0:T(8,128)(2,1)S(1)} %collective-permute-done.refs_7_), channel_id=1, source_target_pairs={{0,8},{8,16},{16,24},{24,28},{28,20},{20,12},{12,4},{4,0},{1,9},{9... | collective-permute-start | bytes 589832 | tf_op jit(solution)/shard_map/ppermute | solution.py:485
  22.6 0.0 collective-permute-done.13.refs_2_
  22.6 0.0 collective-permute-start.14
  22.7 1.1 %collective-permute-done.15.refs_8_.refs_11_ = bf16[784,128]{1,0:T(8,128)(2,1)S(1)} collective-permute-done((bf16[784,128]{1,0:T(8,128)(2,1)S(1)}, bf16[784,128]{1,0:T(8,128)(2,1)S(1)}, u32[]{:S(2)}, u32[]{:S(2)}) %collective-permute-start.15) | collective-permute-done | bytes 200736 | tf_op jit(solution)/shard_map/ppermute | solution.py:488
  23.8 1.9 %collective-permute-start.19 = (bf16[784,128]{1,0:T(8,128)(2,1)S(1)}, bf16[784,128]{1,0:T(8,128)(2,1)S(1)}, u32[]{:S(2)}, u32[]{:S(2)}) collective-permute-start(bf16[784,128]{1,0:T(8,128)(2,1)S(1)} %collective-permute-done.16.refs_9_.refs_12_), channel_id=1, source_target_pairs={{8,0},{16,8},{24,16},{28,24},{20,28},{12,20},{4,12},{0,4},{9,1},{1... | collective-permute-start | bytes 602120 | tf_op jit(solution)/shard_map/ppermute | solution.py:489
  25.6 0.0 collective-permute-done.5.refs_8_
  25.6 0.1 collective-permute-start.17
  25.8 1.0 %collective-permute-done.1.refs_5_ = bf16[768,128]{1,0:T(8,128)(2,1)S(1)} collective-permute-done((bf16[768,128]{1,0:T(8,128)(2,1)S(1)}, bf16[768,128]{1,0:T(8,128)(2,1)S(1)}, u32[]{:S(2)}, u32[]{:S(2)}) %collective-permute-start.1) | collective-permute-done | bytes 196640 | tf_op jit(solution)/shard_map/ppermute | solution.py:485
  26.8 2.3 %collective-permute-start.6 = (bf16[768,128]{1,0:T(8,128)(2,1)S(1)}, bf16[768,128]{1,0:T(8,128)(2,1)S(1)}, u32[]{:S(2)}, u32[]{:S(2)}) collective-permute-start(bf16[768,128]{1,0:T(8,128)(2,1)S(1)} %collective-permute-done.5.refs_8_), channel_id=1, source_target_pairs={{8,0},{16,8},{24,16},{28,24},{20,28},{12,20},{4,12},{0,4},{9,1},{1... | collective-permute-start | bytes 589832 | tf_op jit(solution)/shard_map/ppermute | solution.py:486
  29.1 0.0 collective-permute-done.12.refs_1_
  29.1 0.1 collective-permute-start.2
  29.1 2.1 %zero.1.refs_6_ = bf16[4,36,128,128]{3,2,1,0:T(8,128)(2,1)} custom-call(), custom_call_target="tpu_custom_call" | custom-call | tf_op jit(solution)/shard_map/zero/pallas_call | solution.py:318
  31.2 0.4 collective-permute-done.19.refs_7_.refs_14_
  31.6 4.7 %collective-permute-start.11 = (bf16[16,128]{1,0:T(8,128)(2,1)S(1)}, bf16[16,128]{1,0:T(8,128)(2,1)S(1)}, u32[]{:S(2)}, u32[]{:S(2)}) collective-permute-start(bf16[16,128]{1,0:T(8,128)(2,1)S(1)} %get-tuple-element.17.refs_4_.refs_9_), channel_id=1, source_target_pairs={{0,28},{8,20},{16,12},{24,4},{28,0},{20,8},{12,16},{4,24},{1,29},{... | collective-permute-start | bytes 12296 | tf_op jit(solution)/shard_map/ppermute | solution.py:499
  36.3 0.0 collective-permute-done.17.refs_6_.refs_13_
  36.3 0.8 %collective-permute-start.20 = (bf16[784,128]{1,0:T(8,128)(2,1)S(1)}, bf16[784,128]{1,0:T(8,128)(2,1)S(1)}, u32[]{:S(2)}, u32[]{:S(2)}) collective-permute-start(bf16[784,128]{1,0:T(8,128)(2,1)S(1)} %collective-permute-done.19.refs_7_.refs_14_), channel_id=1, source_target_pairs={{8,0},{16,8},{24,16},{28,24},{20,28},{12,20},{4,12},{0,4},{9,1},{1... | collective-permute-start | bytes 602120 | tf_op jit(solution)/shard_map/ppermute | solution.py:489
  37.0 0.0 collective-permute-done.6.refs_8_
  37.0 1.3 %collective-permute-start.18 = (bf16[784,128]{1,0:T(8,128)(2,1)S(1)}, bf16[784,128]{1,0:T(8,128)(2,1)S(1)}, u32[]{:S(2)}, u32[]{:S(2)}) collective-permute-start(bf16[784,128]{1,0:T(8,128)(2,1)S(1)} %collective-permute-done.17.refs_6_.refs_13_), channel_id=1, source_target_pairs={{0,8},{8,16},{16,24},{24,28},{28,20},{20,12},{12,4},{4,0},{1,9},{9... | collective-permute-start | bytes 602120 | tf_op jit(solution)/shard_map/ppermute | solution.py:488
  38.3 0.0 collective-permute-done.2.refs_5_
  38.3 0.8 %collective-permute-start.7 = (bf16[768,128]{1,0:T(8,128)(2,1)S(1)}, bf16[768,128]{1,0:T(8,128)(2,1)S(1)}, u32[]{:S(2)}, u32[]{:S(2)}) collective-permute-start(bf16[768,128]{1,0:T(8,128)(2,1)S(1)} %collective-permute-done.6.refs_8_), channel_id=1, source_target_pairs={{8,0},{16,8},{24,16},{28,24},{20,28},{12,20},{4,12},{0,4},{9,1},{1... | collective-permute-start | bytes 589832 | tf_op jit(solution)/shard_map/ppermute | solution.py:486
  39.1 0.0 collective-permute-done.14.refs_3_
  39.1 1.3 %collective-permute-start.3 = (bf16[768,128]{1,0:T(8,128)(2,1)S(1)}, bf16[768,128]{1,0:T(8,128)(2,1)S(1)}, u32[]{:S(2)}, u32[]{:S(2)}) collective-permute-start(bf16[768,128]{1,0:T(8,128)(2,1)S(1)} %collective-permute-done.2.refs_5_), channel_id=1, source_target_pairs={{0,8},{8,16},{16,24},{24,28},{28,20},{20,12},{12,4},{4,0},{1,9},{9... | collective-permute-start | bytes 589832 | tf_op jit(solution)/shard_map/ppermute | solution.py:485
  40.4 3.2 %shard_map.49 = (f32[512,1024]{1,0:T(8,128)S(1)}, bf16[512,512]{1,0:T(8,128)(2,1)S(1)}) custom-call(bf16[1536,128]{1,0:T(8,128)(2,1)S(1)} %get-tuple-element.18.refs_0_, bf16[1536,128]{1,0:T(8,128)(2,1)S(1)} %collective-permute-done.12.refs_1_, bf16[1536,128]{1,0:T(8,128)(2,1)S(1)} %collective-permute-done.13.refs_2_, ...), custom_call_target="tpu_custom_call" | custom-call | flops 1610612736 | bytes 4000000 | tf_op jit(solution)/shard_map/pallas_call | solution.py:355
  43.6 2.7 %shard_map.50.refs_17_ = f32[512,1024]{1,0:T(8,128)S(1)} custom-call(bf16[1536,128]{1,0:T(8,128)(2,1)S(1)} %get-tuple-element.18.refs_0_, bf16[1536,128]{1,0:T(8,128)(2,1)S(1)} %collective-permute-done.12.refs_1_, bf16[1536,128]{1,0:T(8,128)(2,1)S(1)} %collective-permute-done.13.refs_2_, ...), custom_call_target="tpu_custom_call", output_to_operand_aliasing={{}: (9, {})} | custom-call | flops 1073741824 | bytes 4000000 | tf_op jit(solution)/shard_map/pallas_call | solution.py:355
  46.2 0.0 collective-permute-done.11.refs_10_.refs_2_
  46.3 0.0 collective-permute-done.20.refs_7_.refs_16_
  46.3 0.0 collective-permute-done.18.refs_6_.refs_15_
  46.3 3.2 %shard_map.51 = (f32[512,1024]{1,0:T(8,128)S(1)}, s32[32]{0:T(128)S(1)}, s32[4,1,36]{2,1,0:T(1,128)}, s32[1,4]{1,0:T(1,128)}) custom-call(bf16[1536,128]{1,0:T(8,128)(2,1)S(1)} %get-tuple-element.18.refs_0_, bf16[1536,128]{1,0:T(8,128)(2,1)S(1)} %collective-permute-done.12.refs_1_, ...), custom_call_target="tpu_custom_call", output_to_operand_aliasing={{0}: (17, {})} | custom-call | flops 1073741824 | bytes 4000000 | tf_op jit(solution)/shard_map/pallas_call | solution.py:355
  49.4 0.0 collective-permute-done.3.refs_0_
  49.5 2.6 %shard_map.52 = bf16[4,36,128,128]{3,2,1,0:T(8,128)(2,1)} custom-call(bf16[768,128]{1,0:T(8,128)(2,1)S(1)} %collective-permute-done.3.refs_0_, bf16[768,128]{1,0:T(8,128)(2,1)S(1)} %collective-permute-done.7.refs_1_, bf16[16,128]{1,0:T(8,128)(2,1)S(1)} %collective-permute-done.11.refs_10_.refs_2_, ...), custom_call_target="tpu_custom_call", output_to_operand_aliasing={{}: (6, {})} | custom-call | flops 536870912 | bytes 4000000 | tf_op jit(solution)/shard_map/pallas_call | solution.py:370
  (1 shorter events, 0.0 us)
Async XLA Ops:
  0.6 4.3 %collective-permute-start.8 = (s32[4,1,3]{0,1,2:T(1,128)}, s32[4,1,3]{0,1,2:T(1,128)S(1)}, u32[]{:S(2)}, u32[]{:S(2)}) collective-permute-start(s32[4,1,3]{0,1,2:T(1,128)} %param.3), channel_id=1, source_target_pairs={{0,1},{1,0},{2,3},{3,2},{4,5},{5,4},{6,7},{7,6},{8,9},{9,8},{10,11... | collective-permute-start | bytes 152 | tf_op jit(solution)/shard_map/ppermute | solution.py:389
  1.2 4.1 %collective-permute-start.10 = (s32[4,1,3]{0,1,2:T(1,128)}, s32[4,1,3]{0,1,2:T(1,128)S(1)}, u32[]{:S(2)}, u32[]{:S(2)}) collective-permute-start(s32[4,1,3]{0,1,2:T(1,128)} %param.3), channel_id=1, source_target_pairs={{0,3},{1,2},{2,1},{3,0},{4,7},{5,6},{6,5},{7,4},{8,11},{9,10},{10,... | collective-permute-start | bytes 152 | tf_op jit(solution)/shard_map/ppermute | solution.py:389
  3.8 3.8 %collective-permute-start.9 = (s32[4,1,3]{0,1,2:T(1,128)}, s32[4,1,3]{0,1,2:T(1,128)S(1)}, u32[]{:S(2)}, u32[]{:S(2)}) collective-permute-start(s32[4,1,3]{0,1,2:T(1,128)} %param.3), channel_id=1, source_target_pairs={{0,2},{1,3},{2,0},{3,1},{4,6},{5,7},{6,4},{7,5},{8,10},{9,11},{10,... | collective-permute-start | bytes 152 | tf_op jit(solution)/shard_map/ppermute | solution.py:389
  8.4 14.3 %collective-permute-start.13 = (bf16[1536,128]{1,0:T(8,128)(2,1)S(1)}, bf16[1536,128]{1,0:T(8,128)(2,1)S(1)}, u32[]{:S(2)}, u32[]{:S(2)}) collective-permute-start(bf16[1536,128]{1,0:T(8,128)(2,1)S(1)} %get-tuple-element.18.refs_0_), channel_id=1, source_target_pairs={{0,2},{1,3},{2,0},{3,1},{4,6},{5,7},{6,4},{7,5},{8,10},{9,11},{10,... | collective-permute-start | bytes 1179656 | tf_op jit(solution)/shard_map/ppermute | solution.py:389
  8.5 7.8 %collective-permute-start.4 = (bf16[768,128]{1,0:T(8,128)(2,1)S(1)}, bf16[768,128]{1,0:T(8,128)(2,1)S(1)}, u32[]{:S(2)}, u32[]{:S(2)}) collective-permute-start(bf16[768,128]{1,0:T(8,128)(2,1)S(1)} %get-tuple-element.16.refs_5_), channel_id=1, source_target_pairs={{8,0},{16,8},{24,16},{28,24},{20,28},{12,20},{4,12},{0,4},{9,1},{1... | collective-permute-start | bytes 589832 | tf_op jit(solution)/shard_map/ppermute | solution.py:486
  10.5 7.8 %collective-permute-start = (bf16[768,128]{1,0:T(8,128)(2,1)S(1)}, bf16[768,128]{1,0:T(8,128)(2,1)S(1)}, u32[]{:S(2)}, u32[]{:S(2)}) collective-permute-start(bf16[768,128]{1,0:T(8,128)(2,1)S(1)} %get-tuple-element.15.refs_4_.refs_5_), channel_id=1, source_target_pairs={{0,8},{8,16},{16,24},{24,28},{28,20},{20,12},{12,4},{4,0},{1,9},{9... | collective-permute-start | bytes 589832 | tf_op jit(solution)/shard_map/ppermute | solution.py:485
  10.6 10.0 %collective-permute-start.16 = (bf16[784,128]{1,0:T(8,128)(2,1)S(1)}, bf16[784,128]{1,0:T(8,128)(2,1)S(1)}, u32[]{:S(2)}, u32[]{:S(2)}) collective-permute-start(bf16[784,128]{1,0:T(8,128)(2,1)S(1)} %get-tuple-element.20), channel_id=1, source_target_pairs={{8,0},{16,8},{24,16},{28,24},{20,28},{12,20},{4,12},{0,4},{9,1},{1... | collective-permute-start | bytes 602120 | tf_op jit(solution)/shard_map/ppermute | solution.py:489
  12.5 16.5 %collective-permute-start.12 = (bf16[1536,128]{1,0:T(8,128)(2,1)S(1)}, bf16[1536,128]{1,0:T(8,128)(2,1)S(1)}, u32[]{:S(2)}, u32[]{:S(2)}) collective-permute-start(bf16[1536,128]{1,0:T(8,128)(2,1)S(1)} %get-tuple-element.18.refs_0_), channel_id=1, source_target_pairs={{0,1},{1,0},{2,3},{3,2},{4,5},{5,4},{6,7},{7,6},{8,9},{9,8},{10,11... | collective-permute-start | bytes 1179656 | tf_op jit(solution)/shard_map/ppermute | solution.py:389
  16.3 7.4 %collective-permute-start.15 = (bf16[784,128]{1,0:T(8,128)(2,1)S(1)}, bf16[784,128]{1,0:T(8,128)(2,1)S(1)}, u32[]{:S(2)}, u32[]{:S(2)}) collective-permute-start(bf16[784,128]{1,0:T(8,128)(2,1)S(1)} %get-tuple-element.19.refs_6_), channel_id=1, source_target_pairs={{0,8},{8,16},{16,24},{24,28},{28,20},{20,12},{12,4},{4,0},{1,9},{9... | collective-permute-start | bytes 602120 | tf_op jit(solution)/shard_map/ppermute | solution.py:488
  18.3 7.3 %collective-permute-start.5 = (bf16[768,128]{1,0:T(8,128)(2,1)S(1)}, bf16[768,128]{1,0:T(8,128)(2,1)S(1)}, u32[]{:S(2)}, u32[]{:S(2)}) collective-permute-start(bf16[768,128]{1,0:T(8,128)(2,1)S(1)} %collective-permute-done.4.refs_10_), channel_id=1, source_target_pairs={{8,0},{16,8},{24,16},{28,24},{20,28},{12,20},{4,12},{0,4},{9,1},{1... | collective-permute-start | bytes 589832 | tf_op jit(solution)/shard_map/ppermute | solution.py:486
  20.6 6.1 %collective-permute-start.1 = (bf16[768,128]{1,0:T(8,128)(2,1)S(1)}, bf16[768,128]{1,0:T(8,128)(2,1)S(1)}, u32[]{:S(2)}, u32[]{:S(2)}) collective-permute-start(bf16[768,128]{1,0:T(8,128)(2,1)S(1)} %collective-permute-done.refs_7_), channel_id=1, source_target_pairs={{0,8},{8,16},{16,24},{24,28},{28,20},{20,12},{12,4},{4,0},{1,9},{9... | collective-permute-start | bytes 589832 | tf_op jit(solution)/shard_map/ppermute | solution.py:485
  22.6 16.4 %collective-permute-start.14 = (bf16[1536,128]{1,0:T(8,128)(2,1)S(1)}, bf16[1536,128]{1,0:T(8,128)(2,1)S(1)}, u32[]{:S(2)}, u32[]{:S(2)}) collective-permute-start(bf16[1536,128]{1,0:T(8,128)(2,1)S(1)} %collective-permute-done.13.refs_2_), channel_id=1, source_target_pairs={{0,1},{1,0},{2,3},{3,2},{4,5},{5,4},{6,7},{7,6},{8,9},{9,8},{10,11... | collective-permute-start | bytes 1179656 | tf_op jit(solution)/shard_map/ppermute | solution.py:389
  23.8 7.9 %collective-permute-start.19 = (bf16[784,128]{1,0:T(8,128)(2,1)S(1)}, bf16[784,128]{1,0:T(8,128)(2,1)S(1)}, u32[]{:S(2)}, u32[]{:S(2)}) collective-permute-start(bf16[784,128]{1,0:T(8,128)(2,1)S(1)} %collective-permute-done.16.refs_9_.refs_12_), channel_id=1, source_target_pairs={{8,0},{16,8},{24,16},{28,24},{20,28},{12,20},{4,12},{0,4},{9,1},{1... | collective-permute-start | bytes 602120 | tf_op jit(solution)/shard_map/ppermute | solution.py:489
  25.6 10.7 %collective-permute-start.17 = (bf16[784,128]{1,0:T(8,128)(2,1)S(1)}, bf16[784,128]{1,0:T(8,128)(2,1)S(1)}, u32[]{:S(2)}, u32[]{:S(2)}) collective-permute-start(bf16[784,128]{1,0:T(8,128)(2,1)S(1)} %collective-permute-done.15.refs_8_.refs_11_), channel_id=1, source_target_pairs={{0,8},{8,16},{16,24},{24,28},{28,20},{20,12},{12,4},{4,0},{1,9},{9... | collective-permute-start | bytes 602120 | tf_op jit(solution)/shard_map/ppermute | solution.py:488
  26.8 10.3 %collective-permute-start.6 = (bf16[768,128]{1,0:T(8,128)(2,1)S(1)}, bf16[768,128]{1,0:T(8,128)(2,1)S(1)}, u32[]{:S(2)}, u32[]{:S(2)}) collective-permute-start(bf16[768,128]{1,0:T(8,128)(2,1)S(1)} %collective-permute-done.5.refs_8_), channel_id=1, source_target_pairs={{8,0},{16,8},{24,16},{28,24},{20,28},{12,20},{4,12},{0,4},{9,1},{1... | collective-permute-start | bytes 589832 | tf_op jit(solution)/shard_map/ppermute | solution.py:486
  29.1 9.3 %collective-permute-start.2 = (bf16[768,128]{1,0:T(8,128)(2,1)S(1)}, bf16[768,128]{1,0:T(8,128)(2,1)S(1)}, u32[]{:S(2)}, u32[]{:S(2)}) collective-permute-start(bf16[768,128]{1,0:T(8,128)(2,1)S(1)} %collective-permute-done.1.refs_5_), channel_id=1, source_target_pairs={{0,8},{8,16},{16,24},{24,28},{28,20},{20,12},{12,4},{4,0},{1,9},{9... | collective-permute-start | bytes 589832 | tf_op jit(solution)/shard_map/ppermute | solution.py:485
  31.6 14.6 %collective-permute-start.11 = (bf16[16,128]{1,0:T(8,128)(2,1)S(1)}, bf16[16,128]{1,0:T(8,128)(2,1)S(1)}, u32[]{:S(2)}, u32[]{:S(2)}) collective-permute-start(bf16[16,128]{1,0:T(8,128)(2,1)S(1)} %get-tuple-element.17.refs_4_.refs_9_), channel_id=1, source_target_pairs={{0,28},{8,20},{16,12},{24,4},{28,0},{20,8},{12,16},{4,24},{1,29},{... | collective-permute-start | bytes 12296 | tf_op jit(solution)/shard_map/ppermute | solution.py:499
  36.3 10.0 %collective-permute-start.20 = (bf16[784,128]{1,0:T(8,128)(2,1)S(1)}, bf16[784,128]{1,0:T(8,128)(2,1)S(1)}, u32[]{:S(2)}, u32[]{:S(2)}) collective-permute-start(bf16[784,128]{1,0:T(8,128)(2,1)S(1)} %collective-permute-done.19.refs_7_.refs_14_), channel_id=1, source_target_pairs={{8,0},{16,8},{24,16},{28,24},{20,28},{12,20},{4,12},{0,4},{9,1},{1... | collective-permute-start | bytes 602120 | tf_op jit(solution)/shard_map/ppermute | solution.py:489
  37.0 9.2 %collective-permute-start.18 = (bf16[784,128]{1,0:T(8,128)(2,1)S(1)}, bf16[784,128]{1,0:T(8,128)(2,1)S(1)}, u32[]{:S(2)}, u32[]{:S(2)}) collective-permute-start(bf16[784,128]{1,0:T(8,128)(2,1)S(1)} %collective-permute-done.17.refs_6_.refs_13_), channel_id=1, source_target_pairs={{0,8},{8,16},{16,24},{24,28},{28,20},{20,12},{12,4},{4,0},{1,9},{9... | collective-permute-start | bytes 602120 | tf_op jit(solution)/shard_map/ppermute | solution.py:488
  38.3 11.1 %collective-permute-start.7 = (bf16[768,128]{1,0:T(8,128)(2,1)S(1)}, bf16[768,128]{1,0:T(8,128)(2,1)S(1)}, u32[]{:S(2)}, u32[]{:S(2)}) collective-permute-start(bf16[768,128]{1,0:T(8,128)(2,1)S(1)} %collective-permute-done.6.refs_8_), channel_id=1, source_target_pairs={{8,0},{16,8},{24,16},{28,24},{20,28},{12,20},{4,12},{0,4},{9,1},{1... | collective-permute-start | bytes 589832 | tf_op jit(solution)/shard_map/ppermute | solution.py:486
  39.1 10.4 %collective-permute-start.3 = (bf16[768,128]{1,0:T(8,128)(2,1)S(1)}, bf16[768,128]{1,0:T(8,128)(2,1)S(1)}, u32[]{:S(2)}, u32[]{:S(2)}) collective-permute-start(bf16[768,128]{1,0:T(8,128)(2,1)S(1)} %collective-permute-done.2.refs_5_), channel_id=1, source_target_pairs={{0,8},{8,16},{16,24},{24,28},{28,20},{20,12},{12,4},{4,0},{1,9},{9... | collective-permute-start | bytes 589832 | tf_op jit(solution)/shard_map/ppermute | solution.py:485
